TPU v7x, 32 devices: a whole 2x2x4 slice. The times are simulated.
32 devices in a mesh: dp: 8 (over z, x), mp: 4 (over y, core).
Axes of the slice: x: 2, y: 2, z: 4, core: 2. Of those that a mesh axis runs over, the one named last changes fastest.
Arguments:
- tokens: bfloat16 [32768, 1024], P(('dp', 'mp')), may hold values from -6 to 6
- segment_ids: int32 [32, 1024], P('dp'), may hold values from 0 to 7, never falling along the last dimension, each value on 1 to 512 neighbouring positions
- time_steps: int32 [32], P('dp'), may hold values from 0 to 999
- w_qkv: bfloat16 [1024, 3, 1024], P(None, None, 'mp'), may hold values from -0.1875 to 0.1875
- b_qv: bfloat16 [2, 1024], P(None, 'mp'), may hold values from -1.796875 to 1.796875
- w_out: bfloat16 [1024, 1024], P('mp'), may hold values from -0.75 to 0.75
- b_out: bfloat16 [1024], replicated, may hold values from -1.796875 to 1.796875
- gain_one: bfloat16 [1024], replicated, may hold values from 0.5 to 1.5
- shift_one: bfloat16 [1024], replicated, may hold values from -1.796875 to 1.796875
- w_up: bfloat16 [1024, 4096], P(None, 'mp'), may hold values from -0.1875 to 0.1875
- b_up: bfloat16 [4096], P('mp'), may hold values from -1.796875 to 1.796875
- w_down: bfloat16 [4096, 1024], P('mp'), may hold values from -0.09375 to 0.09375
- b_down: bfloat16 [1024], replicated, may hold values from -1.796875 to 1.796875
- gain_two: bfloat16 [1024], replicated, may hold values from 0.5 to 1.5
- shift_two: bfloat16 [1024], replicated, may hold values from -1.796875 to 1.796875
- w_time: bfloat16 [1024, 1024], replicated, may hold values from -0.1875 to 0.1875
- b_time: bfloat16 [1024], replicated, may hold values from -1.796875 to 1.796875
- cotangent: bfloat16 [32768, 1024], P(('dp', 'mp')), may hold values from -6 to 6
Outputs:
- out_rows: bfloat16 [32768, 1024], P(('dp', 'mp'))
- grad_tokens: float32 [32768, 1024], P(('dp', 'mp'))
- grad_w_qkv: float32 [1024, 3, 1024], P('dp', None, 'mp')
- grad_b_qv: float32 [2, 4, 256], P(None, 'mp', 'dp')
- grad_w_out: float32 [1024, 1024], P('mp', 'dp')
- grad_b_out: float32 [1024], P(('dp', 'mp'))
- grad_gain_one: float32 [1024], P(('dp', 'mp'))
- grad_shift_one: float32 [1024], P(('dp', 'mp'))
- grad_w_up: float32 [1024, 4096], P('dp', 'mp')
- grad_b_up: float32 [4, 1024], P('mp', 'dp')
- grad_w_down: float32 [4096, 1024], P('mp', 'dp')
- grad_b_down: float32 [1024], P(('dp', 'mp'))
- grad_gain_two: float32 [1024], P(('dp', 'mp'))
- grad_shift_two: float32 [1024], P(('dp', 'mp'))
- grad_w_time: float32 [1024, 1024], P(('dp', 'mp'))
- grad_b_time: float32 [1024], P(('dp', 'mp'))
Inputs may be any that keep to these rules, and one draw needn't show every extreme that they name: `segment_ids`: along a packed row the ids never fall and every id from 0 up occurs; a document holds at most 512 tokens, and some document holds exactly that many.
All inputs are finite; a program needn't handle non-finite values.
Results may differ from a plain program's by a relative error of at most 0.02.
Values may be sent and summed in bfloat16 or wider, within the bound.
A program may use at most 256 MiB of HBM per device.

v0:
```python
import math

import jax
import jax.numpy as jnp
from jax import lax
from jax.sharding import PartitionSpec as P

D = 1024
HEAD_DIM = 64
LEN = 1024


EPS = 1e-05
HIGHEST_PRECISION = lax.Precision.HIGHEST


def time_features(step_values):
    half_width = D // 2
    ladder = jnp.arange(half_width, dtype=jnp.float32)
    frequency = jnp.exp(ladder * (-math.log(10000.0) / half_width))
    angles = step_values.astype(jnp.float32)[:, None] * frequency[None, :]
    return jnp.concatenate([jnp.sin(angles), jnp.cos(angles)], axis=1)


def layer_norm(values, gain_vec, shift_vec):
    center = values - jnp.mean(values, axis=-1, keepdims=True)
    spread = jnp.mean(center * center, axis=-1, keepdims=True)
    return center * lax.rsqrt(spread + EPS) * gain_vec + shift_vec


def exact_gelu(values):
    return jax.nn.gelu(values, approximate=False)


def project_qkv(hidden_full, w_qkv, b_qv):
    width_local = w_qkv.shape[2]
    w_flat = w_qkv.reshape(w_qkv.shape[0], 3 * width_local)
    bias_row = jnp.concatenate([b_qv[0], jnp.zeros((width_local,), b_qv.dtype), b_qv[1]]).astype(
        jnp.float32
    )
    product = jnp.dot(hidden_full, w_flat, preferred_element_type=jnp.float32)
    return (product + bias_row[None, :]).astype(jnp.bfloat16)


def head_parts(qkv_seq):
    width_local = qkv_seq.shape[1] // 3
    head_local = width_local // HEAD_DIM
    shaped = qkv_seq.reshape(qkv_seq.shape[0], 3, head_local, HEAD_DIM)
    return (shaped[:, 0], shaped[:, 1], shaped[:, 2])


def masked_scores(queries, keys_part, segment_row):
    scores = jnp.einsum("qhd,khd->hqk", queries, keys_part, preferred_element_type=jnp.float32)
    scores = scores * (1.0 / math.sqrt(HEAD_DIM))
    same_doc = segment_row[:, None] == segment_row[None, :]
    return jnp.where(same_doc[None, :, :], scores, -1e30)


def attend_forward(inputs):
    qkv_seq, segment_row = inputs
    queries, keys_part, values_part = head_parts(qkv_seq)
    masked = masked_scores(queries, keys_part, segment_row)
    top_score = jnp.max(masked, axis=2, keepdims=True)
    weights_exp = jnp.exp(masked - top_score)
    totals = jnp.sum(weights_exp, axis=2, keepdims=True)
    probability = weights_exp / totals
    context = jnp.einsum(
        "hqk,khd->qhd",
        probability.astype(jnp.bfloat16),
        values_part,
        preferred_element_type=jnp.float32,
    )
    log_total = (top_score + jnp.log(totals))[:, :, 0]
    return (context.reshape(qkv_seq.shape[0], -1).astype(jnp.bfloat16), log_total)


def attend_backward(inputs):
    qkv_seq, grad_seq, log_total, segment_row = inputs
    queries, keys_part, values_part = head_parts(qkv_seq)
    masked = masked_scores(queries, keys_part, segment_row)
    probability = jnp.exp(masked - log_total[:, :, None])
    grad_heads = grad_seq.reshape(grad_seq.shape[0], -1, HEAD_DIM)
    d_values = jnp.einsum(
        "hqk,qhd->khd",
        probability.astype(jnp.bfloat16),
        grad_heads,
        preferred_element_type=jnp.float32,
    )
    d_probs = jnp.einsum(
        "qhd,khd->hqk", grad_heads, values_part, preferred_element_type=jnp.float32
    )
    row_terms = jnp.sum(probability * d_probs, axis=2, keepdims=True)
    d_scores = (probability * (d_probs - row_terms)).astype(jnp.bfloat16)
    score_scale = 1.0 / math.sqrt(HEAD_DIM)
    d_queries = (
        jnp.einsum("hqk,khd->qhd", d_scores, keys_part, preferred_element_type=jnp.float32)
        * score_scale
    )
    d_keys = (
        jnp.einsum("hqk,qhd->khd", d_scores, queries, preferred_element_type=jnp.float32)
        * score_scale
    )
    stacked = jnp.stack([d_queries, d_keys, d_values], axis=1)
    return stacked.reshape(qkv_seq.shape[0], -1).astype(jnp.bfloat16)


def body(
    tokens,
    segment_ids,
    time_steps,
    w_qkv,
    b_qv,
    w_out,
    b_out,
    gain_one,
    shift_one,
    w_up,
    b_up,
    w_down,
    b_down,
    gain_two,
    shift_two,
    w_time,
    b_time,
    cotangent,
):
    row_count = tokens.shape[0]
    seq_local = time_steps.shape[0]
    width_local = w_qkv.shape[2]
    gain_one_f = gain_one.astype(jnp.float32)
    shift_one_f = shift_one.astype(jnp.float32)
    gain_two_f = gain_two.astype(jnp.float32)
    shift_two_f = shift_two.astype(jnp.float32)
    w_flat = w_qkv.reshape(D, 3 * width_local)
    features = time_features(time_steps)
    embed_rows = jnp.dot(features, w_time.astype(jnp.float32), precision=HIGHEST_PRECISION)
    embed_rows = embed_rows + b_time.astype(jnp.float32)[None, :]
    row_seq = (lax.axis_index("mp") * row_count + jnp.arange(row_count, dtype=jnp.int32)) // LEN
    selector = (row_seq[:, None] == jnp.arange(seq_local, dtype=jnp.int32)[None, :]).astype(
        jnp.float32
    )
    hidden_in = tokens.astype(jnp.float32) + jnp.dot(
        selector, embed_rows, precision=HIGHEST_PRECISION
    )
    hidden_low = hidden_in.astype(jnp.bfloat16)
    hidden_full = lax.all_gather(hidden_low, "mp", axis=0, tiled=True)
    qkv_full = project_qkv(hidden_full, w_qkv, b_qv)
    ctx_blocks, log_totals = lax.map(
        attend_forward, (qkv_full.reshape(seq_local, LEN, 3 * width_local), segment_ids)
    )
    context = ctx_blocks.reshape(seq_local * LEN, width_local)
    rows_in = context
    attn_sum = lax.psum_scatter(
        jnp.dot(rows_in, w_out, preferred_element_type=jnp.float32).astype(jnp.bfloat16),
        "mp",
        scatter_dimension=0,
        tiled=True,
    ).astype(jnp.float32)
    attn_out = attn_sum + b_out.astype(jnp.float32)[None, :]
    mid_in = hidden_in + attn_out
    mid_norm = layer_norm(mid_in, gain_one_f, shift_one_f)
    mid_low = mid_norm.astype(jnp.bfloat16)
    mid_full = lax.all_gather(mid_low, "mp", axis=0, tiled=True)
    pre_act = (
        jnp.dot(mid_full, w_up, preferred_element_type=jnp.float32)
        + b_up.astype(jnp.float32)[None, :]
    )
    activated = exact_gelu(pre_act).astype(jnp.bfloat16)
    rows_in = activated
    ffn_part = lax.psum_scatter(
        jnp.dot(rows_in, w_down, preferred_element_type=jnp.float32).astype(jnp.bfloat16),
        "mp",
        scatter_dimension=0,
        tiled=True,
    ).astype(jnp.float32)
    out_in = mid_norm + ffn_part + b_down.astype(jnp.float32)[None, :]
    out_rows, out_back = jax.vjp(layer_norm, out_in, gain_two_f, shift_two_f)
    grad_two, grad_gain_two, grad_shift_two = out_back(cotangent.astype(jnp.float32))
    branch_two = grad_two.astype(jnp.bfloat16)
    grad_b_down = jnp.sum(branch_two.astype(jnp.float32), axis=0)
    gelu_value, gelu_back = jax.vjp(exact_gelu, pre_act)
    cot_full = lax.all_gather(branch_two, "mp", axis=0, tiled=True)
    d_act = jnp.dot(cot_full, w_down.T, preferred_element_type=jnp.float32)
    grad_w_down = jnp.dot(activated.T, cot_full, preferred_element_type=jnp.float32)
    d_pre = gelu_back(d_act)[0].astype(jnp.bfloat16)
    grad_w_up = jnp.dot(mid_full.T, d_pre, preferred_element_type=jnp.float32)
    grad_b_up = jnp.sum(d_pre.astype(jnp.float32), axis=0)
    rows_in = d_pre
    d_mid_part = lax.psum_scatter(
        jnp.dot(rows_in, w_up.T, preferred_element_type=jnp.float32).astype(jnp.bfloat16),
        "mp",
        scatter_dimension=0,
        tiled=True,
    ).astype(jnp.float32)
    mid_value, mid_back = jax.vjp(layer_norm, mid_in, gain_one_f, shift_one_f)
    grad_one, grad_gain_one, grad_shift_one = mid_back(grad_two + d_mid_part)
    branch_one = grad_one.astype(jnp.bfloat16)
    grad_b_out = jnp.sum(branch_one.astype(jnp.float32), axis=0)
    cot_attn = lax.all_gather(branch_one, "mp", axis=0, tiled=True)
    d_context = jnp.dot(cot_attn, w_out.T, preferred_element_type=jnp.float32).astype(jnp.bfloat16)
    grad_w_out = jnp.dot(context.T, cot_attn, preferred_element_type=jnp.float32)
    grad_blocks = lax.map(
        attend_backward,
        (
            qkv_full.reshape(seq_local, LEN, 3 * width_local),
            d_context.reshape(seq_local, LEN, width_local),
            log_totals,
            segment_ids,
        ),
    )
    d_qkv = grad_blocks.reshape(seq_local * LEN, 3 * width_local)
    grad_w_qkv = jnp.dot(hidden_full.T, d_qkv, preferred_element_type=jnp.float32).reshape(
        D, 3, width_local
    )
    qkv_sums = jnp.sum(d_qkv.astype(jnp.float32), axis=0).reshape(3, width_local)
    grad_b_qv = jnp.stack([qkv_sums[0], qkv_sums[2]]).reshape(2, 1, width_local)
    rows_in = d_qkv
    input_part = lax.psum_scatter(
        jnp.dot(rows_in, w_flat.T, preferred_element_type=jnp.float32).astype(jnp.bfloat16),
        "mp",
        scatter_dimension=0,
        tiled=True,
    ).astype(jnp.float32)
    grad_tokens = grad_one + input_part
    grad_embed = jnp.dot(selector.T, grad_tokens, precision=HIGHEST_PRECISION)
    grad_w_time = jnp.dot(features.T, grad_embed, precision=HIGHEST_PRECISION)
    grad_b_time = jnp.sum(grad_embed, axis=0)
    sharded = (
        lax.psum_scatter(
            grad_w_qkv.astype(jnp.bfloat16), "dp", scatter_dimension=0, tiled=True
        ).astype(jnp.float32),
        lax.psum_scatter(
            grad_b_qv.astype(jnp.bfloat16), "dp", scatter_dimension=2, tiled=True
        ).astype(jnp.float32),
        lax.psum_scatter(
            grad_w_out.astype(jnp.bfloat16), "dp", scatter_dimension=1, tiled=True
        ).astype(jnp.float32),
        lax.psum_scatter(
            grad_w_up.astype(jnp.bfloat16), "dp", scatter_dimension=0, tiled=True
        ).astype(jnp.float32),
        lax.psum_scatter(
            grad_b_up.reshape(1, -1).astype(jnp.bfloat16), "dp", scatter_dimension=1, tiled=True
        ).astype(jnp.float32),
        lax.psum_scatter(
            grad_w_down.astype(jnp.bfloat16), "dp", scatter_dimension=1, tiled=True
        ).astype(jnp.float32),
    )
    shared = (
        lax.psum_scatter(grad_w_time, ("dp", "mp"), scatter_dimension=0, tiled=True),
        lax.psum_scatter(grad_b_time, ("dp", "mp"), scatter_dimension=0, tiled=True),
        lax.psum_scatter(grad_gain_one, ("dp", "mp"), scatter_dimension=0, tiled=True),
        lax.psum_scatter(grad_shift_one, ("dp", "mp"), scatter_dimension=0, tiled=True),
        lax.psum_scatter(grad_gain_two, ("dp", "mp"), scatter_dimension=0, tiled=True),
        lax.psum_scatter(grad_shift_two, ("dp", "mp"), scatter_dimension=0, tiled=True),
        lax.psum_scatter(grad_b_out, ("dp", "mp"), scatter_dimension=0, tiled=True),
        lax.psum_scatter(grad_b_down, ("dp", "mp"), scatter_dimension=0, tiled=True),
    )
    return (
        out_rows.astype(jnp.bfloat16),
        grad_tokens,
        sharded[0],
        sharded[1],
        sharded[2],
        shared[6],
        shared[2],
        shared[3],
        sharded[3],
        sharded[4],
        sharded[5],
        shared[7],
        shared[4],
        shared[5],
        shared[0],
        shared[1],
    )


def solution(mesh):
    placed = (
        P(("dp", "mp"), None),
        P("dp", None),
        P("dp"),
        P(None, None, "mp"),
        P(None, "mp"),
        P("mp", None),
        P(),
        P(),
        P(),
        P(None, "mp"),
        P("mp"),
        P("mp", None),
        P(),
        P(),
        P(),
        P(),
        P(),
        P(("dp", "mp"), None),
    )
    return jax.shard_map(
        body,
        mesh=mesh,
        in_specs=placed,
        out_specs=(
            P(("dp", "mp"), None),
            P(("dp", "mp"), None),
            P("dp", None, "mp"),
            P(None, "mp", "dp"),
            P("mp", "dp"),
            P(("dp", "mp")),
            P(("dp", "mp")),
            P(("dp", "mp")),
            P("dp", "mp"),
            P("mp", "dp"),
            P("mp", "dp"),
            P(("dp", "mp")),
            P(("dp", "mp")),
            P(("dp", "mp")),
            P(("dp", "mp"), None),
            P(("dp", "mp")),
        ),
        check_vma=False,
    )
```

profile of v0, /device:TPU:0, one launch (start us, length us, event | category | flops | bytes accessed | tf_op | source)
XLA Modules:
  0.0 1548.9 jit_solution(1779898777233355602)
XLA Ops:
  16.0 6.4 fusion.33
  25.3 58.2 %all-gather.5.cloned.1.call-done = bf16[4096,1024]{0,1:T(8,128)(2,1)} async-done(((bf16[1024,1024]{0,1:T(8,128)(2,1)}), bf16[4096,1024]{0,1:T(8,128)(2,1)}) %all-gather.5.cloned.1.call-update) | async-done | bytes 8388624 | tf_op jit(solution)/shard_map/all_gather | solution.py:146
  83.5 11.5 add_convert_fusion.1
  95.0 8.6 copy.93
  103.6 65.6 %while.22 = (s32[]{:T(128)}, bf16[4,1024,256]{2,1,0:T(8,128)(2,1)}, f32[4,4,1024]{2,1,0:T(4,128)}, bf16[4,1024,768]{1,2,0:T(8,128)(2,1)}, s32[4,1024]{1,0:T(4,128)}, /*index=5*/s32[]{:T(128)}) while((s32[]{:T(128)}, bf16[4,1024,256]{2,1,0:T(8,128)(2,1)}, f32[4,4,1024]{2,1,0:T(4,128)}, bf16[4,1024,768]{1,2,0:T(8,128)(2,1)}, ...), condition=%wide.region_3.4_spmd, body=%wide.region_0.3_spmd.sunk | while | flops 1125380096 | bytes 62009436 | solution.py:148
  169.2 7.3 convolution_convert_fusion.3
  177.2 70.7 %reduce-scatter.20.cloned.1.call-done = bf16[1024,1024]{0,1:T(8,128)(2,1)} async-done(((bf16[4096,1024]{0,1:T(8,128)(2,1)}), bf16[1024,1024]{0,1:T(8,128)(2,1)}) %reduce-scatter.20.cloned.1.call-update) | async-done | bytes 2097168 | tf_op jit(solution)/shard_map/reduce_scatter | solution.py:153
  256.4 58.3 %all-gather.7.cloned.1.call-done = bf16[4096,1024]{0,1:T(8,128)(2,1)} async-done(((bf16[1024,1024]{0,1:T(8,128)(2,1)}), bf16[4096,1024]{0,1:T(8,128)(2,1)}) %all-gather.7.cloned.1.call-update) | async-done | bytes 8388624 | tf_op jit(solution)/shard_map/all_gather | solution.py:163
  314.7 48.1 %multiply_convert_fusion.1 = (bf16[4096,1024]{1,0:T(8,128)(2,1)}, f32[4096,1024]{1,0:T(8,128)}, f32[4096,1024]{1,0:T(8,128)}) fusion(f32[1024]{0:T(1024)S(1)} %convert_element_type.203, bf16[4096,1024]{0,1:T(8,128)(2,1)} %all-gather.7.cloned.1.call-done, bf16[1024,1024]{1,0:T(8,128)(2,1)S(1)} %copy-done), kind=kOutput, calls=%fused_computation.45 | convolution fusion | flops 8866758656 | bytes 52432896 | tf_op jit(solution)/shard_map/dot_general | solution.py:165
  362.8 14.5 convolution_convert_fusion.2
  382.1 66.6 %reduce-scatter.22.cloned.1.call-done = bf16[1024,1024]{0,1:T(8,128)(2,1)} async-done(((bf16[4096,1024]{0,1:T(8,128)(2,1)}), bf16[1024,1024]{0,1:T(8,128)(2,1)}) %reduce-scatter.22.cloned.1.call-update) | async-done | bytes 2097168 | tf_op jit(solution)/shard_map/reduce_scatter | solution.py:170
  462.4 58.4 %all-gather.9.cloned.1.call-done = bf16[4096,1024]{0,1:T(8,128)(2,1)} async-done(((bf16[1024,1024]{0,1:T(8,128)(2,1)}), bf16[4096,1024]{0,1:T(8,128)(2,1)}) %all-gather.9.cloned.1.call-update) | async-done | bytes 8388624 | tf_op jit(solution)/shard_map/all_gather | solution.py:182
  520.8 24.7 %fusion.52 = (bf16[1024]{0:T(1024)(128)(2,1)}, bf16[4096,1024]{1,0:T(8,128)(2,1)}) fusion(f32[4096,1024]{1,0:T(8,128)} %get-tuple-element.237, f32[4096,1024]{1,0:T(8,128)} %get-tuple-element.251, f32[1024]{0:T(1024)S(1)} %convert_element_type.203, bf16[4096,1024]{0,1:T(8,128)(2,1)} %all-gather.9.cloned.1.call-done, bf16[1024,1024]{1,0:T(8,128)(2,1)} %param.33), kind=kOutput, calls=%fused_computation.138 | convolution fusion | flops 8657042432 | bytes 52434944 | tf_op jit(solution)/shard_map/dot_general | solution.py:183
  545.5 14.3 convolution_convert_fusion.1
  559.9 71.3 %reduce-scatter.24.cloned.1.call-done = bf16[1024,1024]{0,1:T(8,128)(2,1)} async-done(((bf16[4096,1024]{0,1:T(8,128)(2,1)}), bf16[1024,1024]{0,1:T(8,128)(2,1)}) %reduce-scatter.24.cloned.1.call-update) | async-done | bytes 2097168 | tf_op jit(solution)/shard_map/reduce_scatter | solution.py:189
  631.2 5.9 multiply_reduce_fusion.1
  644.8 58.4 %all-gather.11.cloned.1.call-done = bf16[4096,1024]{0,1:T(8,128)(2,1)} async-done(((bf16[1024,1024]{0,1:T(8,128)(2,1)}), bf16[4096,1024]{0,1:T(8,128)(2,1)}) %all-gather.11.cloned.1.call-update) | async-done | bytes 8388624 | tf_op jit(solution)/shard_map/all_gather | solution.py:199
  703.2 5.9 convolution_convert_fusion.4
  709.1 189.9 %while.23 = (s32[]{:T(128)}, bf16[4,1024,768]{1,2,0:T(8,128)(2,1)}, bf16[4,1024,768]{1,2,0:T(8,128)(2,1)}, s32[4,1024]{1,0:T(4,128)}, f32[4,4,1024]{2,1,0:T(4,12...) while((s32[]{:T(128)}, bf16[4,1024,768]{1,2,0:T(8,128)(2,1)}, bf16[4,1024,768]{1,2,0:T(8,128)(2,1)}, ...), condition=%wide.region_17.18_spmd, body=%wide.region_15.17_spmd.sunk | while | flops 2726031360 | bytes 195129552 | solution.py:202
  719.1 10.9 multiply_reduce_fusion.6
  729.9 10.4 multiply_convert_fusion.3
  740.3 8.6 fusion.112
  766.4 10.9 multiply_reduce_fusion.6
  777.3 10.4 multiply_convert_fusion.3
  787.7 8.6 fusion.112
  813.7 10.9 multiply_reduce_fusion.6
  824.6 10.4 multiply_convert_fusion.3
  835.0 8.6 fusion.112
  861.1 10.9 multiply_reduce_fusion.6
  872.0 10.4 multiply_convert_fusion.3
  882.4 8.6 fusion.112
  899.0 8.9 copy.101
  907.9 11.7 convolution_convert_fusion
  921.3 14.5 convolution_convert_fusion.5
  938.4 15.5 convolution_convert_fusion.6
  959.2 5.8 convolution_convert_fusion.7
  965.9 8.5 copy.103
  974.5 11.9 fusion.34
  998.8 5.1 fusion.43
  1008.0 49.0 %reduce-scatter.38.cloned.1.call-done = bf16[128,1]{1,0:T(8,128)(2,1)} async-done(((bf16[1024,1]{1,0:T(8,128)(2,1)}), bf16[128,1]{1,0:T(8,128)(2,1)}) %reduce-scatter.38.cloned.1.call-update) | async-done | bytes 272
  1058.4 69.3 %reduce-scatter.40.cloned.1.call-done = bf16[128,1024]{1,0:T(8,128)(2,1)} async-done(((bf16[1024,1024]{1,0:T(8,128)(2,1)}), bf16[128,1024]{1,0:T(8,128)(2,1)}) %reduce-scatter.40.cloned.1.call-update) | async-done | bytes 262160
  1129.7 69.1 %reduce-scatter.30.cloned.1.call-done = bf16[128,1024]{1,0:T(8,128)(2,1)} async-done(((bf16[1024,1024]{1,0:T(8,128)(2,1)}), bf16[128,1024]{1,0:T(8,128)(2,1)}) %reduce-scatter.30.cloned.1.call-update) | async-done | bytes 262160 | tf_op jit(solution)/shard_map/reduce_scatter | solution.py:238
  1200.6 63.6 %reduce-scatter.34.cloned.1.call-done = bf16[32,2]{1,0:T(8,128)(2,1)} async-done(((bf16[256,2]{1,0:T(8,128)(2,1)}), bf16[32,2]{1,0:T(8,128)(2,1)}) %reduce-scatter.34.cloned.1.call-update) | async-done | bytes 144
  1265.6 63.8 %reduce-scatter.36.cloned.1.call-done = bf16[128,256]{1,0:T(8,128)(2,1)} async-done(((bf16[1024,256]{1,0:T(8,128)(2,1)}), bf16[128,256]{1,0:T(8,128)(2,1)}) %reduce-scatter.36.cloned.1.call-update) | async-done | bytes 65552
  1331.0 66.8 %reduce-scatter.28.cloned.1.call-done = bf16[128,3,256]{2,0,1:T(8,128)(2,1)} async-done(((bf16[1024,3,256]{2,0,1:T(8,128)(2,1)}), bf16[128,3,256]{2,0,1:T(8,128)(2,1)}) %reduce-scatter.28.cloned.1.call-update) | async-done | bytes 196624 | tf_op jit(solution)/shard_map/reduce_scatter | solution.py:229
  1399.5 5.3 copy.105
  1404.9 40.5 %all-reduce.7 = (f32[1024]{0:T(1024)S(1)}, f32[1024]{0:T(1024)S(1)}, f32[1024]{0:T(1024)S(1)}, f32[1024]{0:T(1024)S(1)}, f32[1024]{0:T(1024)S(1)}, /*index=5*/f32[1024]{0:T(1024)S(1)}, f32[1024]{0:T(1024)S(1)}) all-reduce(f32[1024]{0:T(1024)S(1)} %copy-done.31, ...), channel_id=9, replica_groups=mesh['dp'=8,'mp'=4] {'dp','mp'}, use_global_device_ids=true, to_apply=%region_24.25.clone | all-reduce | flops 7168 | bytes 57344
  1449.5 92.6 %reduce-scatter.32.cloned.1.call-done = f32[32,1024]{1,0:T(8,128)} async-done(((f32[1024,1024]{1,0:T(8,128)}), f32[32,1024]{1,0:T(8,128)}) %reduce-scatter.32.cloned.1.call-update) | async-done | bytes 131088 | tf_op jit(solution)/shard_map/reduce_scatter | solution.py:249
  (284 shorter events, 222.6 us)
Async XLA Ops:
  7.2 307.5 %copy-start = (bf16[1024,1024]{1,0:T(8,128)(2,1)S(1)}, bf16[1024,1024]{1,0:T(8,128)(2,1)}, u32[]{:S(2)}) copy-start(bf16[1024,1024]{1,0:T(8,128)(2,1)} %param.31) | copy-start | bytes 6291460
  7.2 76.3 %all-gather.5.cloned.1.call-start = ((), (), s32[]{:S(2)}) async-start(), calls=%async_computation.11 | async-start | bytes 10485760 | tf_op jit(solution)/shard_map/all_gather | solution.py:146
  8.1 14.3 copy-start.22
  16.0 9.3 copy-start.32
  22.4 225.6 %reduce-scatter.20.cloned.1.call-start = ((), (), s32[]{:S(2)}) async-start(), calls=%async_computation.12 | async-start | bytes 10485760 | tf_op jit(solution)/shard_map/reduce_scatter | solution.py:153
  176.6 138.2 %all-gather.7.cloned.1.call-start = ((), (), s32[]{:S(2)}) async-start(), calls=%async_computation.13 | async-start | bytes 10485760 | tf_op jit(solution)/shard_map/all_gather | solution.py:163
  252.3 4.1 copy-start.37
  256.3 192.4 %reduce-scatter.22.cloned.1.call-start = ((), (), s32[]{:S(2)}) async-start(), calls=%async_computation.14 | async-start | bytes 10485760 | tf_op jit(solution)/shard_map/reduce_scatter | solution.py:170
  314.7 48.1 %copy-start.41 = (bf16[1024,1024]{1,0:T(8,128)(2,1)S(1)}, bf16[1024,1024]{1,0:T(8,128)(2,1)}, u32[]{:S(2)}) copy-start(bf16[1024,1024]{1,0:T(8,128)(2,1)} %param.33) | copy-start | bytes 6291460
  377.3 143.4 %all-gather.9.cloned.1.call-start = ((), (), s32[]{:S(2)}) async-start(), calls=%async_computation.15 | async-start | bytes 10485760 | tf_op jit(solution)/shard_map/all_gather | solution.py:182
  448.7 4.2 copy-start.9
  462.4 168.9 %reduce-scatter.24.cloned.1.call-start = ((), (), s32[]{:S(2)}) async-start(), calls=%async_computation.16 | async-start | bytes 10485760 | tf_op jit(solution)/shard_map/reduce_scatter | solution.py:189
  559.8 77.3 %copy-start.25 = (f32[1024]{0:T(1024)S(1)}, f32[1024]{0:T(1024)}, u32[]{:S(2)}) copy-start(f32[1024]{0:T(1024)} %copy-done.24) | copy-start | bytes 12292
  559.9 143.3 %all-gather.11.cloned.1.call-start = ((), (), s32[]{:S(2)}) async-start(), calls=%async_computation.17 | async-start | bytes 10485760 | tf_op jit(solution)/shard_map/all_gather | solution.py:199
  631.2 6.0 copy-start.4
  631.2 6.5 copy-start.6
  631.2 7.1 copy-start.10
  640.5 62.7 %copy-start.15 = (bf16[256,1024]{1,0:T(8,128)(2,1)S(1)}, bf16[256,1024]{1,0:T(8,128)(2,1)}, u32[]{:S(2)}) copy-start(bf16[256,1024]{1,0:T(8,128)(2,1)} %param.27) | copy-start | bytes 1572868
  640.5 4.3 copy-start.20
  644.8 346.3 %reduce-scatter.26.cloned.1.call-start = ((), (), s32[]{:S(2)}) async-start(), calls=%async_computation.18 | async-start | bytes 10485760 | tf_op jit(solution)/shard_map/reduce_scatter | solution.py:218
  740.3 8.6 copy-start.2
  751.6 5.3 copy-start.13
  787.7 8.6 copy-start.2
  798.9 5.3 copy-start.13
  835.0 8.6 copy-start.2
  846.3 5.4 copy-start.13
  882.4 8.6 copy-start.2
  893.6 5.3 copy-start.13
  899.0 8.9 copy-start.14
  919.6 137.4 %reduce-scatter.38.cloned.1.call-start = ((), (), s32[]{:S(2)}) async-start(), calls=%async_computation.24 | async-start | bytes 294912
  921.2 206.5 %reduce-scatter.40.cloned.1.call-start = ((), (), s32[]{:S(2)}) async-start(), calls=%async_computation.25 | async-start | bytes 2359296
  938.4 260.4 %reduce-scatter.30.cloned.1.call-start = ((), (), s32[]{:S(2)}) async-start(), calls=%async_computation.20 | async-start | bytes 2359296 | tf_op jit(solution)/shard_map/reduce_scatter | solution.py:238
  953.9 5.2 copy-start.11
  953.9 310.2 %reduce-scatter.34.cloned.1.call-start = ((), (), s32[]{:S(2)}) async-start(), calls=%async_computation.22 | async-start | bytes 73728
  959.1 370.3 %reduce-scatter.36.cloned.1.call-start = ((), (), s32[]{:S(2)}) async-start(), calls=%async_computation.23 | async-start | bytes 589824
  974.5 423.4 %reduce-scatter.28.cloned.1.call-start = ((), (), s32[]{:S(2)}) async-start(), calls=%async_computation.19 | async-start | bytes 1769472 | tf_op jit(solution)/shard_map/reduce_scatter | solution.py:229
  974.5 16.5 %copy-start.21 = (f32[1024]{0:T(1024)S(1)}, f32[1024]{0:T(1024)}, u32[]{:S(2)}) copy-start(f32[1024]{0:T(1024)} %copy-done.20) | copy-start | bytes 12292
  986.5 10.1 copy-start.23
  986.5 12.3 copy-start.17
  986.5 12.3 copy-start.19
  986.5 555.6 %reduce-scatter.32.cloned.1.call-start = ((), (), s32[]{:S(2)}) async-start(), calls=%async_computation.21 | async-start | bytes 4325376 | tf_op jit(solution)/shard_map/reduce_scatter | solution.py:249
  1003.9 538.3 %copy-start.1 = (bf16[1024,1024]{1,0:T(8,128)(2,1)S(1)}, bf16[1024,1024]{1,0:T(8,128)(2,1)}, u32[]{:S(2)}) copy-start(bf16[1024,1024]{1,0:T(8,128)(2,1)} %param.31) | copy-start | bytes 6291460
  1008.0 396.9 %copy-start.26 = (f32[1024]{0:T(1024)S(1)}, f32[1024]{0:T(1024)}, u32[]{:S(2)}) copy-start(f32[1024]{0:T(1024)} %get-tuple-element.189) | copy-start | bytes 12292
  1008.0 396.9 %copy-start.27 = (f32[1024]{0:T(1024)S(1)}, f32[1024]{0:T(1024)}, u32[]{:S(2)}) copy-start(f32[1024]{0:T(1024)} %get-tuple-element.192) | copy-start | bytes 12292
  1008.0 396.9 %copy-start.28 = (f32[1024]{0:T(1024)S(1)}, f32[1024]{0:T(1024)}, u32[]{:S(2)}) copy-start(f32[1024]{0:T(1024)} %get-tuple-element.226) | copy-start | bytes 12292
  1008.0 396.9 %copy-start.29 = (f32[1024]{0:T(1024)S(1)}, f32[1024]{0:T(1024)}, u32[]{:S(2)}) copy-start(f32[1024]{0:T(1024)} %get-tuple-element.187) | copy-start | bytes 12292
  1008.0 396.9 %copy-start.30 = (f32[1024]{0:T(1024)S(1)}, f32[1024]{0:T(1024)}, u32[]{:S(2)}) copy-start(f32[1024]{0:T(1024)} %get-tuple-element.191) | copy-start | bytes 12292
  1008.0 396.9 %copy-start.31 = (f32[1024]{0:T(1024)S(1)}, f32[1024]{0:T(1024)}, u32[]{:S(2)}) copy-start(f32[1024]{0:T(1024)} %get-tuple-element.228) | copy-start | bytes 12292
  (18 other events, 20.8 us)
Sparse Core Ops, SparseCore 0:
  22.5 60.9 all-gather.4
  176.7 71.2 reduce-scatter.19
  256.4 58.2 all-gather.6
  377.5 71.2 reduce-scatter.21
  462.5 58.2 all-gather.8
  560.0 71.2 reduce-scatter.23
  644.9 58.2 all-gather.10
  919.8 71.2 reduce-scatter.25
  994.9 62.0 reduce-scatter.37
  1060.4 67.2 reduce-scatter.39
  1131.3 67.4 reduce-scatter.29
  1202.6 61.4 reduce-scatter.33
  1267.5 61.8 reduce-scatter.35
  1332.7 65.1 reduce-scatter.27
  1400.5 141.5 reduce-scatter.31
where the time goes:
time: 1560 us; the launch traced here: 1550 us
  waiting for transfers between devices  921 us (59%)
  matrix products  351 us (22%)
  other arithmetic  113 us (7%)
  local copies, waits for them, and re-layouts  107 us (7%)
  blocking collectives  40.5 us (3%)
    unnamed x19, waiting for transfers between devices  246 us
    reduce_scatter x1, waiting for transfers between devices, body(): lax.psum_scatter(grad_w_time, ('dp', 'mp'), scatter_dimension=0, tiled=True)  92.6 us
    reduce_scatter x1, waiting for transfers between devices, body(): lax.psum_scatter(jnp.dot(rows_in, w_up.T, preferred_element_type=jnp.floa...  71.3 us
    reduce_scatter x1, waiting for transfers between devices, body(): lax.psum_scatter(jnp.dot(rows_in, w_out, preferred_element_type=jnp.float...  70.7 us
    reduce_scatter x1, waiting for transfers between devices, body(): lax.psum_scatter(grad_w_up.astype(jnp.bfloat16), 'dp', scatter_dimension=...  69.1 us
    reduce_scatter x1, waiting for transfers between devices, body(): lax.psum_scatter(grad_w_qkv.astype(jnp.bfloat16), 'dp', scatter_dimension...  66.8 us
    reduce_scatter x1, waiting for transfers between devices, body(): lax.psum_scatter(jnp.dot(rows_in, w_down, preferred_element_type=jnp.floa...  66.6 us
    all_gather x1, waiting for transfers between devices, body(): cot_full = lax.all_gather(branch_two, 'mp', axis=0, tiled=True)  58.4 us
  transfers between devices with their start and end apart: 15, of which 15 were waited for; matrix products, arithmetic and copies ran while one was open for 7% of the time, Pallas kernels for 0%

commit v1 on v0

--- a/solution.py
+++ b/solution.py
@@ -104,7 +104,7 @@
     return stacked.reshape(qkv_seq.shape[0], -1).astype(jnp.bfloat16)
 
 
-def body(
+def body_split(
     tokens,
     segment_ids,
     time_steps,
@@ -275,6 +275,338 @@
     )
 
 
+GRID_DP = 8
+GRID_MP = 4
+F32 = jnp.float32
+BF16 = jnp.bfloat16
+
+
+def flip_mp(values, bit):
+    return lax.ppermute(values, "mp", [(i, i ^ bit) for i in range(GRID_MP)])
+
+
+def flip_dp(values, bit):
+    return lax.ppermute(values, "dp", [(i, i ^ bit) for i in range(GRID_DP)])
+
+
+def half_of(values, which, axis):
+    size = values.shape[axis] // 2
+    return lax.dynamic_slice_in_dim(values, which * size, size, axis)
+
+
+def fetch_pieces(own, axis, x_at):
+    near = flip_mp(own, 1)
+    far_a = flip_mp(half_of(own, x_at, axis), 2)
+    far_b = flip_dp(far_a, 1)
+    return [own, near, far_a, far_b, flip_mp(far_a, 1), flip_mp(far_b, 1)]
+
+
+def fetch_vectors(own, x_at):
+    near = flip_mp(own, 1)
+    far = flip_mp(own, 2)
+    near_far = flip_mp(far, 1)
+    return [
+        own,
+        near,
+        half_of(far, x_at, 1),
+        half_of(far, 1 - x_at, 1),
+        half_of(near_far, x_at, 1),
+        half_of(near_far, 1 - x_at, 1),
+    ]
+
+
+def x_parts(values, x_at):
+    width = values.shape[1]
+    shaped = values.reshape(4, 2, values.shape[0] // 8, width)
+    keep = lax.dynamic_index_in_dim(shaped, x_at, 1, keepdims=False)
+    leave = lax.dynamic_index_in_dim(shaped, 1 - x_at, 1, keepdims=False)
+    return keep, leave
+
+
+def join_halves(part_a, part_b, x_at):
+    axis = part_a.ndim - 1
+    return jnp.where(
+        x_at == 0,
+        jnp.concatenate([part_a, part_b], axis),
+        jnp.concatenate([part_b, part_a], axis),
+    )
+
+
+def add_low(left, right):
+    return (left.astype(F32) + right.astype(F32)).astype(BF16)
+
+
+def sum_over_z(part, z_at):
+    total = lax.dynamic_index_in_dim(part, z_at, 0, keepdims=False).astype(F32)
+    for bit in (1, 2, 3):
+        sent = lax.dynamic_index_in_dim(part, z_at ^ bit, 0, keepdims=False)
+        total = total + flip_dp(sent, 2 * bit).astype(F32)
+    return total
+
+
+def reduce_pieces(make, join, x_at, z_at, y_first):
+    sent = [flip_mp(make(i, None), 1) for i in (1, 4, 5)]
+    own, far_a, far_b = (make(i, extra) for i, extra in zip((0, 2, 3), sent))
+    if y_first:
+        got_a, got_b = flip_mp(far_a, 2), flip_mp(far_b, 2)
+        block = add_low(own, join(got_a, got_b, x_at))
+        keep, leave = x_parts(block, x_at)
+        part = add_low(keep, flip_dp(leave, 1))
+    else:
+        own_keep, own_leave = x_parts(own, x_at)
+        a_keep, a_leave = x_parts(far_a, x_at)
+        b_keep, b_leave = x_parts(far_b, x_at)
+        got_b, got_a = flip_dp(a_leave, 1), flip_dp(b_leave, 1)
+        got_own = flip_dp(own_leave, 1)
+        far_a, far_b = add_low(a_keep, got_a), add_low(b_keep, got_b)
+        far_a, far_b = flip_mp(far_a, 2), flip_mp(far_b, 2)
+        part = add_low(add_low(own_keep, got_own), join(far_a, far_b, x_at))
+    return sum_over_z(part, z_at)
+
+
+def sum_vectors(rows, place):
+    for flip, bit, at in place:
+        size = rows.shape[0] // 2
+        keep = lax.dynamic_slice_in_dim(rows, at * size, size, 0)
+        leave = lax.dynamic_slice_in_dim(rows, (1 - at) * size, size, 0)
+        rows = keep + flip(leave, bit)
+    return rows[0]
+
+
+def by_device(parts):
+    shaped = parts.reshape(2, 2, 2, 2, 2, -1)
+    return shaped.transpose(4, 3, 2, 0, 1, 5).reshape(32, -1)
+
+
+def gather_all(row, order):
+    index = lax.axis_index("dp") * GRID_MP + lax.axis_index("mp")
+    full = jnp.zeros((GRID_DP * GRID_MP, row.shape[1]), row.dtype)
+    rows = row
+    for flip, bit, shift in order:
+        other = flip(rows, bit)
+        low = (index >> shift) & 1
+        rows = jnp.where(low == 0, jnp.concatenate([rows, other]), jnp.concatenate([other, rows]))
+    return rows
+
+
+def norm_stats(values):
+    center = values - jnp.mean(values, axis=-1, keepdims=True)
+    spread = jnp.mean(center * center, axis=-1, keepdims=True)
+    scale = lax.rsqrt(spread + EPS)
+    return center * scale, scale
+
+
+def norm_back(normal, scale, grad, gain_vec):
+    scaled = grad * gain_vec
+    mean_e = jnp.mean(scaled, axis=-1, keepdims=True)
+    mean_en = jnp.mean(scaled * normal, axis=-1, keepdims=True)
+    return scale * (scaled - mean_e - normal * mean_en)
+
+
+def dot_f32(left, right, dims):
+    return lax.dot_general(left, right, (dims, ((), ())), preferred_element_type=F32)
+
+
+def body_rows(
+    tokens,
+    segment_ids,
+    time_steps,
+    w_qkv,
+    b_qv,
+    w_out,
+    b_out,
+    gain_one,
+    shift_one,
+    w_up,
+    b_up,
+    w_down,
+    b_down,
+    gain_two,
+    shift_two,
+    w_time,
+    b_time,
+    cotangent,
+):
+    dp_at, mp_at = lax.axis_index("dp"), lax.axis_index("mp")
+    x_at, z_at = dp_at % 2, dp_at // 2
+    y_at, c_at = mp_at // 2, mp_at % 2
+    width_local = w_qkv.shape[2]
+    row = lambda v: v.astype(F32)[None, :]
+
+    qkv_w = fetch_pieces(w_qkv, 2, x_at)
+    qkv_w = [w.reshape(D, -1) for w in qkv_w]
+    vectors = fetch_vectors(b_qv, x_at)
+    vec_qkv = [
+        jnp.concatenate([v[0], jnp.zeros_like(v[0]), v[1]]).astype(F32)[None, :] for v in vectors
+    ]
+    out_w = fetch_pieces(w_out, 0, x_at)
+    up_w = fetch_pieces(w_up, 1, x_at)
+    vec_up = [v.astype(F32) for v in fetch_vectors(b_up[None, :], x_at)]
+    down_w = fetch_pieces(w_down, 0, x_at)
+    pieces = range(len(qkv_w))
+
+    own_step = lax.dynamic_slice_in_dim(time_steps, mp_at, 1, 0)
+    segment_row = lax.dynamic_index_in_dim(segment_ids, mp_at, 0, keepdims=False)
+    features = time_features(own_step)
+    embed_row = jnp.dot(features, w_time.astype(F32), precision=HIGHEST_PRECISION)
+    embed_row = embed_row + b_time.astype(F32)[None, :]
+    hidden_in = tokens.astype(F32) + embed_row
+    hidden_low = hidden_in.astype(BF16)
+
+    qkv, context, log_total = [], [], []
+    for i in pieces:
+        product = dot_f32(hidden_low, qkv_w[i], ((1,), (0,)))
+        qkv.append((product + vec_qkv[i]).astype(BF16))
+        ctx, lse = attend_forward((qkv[i], segment_row))
+        context.append(ctx)
+        log_total.append(lse)
+    attn_out = row(b_out)
+    for i in pieces:
+        attn_out = attn_out + dot_f32(context[i], out_w[i], ((1,), (0,)))
+    normal_one, scale_one = norm_stats(hidden_in + attn_out)
+    mid_norm = normal_one * row(gain_one) + row(shift_one)
+    mid_low = mid_norm.astype(BF16)
+
+    act, slope = [], []
+    for i in pieces:
+        pre = dot_f32(mid_low, up_w[i], ((1,), (0,))) + vec_up[i]
+        phi = 0.5 * (1.0 + lax.erf(pre * math.sqrt(0.5)))
+        act.append((pre * phi).astype(BF16))
+        slope.append((phi + pre * jnp.exp(-0.5 * pre * pre) * (1.0 / math.sqrt(2.0 * math.pi))).astype(BF16))
+    ffn = row(b_down)
+    for i in pieces:
+        ffn = ffn + dot_f32(act[i], down_w[i], ((1,), (0,)))
+    normal_two, scale_two = norm_stats(mid_norm + ffn)
+    out_rows = (normal_two * row(gain_two) + row(shift_two)).astype(BF16)
+
+    cot = cotangent.astype(F32)
+    grad_two = norm_back(normal_two, scale_two, cot, row(gain_two))
+    branch_two = grad_two.astype(BF16)
+    d_pre = []
+    for i in pieces:
+        d_act = dot_f32(branch_two, down_w[i], ((1,), (1,)))
+        d_pre.append((d_act * slope[i].astype(F32)).astype(BF16))
+
+    def grad_maker(left, rights):
+        def make(i, extra):
+            total = dot_f32(left, rights[i], ((0,), (0,)))
+            if extra is not None:
+                total = total + extra.astype(F32)
+            return total.astype(BF16)
+
+        return make
+
+    g_w_down = reduce_pieces(grad_maker(branch_two, act), join_halves, x_at, z_at, True)
+    g_w_up = reduce_pieces(grad_maker(mid_low, d_pre), join_halves, x_at, z_at, False)
+    d_mid = grad_two
+    for i in pieces:
+        d_mid = d_mid + dot_f32(d_pre[i], up_w[i], ((1,), (1,)))
+    grad_one = norm_back(normal_one, scale_one, d_mid, row(gain_one))
+    branch_one = grad_one.astype(BF16)
+    d_context = [
+        dot_f32(branch_one, out_w[i], ((1,), (1,))).astype(BF16) for i in pieces
+    ]
+    g_w_out = reduce_pieces(grad_maker(branch_one, context), join_halves, x_at, z_at, True)
+    d_qkv = [
+        attend_backward((qkv[i], d_context[i], log_total[i], segment_row)) for i in pieces
+    ]
+
+    def join_qkv(part_a, part_b, at):
+        lead = part_a.shape[:-1]
+        joined = join_halves(part_a.reshape(lead + (3, -1)), part_b.reshape(lead + (3, -1)), at)
+        return joined.reshape(lead + (3 * width_local,))
+
+    g_w_qkv = reduce_pieces(grad_maker(hidden_low, d_qkv), join_qkv, x_at, z_at, False)
+    grad_tokens = grad_one
+    for i in pieces:
+        grad_tokens = grad_tokens + dot_f32(d_qkv[i], qkv_w[i], ((1,), (1,)))
+
+    place = (
+        (flip_mp, 1, c_at),
+        (flip_mp, 2, y_at),
+        (flip_dp, 1, x_at),
+        (flip_dp, 4, z_at // 2),
+        (flip_dp, 2, z_at % 2),
+    )
+    sum_rows = lambda v: jnp.sum(v.astype(F32), axis=0)
+
+    def natural(parts):
+        far = join_halves(parts[2], parts[3], x_at)
+        near_far = join_halves(parts[4], parts[5], x_at)
+        stacked = jnp.stack([parts[0], parts[1], far, near_far])
+        return jnp.stack([stacked[i ^ mp_at] for i in range(4)])
+
+    def spread(vector):
+        return vector.reshape(8, 4, -1)
+
+    def spread_blocks(blocks):
+        return blocks.reshape(4, 8, -1).transpose(1, 0, 2)
+
+    rows_two = jnp.concatenate(
+        [
+            spread(sum_rows(branch_two)),
+            spread(sum_rows(cot * normal_two)),
+            spread(sum_rows(cot)),
+            spread_blocks(natural([sum_rows(v) for v in d_pre])),
+        ],
+        axis=2,
+    )
+    rows_two = sum_vectors(by_device(rows_two), place)
+    rows_one = jnp.concatenate(
+        [
+            spread(sum_rows(branch_one)),
+            spread(sum_rows(d_mid * normal_one)),
+            spread(sum_rows(d_mid)),
+        ],
+        axis=2,
+    )
+    rows_one = sum_vectors(by_device(rows_one), place)
+    qkv_sums = [sum_rows(v).reshape(3, -1) for v in d_qkv]
+    rows_qkv = jnp.concatenate(
+        [spread_blocks(natural([v[i] for v in qkv_sums])) for i in (0, 2)], axis=2
+    )
+    rows_qkv = sum_vectors(by_device(rows_qkv), place)
+
+    grad_embed = jnp.sum(grad_tokens, axis=0, keepdims=True)
+    tail_row = jnp.concatenate(
+        [grad_embed, jnp.broadcast_to(own_step.astype(F32)[None, :], (1, 128))], axis=1
+    )
+    order = (
+        (flip_mp, 1, 0),
+        (flip_mp, 2, 1),
+        (flip_dp, 1, 2),
+        (flip_dp, 2, 3),
+        (flip_dp, 4, 4),
+    )
+    all_rows = gather_all(tail_row, order)
+    device_at = dp_at * GRID_MP + mp_at
+    span = D // (GRID_DP * GRID_MP)
+    all_grads = all_rows[:, :D]
+    all_features = time_features(all_rows[:, D])
+    own_features = lax.dynamic_slice_in_dim(all_features, device_at * span, span, 1)
+    g_w_time = jnp.dot(own_features.T, all_grads, precision=HIGHEST_PRECISION)
+    g_b_time = lax.dynamic_slice_in_dim(jnp.sum(all_grads, axis=0), device_at * span, span, 0)
+
+    return (
+        out_rows,
+        grad_tokens,
+        g_w_qkv.reshape(-1, 3, width_local),
+        rows_qkv.reshape(2, 1, -1),
+        g_w_out.T,
+        rows_one[:span],
+        rows_one[span : 2 * span],
+        rows_one[2 * span :],
+        g_w_up,
+        rows_two[None, 3 * span :],
+        g_w_down.T,
+        rows_two[:span],
+        rows_two[span : 2 * span],
+        rows_two[2 * span : 3 * span],
+        g_w_time,
+        g_b_time,
+    )
+
+
 def solution(mesh):
     placed = (
         P(("dp", "mp"), None),
@@ -296,6 +628,10 @@
         P(),
         P(("dp", "mp"), None),
     )
+    def body(*args):
+        whole_rows = args[0].shape[0] == LEN and mesh.shape["dp"] == GRID_DP and mesh.shape["mp"] == GRID_MP
+        return (body_rows if whole_rows else body_split)(*args)
+
     return jax.shard_map(
         body,
         mesh=mesh,

time: 1560 us -> 804 us (0.52)
  waiting for transfers between devices: 921 us -> 178 us
  starting transfers between devices: 1.05 us -> 70.9 us
  blocking collectives: 40.5 us -> 0 us
  local copies, waits for them, and re-layouts: 107 us -> 68.8 us
  matrix products: 351 us -> 374 us
  other arithmetic: 113 us -> 96.7 us
    reduce_scatter x7 -> x0, waiting for transfers between devices: 441 us -> none  [the longest x1 92.6 us: body(): lax.psum_scatter(grad_w_time, ('dp', 'mp'), scatter_dimension=0, tiled=True)]
    unnamed x19 -> x0, waiting for transfers between devices: 246 us -> none
    all_gather x4 -> x0, waiting for transfers between devices: 233 us -> none  [the longest x1 58.4 us: body(): cot_full = lax.all_gather(branch_two, 'mp', axis=0, tiled=True)]
    ppermute x0 -> x86, waiting for transfers between devices: none -> 178 us  [the longest x36 120 us: flip_dp(): return lax.ppermute(values, 'dp', [(i, i ^ bit) for i in range(GRID_DP)])]
    ppermute x0 -> x86, starting transfers between devices: none -> 70.9 us  [the longest x36 47.5 us: flip_dp(): return lax.ppermute(values, 'dp', [(i, i ^ bit) for i in range(GRID_DP)])]
    dot_general x16 -> x74, matrix products: 202 us -> 254 us  [the longest x72 252 us: dot_f32(): lax.dot_general(left, right, (dims, ((), ())), preferred_element_type=F32)]
    unnamed x1 -> x0, blocking collectives: 40.5 us -> none
    dot_general x8 -> x6, matrix products: 55.6 us -> 22.8 us  [masked_scores(): jnp.einsum('qhd,khd->hqk', queries, keys_part, preferred_element_type=jnp...]
  transfers between devices with their start and end apart: 15 -> 86, of which waited for: 15 -> 34; matrix products, arithmetic and copies ran while one was open for 7% -> 33% of each run, Pallas kernels for 0% -> 0%
where the time goes in v1:
time: 804 us; the launch traced here: 792 us
  matrix products  374 us (47%)
  waiting for transfers between devices  178 us (22%)
  other arithmetic  96.7 us (12%)
  starting transfers between devices  70.9 us (9%)
  local copies, waits for them, and re-layouts  68.8 us (9%)
    dot_general x72, matrix products, dot_f32(): lax.dot_general(left, right, (dims, ((), ())), preferred_element_type=F32)  252 us
    ppermute x36, waiting for transfers between devices, flip_dp(): return lax.ppermute(values, 'dp', [(i, i ^ bit) for i in range(GRID_DP)])  120 us
    ppermute x50, waiting for transfers between devices, flip_mp(): return lax.ppermute(values, 'mp', [(i, i ^ bit) for i in range(GRID_MP)])  57.6 us
    ppermute x36, starting transfers between devices, flip_dp(): return lax.ppermute(values, 'dp', [(i, i ^ bit) for i in range(GRID_DP)])  47.5 us
    unnamed x376, local copies, waits for them, and re-layouts  42.7 us
    dot_general x6, matrix products, attend_backward(): jnp.einsum('qhd,khd->hqk', grad_heads, values_part, preferred_element_typ...  33.9 us
    convert_element_type x6, other arithmetic, attend_backward(): d_scores = (probability * (d_probs - row_terms)).astype(jnp.bfloat16)  26.3 us
    dot_general x6, matrix products, attend_forward(): jnp.einsum('hqk,khd->qhd', probability.astype(jnp.bfloat16), values_part,...  24.1 us
  transfers between devices with their start and end apart: 86, of which 34 were waited for; matrix products, arithmetic and copies ran while one was open for 33% of the time, Pallas kernels for 0%

profile of v1, /device:TPU:0, one launch (start us, length us, event | category | flops | bytes accessed | tf_op | source)
XLA Modules:
  0.0 792.3 jit_solution(713379392120556897)
XLA Ops:
  37.2 7.4 fusion.214
  44.7 8.0 %fusion = f32[4,1024]{1,0:T(4,128)S(1)} fusion(f32[4,1024,1024]{1,2,0:T(8,128)} %get-tuple-element.178, f32[4,1024]{1,0:T(4,128)S(1)} %get-tuple-element.177), kind=kLoop, calls=%fused_computation.12 | loop fusion | flops 8384512 | bytes 16809984 | tf_op jit(solution)/shard_map/reduce_sum | solution.py:65
  52.7 7.6 fusion.90
  82.1 10.0 %collective-permute-done.6 = bf16[1024,3,128]{0,2,1:T(8,128)(2,1)S(1)} collective-permute-done((bf16[1024,3,128]{0,2,1:T(8,128)(2,1)}, bf16[1024,3,128]{0,2,1:T(8,128)(2,1)S(1)}, u32[]{:S(2)}, u32[]{:S(2)}) %collective-permute-start.6) | collective-permute-done | bytes 786464 | tf_op jit(solution)/shard_map/ppermute | solution.py:289
  114.3 7.7 fusion.213
  121.9 8.0 %fusion.1 = f32[4,1024]{1,0:T(4,128)S(1)} fusion(f32[4,1024,1024]{1,2,0:T(8,128)} %get-tuple-element.176, f32[4,1024]{1,0:T(4,128)S(1)} %get-tuple-element.175), kind=kLoop, calls=%fused_computation.13 | loop fusion | flops 8384512 | bytes 16809984 | tf_op jit(solution)/shard_map/reduce_sum | solution.py:65
  130.0 8.9 %fusion.89 = bf16[4,64,1024]{2,1,0:T(8,128)(2,1)S(1)} fusion(f32[4,1024,1024]{1,2,0:T(8,128)} %get-tuple-element.176, f32[4,1024]{1,0:T(4,128)S(1)} %fusion.1, f32[4,1024]{1,0:T(4,128)S(1)} %get-tuple-element.175, bf16[1024,3,4,64]{0,3,2,1:T(8,128)(2,1)} %bitcast.586), kind=kOutput, calls=%fused_computation.216 | convolution fusion | flops 549715968 | bytes 17858560 | tf_op jit(solution)/shard_map/hqk,khd->qhd/dot_general | solution.py:67
  161.6 12.7 %collective-permute-done.18 = bf16[512,1024]{1,0:T(8,128)(2,1)} collective-permute-done((bf16[512,1024]{1,0:T(8,128)(2,1)S(1)}, bf16[512,1024]{1,0:T(8,128)(2,1)}, u32[]{:S(2)}, u32[]{:S(2)}) %collective-permute-start.18) | collective-permute-done | bytes 1048608 | tf_op jit(solution)/shard_map/ppermute | solution.py:285
  174.6 4.8 fusion.216
  180.8 6.5 multiply_convert_fusion.9
  187.3 4.7 multiply_convert_fusion.17
  194.9 4.5 fusion.224
  199.4 9.6 %collective-permute-done.20 = bf16[512,1024]{1,0:T(8,128)(2,1)S(1)} collective-permute-done((bf16[512,1024]{1,0:T(8,128)(2,1)}, bf16[512,1024]{1,0:T(8,128)(2,1)S(1)}, u32[]{:S(2)}, u32[]{:S(2)}) %collective-permute-start.20) | collective-permute-done | bytes 1048608 | tf_op jit(solution)/shard_map/ppermute | solution.py:289
  215.6 4.9 fusion.226
  220.5 6.0 multiply_convert_fusion.8
  230.5 6.0 fusion.225
  237.8 9.0 %fusion.217 = (f32[1024]{0:T(1024)}, f32[1024,1024]{0,1:T(8,128)S(1)}) fusion(bf16[512,1024]{1,0:T(8,128)(2,1)S(1)} %collective-permute-done.25, f32[1024,512]{1,0:T(8,128)S(1)} %fusion.229, f32[512]{0:T(512)} %bitcast.652, f32[1024,1024]{0,1:T(8,128)} %fusion.228, f32[1024,1024]{0,1:T(8,128)} %fusion.227, f32[1024,1024]{0,1:T(8,128)} %fusion.226, ...), kind=kOutput, calls=%fused_computation.512 | convolution fusion | flops 1089469440 | bytes 32532480 | tf_op jit(solution)/shard_map/dot_general | solution.py:407
  256.5 6.8 convert_reduce_fusion.2
  264.6 6.1 fusion.230
  274.2 5.8 convert_reduce_fusion.1
  280.1 6.8 fusion.231
  286.9 4.0 convert_reduce_fusion.10
  290.9 4.9 fusion.232
  307.9 14.4 %multiply_reduce_fusion.6 = (f32[1024]{0:T(1024)}, f32[1024]{0:T(1024)S(1)}, f32[1024]{0:T(1024)S(1)}, f32[1024]{0:T(1024)}, f32[1024,1024]{0,1:T(8,128)}) fusion(f32[1024,1024]{0,1:T(8,128)} %copy-done.2, f32[1024]{0:T(1024)S(1)} %add_rsqrt_fusion.1, f32[1024]{0:T(1024)S(1)} %broadcast_multiply_fusion.5, f32[1024]{0:T(1024)S(1)} %copy-done.96, ...), kind=kOutput, calls=%fused_computation.86 | convolution fusion | flops 1097854976 | bytes 37797888 | tf_op jit(solution)/shard_map/dot_general | solution.py:407
  322.3 5.6 convert_reduce_fusion.4
  329.8 9.3 %multiply_reduce_fusion.1 = (f32[4,1024]{1,0:T(4,128)}, f32[4,1024,1024]{1,2,0:T(8,128)}) fusion(f32[4,1024,1024]{1,2,0:T(8,128)S(1)} %bitcast.540, f32[4,1024]{1,0:T(4,128)S(1)} %copy-done.87, bf16[1024,4,64]{0,2,1:T(8,128)(2,1)S(1)} %bitcast.571, bf16[1024,3,4,64]{0,3,2,1:T(8,128)(2,1)} %bitcast.582), kind=kOutput, calls=%fused_computation.4 | convolution fusion | flops 549449728 | bytes 34635776 | tf_op jit(solution)/shard_map/qhd,khd->hqk/dot_general | solution.py:89
  339.0 7.9 multiply_convert_fusion.1
  350.3 4.5 fusion.87
  360.3 14.1 %multiply_reduce_fusion = (f32[4,1024]{1,0:T(4,128)}, f32[4,1024,1024]{1,2,0:T(8,128)}) fusion(f32[4,1024,1024]{1,2,0:T(8,128)} %get-tuple-element.176, f32[4,1024]{1,0:T(4,128)} %log_add_fusion, bf16[1024,4,64]{0,2,1:T(8,128)(2,1)S(1)} %bitcast.569, bf16[1024,3,4,64]{0,3,2,1:T(8,128)(2,1)} %bitcast.587), kind=kOutput, calls=%fused_computation.1 | convolution fusion | flops 549449728 | bytes 34635776 | tf_op jit(solution)/shard_map/qhd,khd->hqk/dot_general | solution.py:89
  376.9 7.9 multiply_convert_fusion
  388.2 4.5 fusion.85
  397.7 5.0 multiply_reduce_fusion.5
  468.4 5.3 fusion.236
  481.2 4.6 fusion.237
  493.1 9.7 %fusion.218 = (f32[1024]{0:T(1024)S(1)}, f32[1024,1024]{0,1:T(8,128)}) fusion(bf16[1024,384]{0,1:T(8,128)(2,1)S(1)} %bitcast.560, bf16[1024,384]{0,1:T(8,128)(2,1)} %bitcast.637, f32[1024,1024]{0,1:T(8,128)S(1)} %fusion.239, f32[1024,1024]{0,1:T(8,128)} %fusion.238, f32[1024,1024]{0,1:T(8,128)} %fusion.237, f32[1024,1024]{0,1:T(8,128)} %fusion.236, ...), kind=kOutput, calls=%fused_computation.513 | convolution fusion | flops 819985408 | bytes 35151872 | tf_op jit(solution)/shard_map/dot_general | solution.py:407
  507.2 5.3 copy.224
  591.4 5.2 collective-permute-done.46
  620.7 4.8 add_convert_fusion.8
  634.1 6.1 collective-permute-done.30
  641.6 6.5 collective-permute-done.32
  653.6 9.1 %collective-permute-done.60 = bf16[4,128,512]{2,1,0:T(8,128)(2,1)} collective-permute-done((bf16[4,128,512]{2,1,0:T(8,128)(2,1)S(1)}, bf16[4,128,512]{2,1,0:T(8,128)(2,1)}, u32[]{:S(2)}, u32[]{:S(2)}) %collective-permute-start.60) | collective-permute-done | bytes 524320 | tf_op jit(solution)/shard_map/ppermute | solution.py:289
  667.2 21.9 %collective-permute-done.76 = bf16[1024,512]{1,0:T(8,128)(2,1)} collective-permute-done((bf16[1024,512]{1,0:T(8,128)(2,1)}, bf16[1024,512]{1,0:T(8,128)(2,1)}, u32[]{:S(2)}, u32[]{:S(2)}) %collective-permute-start.76) | collective-permute-done | bytes 1048608 | tf_op jit(solution)/shard_map/ppermute | solution.py:285
  690.5 6.7 add_convert_fusion
  699.9 5.2 add_convert_fusion.2
  717.7 15.0 %collective-permute-done.77 = bf16[4,128,1024]{1,2,0:T(8,128)(2,1)} collective-permute-done((bf16[4,128,1024]{1,2,0:T(8,128)(2,1)}, bf16[4,128,1024]{1,2,0:T(8,128)(2,1)}, u32[]{:S(2)}, u32[]{:S(2)}) %collective-permute-start.77) | collective-permute-done | bytes 1048608 | tf_op jit(solution)/shard_map/ppermute | solution.py:289
  739.0 11.1 %collective-permute-done.57 = bf16[4,128,1024]{2,1,0:T(8,128)(2,1)} collective-permute-done((bf16[4,128,1024]{2,1,0:T(8,128)(2,1)}, bf16[4,128,1024]{2,1,0:T(8,128)(2,1)}, u32[]{:S(2)}, u32[]{:S(2)}) %collective-permute-start.57) | collective-permute-done | bytes 1048608 | tf_op jit(solution)/shard_map/ppermute | solution.py:289
  762.5 16.1 %collective-permute-done.79 = bf16[128,1024]{0,1:T(8,128)(2,1)} collective-permute-done((bf16[128,1024]{0,1:T(8,128)(2,1)}, bf16[128,1024]{0,1:T(8,128)(2,1)}, u32[]{:S(2)}, u32[]{:S(2)}) %collective-permute-start.79) | collective-permute-done | bytes 262176 | tf_op jit(solution)/shard_map/ppermute | solution.py:289
  780.6 9.2 %collective-permute-done.65 = bf16[128,1024]{1,0:T(8,128)(2,1)} collective-permute-done((bf16[128,1024]{1,0:T(8,128)(2,1)}, bf16[128,1024]{1,0:T(8,128)(2,1)}, u32[]{:S(2)}, u32[]{:S(2)}) %collective-permute-start.65) | collective-permute-done | bytes 262176 | tf_op jit(solution)/shard_map/ppermute | solution.py:289
  (811 shorter events, 412.6 us)
Async XLA Ops:
  0.7 62.3 %collective-permute-start.4 = (bf16[2,256]{1,0:T(2,128)(2,1)}, bf16[2,256]{1,0:T(2,128)(2,1)S(1)}, u32[]{:S(2)}, u32[]{:S(2)}) collective-permute-start(bf16[2,256]{1,0:T(2,128)(2,1)} %param.22), channel_id=1, source_target_pairs={{0,2},{1,3},{2,0},{3,1},{4,6},{5,7},{6,4},{7,5},{8,10},{9,11},{10,... | collective-permute-start | bytes 3080 | tf_op jit(solution)/shard_map/ppermute | solution.py:285
  3.8 27.4 %collective-permute-start.1 = (bf16[2,256]{1,0:T(2,128)(2,1)}, bf16[2,256]{1,0:T(2,128)(2,1)S(1)}, u32[]{:S(2)}, u32[]{:S(2)}) collective-permute-start(bf16[2,256]{1,0:T(2,128)(2,1)} %param.22), channel_id=1, source_target_pairs={{0,1},{1,0},{2,3},{3,2},{4,5},{5,4},{6,7},{7,6},{8,9},{9,8},{10,11... | collective-permute-start | bytes 3080 | tf_op jit(solution)/shard_map/ppermute | solution.py:285
  6.4 104.3 %collective-permute-start = (bf16[1024,3,256]{0,2,1:T(8,128)(2,1)}, bf16[1024,3,256]{0,2,1:T(8,128)(2,1)}, u32[]{:S(2)}, u32[]{:S(2)}) collective-permute-start(bf16[1024,3,256]{0,2,1:T(8,128)(2,1)} %copy.158), channel_id=1, source_target_pairs={{0,1},{1,0},{2,3},{3,2},{4,5},{5,4},{6,7},{7,6},{8,9},{9,8},{10,11... | collective-permute-start | bytes 4718600 | tf_op jit(solution)/shard_map/ppermute | solution.py:285
  9.0 58.0 %collective-permute-start.3 = (bf16[1024,3,128]{0,2,1:T(8,128)(2,1)}, bf16[1024,3,128]{0,2,1:T(8,128)(2,1)}, u32[]{:S(2)}, u32[]{:S(2)}) collective-permute-start(bf16[1024,3,128]{0,2,1:T(8,128)(2,1)} %constant_dynamic-slice_fusion.63), channel_id=1, source_target_pairs={{0,2},{1,3},{2,0},{3,1},{4,6},{5,7},{6,4},{7,5},{8,10},{9,11},{10,... | collective-permute-start | bytes 2359304 | tf_op jit(solution)/shard_map/ppermute | solution.py:285
  9.1 139.7 %collective-permute-start.2 = (bf16[256,1024]{1,0:T(8,128)(2,1)}, bf16[256,1024]{1,0:T(8,128)(2,1)}, u32[]{:S(2)}, u32[]{:S(2)}) collective-permute-start(bf16[256,1024]{1,0:T(8,128)(2,1)} %param.23), channel_id=1, source_target_pairs={{0,1},{1,0},{2,3},{3,2},{4,5},{5,4},{6,7},{7,6},{8,9},{9,8},{10,11... | collective-permute-start | bytes 1572872 | tf_op jit(solution)/shard_map/ppermute | solution.py:285
  31.2 33.2 %collective-permute-start.17 = (bf16[1,1024]{1,0:T(2,128)(2,1)S(1)}, bf16[1,1024]{1,0:T(2,128)(2,1)S(1)}, u32[]{:S(2)}, u32[]{:S(2)}) collective-permute-start(bf16[1,1024]{1,0:T(2,128)(2,1)S(1)} %broadcast_in_dim.72), channel_id=1, source_target_pairs={{0,2},{1,3},{2,0},{3,1},{4,6},{5,7},{6,4},{7,5},{8,10},{9,11},{10,... | collective-permute-start | bytes 6152 | tf_op jit(solution)/shard_map/ppermute | solution.py:285
  65.3 155.2 %collective-permute-start.13 = (bf16[1024,1024]{1,0:T(8,128)(2,1)}, bf16[1024,1024]{1,0:T(8,128)(2,1)}, u32[]{:S(2)}, u32[]{:S(2)}) collective-permute-start(bf16[1024,1024]{1,0:T(8,128)(2,1)} %param.27), channel_id=1, source_target_pairs={{0,1},{1,0},{2,3},{3,2},{4,5},{5,4},{6,7},{7,6},{8,9},{9,8},{10,11... | collective-permute-start | bytes 6291464 | tf_op jit(solution)/shard_map/ppermute | solution.py:285
  72.4 19.7 %collective-permute-start.6 = (bf16[1024,3,128]{0,2,1:T(8,128)(2,1)}, bf16[1024,3,128]{0,2,1:T(8,128)(2,1)S(1)}, u32[]{:S(2)}, u32[]{:S(2)}) collective-permute-start(bf16[1024,3,128]{0,2,1:T(8,128)(2,1)} %collective-permute-done.3), channel_id=1, source_target_pairs={{0,4},{4,0},{8,12},{12,8},{16,20},{20,16},{24,28},{28,24},{1,5},{5... | collective-permute-start | bytes 2359304 | tf_op jit(solution)/shard_map/ppermute | solution.py:289
  76.7 75.5 %collective-permute-start.16 = (bf16[1024,512]{1,0:T(8,128)(2,1)}, bf16[1024,512]{1,0:T(8,128)(2,1)}, u32[]{:S(2)}, u32[]{:S(2)}) collective-permute-start(bf16[1024,512]{1,0:T(8,128)(2,1)} %constant_dynamic-slice_fusion.57), channel_id=1, source_target_pairs={{0,2},{1,3},{2,0},{3,1},{4,6},{5,7},{6,4},{7,5},{8,10},{9,11},{10,... | collective-permute-start | bytes 3145736 | tf_op jit(solution)/shard_map/ppermute | solution.py:285
  101.1 39.1 %collective-permute-start.7 = (bf16[128,1024]{1,0:T(8,128)(2,1)}, bf16[128,1024]{1,0:T(8,128)(2,1)}, u32[]{:S(2)}, u32[]{:S(2)}) collective-permute-start(bf16[128,1024]{1,0:T(8,128)(2,1)} %collective-permute-done.5), channel_id=1, source_target_pairs={{0,4},{4,0},{8,12},{12,8},{16,20},{20,16},{24,28},{28,24},{1,5},{5... | collective-permute-start | bytes 786440 | tf_op jit(solution)/shard_map/ppermute | solution.py:289
  110.6 34.2 %collective-permute-start.10 = (bf16[128,1024]{1,0:T(8,128)(2,1)}, bf16[128,1024]{1,0:T(8,128)(2,1)}, u32[]{:S(2)}, u32[]{:S(2)}) collective-permute-start(bf16[128,1024]{1,0:T(8,128)(2,1)} %collective-permute-done.5), channel_id=1, source_target_pairs={{0,1},{1,0},{2,3},{3,2},{4,5},{5,4},{6,7},{7,6},{8,9},{9,8},{10,11... | collective-permute-start | bytes 786440 | tf_op jit(solution)/shard_map/ppermute | solution.py:285
  144.9 85.6 %collective-permute-start.15 = (bf16[1024,1024]{1,0:T(8,128)(2,1)}, bf16[1024,1024]{1,0:T(8,128)(2,1)}, u32[]{:S(2)}, u32[]{:S(2)}) collective-permute-start(bf16[1024,1024]{1,0:T(8,128)(2,1)} %param.29), channel_id=1, source_target_pairs={{0,1},{1,0},{2,3},{3,2},{4,5},{5,4},{6,7},{7,6},{8,9},{9,8},{10,11... | collective-permute-start | bytes 6291464 | tf_op jit(solution)/shard_map/ppermute | solution.py:285
  148.8 25.4 %collective-permute-start.18 = (bf16[512,1024]{1,0:T(8,128)(2,1)S(1)}, bf16[512,1024]{1,0:T(8,128)(2,1)}, u32[]{:S(2)}, u32[]{:S(2)}) collective-permute-start(bf16[512,1024]{1,0:T(8,128)(2,1)S(1)} %copy-done.65), channel_id=1, source_target_pairs={{0,2},{1,3},{2,0},{3,1},{4,6},{5,7},{6,4},{7,5},{8,10},{9,11},{10,... | collective-permute-start | bytes 3145736 | tf_op jit(solution)/shard_map/ppermute | solution.py:285
  152.3 60.0 %collective-permute-start.21 = (bf16[1024,512]{1,0:T(8,128)(2,1)}, bf16[1024,512]{1,0:T(8,128)(2,1)S(1)}, u32[]{:S(2)}, u32[]{:S(2)}) collective-permute-start(bf16[1024,512]{1,0:T(8,128)(2,1)} %collective-permute-done.16), channel_id=1, source_target_pairs={{0,1},{1,0},{2,3},{3,2},{4,5},{5,4},{6,7},{7,6},{8,9},{9,8},{10,11... | collective-permute-start | bytes 3145736 | tf_op jit(solution)/shard_map/ppermute | solution.py:285
  161.0 31.0 %collective-permute-start.19 = (bf16[1024,512]{1,0:T(8,128)(2,1)}, bf16[1024,512]{1,0:T(8,128)(2,1)S(1)}, u32[]{:S(2)}, u32[]{:S(2)}) collective-permute-start(bf16[1024,512]{1,0:T(8,128)(2,1)} %collective-permute-done.16), channel_id=1, source_target_pairs={{0,4},{4,0},{8,12},{12,8},{16,20},{20,16},{24,28},{28,24},{1,5},{5... | collective-permute-start | bytes 3145736 | tf_op jit(solution)/shard_map/ppermute | solution.py:289
  174.3 34.7 %collective-permute-start.20 = (bf16[512,1024]{1,0:T(8,128)(2,1)}, bf16[512,1024]{1,0:T(8,128)(2,1)S(1)}, u32[]{:S(2)}, u32[]{:S(2)}) collective-permute-start(bf16[512,1024]{1,0:T(8,128)(2,1)} %collective-permute-done.18), channel_id=1, source_target_pairs={{0,4},{4,0},{8,12},{12,8},{16,20},{20,16},{24,28},{28,24},{1,5},{5... | collective-permute-start | bytes 3145736 | tf_op jit(solution)/shard_map/ppermute | solution.py:289
  192.1 34.4 %collective-permute-start.23 = (bf16[512,1024]{1,0:T(8,128)(2,1)}, bf16[512,1024]{1,0:T(8,128)(2,1)S(1)}, u32[]{:S(2)}, u32[]{:S(2)}) collective-permute-start(bf16[512,1024]{1,0:T(8,128)(2,1)} %collective-permute-done.18), channel_id=1, source_target_pairs={{0,1},{1,0},{2,3},{3,2},{4,5},{5,4},{6,7},{7,6},{8,9},{9,8},{10,11... | collective-permute-start | bytes 3145736 | tf_op jit(solution)/shard_map/ppermute | solution.py:285
  208.9 27.6 %collective-permute-start.24 = (bf16[1024,512]{1,0:T(8,128)(2,1)S(1)}, bf16[1024,512]{1,0:T(8,128)(2,1)S(1)}, u32[]{:S(2)}, u32[]{:S(2)}) collective-permute-start(bf16[1024,512]{1,0:T(8,128)(2,1)S(1)} %collective-permute-done.19), channel_id=1, source_target_pairs={{0,1},{1,0},{2,3},{3,2},{4,5},{5,4},{6,7},{7,6},{8,9},{9,8},{10,11... | collective-permute-start | bytes 3145736 | tf_op jit(solution)/shard_map/ppermute | solution.py:285
  212.3 25.5 %collective-permute-start.25 = (bf16[512,1024]{1,0:T(8,128)(2,1)S(1)}, bf16[512,1024]{1,0:T(8,128)(2,1)S(1)}, u32[]{:S(2)}, u32[]{:S(2)}) collective-permute-start(bf16[512,1024]{1,0:T(8,128)(2,1)S(1)} %collective-permute-done.20), channel_id=1, source_target_pairs={{0,1},{1,0},{2,3},{3,2},{4,5},{5,4},{6,7},{7,6},{8,9},{9,8},{10,11... | collective-permute-start | bytes 3145736 | tf_op jit(solution)/shard_map/ppermute | solution.py:285
  502.9 117.2 %collective-permute-start.73 = (bf16[1024,512]{1,0:T(8,128)(2,1)}, bf16[1024,512]{1,0:T(8,128)(2,1)}, u32[]{:S(2)}, u32[]{:S(2)}) collective-permute-start(bf16[1024,512]{1,0:T(8,128)(2,1)} %convolution_convert_fusion.4), channel_id=1, source_target_pairs={{0,1},{1,0},{2,3},{3,2},{4,5},{5,4},{6,7},{7,6},{8,9},{9,8},{10,11... | collective-permute-start | bytes 3145736 | tf_op jit(solution)/shard_map/ppermute | solution.py:285
  504.2 40.1 %collective-permute-start.67 = (f32[16,224]{1,0:T(8,128)S(1)}, f32[16,224]{1,0:T(8,128)S(1)}, u32[]{:S(2)}, u32[]{:S(2)}) collective-permute-start(f32[16,224]{1,0:T(8,128)S(1)} %constant_dynamic-slice_fusion.10), channel_id=1, source_target_pairs={{0,1},{1,0},{2,3},{3,2},{4,5},{5,4},{6,7},{7,6},{8,9},{9,8},{10,11... | collective-permute-start | bytes 43016 | tf_op jit(solution)/shard_map/ppermute | solution.py:285
  516.5 63.9 %collective-permute-start.43 = (bf16[1024,128]{1,0:T(8,128)(2,1)}, bf16[1024,128]{1,0:T(8,128)(2,1)}, u32[]{:S(2)}, u32[]{:S(2)}) collective-permute-start(bf16[1024,128]{1,0:T(8,128)(2,1)} %convolution_convert_fusion.17), channel_id=1, source_target_pairs={{0,1},{1,0},{2,3},{3,2},{4,5},{5,4},{6,7},{7,6},{8,9},{9,8},{10,11... | collective-permute-start | bytes 786440 | tf_op jit(solution)/shard_map/ppermute | solution.py:285
  520.6 62.1 %collective-permute-start.45 = (bf16[1024,128]{1,0:T(8,128)(2,1)}, bf16[1024,128]{1,0:T(8,128)(2,1)}, u32[]{:S(2)}, u32[]{:S(2)}) collective-permute-start(bf16[1024,128]{1,0:T(8,128)(2,1)} %convolution_convert_fusion.16), channel_id=1, source_target_pairs={{0,1},{1,0},{2,3},{3,2},{4,5},{5,4},{6,7},{7,6},{8,9},{9,8},{10,11... | collective-permute-start | bytes 786440 | tf_op jit(solution)/shard_map/ppermute | solution.py:285
  544.2 43.6 %collective-permute-start.42 = (bf16[1024,256]{1,0:T(8,128)(2,1)}, bf16[1024,256]{1,0:T(8,128)(2,1)S(1)}, u32[]{:S(2)}, u32[]{:S(2)}) collective-permute-start(bf16[1024,256]{1,0:T(8,128)(2,1)} %convolution_convert_fusion.11), channel_id=1, source_target_pairs={{0,1},{1,0},{2,3},{3,2},{4,5},{5,4},{6,7},{7,6},{8,9},{9,8},{10,11... | collective-permute-start | bytes 1572872 | tf_op jit(solution)/shard_map/ppermute | solution.py:285
  580.0 19.0 %collective-permute-start.29 = (bf16[1024,384]{1,0:T(8,128)(2,1)}, bf16[1024,384]{1,0:T(8,128)(2,1)}, u32[]{:S(2)}, u32[]{:S(2)}) collective-permute-start(bf16[1024,384]{1,0:T(8,128)(2,1)} %convolution_convert_fusion.7), channel_id=1, source_target_pairs={{0,1},{1,0},{2,3},{3,2},{4,5},{5,4},{6,7},{7,6},{8,9},{9,8},{10,11... | collective-permute-start | bytes 2359304 | tf_op jit(solution)/shard_map/ppermute | solution.py:285
  587.7 37.7 %collective-permute-start.59 = (bf16[1024,512]{1,0:T(8,128)(2,1)}, bf16[1024,512]{1,0:T(8,128)(2,1)}, u32[]{:S(2)}, u32[]{:S(2)}) collective-permute-start(bf16[1024,512]{1,0:T(8,128)(2,1)} %convolution_convert_fusion.5), channel_id=1, source_target_pairs={{0,1},{1,0},{2,3},{3,2},{4,5},{5,4},{6,7},{7,6},{8,9},{9,8},{10,11... | collective-permute-start | bytes 3145736 | tf_op jit(solution)/shard_map/ppermute | solution.py:285
  617.4 72.1 %collective-permute-start.72 = (bf16[1024,1024]{1,0:T(8,128)(2,1)}, bf16[1024,1024]{1,0:T(8,128)(2,1)}, u32[]{:S(2)}, u32[]{:S(2)}) collective-permute-start(bf16[1024,1024]{1,0:T(8,128)(2,1)} %convolution_convert_fusion), channel_id=1, source_target_pairs={{0,1},{1,0},{2,3},{3,2},{4,5},{5,4},{6,7},{7,6},{8,9},{9,8},{10,11... | collective-permute-start | bytes 6291464 | tf_op jit(solution)/shard_map/ppermute | solution.py:285
  620.1 78.6 %collective-permute-start.56 = (bf16[1024,1024]{1,0:T(8,128)(2,1)}, bf16[1024,1024]{1,0:T(8,128)(2,1)}, u32[]{:S(2)}, u32[]{:S(2)}) collective-permute-start(bf16[1024,1024]{1,0:T(8,128)(2,1)} %convolution_convert_fusion.1), channel_id=1, source_target_pairs={{0,1},{1,0},{2,3},{3,2},{4,5},{5,4},{6,7},{7,6},{8,9},{9,8},{10,11... | collective-permute-start | bytes 6291464 | tf_op jit(solution)/shard_map/ppermute | solution.py:285
  625.5 24.0 %collective-permute-start.26 = (bf16[1024,768]{1,0:T(8,128)(2,1)S(1)}, bf16[1024,768]{1,0:T(8,128)(2,1)S(1)}, u32[]{:S(2)}, u32[]{:S(2)}) collective-permute-start(bf16[1024,768]{1,0:T(8,128)(2,1)S(1)} %copy-done.144), channel_id=1, source_target_pairs={{0,1},{1,0},{2,3},{3,2},{4,5},{5,4},{6,7},{7,6},{8,9},{9,8},{10,11... | collective-permute-start | bytes 4718600 | tf_op jit(solution)/shard_map/ppermute | solution.py:285
  640.2 26.3 %collective-permute-start.74 = (bf16[1024,512]{1,0:T(8,128)(2,1)}, bf16[1024,512]{1,0:T(8,128)(2,1)}, u32[]{:S(2)}, u32[]{:S(2)}) collective-permute-start(bf16[1024,512]{1,0:T(8,128)(2,1)} %add_convert_fusion.8), channel_id=1, source_target_pairs={{0,2},{1,3},{2,0},{3,1},{4,6},{5,7},{6,4},{7,5},{8,10},{9,11},{10,... | collective-permute-start | bytes 3145736 | tf_op jit(solution)/shard_map/ppermute | solution.py:285
  648.1 41.0 %collective-permute-start.76 = (bf16[1024,512]{1,0:T(8,128)(2,1)}, bf16[1024,512]{1,0:T(8,128)(2,1)}, u32[]{:S(2)}, u32[]{:S(2)}) collective-permute-start(bf16[1024,512]{1,0:T(8,128)(2,1)} %add_convert_fusion.7), channel_id=1, source_target_pairs={{0,2},{1,3},{2,0},{3,1},{4,6},{5,7},{6,4},{7,5},{8,10},{9,11},{10,... | collective-permute-start | bytes 3145736 | tf_op jit(solution)/shard_map/ppermute | solution.py:285
  662.7 44.8 %collective-permute-start.62 = (bf16[4,128,512]{2,1,0:T(8,128)(2,1)}, bf16[4,128,512]{2,1,0:T(8,128)(2,1)S(1)}, u32[]{:S(2)}, u32[]{:S(2)}) collective-permute-start(bf16[4,128,512]{2,1,0:T(8,128)(2,1)} %dynamic-slice_bitcast_fusion.1), channel_id=1, source_target_pairs={{0,4},{4,0},{8,12},{12,8},{16,20},{20,16},{24,28},{28,24},{1,5},{5... | collective-permute-start | bytes 1572872 | tf_op jit(solution)/shard_map/ppermute | solution.py:289
  666.6 43.9 %collective-permute-start.31 = (bf16[4,128,384]{1,2,0:T(8,128)(2,1)}, bf16[4,128,384]{1,2,0:T(8,128)(2,1)}, u32[]{:S(2)}, u32[]{:S(2)}) collective-permute-start(bf16[4,128,384]{1,2,0:T(8,128)(2,1)} %fusion.118), channel_id=1, source_target_pairs={{0,2},{1,3},{2,0},{3,1},{4,6},{5,7},{6,4},{7,5},{8,10},{9,11},{10,... | collective-permute-start | bytes 1179656 | tf_op jit(solution)/shard_map/ppermute | solution.py:285
  689.0 23.0 %collective-permute-start.33 = (bf16[4,128,384]{1,2,0:T(8,128)(2,1)}, bf16[4,128,384]{1,2,0:T(8,128)(2,1)}, u32[]{:S(2)}, u32[]{:S(2)}) collective-permute-start(bf16[4,128,384]{1,2,0:T(8,128)(2,1)} %fusion.117), channel_id=1, source_target_pairs={{0,2},{1,3},{2,0},{3,1},{4,6},{5,7},{6,4},{7,5},{8,10},{9,11},{10,... | collective-permute-start | bytes 1179656 | tf_op jit(solution)/shard_map/ppermute | solution.py:285
  689.5 26.2 %collective-permute-start.27 = (bf16[4,128,768]{1,2,0:T(8,128)(2,1)}, bf16[4,128,768]{1,2,0:T(8,128)(2,1)}, u32[]{:S(2)}, u32[]{:S(2)}) collective-permute-start(bf16[4,128,768]{1,2,0:T(8,128)(2,1)} %bitcast.629), channel_id=1, source_target_pairs={{0,4},{4,0},{8,12},{12,8},{16,20},{20,16},{24,28},{28,24},{1,5},{5... | collective-permute-start | bytes 2359304 | tf_op jit(solution)/shard_map/ppermute | solution.py:289
  698.8 34.0 %collective-permute-start.77 = (bf16[4,128,1024]{1,2,0:T(8,128)(2,1)}, bf16[4,128,1024]{1,2,0:T(8,128)(2,1)}, u32[]{:S(2)}, u32[]{:S(2)}) collective-permute-start(bf16[4,128,1024]{1,2,0:T(8,128)(2,1)} %bitcast.620), channel_id=1, source_target_pairs={{0,4},{4,0},{8,12},{12,8},{16,20},{20,16},{24,28},{28,24},{1,5},{5... | collective-permute-start | bytes 3145736 | tf_op jit(solution)/shard_map/ppermute | solution.py:289
  707.5 42.6 %collective-permute-start.57 = (bf16[4,128,1024]{2,1,0:T(8,128)(2,1)}, bf16[4,128,1024]{2,1,0:T(8,128)(2,1)}, u32[]{:S(2)}, u32[]{:S(2)}) collective-permute-start(bf16[4,128,1024]{2,1,0:T(8,128)(2,1)} %dynamic-slice_bitcast_fusion), channel_id=1, source_target_pairs={{0,4},{4,0},{8,12},{12,8},{16,20},{20,16},{24,28},{28,24},{1,5},{5... | collective-permute-start | bytes 3145736 | tf_op jit(solution)/shard_map/ppermute | solution.py:289
  710.5 25.5 %collective-permute-start.61 = (bf16[4,128,512]{2,1,0:T(8,128)(2,1)}, bf16[4,128,512]{2,1,0:T(8,128)(2,1)}, u32[]{:S(2)}, u32[]{:S(2)}) collective-permute-start(bf16[4,128,512]{2,1,0:T(8,128)(2,1)} %fusion.116), channel_id=1, source_target_pairs={{0,2},{1,3},{2,0},{3,1},{4,6},{5,7},{6,4},{7,5},{8,10},{9,11},{10,... | collective-permute-start | bytes 1572872 | tf_op jit(solution)/shard_map/ppermute | solution.py:285
  712.0 26.3 %collective-permute-start.63 = (bf16[4,128,512]{2,1,0:T(8,128)(2,1)}, bf16[4,128,512]{2,1,0:T(8,128)(2,1)}, u32[]{:S(2)}, u32[]{:S(2)}) collective-permute-start(bf16[4,128,512]{2,1,0:T(8,128)(2,1)} %fusion.115), channel_id=1, source_target_pairs={{0,2},{1,3},{2,0},{3,1},{4,6},{5,7},{6,4},{7,5},{8,10},{9,11},{10,... | collective-permute-start | bytes 1572872 | tf_op jit(solution)/shard_map/ppermute | solution.py:285
  717.6 36.1 %collective-permute-start.34 = (bf16[128,768]{0,1:T(8,128)(2,1)S(1)}, bf16[128,768]{0,1:T(8,128)(2,1)S(1)}, u32[]{:S(2)}, u32[]{:S(2)}) collective-permute-start(bf16[128,768]{0,1:T(8,128)(2,1)S(1)} %get-tuple-element.103), channel_id=1, source_target_pairs={{0,8},{4,12},{8,0},{12,4},{16,24},{20,28},{24,16},{28,20},{1,9},{5... | collective-permute-start | bytes 589832 | tf_op jit(solution)/shard_map/ppermute | solution.py:289
  732.7 24.3 %collective-permute-start.35 = (bf16[128,768]{0,1:T(8,128)(2,1)S(1)}, bf16[128,768]{0,1:T(8,128)(2,1)S(1)}, u32[]{:S(2)}, u32[]{:S(2)}) collective-permute-start(bf16[128,768]{0,1:T(8,128)(2,1)S(1)} %get-tuple-element.105), channel_id=1, source_target_pairs={{0,16},{4,20},{8,24},{12,28},{16,0},{20,4},{24,8},{28,12},{1,17},{... | collective-permute-start | bytes 589832 | tf_op jit(solution)/shard_map/ppermute | solution.py:289
  736.0 22.5 %collective-permute-start.36 = (bf16[128,768]{0,1:T(8,128)(2,1)S(1)}, bf16[128,768]{0,1:T(8,128)(2,1)S(1)}, u32[]{:S(2)}, u32[]{:S(2)}) collective-permute-start(bf16[128,768]{0,1:T(8,128)(2,1)S(1)} %get-tuple-element.104), channel_id=1, source_target_pairs={{0,24},{4,28},{8,16},{12,20},{16,8},{20,12},{24,0},{28,4},{1,25},{... | collective-permute-start | bytes 589832 | tf_op jit(solution)/shard_map/ppermute | solution.py:289
  738.3 20.8 %collective-permute-start.78 = (bf16[128,1024]{0,1:T(8,128)(2,1)S(1)}, bf16[128,1024]{0,1:T(8,128)(2,1)S(1)}, u32[]{:S(2)}, u32[]{:S(2)}) collective-permute-start(bf16[128,1024]{0,1:T(8,128)(2,1)S(1)} %get-tuple-element.97), channel_id=1, source_target_pairs={{0,8},{4,12},{8,0},{12,4},{16,24},{20,28},{24,16},{28,20},{1,9},{5... | collective-permute-start | bytes 786440 | tf_op jit(solution)/shard_map/ppermute | solution.py:289
  750.1 28.5 %collective-permute-start.79 = (bf16[128,1024]{0,1:T(8,128)(2,1)}, bf16[128,1024]{0,1:T(8,128)(2,1)}, u32[]{:S(2)}, u32[]{:S(2)}) collective-permute-start(bf16[128,1024]{0,1:T(8,128)(2,1)} %get-tuple-element.99), channel_id=1, source_target_pairs={{0,16},{4,20},{8,24},{12,28},{16,0},{20,4},{24,8},{28,12},{1,17},{... | collective-permute-start | bytes 786440 | tf_op jit(solution)/shard_map/ppermute | solution.py:289
  753.7 24.8 %collective-permute-start.80 = (bf16[128,1024]{0,1:T(8,128)(2,1)}, bf16[128,1024]{0,1:T(8,128)(2,1)}, u32[]{:S(2)}, u32[]{:S(2)}) collective-permute-start(bf16[128,1024]{0,1:T(8,128)(2,1)} %get-tuple-element.98), channel_id=1, source_target_pairs={{0,24},{4,28},{8,16},{12,20},{16,8},{20,12},{24,0},{28,4},{1,25},{... | collective-permute-start | bytes 786440 | tf_op jit(solution)/shard_map/ppermute | solution.py:289
  757.1 23.5 %collective-permute-start.64 = (bf16[128,1024]{1,0:T(8,128)(2,1)}, bf16[128,1024]{1,0:T(8,128)(2,1)}, u32[]{:S(2)}, u32[]{:S(2)}) collective-permute-start(bf16[128,1024]{1,0:T(8,128)(2,1)} %get-tuple-element.100), channel_id=1, source_target_pairs={{0,8},{4,12},{8,0},{12,4},{16,24},{20,28},{24,16},{28,20},{1,9},{5... | collective-permute-start | bytes 786440 | tf_op jit(solution)/shard_map/ppermute | solution.py:289
  758.5 31.3 %collective-permute-start.65 = (bf16[128,1024]{1,0:T(8,128)(2,1)}, bf16[128,1024]{1,0:T(8,128)(2,1)}, u32[]{:S(2)}, u32[]{:S(2)}) collective-permute-start(bf16[128,1024]{1,0:T(8,128)(2,1)} %get-tuple-element.102), channel_id=1, source_target_pairs={{0,16},{4,20},{8,24},{12,28},{16,0},{20,4},{24,8},{28,12},{1,17},{... | collective-permute-start | bytes 786440 | tf_op jit(solution)/shard_map/ppermute | solution.py:289
  759.1 30.6 %collective-permute-start.66 = (bf16[128,1024]{1,0:T(8,128)(2,1)}, bf16[128,1024]{1,0:T(8,128)(2,1)}, u32[]{:S(2)}, u32[]{:S(2)}) collective-permute-start(bf16[128,1024]{1,0:T(8,128)(2,1)} %get-tuple-element.101), channel_id=1, source_target_pairs={{0,24},{4,28},{8,16},{12,20},{16,8},{20,12},{24,0},{28,4},{1,25},{... | collective-permute-start | bytes 786440 | tf_op jit(solution)/shard_map/ppermute | solution.py:289
  (220 other events, 2519.1 us)

commit v2 on v0

--- a/solution.py
+++ b/solution.py
@@ -1,8 +1,11 @@
+import functools
 import math
 
 import jax
 import jax.numpy as jnp
 from jax import lax
+from jax.experimental import pallas as pl
+from jax.experimental.pallas import tpu as pltpu
 from jax.sharding import PartitionSpec as P
 
 D = 1024
@@ -104,7 +107,7 @@
     return stacked.reshape(qkv_seq.shape[0], -1).astype(jnp.bfloat16)
 
 
-def body(
+def body_split(
     tokens,
     segment_ids,
     time_steps,
@@ -275,6 +278,952 @@
     )
 
 
+GRID_DP = 8
+GRID_MP = 4
+HALF = 2
+UNIT = 128
+F32 = jnp.float32
+BF16 = jnp.bfloat16
+TILE_F = 512
+TILE_B = 256
+ROWS = 256
+GRAIN = 256
+STEP = 128
+FAR = -(2.0**100)
+NN = (((1,), (0,)), ((), ()))
+NT = (((1,), (1,)), ((), ()))
+
+
+def dot(left, right, dims=NN):
+    return lax.dot_general(left, right, dims, preferred_element_type=F32)
+
+
+def flip_mp(values, bit):
+    return lax.ppermute(values, "mp", [(i, i ^ bit) for i in range(GRID_MP)])
+
+
+def flip_dp(values, bit):
+    return lax.ppermute(values, "dp", [(i, i ^ bit) for i in range(GRID_DP)])
+
+
+def after(values, others):
+    return lax.optimization_barrier((values, others))[0]
+
+
+def half_of(values, which, axis):
+    size = values.shape[axis] // 2
+    return lax.dynamic_slice_in_dim(values, which * size, size, axis)
+
+
+def whole(shape):
+    return pl.BlockSpec(shape, lambda *_: (0,) * len(shape))
+
+
+def struct(shape, kind=BF16):
+    return jax.ShapeDtypeStruct(shape, kind)
+
+
+def cost(flops, moved):
+    return pl.CostEstimate(flops=int(flops), bytes_accessed=int(moved), transcendentals=0)
+
+
+def fetch(own, axis, x_at, wait_for):
+    half = half_of(own, x_at, axis)
+    if wait_for is not None:
+        half = after(half, wait_for)
+    far_a = flip_mp(half, 2)
+    far_b = flip_dp(far_a, 1)
+    near = flip_mp(own, 1)
+    return [own, near, far_a, flip_mp(far_a, 1), far_b, flip_mp(far_b, 1)]
+
+
+def fetch_rows(own, x_at):
+    near, far = flip_mp(own, 1), flip_mp(own, 2)
+    near_far = flip_mp(far, 1)
+    cut = lambda v, at: half_of(v, at, 1)
+    order = ((own, near), (far, near_far))
+    first = [cut(v, at) for v in order[0] for at in (x_at, 1 - x_at)]
+    return first + [cut(v, at) for at in (x_at, 1 - x_at) for v in order[1]]
+
+
+def piece_specs(shape, column, skip):
+    def spec(which):
+        def index(*args):
+            at = 0 if which is None else args[skip][which]
+            return (0, at) if column else (at, 0)
+
+        return pl.BlockSpec(shape, index)
+
+    return [spec(w) for w in (0, 1, 0, 1, None, None, None, None)]
+
+
+def eight(pieces):
+    own, near, far_a, near_a, far_b, near_b = pieces
+    return [own, own, near, near, far_a, near_a, far_b, near_b]
+
+
+def mark_segments(segment_row):
+    lane = jnp.arange(UNIT, dtype=jnp.int32)[None, :]
+    hot = segment_row[:, None] == (lane % HEAD_DIM)
+    used = (lane % HEAD_DIM) < 8
+    return (
+        jnp.where(hot & used, 1.0, 0.0).astype(BF16),
+        jnp.where(used & ~hot, FAR, 0.0).astype(BF16),
+    )
+
+
+def windows(segment_row, tile):
+    first, last = segment_row[::tile], segment_row[tile - 1 :: tile]
+    low = jnp.sum(segment_row[None, :] < first[:, None], axis=1) // STEP * STEP
+    high = jnp.sum(segment_row[None, :] <= last[:, None], axis=1)
+    count = jnp.maximum((high - low + GRAIN - 1) // GRAIN, tile // GRAIN)
+    low = jnp.minimum(low, LEN - count * GRAIN)
+    return jnp.stack([low, count]).astype(jnp.int32)
+
+
+def variants(count, tile, run):
+    for n in range(tile // GRAIN, LEN // GRAIN + 1):
+
+        @pl.when(count == n)
+        def _(n=n):
+            run(n * GRAIN)
+
+
+def lanes_at(at, base=0):
+    return pl.ds(pl.multiple_of(base + at * UNIT, UNIT), UNIT)
+
+
+def attend_kernel(
+    win_ref, info_ref, x_ref, *refs
+):
+    weights, (bias_ref, hotq_ref, hotk_ref, qkv_ref, ctx_ref, lse_ref, w_ref, kx) = refs[:6], refs[6:]
+    unit, step = pl.program_id(0), pl.program_id(1)
+
+    @pl.when((unit == 0) & (step == 0))
+    def _():
+        for j in range(3):
+            for u in range(HALF):
+                at = (2 * j + u) * UNIT
+                w_ref[:, at : at + UNIT] = weights[3 * u + j][...]
+        for r in range(LEN // ROWS):
+            rows = slice(r * ROWS, (r + 1) * ROWS)
+            qkv_ref[rows, :] = (dot(x_ref[rows, :], w_ref[...]) + bias_ref[...]).astype(BF16)
+
+    @pl.when(step == 0)
+    def _():
+        lane = lax.broadcasted_iota(jnp.int32, (LEN, UNIT), 1)
+        keys = qkv_ref[:, lanes_at(unit, 2 * UNIT)]
+        for h in range(HALF):
+            kx[h] = jnp.where((lane // HEAD_DIM) == h, keys, hotk_ref[...])
+
+    lane = lax.broadcasted_iota(jnp.int32, (TILE_F, UNIT), 1)
+    rows = pl.ds(pl.multiple_of(step * TILE_F, TILE_F), TILE_F)
+    queries = qkv_ref[rows, lanes_at(unit)] * jnp.asarray(1.0 / math.sqrt(HEAD_DIM), BF16)
+    start = pl.multiple_of(win_ref[0, step], STEP)
+
+    def run(width):
+        window = pl.ds(start, width)
+        values = qkv_ref[window, lanes_at(unit, 4 * UNIT)]
+        scores = [
+            dot(
+                jnp.where((lane // HEAD_DIM) == h, queries, hotq_ref[...]), kx[h, window, :], NT
+            )
+            for h in range(HALF)
+        ]
+        outs = []
+        for h in range(HALF):
+            top = jnp.max(scores[h], axis=1, keepdims=True)
+            weight = jnp.exp(scores[h] - top)
+            total = jnp.sum(weight, axis=1, keepdims=True)
+            outs.append(dot(weight.astype(BF16), values) * (1.0 / total))
+            lse_ref[0, h : h + 1, :] = (top + jnp.log(total)).T
+        ctx_ref[...] = jnp.where(lane < HEAD_DIM, outs[0], outs[1]).astype(BF16)
+
+    variants(win_ref[1, step], TILE_F, run)
+
+
+def attend_pair(win, info, hidden_low, pair, far, bias, hotq, hotk):
+    def w_spec(j, u):
+        if far:
+            return pl.BlockSpec((D, UNIT), lambda n, i, win, info: (0, j))
+        return pl.BlockSpec((D, UNIT), lambda n, i, win, info: (0, 2 * j + info[u]))
+
+    return pl.pallas_call(
+        attend_kernel,
+        out_shape=(
+            struct((LEN, 6 * UNIT)),
+            struct((LEN, 2 * UNIT)),
+            struct((HALF, 8, LEN), F32),
+            struct((D, 6 * UNIT)),
+        ),
+        grid_spec=pltpu.PrefetchScalarGridSpec(
+            num_scalar_prefetch=2,
+            grid=(HALF, LEN // TILE_F),
+            in_specs=[whole((LEN, D))]
+            + [w_spec(j, u) for u in range(HALF) for j in range(3)]
+            + [
+                whole((1, 6 * UNIT)),
+                pl.BlockSpec((TILE_F, UNIT), lambda n, i, win, info: (i, 0)),
+                whole((LEN, UNIT)),
+            ],
+            out_specs=[
+                whole((LEN, 6 * UNIT)),
+                pl.BlockSpec((TILE_F, UNIT), lambda n, i, win, info: (i, n)),
+                pl.BlockSpec((1, 8, TILE_F), lambda n, i, win, info: (n, 0, i)),
+                whole((D, 6 * UNIT)),
+            ],
+            scratch_shapes=[pltpu.VMEM((HALF, LEN, UNIT), BF16)],
+        ),
+        cost_estimate=cost(6e9, 8e6),
+        name="attend",
+    )(win, info, hidden_low, *[pair[u] for u in range(HALF) for _ in range(3)], bias, hotq, hotk)
+
+
+def attend_back_kernel(
+    win_ref,
+    qkv_ref,
+    hotq_ref,
+    hotk_ref,
+    branch_ref,
+    wout_ref,
+    ctx_ref,
+    lse_ref,
+    out_ref,
+    sum_ref,
+    kx,
+    kt,
+    grads,
+    dk,
+    dv,
+):
+    unit, step = pl.program_id(0), pl.program_id(1)
+    scale = jnp.asarray(1.0 / math.sqrt(HEAD_DIM), BF16)
+
+    @pl.when((unit == 0) & (step == 0))
+    def _():
+        for r in range(LEN // ROWS):
+            rows = slice(r * ROWS, (r + 1) * ROWS)
+            grads[rows, :] = dot(branch_ref[rows, :], wout_ref[...], NT).astype(BF16)
+
+    @pl.when(step == 0)
+    def _():
+        lane = lax.broadcasted_iota(jnp.int32, (LEN, UNIT), 1)
+        keys = qkv_ref[:, lanes_at(unit, 2 * UNIT)]
+        for h in range(HALF):
+            kx[h] = jnp.where((lane // HEAD_DIM) == h, keys, hotk_ref[...])
+        kt[...] = (keys * scale).T
+        dk[...] = jnp.zeros_like(dk)
+        dv[...] = jnp.zeros_like(dv)
+
+    lane = lax.broadcasted_iota(jnp.int32, (TILE_B, UNIT), 1)
+    rows = pl.ds(pl.multiple_of(step * TILE_B, TILE_B), TILE_B)
+    queries = qkv_ref[rows, lanes_at(unit)] * scale
+    grad = grads[rows, lanes_at(unit)]
+    product = (grad.astype(F32) * ctx_ref[...].astype(F32)).T
+    start = pl.multiple_of(win_ref[0, step], STEP)
+
+    def run(width):
+        window = pl.ds(start, width)
+        values = qkv_ref[window, lanes_at(unit, 4 * UNIT)]
+        d_queries, d_keys, d_values = [], [], []
+        for h in range(HALF):
+            mine = (lane // HEAD_DIM) == h
+            q_mine = jnp.where(mine, queries, jnp.zeros_like(queries))
+            g_mine = jnp.where(mine, grad, jnp.zeros_like(grad))
+            scores = dot(kx[h, window, :], jnp.where(mine, queries, hotq_ref[...]), NT)
+            weight = jnp.exp(scores - lse_ref[0, h : h + 1, :])
+            d_weight = dot(values, g_mine, NT)
+            row_term = jnp.sum(
+                product[h * HEAD_DIM : (h + 1) * HEAD_DIM], axis=0, keepdims=True
+            )
+            d_scores = (weight * (d_weight - row_term)).astype(BF16)
+            d_values.append(dot(weight.astype(BF16), g_mine))
+            d_keys.append(dot(d_scores, q_mine))
+            d_queries.append(dot(kt[h * HEAD_DIM : (h + 1) * HEAD_DIM, window], d_scores))
+        dv[window, :] += d_values[0] + d_values[1]
+        dk[window, :] += d_keys[0] + d_keys[1]
+        out_ref[rows, lanes_at(unit)] = jnp.concatenate(d_queries, 0).T.astype(BF16)
+
+    variants(win_ref[1, step], TILE_B, run)
+
+    @pl.when(step == LEN // TILE_B - 1)
+    def _():
+        out_ref[:, lanes_at(unit, 2 * UNIT)] = dk[...].astype(BF16)
+        out_ref[:, lanes_at(unit, 4 * UNIT)] = dv[...].astype(BF16)
+
+    @pl.when((unit == HALF - 1) & (step == LEN // TILE_B - 1))
+    def _():
+        total = jnp.sum(out_ref[...].astype(F32), axis=0, keepdims=True)
+        sum_ref[...] = jnp.broadcast_to(total, sum_ref.shape)
+
+
+def attend_back_pair(win, qkv, hotq, hotk, branch_one, wout_all, pair, ctx, lse):
+    return pl.pallas_call(
+        attend_back_kernel,
+        out_shape=(struct((LEN, 6 * UNIT)), struct((8, 6 * UNIT), F32)),
+        grid_spec=pltpu.PrefetchScalarGridSpec(
+            num_scalar_prefetch=1,
+            grid=(HALF, LEN // TILE_B),
+            in_specs=[
+                whole((LEN, 6 * UNIT)),
+                pl.BlockSpec((TILE_B, UNIT), lambda n, i, win: (i, 0)),
+                whole((LEN, UNIT)),
+                whole((LEN, D)),
+                pl.BlockSpec((2 * UNIT, D), lambda n, i, win: (pair, 0)),
+                pl.BlockSpec((TILE_B, UNIT), lambda n, i, win: (i, n)),
+                pl.BlockSpec((1, 8, TILE_B), lambda n, i, win: (n, 0, i)),
+            ],
+            out_specs=[whole((LEN, 6 * UNIT)), whole((8, 6 * UNIT))],
+            scratch_shapes=[
+                pltpu.VMEM((HALF, LEN, UNIT), BF16),
+                pltpu.VMEM((UNIT, LEN), BF16),
+                pltpu.VMEM((LEN, 2 * UNIT), BF16),
+                pltpu.VMEM((LEN, UNIT), F32),
+                pltpu.VMEM((LEN, UNIT), F32),
+            ],
+        ),
+        cost_estimate=cost(8e9, 8e6),
+        name="attend_back",
+    )(win, qkv, hotq, hotk, branch_one, wout_all, ctx, lse)
+
+
+def norm_of(values):
+    center = values - jnp.mean(values, axis=-1, keepdims=True)
+    spread = jnp.mean(center * center, axis=-1, keepdims=True)
+    scale = lax.rsqrt(spread + EPS)
+    return center * scale, scale
+
+
+def norm_back(normal, scale, grad, gain_row):
+    scaled = grad * gain_row
+    mean_e = jnp.mean(scaled, axis=-1, keepdims=True)
+    mean_en = jnp.mean(scaled * normal, axis=-1, keepdims=True)
+    return scale * (scaled - mean_e - normal * mean_en)
+
+
+def first_norm_kernel(info_ref, tok_ref, *refs):
+    ctx_refs, weights, refs = refs[:4], refs[4:12], refs[12:]
+    embed_ref, bout_ref, gain_ref, shift_ref, normal_ref, scale_ref, mid_ref, mid_t, hid_t, wout_ref = refs
+
+    @pl.when(pl.program_id(0) == 0)
+    def _():
+        for j in range(8):
+            wout_ref[j * UNIT : (j + 1) * UNIT, :] = weights[j][...]
+
+    hidden = tok_ref[...].astype(F32) + embed_ref[...]
+    hid_t[...] = hidden.astype(BF16).T
+    total = bout_ref[...]
+    for p in range(4):
+        total = total + dot(ctx_refs[p][...], wout_ref[2 * p * UNIT : 2 * (p + 1) * UNIT, :])
+    normal, scale = norm_of(hidden + total)
+    normal_ref[...] = normal
+    scale_ref[...] = scale
+    mid = (normal * gain_ref[...] + shift_ref[...]).astype(BF16)
+    mid_ref[...] = mid
+    mid_t[...] = mid.T
+
+
+def first_norm(info, tokens, contexts, w_out, embed_row, b_out, gain, shift):
+    tile = pl.BlockSpec((ROWS, D), lambda i, info: (i, 0))
+    column = pl.BlockSpec((D, ROWS), lambda i, info: (0, i))
+    return pl.pallas_call(
+        first_norm_kernel,
+        out_shape=(
+            struct((LEN, D), F32),
+            struct((LEN, 1), F32),
+            struct((LEN, D)),
+            struct((D, LEN)),
+            struct((D, LEN)),
+            struct((D, D)),
+        ),
+        grid_spec=pltpu.PrefetchScalarGridSpec(
+            num_scalar_prefetch=1,
+            grid=(LEN // ROWS,),
+            in_specs=[tile]
+            + [pl.BlockSpec((ROWS, 2 * UNIT), lambda i, info: (i, 0))] * 4
+            + piece_specs((UNIT, D), False, 1)
+            + [whole((1, D))] * 4,
+            out_specs=[
+                tile,
+                pl.BlockSpec((ROWS, 1), lambda i, info: (i, 0)),
+                tile,
+                column,
+                column,
+                whole((D, D)),
+            ],
+        ),
+        cost_estimate=cost(2.2e9, 20e6),
+        name="first_norm",
+    )(info, tokens, *contexts, *eight(w_out), embed_row, b_out, gain, shift)
+
+
+def second_norm_kernel(
+    ffn_ref, one_ref, cot_ref, gain1, shift1, gain2, shift2, out_ref, grad_ref, low_ref, low_t, sum_ref
+):
+    @pl.when(pl.program_id(0) == 0)
+    def _():
+        sum_ref[...] = jnp.zeros_like(sum_ref)
+
+    mid = one_ref[...] * gain1[...] + shift1[...]
+    normal, scale = norm_of(mid + ffn_ref[...])
+    out_ref[...] = (normal * gain2[...] + shift2[...]).astype(BF16)
+    cot = cot_ref[...].astype(F32)
+    grad = norm_back(normal, scale, cot, gain2[...])
+    grad_ref[...] = grad
+    low = grad.astype(BF16)
+    low_ref[...] = low
+    low_t[...] = low.T
+    sums = [jnp.sum(v, axis=0, keepdims=True) for v in (low.astype(F32), cot * normal, cot)]
+    for j in range(3):
+        sum_ref[j : j + 1, :] += sums[j]
+
+
+def second_norm(ffn, normal_one, cot, *rows):
+    tile = pl.BlockSpec((ROWS, D), lambda i: (i, 0))
+    return pl.pallas_call(
+        second_norm_kernel,
+        out_shape=(
+            struct((LEN, D)),
+            struct((LEN, D), F32),
+            struct((LEN, D)),
+            struct((D, LEN)),
+            struct((8, D), F32),
+        ),
+        grid=(LEN // ROWS,),
+        in_specs=[tile] * 3 + [whole((1, D))] * 4,
+        out_specs=[tile] * 3 + [pl.BlockSpec((D, ROWS), lambda i: (0, i)), whole((8, D))],
+        cost_estimate=cost(1e8, 20e6),
+        name="second_norm",
+    )(ffn, normal_one, cot, *rows)
+
+
+def first_back_kernel(
+    part_ref, grad_ref, one_ref, scale_ref, gain_ref, out_ref, low_ref, low_t, sum_ref
+):
+    @pl.when(pl.program_id(0) == 0)
+    def _():
+        sum_ref[...] = jnp.zeros_like(sum_ref)
+
+    d_mid = part_ref[...] + grad_ref[...]
+    normal = one_ref[...]
+    grad = norm_back(normal, scale_ref[...], d_mid, gain_ref[...])
+    out_ref[...] = grad
+    low = grad.astype(BF16)
+    low_ref[...] = low
+    low_t[...] = low.T
+    sums = [jnp.sum(v, axis=0, keepdims=True) for v in (low.astype(F32), d_mid * normal, d_mid)]
+    for j in range(3):
+        sum_ref[j : j + 1, :] += sums[j]
+
+
+def first_back(part, grad_two, normal_one, scale_one, gain):
+    tile = pl.BlockSpec((ROWS, D), lambda i: (i, 0))
+    return pl.pallas_call(
+        first_back_kernel,
+        out_shape=(struct((LEN, D), F32), struct((LEN, D)), struct((D, LEN)), struct((8, D), F32)),
+        grid=(LEN // ROWS,),
+        in_specs=[tile] * 3 + [pl.BlockSpec((ROWS, 1), lambda i: (i, 0)), whole((1, D))],
+        out_specs=[tile, tile, pl.BlockSpec((D, ROWS), lambda i: (0, i)), whole((8, D))],
+        cost_estimate=cost(1e8, 20e6),
+        name="first_back",
+    )(part, grad_two, normal_one, scale_one, gain)
+
+
+def ffn_kernel(info_ref, mid_ref, *refs):
+    up_refs, down_refs, bias_refs = refs[0:2], refs[2:4], refs[4:6]
+    into_ref, act_ref, slope_ref, total_ref = refs[6:]
+    size = up_refs[0].shape[1]
+    for u in range(HALF):
+        columns = slice(u * size, (u + 1) * size)
+        for r in range(LEN // ROWS):
+            rows = slice(r * ROWS, (r + 1) * ROWS)
+            pre = dot(mid_ref[rows, :], up_refs[u][...]) + bias_refs[u][...]
+            phi = 0.5 * (1.0 + lax.erf(pre * math.sqrt(0.5)))
+            bell = jnp.exp(-0.5 * pre * pre) * (1.0 / math.sqrt(2.0 * math.pi))
+            act = (pre * phi).astype(BF16)
+            act_ref[rows, columns] = act
+            slope_ref[rows, columns] = (phi + pre * bell).astype(BF16)
+            before = into_ref[rows, :] if u == 0 else total_ref[rows, :]
+            total_ref[rows, :] = before + dot(act, down_refs[u][...])
+
+
+def ffn_pair(info, mid_low, up, down, bias, into, far):
+    def spec(shape, u, column):
+        if far:
+            return whole(shape)
+        return pl.BlockSpec(shape, lambda i, info: (0, info[u]) if column else (info[u], 0))
+
+    size = up[0].shape[1] if far else up[0].shape[1] // 2
+    return pl.pallas_call(
+        ffn_kernel,
+        out_shape=(
+            struct((LEN, 2 * size)),
+            struct((LEN, 2 * size)),
+            struct((LEN, D), F32),
+        ),
+        grid_spec=pltpu.PrefetchScalarGridSpec(
+            num_scalar_prefetch=1,
+            grid=(1,),
+            in_specs=[whole((LEN, D))]
+            + [spec((D, size), u, True) for u in range(HALF)]
+            + [spec((size, D), u, False) for u in range(HALF)]
+            + [whole((1, size))] * 2
+            + [whole((LEN, D))],
+            out_specs=[whole((LEN, 2 * size)), whole((LEN, 2 * size)), whole((LEN, D))],
+        ),
+        cost_estimate=cost(4.3e9, 18e6),
+        name="ffn",
+    )(info, mid_low, *up, *down, *bias, into)
+
+
+def ffn_back_kernel(info_ref, branch_hbm, *refs):
+    down_hbm, up_hbm, slope_hbm, refs = refs[0:6], refs[6:12], refs[12:16], refs[16:]
+    pre_refs, total_ref, sum_ref, refs = refs[0:4], refs[4], refs[5], refs[6:]
+    branch, down, up, slope, sems = refs
+    size = up.shape[2]
+    plan = ((0, 0), (0, 1), (1, 0), (1, 1), (2, None), (3, None), (4, None), (5, None))
+    first = pltpu.make_async_copy(branch_hbm, branch, sems.at[0])
+    first.start()
+    copies = []
+    for j, (piece, which) in enumerate(plan):
+        if which is None:
+            down_part, up_part = down_hbm[piece], up_hbm[piece]
+        else:
+            part = pl.ds(pl.multiple_of(info_ref[which] * size, size), size)
+            down_part, up_part = down_hbm[piece].at[part, :], up_hbm[piece].at[:, part]
+        group = [
+            pltpu.make_async_copy(down_part, down.at[j], sems.at[1 + 3 * j]),
+            pltpu.make_async_copy(
+                slope_hbm[j // 2].at[:, (j % 2) * size : (j % 2 + 1) * size],
+                slope.at[j],
+                sems.at[2 + 3 * j],
+            ),
+            pltpu.make_async_copy(up_part, up.at[j], sems.at[3 + 3 * j]),
+        ]
+        for copy in group:
+            copy.start()
+        copies.append(group)
+    first.wait()
+    for j in range(len(plan)):
+        for copy in copies[j]:
+            copy.wait()
+        columns = slice((j % 2) * size, (j % 2 + 1) * size)
+        sums = 0.0
+        for r in range(LEN // ROWS):
+            rows = slice(r * ROWS, (r + 1) * ROWS)
+            d_act = dot(branch[rows, :], down[j], NT)
+            d_pre = (d_act * slope[j, rows, :].astype(F32)).astype(BF16)
+            pre_refs[j // 2][rows, columns] = d_pre
+            sums = sums + jnp.sum(d_pre.astype(F32), axis=0, keepdims=True)
+            part = dot(d_pre, up[j], NT)
+            if j == 0:
+                total_ref[rows, :] = part
+            else:
+                total_ref[rows, :] += part
+        sum_ref[j : j + 1, :] = sums
+
+
+def ffn_back(info, branch_two, down, up, slopes):
+    size = down[2].shape[0]
+    hbm = pl.BlockSpec(memory_space=pl.ANY)
+    return pl.pallas_call(
+        ffn_back_kernel,
+        out_shape=(struct((LEN, 2 * size)),) * 4 + (struct((LEN, D), F32), struct((8, size), F32)),
+        grid_spec=pltpu.PrefetchScalarGridSpec(
+            num_scalar_prefetch=1,
+            grid=(1,),
+            in_specs=[hbm] * 17,
+            out_specs=[whole((LEN, 2 * size))] * 4 + [whole((LEN, D)), whole((8, size))],
+            scratch_shapes=[
+                pltpu.VMEM((LEN, D), BF16),
+                pltpu.VMEM((8, size, D), BF16),
+                pltpu.VMEM((8, D, size), BF16),
+                pltpu.VMEM((8, LEN, size), BF16),
+                pltpu.SemaphoreType.DMA((25,)),
+            ],
+        ),
+        cost_estimate=cost(17e9, 40e6),
+        name="ffn_back",
+    )(info, branch_two, *down, *up, *slopes)
+
+
+def grad_columns(refs, group, size, which):
+    full, part_a, part_b = refs
+    for at in range(0, size, 2 * group):
+        yield full, at, at, 2 * group
+    for at in range(0, size, 2 * group):
+        yield part_a, at + which * group, size + at, group
+        yield part_b, at + which * group, size + at + group, group
+
+
+def grad_send_kernel(group, info_ref, left_ref, *refs):
+    *rights, out_ref = refs
+    size = rights[0].shape[1]
+    left = left_ref[...].reshape(D // 2, LEN)
+    for right, source, target, width in grad_columns(rights, group, size, 1):
+        out_ref[0, :, target : target + width] = dot(left, right[:, source : source + width]).astype(
+            BF16
+        )
+
+
+def left_spec():
+    return pl.BlockSpec((4, 1, D // 8, LEN), lambda i, info: (0, i ^ info[0], 0, 0))
+
+
+def grad_send(info, left_t, near, part_a, part_b, group):
+    size = near.shape[1]
+    return pl.pallas_call(
+        functools.partial(grad_send_kernel, group),
+        out_shape=struct((2, D // 2, 2 * size)),
+        grid_spec=pltpu.PrefetchScalarGridSpec(
+            num_scalar_prefetch=1,
+            grid=(2,),
+            in_specs=[left_spec()] + [whole((LEN, size))] * 3,
+            out_specs=pl.BlockSpec((1, D // 2, 2 * size), lambda i, info: (i, 0, 0)),
+        ),
+        cost_estimate=cost(4 * D * LEN * size, 10e6),
+        name="grad_send",
+    )(info, left_t.reshape(4, 2, D // 8, LEN), near, part_a, part_b)
+
+
+def grad_keep_kernel(group, info_ref, left_ref, *refs):
+    rights, got_ref, outs = refs[:3], refs[3], refs[4:]
+    size = rights[0].shape[1]
+    left = left_ref[...].reshape(D // 2, LEN)
+    for side in range(2):
+
+        @pl.when(pl.program_id(0) == side)
+        def _():
+            for right, source, target, width in grad_columns(rights, group, size, 0):
+                total = dot(left, right[:, source : source + width])
+                total = total + got_ref[0, :, target : target + width].astype(F32)
+                out_ref = outs[side + 2 * (target // size)]
+                at = target % size
+                out_ref[:, at : at + width] = total.astype(BF16)
+
+
+def grad_keep(info, left_t, own, part_a, part_b, got, group):
+    size = own.shape[1]
+    return pl.pallas_call(
+        functools.partial(grad_keep_kernel, group),
+        out_shape=(struct((D // 2, size)),) * 4,
+        grid_spec=pltpu.PrefetchScalarGridSpec(
+            num_scalar_prefetch=1,
+            grid=(2,),
+            in_specs=[left_spec()]
+            + [whole((LEN, size))] * 3
+            + [pl.BlockSpec((1, D // 2, 2 * size), lambda i, info: (i, 0, 0))],
+            out_specs=[whole((D // 2, size))] * 4,
+        ),
+        cost_estimate=cost(4 * D * LEN * size, 14e6),
+        name="grad_keep",
+    )(info, left_t.reshape(4, 2, D // 8, LEN), own, part_a, part_b, got)
+
+
+def swapped(ref, group, rows=slice(None)):
+    size = ref.shape[-1]
+    return [(at, ref[rows, at ^ group : (at ^ group) + group]) for at in range(0, size, group)]
+
+
+def add_kernel(group, swap, mine_ref, got_ref, out_ref):
+    for at in range(0, mine_ref.shape[1], group):
+        source = at ^ group if swap else at
+        total = mine_ref[:, at : at + group].astype(F32) + got_ref[:, source : source + group].astype(F32)
+        out_ref[:, at : at + group] = total.astype(BF16)
+
+
+def add_parts(mine, got, group, swap):
+    return pl.pallas_call(
+        functools.partial(add_kernel, group, swap),
+        out_shape=struct(mine.shape),
+        cost_estimate=cost(1e6, 3e6),
+        name="add_parts",
+    )(mine, got)
+
+
+def split_kernel(group, info_ref, mine_ref, x_ref, y_ref, *out_refs):
+    span = mine_ref.shape[0] // 4
+    for k in range(4):
+        rows = pl.ds(pl.multiple_of((info_ref[2] ^ k) * span, span), span)
+        for at in range(0, mine_ref.shape[1], group):
+            swap = at ^ group
+            total = mine_ref[rows, at : at + group].astype(F32)
+            total = total + x_ref[rows, swap : swap + group].astype(F32)
+            total = total + y_ref[rows, at : at + group].astype(F32)
+            out_refs[k][:, at : at + group] = total.astype(BF16)
+
+
+def split_z(info, mine, from_x, from_y, group):
+    rows, size = mine.shape
+    return pl.pallas_call(
+        functools.partial(split_kernel, group),
+        out_shape=(struct((rows // 4, size)),) * 4,
+        grid_spec=pltpu.PrefetchScalarGridSpec(
+            num_scalar_prefetch=1,
+            grid=(1,),
+            in_specs=[whole((rows, size))] * 3,
+            out_specs=[whole((rows // 4, size))] * 4,
+        ),
+        cost_estimate=cost(1e6, 4e6),
+        name="split_z",
+    )(info, mine, from_x, from_y)
+
+
+def reduce_parts(info, parts, group, y_first):
+    own_keep, own_leave, far_keep, far_leave = parts
+    if y_first:
+        from_y_leave = flip_mp(far_leave, 2)
+        from_y = flip_mp(after(far_keep, from_y_leave), 2)
+        from_x = flip_dp(add_parts(own_leave, from_y_leave, group, False), 1)
+    else:
+        from_x_far = flip_dp(far_leave, 1)
+        from_x = flip_dp(after(own_leave, from_x_far), 1)
+        from_y = flip_mp(add_parts(far_keep, from_x_far, group, True), 2)
+    mine, *others = split_z(info, own_keep, from_x, from_y, group)
+    total = mine.astype(F32)
+    for k, other in enumerate(others):
+        total = total + flip_dp(other, 2 * (k + 1)).astype(F32)
+    return total
+
+
+def natural_columns(values, group, x_at):
+    rows = values.shape[0]
+    shaped = values.reshape(rows, -1, 2, group)
+    return jnp.where(x_at == 0, shaped, shaped[:, :, ::-1]).reshape(rows, -1)
+
+
+def input_grad_kernel(one_ref, *refs):
+    grads, weights, out_ref, sum_ref = refs[:4], refs[4:8], refs[8], refs[9]
+
+    @pl.when(pl.program_id(0) == 0)
+    def _():
+        sum_ref[...] = jnp.zeros_like(sum_ref)
+
+    total = one_ref[...]
+    for p in range(4):
+        total = total + dot(grads[p][...], weights[p][...], NT)
+    out_ref[...] = total
+    sum_ref[0:1, :] += jnp.sum(total, axis=0, keepdims=True)
+
+
+def input_grad(grad_one, d_qkv, weights):
+    tile = pl.BlockSpec((ROWS, D), lambda i: (i, 0))
+    width = d_qkv[0].shape[1]
+    return pl.pallas_call(
+        input_grad_kernel,
+        out_shape=(struct((LEN, D), F32), struct((8, D), F32)),
+        grid=(LEN // ROWS,),
+        in_specs=[tile]
+        + [pl.BlockSpec((ROWS, width), lambda i: (i, 0))] * 4
+        + [whole((D, width))] * 4,
+        out_specs=[tile, whole((8, D))],
+        cost_estimate=cost(6.4e9, 20e6),
+        name="input_grad",
+    )(grad_one, *d_qkv, *weights)
+
+
+def sum_vectors(rows, place):
+    for flip, bit, at in place:
+        size = rows.shape[0] // 2
+        keep = lax.dynamic_slice_in_dim(rows, at * size, size, 0)
+        leave = lax.dynamic_slice_in_dim(rows, (1 - at) * size, size, 0)
+        rows = keep + flip(leave, bit)
+    return rows[0]
+
+
+def by_device(parts):
+    shaped = parts.reshape(2, 2, 2, 2, 2, -1)
+    return shaped.transpose(4, 3, 2, 0, 1, 5).reshape(32, -1)
+
+
+def gather_rows(rows, order, index):
+    for flip, bit, shift in order:
+        other = flip(rows, bit)
+        low = (index >> shift) & 1
+        rows = jnp.where(low == 0, jnp.concatenate([rows, other]), jnp.concatenate([other, rows]))
+    return rows
+
+
+def natural_blocks(halves, x_at, mp_at):
+    join = lambda a, b: jnp.where(x_at == 0, jnp.concatenate([a, b]), jnp.concatenate([b, a]))
+    stacked = jnp.stack(
+        [
+            join(halves[0], halves[1]),
+            join(halves[2], halves[3]),
+            join(halves[4], halves[6]),
+            join(halves[5], halves[7]),
+        ]
+    )
+    return jnp.stack([stacked[i ^ mp_at] for i in range(4)])
+
+
+def body_rows(
+    tokens,
+    segment_ids,
+    time_steps,
+    w_qkv,
+    b_qv,
+    w_out,
+    b_out,
+    gain_one,
+    shift_one,
+    w_up,
+    b_up,
+    w_down,
+    b_down,
+    gain_two,
+    shift_two,
+    w_time,
+    b_time,
+    cotangent,
+):
+    dp_at, mp_at = lax.axis_index("dp"), lax.axis_index("mp")
+    x_at, z_at = dp_at % 2, dp_at // 2
+    y_at, c_at = mp_at // 2, mp_at % 2
+    info = jnp.stack([x_at, 1 - x_at, z_at, mp_at]).astype(jnp.int32)
+    row = lambda v: v.astype(F32)[None, :]
+    width = w_qkv.shape[2]
+    flat = lambda w: w.reshape(D, -1)
+
+    w_all = fetch(w_qkv, 2, x_at, None)
+    qkv_w = [flat(w) for w in w_all]
+    out_w = fetch(w_out, 0, x_at, w_all[2])
+    up_w = fetch(w_up, 1, x_at, out_w[2])
+    down_w = fetch(w_down, 0, x_at, up_w[2])
+    qv_rows = [v.astype(F32) for v in fetch_rows(b_qv, x_at)]
+    up_rows = [v.astype(F32) for v in fetch_rows(b_up[None, :], x_at)]
+    zero = jnp.zeros((1, width // 2), F32)
+
+    own_step = lax.dynamic_slice_in_dim(time_steps, mp_at, 1, 0)
+    segment_row = lax.dynamic_index_in_dim(segment_ids, mp_at, 0, keepdims=False)
+    features = time_features(own_step)
+    embed_row = jnp.dot(features, w_time.astype(F32), precision=HIGHEST_PRECISION)
+    embed_row = embed_row + row(b_time)
+    hidden_low = (tokens.astype(F32) + embed_row).astype(BF16)
+    hotq, hotk = mark_segments(segment_row)
+    win_f, win_b = windows(segment_row, TILE_F), windows(segment_row, TILE_B)
+
+    qkv, ctx, lse, qkv_cat = [], [], [], []
+    pairs = [(qkv_w[0],) * 2, (qkv_w[1],) * 2, qkv_w[2:4], qkv_w[4:6]]
+    for p in range(4):
+        first, second = qv_rows[2 * p : 2 * p + 2]
+        bias = jnp.concatenate(
+            [first[0:1], second[0:1], zero, zero, first[1:2], second[1:2]], axis=1
+        )
+        parts = attend_pair(win_f, info, hidden_low, pairs[p], p >= 2, bias, hotq, hotk)
+        for kept, part in zip((qkv, ctx, lse, qkv_cat), parts):
+            kept.append(part)
+    normal_one, scale_one, mid_low, mid_t, hidden_t, out_cat = first_norm(
+        info, tokens, ctx, out_w, embed_row, row(b_out), row(gain_one), row(shift_one)
+    )
+
+    up_pairs = [(up_w[0],) * 2, (up_w[1],) * 2, up_w[2:4], up_w[4:6]]
+    down_pairs = [(down_w[0],) * 2, (down_w[1],) * 2, down_w[2:4], down_w[4:6]]
+    act, slope = [], []
+    ffn = jnp.broadcast_to(row(b_down), (LEN, D))
+    for p in range(4):
+        act_p, slope_p, ffn = ffn_pair(
+            info, mid_low, up_pairs[p], down_pairs[p], up_rows[2 * p : 2 * p + 2], ffn, p >= 2
+        )
+        act.append(act_p)
+        slope.append(slope_p)
+    out_rows, grad_two, branch_two, branch_two_t, sums_two = second_norm(
+        ffn, normal_one, cotangent, row(gain_one), row(shift_one), row(gain_two), row(shift_two)
+    )
+
+    ff_group = act[0].shape[1] // 2
+    sent_down = flip_mp(grad_send(info, branch_two_t, act[1], act[2], act[3], ff_group), 1)
+    *d_pre, d_mid, sums_up = ffn_back(info, branch_two, down_w, up_w, slope)
+    parts_down = grad_keep(info, branch_two_t, act[0], act[2], act[3], sent_down, ff_group)
+    g_w_down = reduce_parts(info, parts_down, ff_group, True)
+    sent_up = flip_mp(grad_send(info, mid_t, d_pre[1], d_pre[2], d_pre[3], ff_group), 1)
+    grad_one, branch_one, branch_one_t, sums_one = first_back(
+        d_mid, grad_two, normal_one, scale_one, row(gain_one)
+    )
+    parts_up = grad_keep(info, mid_t, d_pre[0], d_pre[2], d_pre[3], sent_up, ff_group)
+    g_w_up = reduce_parts(info, parts_up, ff_group, False)
+    sent_out = flip_mp(grad_send(info, branch_one_t, ctx[1], ctx[2], ctx[3], UNIT), 1)
+    d_qkv, qkv_sums = [None] * 4, [None] * 4
+    for p in (1, 2, 3, 0):
+        d_qkv[p], qkv_sums[p] = attend_back_pair(
+            win_b, qkv[p], hotq, hotk, branch_one, out_cat, p, ctx[p], lse[p]
+        )
+        if p == 1:
+            parts_out = grad_keep(info, branch_one_t, ctx[0], ctx[2], ctx[3], sent_out, UNIT)
+            g_w_out = reduce_parts(info, parts_out, UNIT, True)
+        if p == 3:
+            sent_qkv = flip_mp(grad_send(info, hidden_t, d_qkv[1], d_qkv[2], d_qkv[3], UNIT), 1)
+    parts_qkv = grad_keep(info, hidden_t, d_qkv[0], d_qkv[2], d_qkv[3], sent_qkv, UNIT)
+    g_w_qkv = reduce_parts(info, parts_qkv, UNIT, False)
+    grad_tokens, sums_in = input_grad(grad_one, d_qkv, qkv_cat)
+
+    place = (
+        (flip_mp, 1, c_at),
+        (flip_mp, 2, y_at),
+        (flip_dp, 1, x_at),
+        (flip_dp, 4, z_at // 2),
+        (flip_dp, 2, z_at % 2),
+    )
+    spread = lambda v: v.reshape(8, 4, -1)
+    spread_blocks = lambda b: b.reshape(4, 8, -1).transpose(1, 0, 2)
+    rows_two = jnp.concatenate(
+        [spread(sums_two[j]) for j in range(3)]
+        + [spread_blocks(natural_blocks([sums_up[j] for j in range(8)], x_at, mp_at))],
+        axis=2,
+    )
+    rows_two = sum_vectors(by_device(rows_two), place)
+    rows_one = jnp.concatenate([spread(sums_one[j]) for j in range(3)], axis=2)
+    rows_one = sum_vectors(by_device(rows_one), place)
+    rows_qkv = []
+    for j in (0, 2):
+        halves = [
+            qkv_sums[p][0, (2 * j + u) * UNIT : (2 * j + u + 1) * UNIT]
+            for p in range(4)
+            for u in range(HALF)
+        ]
+        rows_qkv.append(spread_blocks(natural_blocks(halves, x_at, mp_at)))
+    rows_qkv = sum_vectors(by_device(jnp.concatenate(rows_qkv, axis=2)), place)
+
+    tail_row = jnp.concatenate(
+        [sums_in[0:1], jnp.broadcast_to(own_step.astype(F32)[None, :], (1, UNIT))], axis=1
+    )
+    order = (
+        (flip_mp, 1, 0),
+        (flip_mp, 2, 1),
+        (flip_dp, 1, 2),
+        (flip_dp, 2, 3),
+        (flip_dp, 4, 4),
+    )
+    device_at = dp_at * GRID_MP + mp_at
+    all_rows = gather_rows(tail_row, order, device_at)
+    span = D // (GRID_DP * GRID_MP)
+    all_grads = all_rows[:, :D]
+    own_features = lax.dynamic_slice_in_dim(
+        time_features(all_rows[:, D]), device_at * span, span, 1
+    )
+    g_w_time = jnp.dot(own_features.T, all_grads, precision=HIGHEST_PRECISION)
+    g_b_time = lax.dynamic_slice_in_dim(jnp.sum(all_grads, axis=0), device_at * span, span, 0)
+
+    return (
+        out_rows,
+        grad_tokens,
+        natural_columns(g_w_qkv, UNIT, x_at).reshape(-1, 3, width),
+        rows_qkv.reshape(2, 1, -1),
+        natural_columns(g_w_out, UNIT, x_at).T,
+        rows_one[:span],
+        rows_one[span : 2 * span],
+        rows_one[2 * span :],
+        natural_columns(g_w_up, ff_group, x_at),
+        rows_two[None, 3 * span :],
+        natural_columns(g_w_down, ff_group, x_at).T,
+        rows_two[:span],
+        rows_two[span : 2 * span],
+        rows_two[2 * span : 3 * span],
+        g_w_time,
+        g_b_time,
+    )
+
+
 def solution(mesh):
     placed = (
         P(("dp", "mp"), None),
@@ -296,6 +1245,10 @@
         P(),
         P(("dp", "mp"), None),
     )
+    def body(*args):
+        whole_rows = args[0].shape[0] == LEN and (mesh.shape["dp"], mesh.shape["mp"]) == (GRID_DP, GRID_MP)
+        return (body_rows if whole_rows else body_split)(*args)
+
     return jax.shard_map(
         body,
         mesh=mesh,

time: 1560 us -> 646 us (0.41)
  waiting for transfers between devices: 921 us -> 143 us
  matrix products: 351 us -> 1.97 us
  Pallas kernels: 0 us -> 328 us
  other arithmetic: 113 us -> 15 us
  starting transfers between devices: 1.05 us -> 96.8 us
  local copies, waits for them, and re-layouts: 107 us -> 47.1 us
  blocking collectives: 40.5 us -> 0 us
    reduce_scatter x7 -> x0, waiting for transfers between devices: 441 us -> none  [the longest x1 92.6 us: body(): lax.psum_scatter(grad_w_time, ('dp', 'mp'), scatter_dimension=0, tiled=True)]
    dot_general x44 -> x2, matrix products: 351 us -> 1.97 us  [the longest x1 1.05 us: body_rows(): g_w_time = jnp.dot(own_features.T, all_grads, precision=HIGHEST_PRECISION)]
    pallas_call x0 -> x33, Pallas kernels: none -> 328 us  [the longest x4 60.3 us: attend_back_pair(): pl.pallas_call(attend_back_kernel, out_shape=(struct((LEN, 6 * UNIT)), st...]
    unnamed x19 -> x0, waiting for transfers between devices: 246 us -> none
    all_gather x4 -> x0, waiting for transfers between devices: 233 us -> none  [the longest x1 58.4 us: body(): cot_full = lax.all_gather(branch_two, 'mp', axis=0, tiled=True)]
    ppermute x0 -> x74, waiting for transfers between devices: none -> 143 us  [the longest x34 83.1 us: flip_dp(): return lax.ppermute(values, 'dp', [(i, i ^ bit) for i in range(GRID_DP)])]
    ppermute x0 -> x74, starting transfers between devices: none -> 96.8 us  [the longest x34 59.8 us: flip_dp(): return lax.ppermute(values, 'dp', [(i, i ^ bit) for i in range(GRID_DP)])]
    convert_element_type x21 -> x10, other arithmetic: 51.2 us -> 5.44 us  [the longest x4 2.46 us: body_rows(): up_rows = [v.astype(F32) for v in fetch_rows(b_up[None, :], x_at)]]
  transfers between devices with their start and end apart: 15 -> 74, of which waited for: 15 -> 24; matrix products, arithmetic and copies ran while one was open for 7% -> 9% of each run, Pallas kernels for 0% -> 31%
where the time goes in v2:
time: 646 us; the launch traced here: 635 us
  Pallas kernels  328 us (51%)
  waiting for transfers between devices  143 us (22%)
  starting transfers between devices  96.8 us (15%)
  local copies, waits for them, and re-layouts  47.1 us (7%)
  other arithmetic  15 us (2%)
    ppermute x34, waiting for transfers between devices, flip_dp(): return lax.ppermute(values, 'dp', [(i, i ^ bit) for i in range(GRID_DP)])  83.1 us
    pallas_call x4, Pallas kernels, attend_back_pair(): pl.pallas_call(attend_back_kernel, out_shape=(struct((LEN, 6 * UNIT)), st...  60.3 us
    ppermute x40, waiting for transfers between devices, flip_mp(): return lax.ppermute(values, 'mp', [(i, i ^ bit) for i in range(GRID_MP)])  60.1 us
    ppermute x34, starting transfers between devices, flip_dp(): return lax.ppermute(values, 'dp', [(i, i ^ bit) for i in range(GRID_DP)])  59.8 us
    pallas_call x4, Pallas kernels, ffn_pair(): pl.pallas_call(ffn_kernel, out_shape=(struct((LEN, 2 * size)), struct((LE...  56.2 us
    pallas_call x4, Pallas kernels, attend_pair(): pl.pallas_call(attend_kernel, out_shape=(struct((LEN, 6 * UNIT)), struct(...  44.5 us
    pallas_call x4, Pallas kernels, grad_keep(): pl.pallas_call(functools.partial(grad_keep_kernel, group), out_shape=(str...  39.4 us
    ppermute x40, starting transfers between devices, flip_mp(): return lax.ppermute(values, 'mp', [(i, i ^ bit) for i in range(GRID_MP)])  37 us
  transfers between devices with their start and end apart: 74, of which 24 were waited for; matrix products, arithmetic and copies ran while one was open for 9% of the time, Pallas kernels for 31%

profile of v2, /device:TPU:0, one launch (start us, length us, event | category | flops | bytes accessed | tf_op | source)
XLA Modules:
  0.0 635.4 jit_solution(468142858915469460)
XLA Ops:
  0.7 3.1 collective-permute-start.4
  27.4 11.2 %attend.4 = (bf16[1024,768]{1,0:T(8,128)(2,1)}, bf16[1024,256]{1,0:T(8,128)(2,1)}, f32[2,8,1024]{2,1,0:T(8,128)}, bf16[1024,768]{1,0:T(8,128)(2,1)}) custom-call(s32[2,2]{1,0:T(2,128)} %pad_add_fusion.win_ref, s32[4]{0:T(128)} %pad_add_fusion.2.info_ref, bf16[1024,1024]{1,0:T(8,128)(2,1)} %add_convert_fusion.x_ref, ...), custom_call_target="tpu_custom_call" | custom-call | flops 6000000000 | bytes 8000000 | tf_op jit(solution)/shard_map/attend/pallas_call | solution.py:451
  38.7 4.3 collective-permute-start.2
  43.0 18.3 %collective-permute-done.2 = bf16[1024,3,128]{0,2,1:T(8,128)(2,1)} collective-permute-done((bf16[1024,3,128]{0,2,1:T(8,128)(2,1)S(1)}, bf16[1024,3,128]{0,2,1:T(8,128)(2,1)}, u32[]{:S(2)}, u32[]{:S(2)}) %collective-permute-start.2) | collective-permute-done | bytes 786464 | tf_op jit(solution)/shard_map/ppermute | solution.py:302
  63.1 6.4 %collective-permute-done.9.refs_8_ = bf16[128,1024]{1,0:T(8,128)(2,1)S(1)} collective-permute-done((bf16[128,1024]{1,0:T(8,128)(2,1)S(1)}, bf16[128,1024]{1,0:T(8,128)(2,1)S(1)}, u32[]{:S(2)}, u32[]{:S(2)}) %collective-permute-start.9) | collective-permute-done | bytes 262176 | tf_op jit(solution)/shard_map/ppermute | solution.py:302
  73.2 20.5 %collective-permute-done.13.refs_0_.refs_8_ = bf16[1024,512]{1,0:T(8,128)(2,1)S(1)} collective-permute-done((bf16[1024,512]{1,0:T(8,128)(2,1)S(1)}, bf16[1024,512]{1,0:T(8,128)(2,1)S(1)}, u32[]{:S(2)}, u32[]{:S(2)}) %collective-permute-start.13) | collective-permute-done | bytes 1048608 | tf_op jit(solution)/shard_map/ppermute | solution.py:302
  104.0 11.2 %attend.5 = (bf16[1024,768]{1,0:T(8,128)(2,1)}, bf16[1024,256]{1,0:T(8,128)(2,1)}, f32[2,8,1024]{2,1,0:T(8,128)}, bf16[1024,768]{1,0:T(8,128)(2,1)}) custom-call(s32[2,2]{1,0:T(2,128)} %pad_add_fusion.win_ref, s32[4]{0:T(128)} %pad_add_fusion.2.info_ref, bf16[1024,1024]{1,0:T(8,128)(2,1)} %add_convert_fusion.x_ref, ...), custom_call_target="tpu_custom_call" | custom-call | flops 6000000000 | bytes 8000000 | tf_op jit(solution)/shard_map/attend/pallas_call | solution.py:451
  116.7 3.5 collective-permute-start.14
  120.6 11.2 %attend.6 = (bf16[1024,768]{1,0:T(8,128)(2,1)}, bf16[1024,256]{1,0:T(8,128)(2,1)}, f32[2,8,1024]{2,1,0:T(8,128)}, bf16[1024,768]{1,0:T(8,128)(2,1)}) custom-call(s32[2,2]{1,0:T(2,128)} %pad_add_fusion.win_ref, s32[4]{0:T(128)} %pad_add_fusion.2.info_ref, bf16[1024,1024]{1,0:T(8,128)(2,1)} %add_convert_fusion.x_ref, ...), custom_call_target="tpu_custom_call" | custom-call | flops 6000000000 | bytes 8000000 | tf_op jit(solution)/shard_map/attend/pallas_call | solution.py:451
  135.8 10.9 %attend.7 = (bf16[1024,768]{1,0:T(8,128)(2,1)}, bf16[1024,256]{1,0:T(8,128)(2,1)}, f32[2,8,1024]{2,1,0:T(8,128)}, bf16[1024,768]{1,0:T(8,128)(2,1)}) custom-call(s32[2,2]{1,0:T(2,128)} %pad_add_fusion.win_ref, s32[4]{0:T(128)} %pad_add_fusion.2.info_ref, bf16[1024,1024]{1,0:T(8,128)(2,1)} %add_convert_fusion.x_ref, ...), custom_call_target="tpu_custom_call" | custom-call | flops 6000000000 | bytes 8000000 | tf_op jit(solution)/shard_map/attend/pallas_call | solution.py:451
  146.7 10.7 %first_norm.1 = (f32[1024,1024]{1,0:T(8,128)}, f32[1024,1]{1,0:T(8,128)}, bf16[1024,1024]{1,0:T(8,128)(2,1)}, bf16[1024,1024]{1,0:T(8,128)(2,1)}, bf16[1024,1024...) custom-call(s32[4]{0:T(128)} %pad_add_fusion.2.info_ref, bf16[1024,1024]{1,0:T(8,128)(2,1)} %tok_ref.1, ...), custom_call_target="tpu_custom_call" | custom-call | flops 2200000000 | bytes 20000000 | tf_op jit(solution)/shard_map/first_norm/pallas_call | solution.py:629
  157.5 9.1 %collective-permute-done.17.refs_2_.refs_4_ = bf16[512,1024]{1,0:T(8,128)(2,1)S(1)} collective-permute-done((bf16[512,1024]{1,0:T(8,128)(2,1)}, bf16[512,1024]{1,0:T(8,128)(2,1)S(1)}, u32[]{:S(2)}, u32[]{:S(2)}) %collective-permute-start.17) | collective-permute-done | bytes 1048608 | tf_op jit(solution)/shard_map/ppermute | solution.py:306
  169.2 14.0 %ffn.4 = (bf16[1024,1024]{1,0:T(8,128)(2,1)}, bf16[1024,1024]{1,0:T(8,128)(2,1)}, f32[1024,1024]{1,0:T(8,128)}) custom-call(s32[4]{0:T(128)} %pad_add_fusion.2.info_ref, bf16[1024,1024]{1,0:T(8,128)(2,1)} %get-tuple-element.119.mid_ref, bf16[1024,1024]{1,0:T(8,128)(2,1)} %refs_6_.1, bf16[1024,1024]{1,0:T(8,128)(2,1)} %refs_6_.1, bf16[1024,1024]{1,0:T(8,128)(2,1)} %refs_0_.3, ...), custom_call_target="tpu_custom_call" | custom-call | flops 4300000256 | bytes 18000000 | tf_op jit(solution)/shard_map/ffn/pallas_call | solution.py:757
  183.1 13.9 %ffn.5 = (bf16[1024,1024]{1,0:T(8,128)(2,1)}, bf16[1024,1024]{1,0:T(8,128)(2,1)}, f32[1024,1024]{1,0:T(8,128)}) custom-call(s32[4]{0:T(128)} %pad_add_fusion.2.info_ref, bf16[1024,1024]{1,0:T(8,128)(2,1)} %get-tuple-element.119.mid_ref, bf16[1024,1024]{1,0:T(8,128)(2,1)} %collective-permute-done.23.refs_0_.refs_1_.refs_7_, ...), custom_call_target="tpu_custom_call" | custom-call | flops 4300000256 | bytes 18000000 | tf_op jit(solution)/shard_map/ffn/pallas_call | solution.py:757
  198.1 14.3 %ffn.6 = (bf16[1024,1024]{1,0:T(8,128)(2,1)}, bf16[1024,1024]{1,0:T(8,128)(2,1)}, f32[1024,1024]{1,0:T(8,128)}) custom-call(s32[4]{0:T(128)} %pad_add_fusion.2.info_ref, bf16[1024,1024]{1,0:T(8,128)(2,1)} %get-tuple-element.119.mid_ref, bf16[1024,512]{1,0:T(8,128)(2,1)} %copy-done.30, bf16[1024,512]{1,0:T(8,128)(2,1)} %copy-done.33, ...), custom_call_target="tpu_custom_call" | custom-call | flops 4300000256 | bytes 18000000 | tf_op jit(solution)/shard_map/ffn/pallas_call | solution.py:757
  212.4 14.0 %ffn.7 = (bf16[1024,1024]{1,0:T(8,128)(2,1)}, bf16[1024,1024]{1,0:T(8,128)(2,1)}, f32[1024,1024]{1,0:T(8,128)}) custom-call(s32[4]{0:T(128)} %pad_add_fusion.2.info_ref, bf16[1024,1024]{1,0:T(8,128)(2,1)} %get-tuple-element.119.mid_ref, bf16[1024,512]{1,0:T(8,128)(2,1)} %collective-permute-done.14.refs_0_.refs_10_, ...), custom_call_target="tpu_custom_call" | custom-call | flops 4300000256 | bytes 18000000 | tf_op jit(solution)/shard_map/ffn/pallas_call | solution.py:757
  226.4 10.1 %second_norm.1 = (bf16[1024,1024]{1,0:T(8,128)(2,1)}, f32[1024,1024]{1,0:T(8,128)}, bf16[1024,1024]{1,0:T(8,128)(2,1)}, bf16[1024,1024]{1,0:T(8,128)(2,1)}, f32[8,1024]{1,0:T(8,128)}) custom-call(f32[1024,1024]{1,0:T(8,128)} %get-tuple-element.125.ffn_ref, f32[1024,1024]{1,0:T(8,128)} %get-tuple-element.126.one_ref, bf16[1024,1024]{1,0:T(8,128)(2,1)} %cot_ref.1, ...), custom_call_target="tpu_custom_call" | custom-call | flops 100000000 | bytes 20000000 | tf_op jit(solution)/shard_map/second_norm/pallas_call | solution.py:683
  236.5 27.3 %ffn_back.1 = (bf16[1024,1024]{1,0:T(8,128)(2,1)}, bf16[1024,1024]{1,0:T(8,128)(2,1)}, bf16[1024,1024]{1,0:T(8,128)(2,1)}, bf16[1024,1024]{1,0:T(8,128)(2,1)}, f32[1024,1024]{1,0:T(8,128)}, /*index=5*/f32[8,512]{1,0:T(8,128)}) custom-call(s32[4]{0:T(128)} %pad_add_fusion.2.info_ref, bf16[1024,1024]{1,0:T(8,128)(2,1)} %get-tuple-element.128.branch_hbm, ...), custom_call_target="tpu_custom_call" | custom-call | flops 16999999488 | bytes 40000000 | tf_op jit(solution)/shard_map/ffn_back/pallas_call | solution.py:829
  263.8 9.6 %first_back.1 = (f32[1024,1024]{1,0:T(8,128)}, bf16[1024,1024]{1,0:T(8,128)(2,1)}, bf16[1024,1024]{1,0:T(8,128)(2,1)}, f32[8,1024]{1,0:T(8,128)}) custom-call(f32[1024,1024]{1,0:T(8,128)} %get-tuple-element.133.part_ref, f32[1024,1024]{1,0:T(8,128)} %get-tuple-element.134.grad_ref, f32[1024,1024]{1,0:T(8,128)} %get-tuple-element.126.one_ref, ...), custom_call_target="tpu_custom_call" | custom-call | flops 100000000 | bytes 20000000 | tf_op jit(solution)/shard_map/first_back/pallas_call | solution.py:721
  273.4 14.9 %attend_back.7 = (bf16[1024,768]{1,0:T(8,128)(2,1)}, f32[8,768]{1,0:T(8,128)}) custom-call(s32[2,4]{1,0:T(2,128)} %pad_add_fusion.1.win_ref, bf16[1024,768]{1,0:T(8,128)(2,1)} %get-tuple-element.148.qkv_ref, bf16[1024,128]{1,0:T(8,128)(2,1)} %get-tuple-element.303.refs_7_.hotq_ref, bf16[1024,128]{1,0:T(8,128)(2,1)} %get-tuple-element.302.refs_8_.hotk_ref, ...), custom_call_target="tpu_custom_call" | custom-call | flops 8000000000 | bytes 8000000 | tf_op jit(solution)/shard_map/attend_back/pallas_call | solution.py:561
  288.3 15.1 %attend_back.6 = (bf16[1024,768]{1,0:T(8,128)(2,1)}, f32[8,768]{1,0:T(8,128)}) custom-call(s32[2,4]{1,0:T(2,128)} %pad_add_fusion.1.win_ref, bf16[1024,768]{1,0:T(8,128)(2,1)} %get-tuple-element.145.qkv_ref, bf16[1024,128]{1,0:T(8,128)(2,1)} %get-tuple-element.303.refs_7_.hotq_ref, bf16[1024,128]{1,0:T(8,128)(2,1)} %get-tuple-element.302.refs_8_.hotk_ref, ...), custom_call_target="tpu_custom_call" | custom-call | flops 8000000000 | bytes 8000000 | tf_op jit(solution)/shard_map/attend_back/pallas_call | solution.py:561
  303.4 15.0 %attend_back.5 = (bf16[1024,768]{1,0:T(8,128)(2,1)}, f32[8,768]{1,0:T(8,128)}) custom-call(s32[2,4]{1,0:T(2,128)} %pad_add_fusion.1.win_ref, bf16[1024,768]{1,0:T(8,128)(2,1)} %get-tuple-element.142.qkv_ref, bf16[1024,128]{1,0:T(8,128)(2,1)} %get-tuple-element.303.refs_7_.hotq_ref, bf16[1024,128]{1,0:T(8,128)(2,1)} %get-tuple-element.302.refs_8_.hotk_ref, ...), custom_call_target="tpu_custom_call" | custom-call | flops 8000000000 | bytes 8000000 | tf_op jit(solution)/shard_map/attend_back/pallas_call | solution.py:561
  318.4 15.3 %attend_back.4 = (bf16[1024,768]{1,0:T(8,128)(2,1)}, f32[8,768]{1,0:T(8,128)}) custom-call(s32[2,4]{1,0:T(2,128)} %pad_add_fusion.1.win_ref, bf16[1024,768]{1,0:T(8,128)(2,1)} %get-tuple-element.137.qkv_ref, bf16[1024,128]{1,0:T(8,128)(2,1)} %get-tuple-element.303.refs_7_.hotq_ref, bf16[1024,128]{1,0:T(8,128)(2,1)} %get-tuple-element.302.refs_8_.hotk_ref, ...), custom_call_target="tpu_custom_call" | custom-call | flops 8000000000 | bytes 8000000 | tf_op jit(solution)/shard_map/attend_back/pallas_call | solution.py:561
  333.7 12.4 %input_grad.1 = (f32[1024,1024]{1,0:T(8,128)}, f32[8,1024]{1,0:T(8,128)}) custom-call(f32[1024,1024]{1,0:T(8,128)} %get-tuple-element.136.one_ref, bf16[1024,768]{1,0:T(8,128)(2,1)} %get-tuple-element.141.refs_0_, bf16[1024,768]{1,0:T(8,128)(2,1)} %get-tuple-element.144.refs_1_.refs_0_, bf16[1024,768]{1,0:T(8,128)(2,1)} %get-tuple-element.147.refs_2_.refs_1_, ...), custom_call_target="tpu_custom_call" | custom-call | flops 6400000000 | bytes 20000000 | tf_op jit(solution)/shard_map/input_grad/pallas_call | solution.py:1012
  347.5 10.0 %grad_send.7 = bf16[2,512,2048]{2,1,0:T(8,128)(2,1)} custom-call(s32[4]{0:T(128)} %pad_add_fusion.2.info_ref, bf16[4,2,128,1024]{3,2,1,0:T(8,128)(2,1)} %bitcast.179, bf16[1024,1024]{1,0:T(8,128)(2,1)} %get-tuple-element.201.refs_0_, bf16[1024,1024]{1,0:T(8,128)(2,1)} %get-tuple-element.199.refs_1_, bf16[1024,1024]{1,0:T(8,128)(2,1)} %get-tuple-element.200.refs_2_), custom_call_target="tpu_custom_call" | custom-call | flops 4294967296 | bytes 10000000 | tf_op jit(solution)/shard_map/grad_send/pallas_call | solution.py:875
  359.6 9.9 %grad_send.6 = bf16[2,512,2048]{2,1,0:T(8,128)(2,1)} custom-call(s32[4]{0:T(128)} %pad_add_fusion.2.info_ref, bf16[4,2,128,1024]{3,2,1,0:T(8,128)(2,1)} %bitcast.181, bf16[1024,1024]{1,0:T(8,128)(2,1)} %get-tuple-element.185.refs_0_, bf16[1024,1024]{1,0:T(8,128)(2,1)} %get-tuple-element.183.refs_1_, bf16[1024,1024]{1,0:T(8,128)(2,1)} %get-tuple-element.184.refs_2_), custom_call_target="tpu_custom_call" | custom-call | flops 4294967296 | bytes 10000000 | tf_op jit(solution)/shard_map/grad_send/pallas_call | solution.py:875
  376.1 10.0 %grad_send.4 = bf16[2,512,1536]{2,1,0:T(8,128)(2,1)} custom-call(s32[4]{0:T(128)} %pad_add_fusion.2.info_ref, bf16[4,2,128,1024]{3,2,1,0:T(8,128)(2,1)} %bitcast.183, bf16[1024,768]{1,0:T(8,128)(2,1)} %get-tuple-element.144.refs_1_.refs_0_, bf16[1024,768]{1,0:T(8,128)(2,1)} %get-tuple-element.147.refs_2_.refs_1_, ...), custom_call_target="tpu_custom_call" | custom-call | flops 3221225472 | bytes 10000000 | tf_op jit(solution)/shard_map/grad_send/pallas_call | solution.py:875
  386.1 5.1 grad_send.5
  391.3 9.4 %collective-permute-start.34 = (f32[8,64]{1,0:T(8,128)S(1)}, f32[8,64]{1,0:T(8,128)S(1)}, u32[]{:S(2)}, u32[]{:S(2)}) collective-permute-start(f32[8,64]{1,0:T(8,128)S(1)} %constant_dynamic-slice_fusion.29), channel_id=1, source_target_pairs={{0,2},{1,3},{2,0},{3,1},{4,6},{5,7},{6,4},{7,5},{8,10},{9,11},{10,... | collective-permute-start | bytes 6152 | tf_op jit(solution)/shard_map/ppermute | solution.py:302
  406.0 3.2 collective-permute-start.36
  448.3 5.6 grad_keep.5
  456.0 6.9 %collective-permute-done.39.got_ref = bf16[512,256]{1,0:T(8,128)(2,1)S(1)} collective-permute-done((bf16[512,256]{1,0:T(8,128)(2,1)}, bf16[512,256]{1,0:T(8,128)(2,1)S(1)}, u32[]{:S(2)}, u32[]{:S(2)}) %collective-permute-start.39) | collective-permute-done | bytes 262176 | tf_op jit(solution)/shard_map/ppermute | solution.py:302
  464.8 10.9 %grad_keep.4 = (bf16[512,768]{1,0:T(8,128)(2,1)}, bf16[512,768]{1,0:T(8,128)(2,1)}, bf16[512,768]{1,0:T(8,128)(2,1)}, bf16[512,768]{1,0:T(8,128)(2,1)}) custom-call(s32[4]{0:T(128)} %pad_add_fusion.2.info_ref, bf16[4,2,128,1024]{3,2,1,0:T(8,128)(2,1)} %bitcast.184, bf16[1024,768]{1,0:T(8,128)(2,1)} %get-tuple-element.141.refs_0_, ...), custom_call_target="tpu_custom_call" | custom-call | flops 3221225472 | bytes 14000000 | tf_op jit(solution)/shard_map/grad_keep/pallas_call | solution.py:907
  476.7 11.5 %grad_keep.7 = (bf16[512,1024]{1,0:T(8,128)(2,1)}, bf16[512,1024]{1,0:T(8,128)(2,1)}, bf16[512,1024]{1,0:T(8,128)(2,1)}, bf16[512,1024]{1,0:T(8,128)(2,1)}) custom-call(s32[4]{0:T(128)} %pad_add_fusion.2.info_ref, bf16[4,2,128,1024]{3,2,1,0:T(8,128)(2,1)} %bitcast.180, bf16[1024,1024]{1,0:T(8,128)(2,1)} %get-tuple-element.198.refs_0_, ...), custom_call_target="tpu_custom_call" | custom-call | flops 4294967296 | bytes 14000000 | tf_op jit(solution)/shard_map/grad_keep/pallas_call | solution.py:907
  489.5 11.3 %grad_keep.6 = (bf16[512,1024]{1,0:T(8,128)(2,1)}, bf16[512,1024]{1,0:T(8,128)(2,1)}, bf16[512,1024]{1,0:T(8,128)(2,1)}, bf16[512,1024]{1,0:T(8,128)(2,1)}) custom-call(s32[4]{0:T(128)} %pad_add_fusion.2.info_ref, bf16[4,2,128,1024]{3,2,1,0:T(8,128)(2,1)} %bitcast.182, bf16[1024,1024]{1,0:T(8,128)(2,1)} %get-tuple-element.182.refs_0_, ...), custom_call_target="tpu_custom_call" | custom-call | flops 4294967296 | bytes 14000000 | tf_op jit(solution)/shard_map/grad_keep/pallas_call | solution.py:907
  506.9 15.1 %collective-permute-done.40.x_ref = bf16[512,256]{1,0:T(8,128)(2,1)} collective-permute-done((bf16[512,256]{1,0:T(8,128)(2,1)}, bf16[512,256]{1,0:T(8,128)(2,1)}, u32[]{:S(2)}, u32[]{:S(2)}) %collective-permute-start.40) | collective-permute-done | bytes 262176 | tf_op jit(solution)/shard_map/ppermute | solution.py:306
  530.4 2.8 add_parts.7
  537.4 3.1 collective-permute-done.43
  540.8 3.7 collective-permute-start.44
  545.5 2.8 add_parts.6
  551.9 23.6 %collective-permute-done.28.x_ref = bf16[512,768]{1,0:T(8,128)(2,1)} collective-permute-done((bf16[512,768]{1,0:T(8,128)(2,1)}, bf16[512,768]{1,0:T(8,128)(2,1)}, u32[]{:S(2)}, u32[]{:S(2)}) %collective-permute-start.28) | collective-permute-done | bytes 786464 | tf_op jit(solution)/shard_map/ppermute | solution.py:306
  575.5 3.2 split_z.4
  583.9 3.6 split_z.7
  587.5 2.8 collective-permute-done.30
  590.4 8.2 %collective-permute-done.31 = bf16[128,768]{1,0:T(8,128)(2,1)S(1)} collective-permute-done((bf16[128,768]{1,0:T(8,128)(2,1)}, bf16[128,768]{1,0:T(8,128)(2,1)S(1)}, u32[]{:S(2)}, u32[]{:S(2)}) %collective-permute-start.31) | collective-permute-done | bytes 196640 | tf_op jit(solution)/shard_map/ppermute | solution.py:306
  605.3 3.6 split_z.6
  608.9 9.0 %collective-permute-start.54 = (bf16[128,1024]{1,0:T(8,128)(2,1)}, bf16[128,1024]{1,0:T(8,128)(2,1)S(1)}, u32[]{:S(2)}, u32[]{:S(2)}) collective-permute-start(bf16[128,1024]{1,0:T(8,128)(2,1)} %get-tuple-element.192), channel_id=1, source_target_pairs={{0,8},{4,12},{8,0},{12,4},{16,24},{20,28},{24,16},{28,20},{1,9},{5... | collective-permute-start | bytes 786440 | tf_op jit(solution)/shard_map/ppermute | solution.py:306
  623.4 7.6 %collective-permute-done.55 = bf16[128,1024]{1,0:T(8,128)(2,1)S(1)} collective-permute-done((bf16[128,1024]{1,0:T(8,128)(2,1)}, bf16[128,1024]{1,0:T(8,128)(2,1)S(1)}, u32[]{:S(2)}, u32[]{:S(2)}) %collective-permute-start.55) | collective-permute-done | bytes 262176 | tf_op jit(solution)/shard_map/ppermute | solution.py:306
  (400 shorter events, 153.3 us)
Async XLA Ops:
  0.7 42.3 %collective-permute-start.4 = (bf16[2,256]{1,0:T(2,128)(2,1)}, bf16[2,256]{1,0:T(2,128)(2,1)S(1)}, u32[]{:S(2)}, u32[]{:S(2)}) collective-permute-start(bf16[2,256]{1,0:T(2,128)(2,1)} %param.22), channel_id=1, source_target_pairs={{0,2},{1,3},{2,0},{3,1},{4,6},{5,7},{6,4},{7,5},{8,10},{9,11},{10,... | collective-permute-start | bytes 3080 | tf_op jit(solution)/shard_map/ppermute | solution.py:302
  3.7 34.9 %collective-permute-start.1 = (bf16[2,256]{1,0:T(2,128)(2,1)}, bf16[2,256]{1,0:T(2,128)(2,1)S(1)}, u32[]{:S(2)}, u32[]{:S(2)}) collective-permute-start(bf16[2,256]{1,0:T(2,128)(2,1)} %param.22), channel_id=1, source_target_pairs={{0,1},{1,0},{2,3},{3,2},{4,5},{5,4},{6,7},{7,6},{8,9},{9,8},{10,11... | collective-permute-start | bytes 3080 | tf_op jit(solution)/shard_map/ppermute | solution.py:302
  4.4 68.2 %collective-permute-start.25 = (bf16[1,1024]{1,0:T(2,128)(2,1)S(1)}, bf16[1,1024]{1,0:T(2,128)(2,1)S(1)}, u32[]{:S(2)}, u32[]{:S(2)}) collective-permute-start(bf16[1,1024]{1,0:T(2,128)(2,1)S(1)} %broadcast_in_dim.77), channel_id=1, source_target_pairs={{0,1},{1,0},{2,3},{3,2},{4,5},{5,4},{6,7},{7,6},{8,9},{9,8},{10,11... | collective-permute-start | bytes 6152 | tf_op jit(solution)/shard_map/ppermute | solution.py:302
  4.9 66.0 %collective-permute-start.19 = (bf16[1,1024]{1,0:T(2,128)(2,1)S(1)}, bf16[1,1024]{1,0:T(2,128)(2,1)S(1)}, u32[]{:S(2)}, u32[]{:S(2)}) collective-permute-start(bf16[1,1024]{1,0:T(2,128)(2,1)S(1)} %broadcast_in_dim.77), channel_id=1, source_target_pairs={{0,2},{1,3},{2,0},{3,1},{4,6},{5,7},{6,4},{7,5},{8,10},{9,11},{10,... | collective-permute-start | bytes 6152 | tf_op jit(solution)/shard_map/ppermute | solution.py:302
  7.6 89.5 %collective-permute-start = (bf16[1024,3,256]{0,2,1:T(8,128)(2,1)}, bf16[1024,3,256]{0,2,1:T(8,128)(2,1)}, u32[]{:S(2)}, u32[]{:S(2)}) collective-permute-start(bf16[1024,3,256]{0,2,1:T(8,128)(2,1)} %copy.87), channel_id=1, source_target_pairs={{0,1},{1,0},{2,3},{3,2},{4,5},{5,4},{6,7},{7,6},{8,9},{9,8},{10,11... | collective-permute-start | bytes 4718600 | tf_op jit(solution)/shard_map/ppermute | solution.py:302
  38.7 22.6 %collective-permute-start.2 = (bf16[1024,3,128]{0,2,1:T(8,128)(2,1)S(1)}, bf16[1024,3,128]{0,2,1:T(8,128)(2,1)}, u32[]{:S(2)}, u32[]{:S(2)}) collective-permute-start(bf16[1024,3,128]{0,2,1:T(8,128)(2,1)S(1)} %copy-done.9), channel_id=1, source_target_pairs={{0,2},{1,3},{2,0},{3,1},{4,6},{5,7},{6,4},{7,5},{8,10},{9,11},{10,... | collective-permute-start | bytes 2359304 | tf_op jit(solution)/shard_map/ppermute | solution.py:302
  69.5 24.2 %collective-permute-start.13 = (bf16[1024,512]{1,0:T(8,128)(2,1)S(1)}, bf16[1024,512]{1,0:T(8,128)(2,1)S(1)}, u32[]{:S(2)}, u32[]{:S(2)}) collective-permute-start(bf16[1024,512]{1,0:T(8,128)(2,1)S(1)} %copy-done.6), channel_id=1, source_target_pairs={{0,2},{1,3},{2,0},{3,1},{4,6},{5,7},{6,4},{7,5},{8,10},{9,11},{10,... | collective-permute-start | bytes 3145736 | tf_op jit(solution)/shard_map/ppermute | solution.py:302
  71.1 23.9 %collective-permute-start.6 = (bf16[1024,3,128]{0,2,1:T(8,128)(2,1)}, bf16[1024,3,128]{0,2,1:T(8,128)(2,1)S(1)}, u32[]{:S(2)}, u32[]{:S(2)}) collective-permute-start(bf16[1024,3,128]{0,2,1:T(8,128)(2,1)} %collective-permute-done.2), channel_id=1, source_target_pairs={{0,4},{4,0},{8,12},{12,8},{16,20},{20,16},{24,28},{28,24},{1,5},{5... | collective-permute-start | bytes 2359304 | tf_op jit(solution)/shard_map/ppermute | solution.py:306
  72.6 21.1 %collective-permute-start.8 = (bf16[256,1024]{1,0:T(8,128)(2,1)}, bf16[256,1024]{1,0:T(8,128)(2,1)S(1)}, u32[]{:S(2)}, u32[]{:S(2)}) collective-permute-start(bf16[256,1024]{1,0:T(8,128)(2,1)} %refs_5_.1), channel_id=1, source_target_pairs={{0,1},{1,0},{2,3},{3,2},{4,5},{5,4},{6,7},{7,6},{8,9},{9,8},{10,11... | collective-permute-start | bytes 1572872 | tf_op jit(solution)/shard_map/ppermute | solution.py:302
  72.9 62.4 %collective-permute-start.23 = (bf16[1024,1024]{1,0:T(8,128)(2,1)}, bf16[1024,1024]{1,0:T(8,128)(2,1)}, u32[]{:S(2)}, u32[]{:S(2)}) collective-permute-start(bf16[1024,1024]{1,0:T(8,128)(2,1)} %refs_6_.1), channel_id=1, source_target_pairs={{0,1},{1,0},{2,3},{3,2},{4,5},{5,4},{6,7},{7,6},{8,9},{9,8},{10,11... | collective-permute-start | bytes 6291464 | tf_op jit(solution)/shard_map/ppermute | solution.py:302
  93.7 26.5 %collective-permute-start.16 = (bf16[512,1024]{1,0:T(8,128)(2,1)S(1)}, bf16[512,1024]{1,0:T(8,128)(2,1)}, u32[]{:S(2)}, u32[]{:S(2)}) collective-permute-start(bf16[512,1024]{1,0:T(8,128)(2,1)S(1)} %constant_dynamic-slice_fusion.47), channel_id=1, source_target_pairs={{0,2},{1,3},{2,0},{3,1},{4,6},{5,7},{6,4},{7,5},{8,10},{9,11},{10,... | collective-permute-start | bytes 3145736 | tf_op jit(solution)/shard_map/ppermute | solution.py:302
  97.0 19.7 %collective-permute-start.7 = (bf16[1024,3,128]{0,2,1:T(8,128)(2,1)S(1)}, bf16[1024,3,128]{0,2,1:T(8,128)(2,1)}, u32[]{:S(2)}, u32[]{:S(2)}) collective-permute-start(bf16[1024,3,128]{0,2,1:T(8,128)(2,1)S(1)} %collective-permute-done.6), channel_id=1, source_target_pairs={{0,1},{1,0},{2,3},{3,2},{4,5},{5,4},{6,7},{7,6},{8,9},{9,8},{10,11... | collective-permute-start | bytes 2359304 | tf_op jit(solution)/shard_map/ppermute | solution.py:302
  103.4 79.7 %collective-permute-start.24 = (bf16[1024,1024]{1,0:T(8,128)(2,1)}, bf16[1024,1024]{1,0:T(8,128)(2,1)}, u32[]{:S(2)}, u32[]{:S(2)}) collective-permute-start(bf16[1024,1024]{1,0:T(8,128)(2,1)} %refs_0_.3), channel_id=1, source_target_pairs={{0,1},{1,0},{2,3},{3,2},{4,5},{5,4},{6,7},{7,6},{8,9},{9,8},{10,11... | collective-permute-start | bytes 6291464 | tf_op jit(solution)/shard_map/ppermute | solution.py:302
  116.4 18.9 %collective-permute-start.12 = (bf16[128,1024]{1,0:T(8,128)(2,1)S(1)}, bf16[128,1024]{1,0:T(8,128)(2,1)}, u32[]{:S(2)}, u32[]{:S(2)}) collective-permute-start(bf16[128,1024]{1,0:T(8,128)(2,1)S(1)} %collective-permute-done.11.refs_10_), channel_id=1, source_target_pairs={{0,1},{1,0},{2,3},{3,2},{4,5},{5,4},{6,7},{7,6},{8,9},{9,8},{10,11... | collective-permute-start | bytes 786440 | tf_op jit(solution)/shard_map/ppermute | solution.py:302
  116.7 40.7 %collective-permute-start.14 = (bf16[1024,512]{1,0:T(8,128)(2,1)}, bf16[1024,512]{1,0:T(8,128)(2,1)}, u32[]{:S(2)}, u32[]{:S(2)}) collective-permute-start(bf16[1024,512]{1,0:T(8,128)(2,1)} %copy-done.30), channel_id=1, source_target_pairs={{0,4},{4,0},{8,12},{12,8},{16,20},{20,16},{24,28},{28,24},{1,5},{5... | collective-permute-start | bytes 3145736 | tf_op jit(solution)/shard_map/ppermute | solution.py:306
  120.2 46.4 %collective-permute-start.17 = (bf16[512,1024]{1,0:T(8,128)(2,1)}, bf16[512,1024]{1,0:T(8,128)(2,1)S(1)}, u32[]{:S(2)}, u32[]{:S(2)}) collective-permute-start(bf16[512,1024]{1,0:T(8,128)(2,1)} %collective-permute-done.16.refs_2_), channel_id=1, source_target_pairs={{0,4},{4,0},{8,12},{12,8},{16,20},{20,16},{24,28},{28,24},{1,5},{5... | collective-permute-start | bytes 3145736 | tf_op jit(solution)/shard_map/ppermute | solution.py:306
  135.3 61.8 %collective-permute-start.21 = (bf16[1024,512]{1,0:T(8,128)(2,1)S(1)}, bf16[1024,512]{1,0:T(8,128)(2,1)S(1)}, u32[]{:S(2)}, u32[]{:S(2)}) collective-permute-start(bf16[1024,512]{1,0:T(8,128)(2,1)S(1)} %copy-done.31), channel_id=1, source_target_pairs={{0,1},{1,0},{2,3},{3,2},{4,5},{5,4},{6,7},{7,6},{8,9},{9,8},{10,11... | collective-permute-start | bytes 3145736 | tf_op jit(solution)/shard_map/ppermute | solution.py:302
  135.3 61.8 %collective-permute-start.22 = (bf16[512,1024]{1,0:T(8,128)(2,1)}, bf16[512,1024]{1,0:T(8,128)(2,1)}, u32[]{:S(2)}, u32[]{:S(2)}) collective-permute-start(bf16[512,1024]{1,0:T(8,128)(2,1)} %collective-permute-done.16.refs_2_), channel_id=1, source_target_pairs={{0,1},{1,0},{2,3},{3,2},{4,5},{5,4},{6,7},{7,6},{8,9},{9,8},{10,11... | collective-permute-start | bytes 3145736 | tf_op jit(solution)/shard_map/ppermute | solution.py:302
  157.4 55.0 %collective-permute-start.15 = (bf16[1024,512]{1,0:T(8,128)(2,1)}, bf16[1024,512]{1,0:T(8,128)(2,1)}, u32[]{:S(2)}, u32[]{:S(2)}) collective-permute-start(bf16[1024,512]{1,0:T(8,128)(2,1)} %collective-permute-done.14.refs_0_.refs_10_), channel_id=1, source_target_pairs={{0,1},{1,0},{2,3},{3,2},{4,5},{5,4},{6,7},{7,6},{8,9},{9,8},{10,11... | collective-permute-start | bytes 3145736 | tf_op jit(solution)/shard_map/ppermute | solution.py:302
  166.6 45.7 %collective-permute-start.18 = (bf16[512,1024]{1,0:T(8,128)(2,1)S(1)}, bf16[512,1024]{1,0:T(8,128)(2,1)}, u32[]{:S(2)}, u32[]{:S(2)}) collective-permute-start(bf16[512,1024]{1,0:T(8,128)(2,1)S(1)} %collective-permute-done.17.refs_2_.refs_4_), channel_id=1, source_target_pairs={{0,1},{1,0},{2,3},{3,2},{4,5},{5,4},{6,7},{7,6},{8,9},{9,8},{10,11... | collective-permute-start | bytes 3145736 | tf_op jit(solution)/shard_map/ppermute | solution.py:302
  346.9 44.4 %collective-permute-start.69 = (f32[1,1152]{1,0:T(1,128)S(1)}, f32[1,1152]{1,0:T(1,128)S(1)}, u32[]{:S(2)}, u32[]{:S(2)}) collective-permute-start(f32[1,1152]{1,0:T(1,128)S(1)} %concatenate.307), channel_id=1, source_target_pairs={{0,1},{1,0},{2,3},{3,2},{4,5},{5,4},{6,7},{7,6},{8,9},{9,8},{10,11... | collective-permute-start | bytes 13832 | tf_op jit(solution)/shard_map/ppermute | solution.py:302
  357.5 118.3 %collective-permute-start.62 = (bf16[2,512,2048]{2,1,0:T(8,128)(2,1)}, bf16[2,512,2048]{2,1,0:T(8,128)(2,1)}, u32[]{:S(2)}, u32[]{:S(2)}) collective-permute-start(bf16[2,512,2048]{2,1,0:T(8,128)(2,1)} %grad_send.7), channel_id=1, source_target_pairs={{0,1},{1,0},{2,3},{3,2},{4,5},{5,4},{6,7},{7,6},{8,9},{9,8},{10,11... | collective-permute-start | bytes 12582920 | tf_op jit(solution)/shard_map/ppermute | solution.py:302
  359.1 67.5 %collective-permute-start.57 = (f32[16,224]{1,0:T(8,128)S(1)}, f32[16,224]{1,0:T(8,128)S(1)}, u32[]{:S(2)}, u32[]{:S(2)}) collective-permute-start(f32[16,224]{1,0:T(8,128)S(1)} %constant_dynamic-slice_fusion.8), channel_id=1, source_target_pairs={{0,1},{1,0},{2,3},{3,2},{4,5},{5,4},{6,7},{7,6},{8,9},{9,8},{10,11... | collective-permute-start | bytes 43016 | tf_op jit(solution)/shard_map/ppermute | solution.py:302
  369.5 118.7 %collective-permute-start.50 = (bf16[2,512,2048]{2,1,0:T(8,128)(2,1)}, bf16[2,512,2048]{2,1,0:T(8,128)(2,1)}, u32[]{:S(2)}, u32[]{:S(2)}) collective-permute-start(bf16[2,512,2048]{2,1,0:T(8,128)(2,1)} %grad_send.6), channel_id=1, source_target_pairs={{0,1},{1,0},{2,3},{3,2},{4,5},{5,4},{6,7},{7,6},{8,9},{9,8},{10,11... | collective-permute-start | bytes 12582920 | tf_op jit(solution)/shard_map/ppermute | solution.py:302
  375.6 15.7 %collective-permute-start.33 = (f32[16,64]{1,0:T(8,128)S(1)}, f32[16,64]{1,0:T(8,128)S(1)}, u32[]{:S(2)}, u32[]{:S(2)}) collective-permute-start(f32[16,64]{1,0:T(8,128)S(1)} %constant_dynamic-slice_fusion.31), channel_id=1, source_target_pairs={{0,1},{1,0},{2,3},{3,2},{4,5},{5,4},{6,7},{7,6},{8,9},{9,8},{10,11... | collective-permute-start | bytes 12296 | tf_op jit(solution)/shard_map/ppermute | solution.py:302
  402.3 60.9 %collective-permute-start.26 = (bf16[2,512,1536]{2,1,0:T(8,128)(2,1)}, bf16[2,512,1536]{2,1,0:T(8,128)(2,1)}, u32[]{:S(2)}, u32[]{:S(2)}) collective-permute-start(bf16[2,512,1536]{2,1,0:T(8,128)(2,1)} %grad_send.4), channel_id=1, source_target_pairs={{0,1},{1,0},{2,3},{3,2},{4,5},{5,4},{6,7},{7,6},{8,9},{9,8},{10,11... | collective-permute-start | bytes 9437192 | tf_op jit(solution)/shard_map/ppermute | solution.py:302
  426.5 20.8 %collective-permute-start.38 = (bf16[2,512,512]{2,1,0:T(8,128)(2,1)}, bf16[2,512,512]{2,1,0:T(8,128)(2,1)S(1)}, u32[]{:S(2)}, u32[]{:S(2)}) collective-permute-start(bf16[2,512,512]{2,1,0:T(8,128)(2,1)} %grad_send.5), channel_id=1, source_target_pairs={{0,1},{1,0},{2,3},{3,2},{4,5},{5,4},{6,7},{7,6},{8,9},{9,8},{10,11... | collective-permute-start | bytes 3145736 | tf_op jit(solution)/shard_map/ppermute | solution.py:302
  454.8 46.0 %collective-permute-start.61 = (f32[1,224]{1,0:T(1,128)S(1)}, f32[1,224]{1,0:T(1,128)S(1)}, u32[]{:S(2)}, u32[]{:S(2)}) collective-permute-start(f32[1,224]{1,0:T(1,128)S(1)} %constant_dynamic-slice_fusion), channel_id=1, source_target_pairs={{0,8},{4,12},{8,0},{12,4},{16,24},{20,28},{24,16},{28,20},{1,9},{5... | collective-permute-start | bytes 2696 | tf_op jit(solution)/shard_map/ppermute | solution.py:306
  462.9 39.9 %collective-permute-start.72 = (f32[8,1152]{1,0:T(8,128)S(1)}, f32[8,1152]{1,0:T(8,128)S(1)}, u32[]{:S(2)}, u32[]{:S(2)}) collective-permute-start(f32[8,1152]{1,0:T(8,128)S(1)} %maximum_select_fusion.2), channel_id=1, source_target_pairs={{0,8},{4,12},{8,0},{12,4},{16,24},{20,28},{24,16},{28,20},{1,9},{5... | collective-permute-start | bytes 110600 | tf_op jit(solution)/shard_map/ppermute | solution.py:306
  463.2 41.5 %collective-permute-start.41 = (bf16[512,256]{1,0:T(8,128)(2,1)}, bf16[512,256]{1,0:T(8,128)(2,1)S(1)}, u32[]{:S(2)}, u32[]{:S(2)}) collective-permute-start(bf16[512,256]{1,0:T(8,128)(2,1)} %get-tuple-element.175), channel_id=1, source_target_pairs={{0,2},{1,3},{2,0},{3,1},{4,6},{5,7},{6,4},{7,5},{8,10},{9,11},{10,... | collective-permute-start | bytes 786440 | tf_op jit(solution)/shard_map/ppermute | solution.py:302
  475.7 49.3 %collective-permute-start.27 = (bf16[512,768]{1,0:T(8,128)(2,1)}, bf16[512,768]{1,0:T(8,128)(2,1)S(1)}, u32[]{:S(2)}, u32[]{:S(2)}) collective-permute-start(bf16[512,768]{1,0:T(8,128)(2,1)} %get-tuple-element.159), channel_id=1, source_target_pairs={{0,4},{4,0},{8,12},{12,8},{16,20},{20,16},{24,28},{28,24},{1,5},{5... | collective-permute-start | bytes 2359304 | tf_op jit(solution)/shard_map/ppermute | solution.py:306
  488.3 41.0 %collective-permute-start.63 = (bf16[512,1024]{1,0:T(8,128)(2,1)}, bf16[512,1024]{1,0:T(8,128)(2,1)S(1)}, u32[]{:S(2)}, u32[]{:S(2)}) collective-permute-start(bf16[512,1024]{1,0:T(8,128)(2,1)} %get-tuple-element.204), channel_id=1, source_target_pairs={{0,2},{1,3},{2,0},{3,1},{4,6},{5,7},{6,4},{7,5},{8,10},{9,11},{10,... | collective-permute-start | bytes 3145736 | tf_op jit(solution)/shard_map/ppermute | solution.py:302
  500.8 40.0 %collective-permute-start.51 = (bf16[512,1024]{1,0:T(8,128)(2,1)}, bf16[512,1024]{1,0:T(8,128)(2,1)S(1)}, u32[]{:S(2)}, u32[]{:S(2)}) collective-permute-start(bf16[512,1024]{1,0:T(8,128)(2,1)} %get-tuple-element.188), channel_id=1, source_target_pairs={{0,4},{4,0},{8,12},{12,8},{16,20},{20,16},{24,28},{28,24},{1,5},{5... | collective-permute-start | bytes 3145736 | tf_op jit(solution)/shard_map/ppermute | solution.py:306
  502.9 19.1 %collective-permute-start.40 = (bf16[512,256]{1,0:T(8,128)(2,1)}, bf16[512,256]{1,0:T(8,128)(2,1)}, u32[]{:S(2)}, u32[]{:S(2)}) collective-permute-start(bf16[512,256]{1,0:T(8,128)(2,1)} %add_parts.5), channel_id=1, source_target_pairs={{0,4},{4,0},{8,12},{12,8},{16,20},{20,16},{24,28},{28,24},{1,5},{5... | collective-permute-start | bytes 786440 | tf_op jit(solution)/shard_map/ppermute | solution.py:306
  504.7 28.5 %collective-permute-start.73 = (f32[16,1152]{1,0:T(8,128)S(1)}, f32[16,1152]{1,0:T(8,128)S(1)}, u32[]{:S(2)}, u32[]{:S(2)}) collective-permute-start(f32[16,1152]{1,0:T(8,128)S(1)} %maximum_select_fusion.1), channel_id=1, source_target_pairs={{0,16},{4,20},{8,24},{12,28},{16,0},{20,4},{24,8},{28,12},{1,17},{... | collective-permute-start | bytes 221192 | tf_op jit(solution)/shard_map/ppermute | solution.py:306
  528.4 21.0 %collective-permute-start.29 = (bf16[512,768]{1,0:T(8,128)(2,1)}, bf16[512,768]{1,0:T(8,128)(2,1)S(1)}, u32[]{:S(2)}, u32[]{:S(2)}) collective-permute-start(bf16[512,768]{1,0:T(8,128)(2,1)} %add_parts.4), channel_id=1, source_target_pairs={{0,2},{1,3},{2,0},{3,1},{4,6},{5,7},{6,4},{7,5},{8,10},{9,11},{10,... | collective-permute-start | bytes 2359304 | tf_op jit(solution)/shard_map/ppermute | solution.py:302
  529.2 50.6 %collective-permute-start.65 = (bf16[512,1024]{1,0:T(8,128)(2,1)}, bf16[512,1024]{1,0:T(8,128)(2,1)}, u32[]{:S(2)}, u32[]{:S(2)}) collective-permute-start(bf16[512,1024]{1,0:T(8,128)(2,1)} %get-tuple-element.206), channel_id=1, source_target_pairs={{0,2},{1,3},{2,0},{3,1},{4,6},{5,7},{6,4},{7,5},{8,10},{9,11},{10,... | collective-permute-start | bytes 3145736 | tf_op jit(solution)/shard_map/ppermute | solution.py:302
  533.2 48.9 %collective-permute-start.64 = (bf16[512,1024]{1,0:T(8,128)(2,1)}, bf16[512,1024]{1,0:T(8,128)(2,1)}, u32[]{:S(2)}, u32[]{:S(2)}) collective-permute-start(bf16[512,1024]{1,0:T(8,128)(2,1)} %add_parts.7), channel_id=1, source_target_pairs={{0,4},{4,0},{8,12},{12,8},{16,20},{20,16},{24,28},{28,24},{1,5},{5... | collective-permute-start | bytes 3145736 | tf_op jit(solution)/shard_map/ppermute | solution.py:306
  540.5 35.0 %collective-permute-start.28 = (bf16[512,768]{1,0:T(8,128)(2,1)}, bf16[512,768]{1,0:T(8,128)(2,1)}, u32[]{:S(2)}, u32[]{:S(2)}) collective-permute-start(bf16[512,768]{1,0:T(8,128)(2,1)} %get-tuple-element.160), channel_id=1, source_target_pairs={{0,4},{4,0},{8,12},{12,8},{16,20},{20,16},{24,28},{28,24},{1,5},{5... | collective-permute-start | bytes 2359304 | tf_op jit(solution)/shard_map/ppermute | solution.py:306
  548.3 56.0 %collective-permute-start.53 = (bf16[512,1024]{1,0:T(8,128)(2,1)}, bf16[512,1024]{1,0:T(8,128)(2,1)S(1)}, u32[]{:S(2)}, u32[]{:S(2)}) collective-permute-start(bf16[512,1024]{1,0:T(8,128)(2,1)} %add_parts.6), channel_id=1, source_target_pairs={{0,2},{1,3},{2,0},{3,1},{4,6},{5,7},{6,4},{7,5},{8,10},{9,11},{10,... | collective-permute-start | bytes 3145736 | tf_op jit(solution)/shard_map/ppermute | solution.py:302
  549.4 54.9 %collective-permute-start.52 = (bf16[512,1024]{1,0:T(8,128)(2,1)}, bf16[512,1024]{1,0:T(8,128)(2,1)}, u32[]{:S(2)}, u32[]{:S(2)}) collective-permute-start(bf16[512,1024]{1,0:T(8,128)(2,1)} %get-tuple-element.189), channel_id=1, source_target_pairs={{0,4},{4,0},{8,12},{12,8},{16,20},{20,16},{24,28},{28,24},{1,5},{5... | collective-permute-start | bytes 3145736 | tf_op jit(solution)/shard_map/ppermute | solution.py:306
  579.8 18.8 %collective-permute-start.31 = (bf16[128,768]{1,0:T(8,128)(2,1)}, bf16[128,768]{1,0:T(8,128)(2,1)S(1)}, u32[]{:S(2)}, u32[]{:S(2)}) collective-permute-start(bf16[128,768]{1,0:T(8,128)(2,1)} %get-tuple-element.164), channel_id=1, source_target_pairs={{0,16},{4,20},{8,24},{12,28},{16,0},{20,4},{24,8},{28,12},{1,17},{... | collective-permute-start | bytes 589832 | tf_op jit(solution)/shard_map/ppermute | solution.py:306
  582.1 16.4 %collective-permute-start.32 = (bf16[128,768]{1,0:T(8,128)(2,1)}, bf16[128,768]{1,0:T(8,128)(2,1)S(1)}, u32[]{:S(2)}, u32[]{:S(2)}) collective-permute-start(bf16[128,768]{1,0:T(8,128)(2,1)} %get-tuple-element.165), channel_id=1, source_target_pairs={{0,24},{4,28},{8,16},{12,20},{16,8},{20,12},{24,0},{28,4},{1,25},{... | collective-permute-start | bytes 589832 | tf_op jit(solution)/shard_map/ppermute | solution.py:306
  590.4 27.5 %collective-permute-start.66 = (bf16[128,1024]{1,0:T(8,128)(2,1)}, bf16[128,1024]{1,0:T(8,128)(2,1)S(1)}, u32[]{:S(2)}, u32[]{:S(2)}) collective-permute-start(bf16[128,1024]{1,0:T(8,128)(2,1)} %get-tuple-element.208), channel_id=1, source_target_pairs={{0,8},{4,12},{8,0},{12,4},{16,24},{20,28},{24,16},{28,20},{1,9},{5... | collective-permute-start | bytes 786440 | tf_op jit(solution)/shard_map/ppermute | solution.py:306
  598.5 21.7 %collective-permute-start.67 = (bf16[128,1024]{1,0:T(8,128)(2,1)}, bf16[128,1024]{1,0:T(8,128)(2,1)S(1)}, u32[]{:S(2)}, u32[]{:S(2)}) collective-permute-start(bf16[128,1024]{1,0:T(8,128)(2,1)} %get-tuple-element.209), channel_id=1, source_target_pairs={{0,16},{4,20},{8,24},{12,28},{16,0},{20,4},{24,8},{28,12},{1,17},{... | collective-permute-start | bytes 786440 | tf_op jit(solution)/shard_map/ppermute | solution.py:306
  598.5 21.7 %collective-permute-start.68 = (bf16[128,1024]{1,0:T(8,128)(2,1)}, bf16[128,1024]{1,0:T(8,128)(2,1)S(1)}, u32[]{:S(2)}, u32[]{:S(2)}) collective-permute-start(bf16[128,1024]{1,0:T(8,128)(2,1)} %get-tuple-element.210), channel_id=1, source_target_pairs={{0,24},{4,28},{8,16},{12,20},{16,8},{20,12},{24,0},{28,4},{1,25},{... | collective-permute-start | bytes 786440 | tf_op jit(solution)/shard_map/ppermute | solution.py:306
  608.9 14.5 %collective-permute-start.54 = (bf16[128,1024]{1,0:T(8,128)(2,1)}, bf16[128,1024]{1,0:T(8,128)(2,1)S(1)}, u32[]{:S(2)}, u32[]{:S(2)}) collective-permute-start(bf16[128,1024]{1,0:T(8,128)(2,1)} %get-tuple-element.192), channel_id=1, source_target_pairs={{0,8},{4,12},{8,0},{12,4},{16,24},{20,28},{24,16},{28,20},{1,9},{5... | collective-permute-start | bytes 786440 | tf_op jit(solution)/shard_map/ppermute | solution.py:306
  617.9 13.1 %collective-permute-start.55 = (bf16[128,1024]{1,0:T(8,128)(2,1)}, bf16[128,1024]{1,0:T(8,128)(2,1)S(1)}, u32[]{:S(2)}, u32[]{:S(2)}) collective-permute-start(bf16[128,1024]{1,0:T(8,128)(2,1)} %get-tuple-element.193), channel_id=1, source_target_pairs={{0,16},{4,20},{8,24},{12,28},{16,0},{20,4},{24,8},{28,12},{1,17},{... | collective-permute-start | bytes 786440 | tf_op jit(solution)/shard_map/ppermute | solution.py:306
  (71 other events, 655.7 us)

commit v3 on v2

--- a/solution.py
+++ b/solution.py
@@ -1,5 +1,6 @@
 import functools
 import math
+from typing import NamedTuple
 
 import jax
 import jax.numpy as jnp
@@ -7,6 +8,7 @@
 from jax.experimental import pallas as pl
 from jax.experimental.pallas import tpu as pltpu
 from jax.sharding import PartitionSpec as P
+
 
 D = 1024
 HEAD_DIM = 64
@@ -181,7 +183,7 @@
     grad_two, grad_gain_two, grad_shift_two = out_back(cotangent.astype(jnp.float32))
     branch_two = grad_two.astype(jnp.bfloat16)
     grad_b_down = jnp.sum(branch_two.astype(jnp.float32), axis=0)
-    gelu_value, gelu_back = jax.vjp(exact_gelu, pre_act)
+    _, gelu_back = jax.vjp(exact_gelu, pre_act)
     cot_full = lax.all_gather(branch_two, "mp", axis=0, tiled=True)
     d_act = jnp.dot(cot_full, w_down.T, preferred_element_type=jnp.float32)
     grad_w_down = jnp.dot(activated.T, cot_full, preferred_element_type=jnp.float32)
@@ -195,7 +197,7 @@
         scatter_dimension=0,
         tiled=True,
     ).astype(jnp.float32)
-    mid_value, mid_back = jax.vjp(layer_norm, mid_in, gain_one_f, shift_one_f)
+    _, mid_back = jax.vjp(layer_norm, mid_in, gain_one_f, shift_one_f)
     grad_one, grad_gain_one, grad_shift_one = mid_back(grad_two + d_mid_part)
     branch_one = grad_one.astype(jnp.bfloat16)
     grad_b_out = jnp.sum(branch_one.astype(jnp.float32), axis=0)
@@ -298,18 +300,6 @@
     return lax.dot_general(left, right, dims, preferred_element_type=F32)
 
 
-def flip_mp(values, bit):
-    return lax.ppermute(values, "mp", [(i, i ^ bit) for i in range(GRID_MP)])
-
-
-def flip_dp(values, bit):
-    return lax.ppermute(values, "dp", [(i, i ^ bit) for i in range(GRID_DP)])
-
-
-def after(values, others):
-    return lax.optimization_barrier((values, others))[0]
-
-
 def half_of(values, which, axis):
     size = values.shape[axis] // 2
     return lax.dynamic_slice_in_dim(values, which * size, size, axis)
@@ -327,39 +317,113 @@
     return pl.CostEstimate(flops=int(flops), bytes_accessed=int(moved), transcendentals=0)
 
 
-def fetch(own, axis, x_at, wait_for):
-    half = half_of(own, x_at, axis)
-    if wait_for is not None:
-        half = after(half, wait_for)
-    far_a = flip_mp(half, 2)
-    far_b = flip_dp(far_a, 1)
-    near = flip_mp(own, 1)
-    return [own, near, far_a, flip_mp(far_a, 1), far_b, flip_mp(far_b, 1)]
-
-
-def fetch_rows(own, x_at):
-    near, far = flip_mp(own, 1), flip_mp(own, 2)
-    near_far = flip_mp(far, 1)
-    cut = lambda v, at: half_of(v, at, 1)
-    order = ((own, near), (far, near_far))
-    first = [cut(v, at) for v in order[0] for at in (x_at, 1 - x_at)]
-    return first + [cut(v, at) for at in (x_at, 1 - x_at) for v in order[1]]
-
-
-def piece_specs(shape, column, skip):
-    def spec(which):
-        def index(*args):
-            at = 0 if which is None else args[skip][which]
-            return (0, at) if column else (at, 0)
-
-        return pl.BlockSpec(shape, index)
-
-    return [spec(w) for w in (0, 1, 0, 1, None, None, None, None)]
+def send_mp(values, bit):
+    return lax.ppermute(values, "mp", [(i, i ^ bit) for i in range(GRID_MP)])
+
+
+def send_dp(values, bit):
+    return lax.ppermute(values, "dp", [(i, i ^ bit) for i in range(GRID_DP)])
+
+
+def fetch(own, first_half):
+    near = send_mp(own, 1)
+    far_a = send_mp(first_half, 2)
+    near_a = send_mp(far_a, 1)
+    far_b = send_dp(far_a, 1)
+    near_b = send_mp(far_b, 1)
+    return [own, near, far_a, near_a, far_b, near_b]
+
+
+def pack_heads_kernel(info_ref, qkv_ref, out_ref, both_ref, first_ref):
+    for u in range(HALF):
+        for j in range(3):
+            at = pl.ds(pl.multiple_of(info_ref[u] * UNIT, UNIT), UNIT)
+            both_ref[u, j * UNIT : (j + 1) * UNIT, :] = qkv_ref[j, :, at].T
+        at = pl.ds(pl.multiple_of(info_ref[u] * UNIT, UNIT), UNIT)
+        both_ref[u, 3 * UNIT :, :] = out_ref[at, :]
+    first_ref[...] = both_ref[0]
+
+
+def pack_heads(info, w_qkv, w_out):
+    return pl.pallas_call(
+        pack_heads_kernel,
+        out_shape=(struct((HALF, 4 * UNIT, D)), struct((4 * UNIT, D))),
+        grid_spec=pltpu.PrefetchScalarGridSpec(
+            num_scalar_prefetch=1,
+            grid=(1,),
+            in_specs=[whole((3, D, 2 * UNIT)), whole((2 * UNIT, D))],
+            out_specs=[whole((HALF, 4 * UNIT, D)), whole((4 * UNIT, D))],
+        ),
+        cost_estimate=cost(1e6, 5e6),
+    )(info, w_qkv.transpose(1, 0, 2), w_out)
+
+
+def pack_units_kernel(info_ref, up_ref, down_ref, up_both, up_first, down_both, down_first):
+    step = pl.program_id(0)
+    up = up_ref[...].T
+    up_both[0] = up
+    down_both[0] = down_ref[...]
+
+    @pl.when(step == 0)
+    def _():
+        up_first[...] = up
+        down_first[...] = down_ref[...]
+
+
+def pack_units(info, w_up, w_down):
+    size = w_down.shape[0] // 2
+    return pl.pallas_call(
+        pack_units_kernel,
+        out_shape=(struct((HALF, size, D)), struct((size, D))) * 2,
+        grid_spec=pltpu.PrefetchScalarGridSpec(
+            num_scalar_prefetch=1,
+            grid=(HALF,),
+            in_specs=[
+                pl.BlockSpec((D, size), lambda i, info: (0, info[i])),
+                pl.BlockSpec((size, D), lambda i, info: (info[i], 0)),
+            ],
+            out_specs=[pl.BlockSpec((1, size, D), lambda i, info: (i, 0, 0)), whole((size, D))] * 2,
+        ),
+        cost_estimate=cost(1e6, 10e6),
+    )(info, w_up, w_down)
+
+
+def fetch_bias(own, x_at):
+    packed = jnp.concatenate(own, axis=1)
+    near, far = send_mp(packed, 1), send_mp(packed, 2)
+    near_far = send_mp(far, 1)
+    order = [(packed, x_at), (packed, 1 - x_at), (near, x_at), (near, 1 - x_at)]
+    order += [(v, at) for at in (x_at, 1 - x_at) for v in (far, near_far)]
+    pieces, start = [], 0
+    for row in own:
+        size = row.shape[1]
+        pieces.append(
+            [half_of(v[:, start : start + size], at, 1).astype(F32) for v, at in order]
+        )
+        start += size
+    return pieces
+
+
+def half_specs(rows, block):
+    both = [pl.BlockSpec((1, rows, D), lambda *_, u=u: (u, block, 0)) for u in range(HALF)]
+    return both * 2 + [pl.BlockSpec((rows, D), lambda *_: (block, 0))] * 4
 
 
 def eight(pieces):
     own, near, far_a, near_a, far_b, near_b = pieces
     return [own, own, near, near, far_a, near_a, far_b, near_b]
+
+
+def pair_specs(rows, block, pair):
+    return half_specs(rows, block)[2 * pair : 2 * pair + 2]
+
+
+def pair_of(pieces, pair):
+    return eight(pieces)[2 * pair : 2 * pair + 2]
+
+
+def rows_of(ref):
+    return ref[...].reshape(-1, D)
 
 
 def mark_segments(segment_row):
@@ -394,20 +458,21 @@
 
 
 def attend_kernel(
-    win_ref, info_ref, x_ref, *refs
+    win_ref, x_ref, *refs
 ):
-    weights, (bias_ref, hotq_ref, hotk_ref, qkv_ref, ctx_ref, lse_ref, w_ref, kx) = refs[:6], refs[6:]
+    weights, (bias_ref, hotq_ref, hotk_ref, qkv_ref, ctx_ref, lse_ref, w_ref, kx) = refs[:2], refs[2:]
     unit, step = pl.program_id(0), pl.program_id(1)
 
     @pl.when((unit == 0) & (step == 0))
     def _():
-        for j in range(3):
-            for u in range(HALF):
+        for u in range(HALF):
+            part = rows_of(weights[u])
+            for j in range(3):
                 at = (2 * j + u) * UNIT
-                w_ref[:, at : at + UNIT] = weights[3 * u + j][...]
+                w_ref[at : at + UNIT, :] = part[j * UNIT : (j + 1) * UNIT]
         for r in range(LEN // ROWS):
             rows = slice(r * ROWS, (r + 1) * ROWS)
-            qkv_ref[rows, :] = (dot(x_ref[rows, :], w_ref[...]) + bias_ref[...]).astype(BF16)
+            qkv_ref[rows, :] = (dot(x_ref[rows, :], w_ref[...], NT) + bias_ref[...]).astype(BF16)
 
     @pl.when(step == 0)
     def _():
@@ -442,41 +507,35 @@
     variants(win_ref[1, step], TILE_F, run)
 
 
-def attend_pair(win, info, hidden_low, pair, far, bias, hotq, hotk):
-    def w_spec(j, u):
-        if far:
-            return pl.BlockSpec((D, UNIT), lambda n, i, win, info: (0, j))
-        return pl.BlockSpec((D, UNIT), lambda n, i, win, info: (0, 2 * j + info[u]))
-
+def attend_pair(win, hidden_low, heads, pair, bias, hotq, hotk):
     return pl.pallas_call(
         attend_kernel,
         out_shape=(
             struct((LEN, 6 * UNIT)),
             struct((LEN, 2 * UNIT)),
             struct((HALF, 8, LEN), F32),
-            struct((D, 6 * UNIT)),
+            struct((6 * UNIT, D)),
         ),
         grid_spec=pltpu.PrefetchScalarGridSpec(
-            num_scalar_prefetch=2,
+            num_scalar_prefetch=1,
             grid=(HALF, LEN // TILE_F),
             in_specs=[whole((LEN, D))]
-            + [w_spec(j, u) for u in range(HALF) for j in range(3)]
+            + pair_specs(4 * UNIT, 0, pair)
             + [
                 whole((1, 6 * UNIT)),
-                pl.BlockSpec((TILE_F, UNIT), lambda n, i, win, info: (i, 0)),
+                pl.BlockSpec((TILE_F, UNIT), lambda n, i, win: (i, 0)),
                 whole((LEN, UNIT)),
             ],
             out_specs=[
                 whole((LEN, 6 * UNIT)),
-                pl.BlockSpec((TILE_F, UNIT), lambda n, i, win, info: (i, n)),
-                pl.BlockSpec((1, 8, TILE_F), lambda n, i, win, info: (n, 0, i)),
-                whole((D, 6 * UNIT)),
+                pl.BlockSpec((TILE_F, UNIT), lambda n, i, win: (i, n)),
+                pl.BlockSpec((1, 8, TILE_F), lambda n, i, win: (n, 0, i)),
+                whole((6 * UNIT, D)),
             ],
             scratch_shapes=[pltpu.VMEM((HALF, LEN, UNIT), BF16)],
         ),
         cost_estimate=cost(6e9, 8e6),
-        name="attend",
-    )(win, info, hidden_low, *[pair[u] for u in range(HALF) for _ in range(3)], bias, hotq, hotk)
+    )(win, hidden_low, *pair_of(heads, pair), bias, hotq, hotk)
 
 
 def attend_back_kernel(
@@ -583,7 +642,6 @@
             ],
         ),
         cost_estimate=cost(8e9, 8e6),
-        name="attend_back",
     )(win, qkv, hotq, hotk, branch_one, wout_all, ctx, lse)
 
 
@@ -601,14 +659,14 @@
     return scale * (scaled - mean_e - normal * mean_en)
 
 
-def first_norm_kernel(info_ref, tok_ref, *refs):
+def first_norm_kernel(tok_ref, *refs):
     ctx_refs, weights, refs = refs[:4], refs[4:12], refs[12:]
     embed_ref, bout_ref, gain_ref, shift_ref, normal_ref, scale_ref, mid_ref, mid_t, hid_t, wout_ref = refs
 
     @pl.when(pl.program_id(0) == 0)
     def _():
         for j in range(8):
-            wout_ref[j * UNIT : (j + 1) * UNIT, :] = weights[j][...]
+            wout_ref[j * UNIT : (j + 1) * UNIT, :] = rows_of(weights[j])
 
     hidden = tok_ref[...].astype(F32) + embed_ref[...]
     hid_t[...] = hidden.astype(BF16).T
@@ -623,9 +681,9 @@
     mid_t[...] = mid.T
 
 
-def first_norm(info, tokens, contexts, w_out, embed_row, b_out, gain, shift):
-    tile = pl.BlockSpec((ROWS, D), lambda i, info: (i, 0))
-    column = pl.BlockSpec((D, ROWS), lambda i, info: (0, i))
+def first_norm(tokens, contexts, heads, embed_row, b_out, gain, shift):
+    tile = pl.BlockSpec((ROWS, D), lambda i: (i, 0))
+    column = pl.BlockSpec((D, ROWS), lambda i: (0, i))
     return pl.pallas_call(
         first_norm_kernel,
         out_shape=(
@@ -636,25 +694,21 @@
             struct((D, LEN)),
             struct((D, D)),
         ),
-        grid_spec=pltpu.PrefetchScalarGridSpec(
-            num_scalar_prefetch=1,
-            grid=(LEN // ROWS,),
-            in_specs=[tile]
-            + [pl.BlockSpec((ROWS, 2 * UNIT), lambda i, info: (i, 0))] * 4
-            + piece_specs((UNIT, D), False, 1)
-            + [whole((1, D))] * 4,
-            out_specs=[
-                tile,
-                pl.BlockSpec((ROWS, 1), lambda i, info: (i, 0)),
-                tile,
-                column,
-                column,
-                whole((D, D)),
-            ],
-        ),
+        grid=(LEN // ROWS,),
+        in_specs=[tile]
+        + [pl.BlockSpec((ROWS, 2 * UNIT), lambda i: (i, 0))] * 4
+        + half_specs(UNIT, 3)
+        + [whole((1, D))] * 4,
+        out_specs=[
+            tile,
+            pl.BlockSpec((ROWS, 1), lambda i: (i, 0)),
+            tile,
+            column,
+            column,
+            whole((D, D)),
+        ],
         cost_estimate=cost(2.2e9, 20e6),
-        name="first_norm",
-    )(info, tokens, *contexts, *eight(w_out), embed_row, b_out, gain, shift)
+    )(tokens, *contexts, *eight(heads), embed_row, b_out, gain, shift)
 
 
 def second_norm_kernel(
@@ -693,7 +747,6 @@
         in_specs=[tile] * 3 + [whole((1, D))] * 4,
         out_specs=[tile] * 3 + [pl.BlockSpec((D, ROWS), lambda i: (0, i)), whole((8, D))],
         cost_estimate=cost(1e8, 20e6),
-        name="second_norm",
     )(ffn, normal_one, cot, *rows)
 
 
@@ -725,35 +778,30 @@
         in_specs=[tile] * 3 + [pl.BlockSpec((ROWS, 1), lambda i: (i, 0)), whole((1, D))],
         out_specs=[tile, tile, pl.BlockSpec((D, ROWS), lambda i: (0, i)), whole((8, D))],
         cost_estimate=cost(1e8, 20e6),
-        name="first_back",
     )(part, grad_two, normal_one, scale_one, gain)
 
 
-def ffn_kernel(info_ref, mid_ref, *refs):
+def ffn_kernel(mid_ref, *refs):
     up_refs, down_refs, bias_refs = refs[0:2], refs[2:4], refs[4:6]
     into_ref, act_ref, slope_ref, total_ref = refs[6:]
-    size = up_refs[0].shape[1]
+    size = bias_refs[0].shape[1]
     for u in range(HALF):
+        up, down = rows_of(up_refs[u]), rows_of(down_refs[u])
         columns = slice(u * size, (u + 1) * size)
         for r in range(LEN // ROWS):
             rows = slice(r * ROWS, (r + 1) * ROWS)
-            pre = dot(mid_ref[rows, :], up_refs[u][...]) + bias_refs[u][...]
+            pre = dot(mid_ref[rows, :], up, NT) + bias_refs[u][...]
             phi = 0.5 * (1.0 + lax.erf(pre * math.sqrt(0.5)))
             bell = jnp.exp(-0.5 * pre * pre) * (1.0 / math.sqrt(2.0 * math.pi))
             act = (pre * phi).astype(BF16)
             act_ref[rows, columns] = act
             slope_ref[rows, columns] = (phi + pre * bell).astype(BF16)
             before = into_ref[rows, :] if u == 0 else total_ref[rows, :]
-            total_ref[rows, :] = before + dot(act, down_refs[u][...])
-
-
-def ffn_pair(info, mid_low, up, down, bias, into, far):
-    def spec(shape, u, column):
-        if far:
-            return whole(shape)
-        return pl.BlockSpec(shape, lambda i, info: (0, info[u]) if column else (info[u], 0))
-
-    size = up[0].shape[1] if far else up[0].shape[1] // 2
+            total_ref[rows, :] = before + dot(act, down)
+
+
+def ffn_pair(mid_low, up, down, pair, bias, into):
+    size = bias[0].shape[1]
     return pl.pallas_call(
         ffn_kernel,
         out_shape=(
@@ -761,26 +809,21 @@
             struct((LEN, 2 * size)),
             struct((LEN, D), F32),
         ),
-        grid_spec=pltpu.PrefetchScalarGridSpec(
-            num_scalar_prefetch=1,
-            grid=(1,),
-            in_specs=[whole((LEN, D))]
-            + [spec((D, size), u, True) for u in range(HALF)]
-            + [spec((size, D), u, False) for u in range(HALF)]
-            + [whole((1, size))] * 2
-            + [whole((LEN, D))],
-            out_specs=[whole((LEN, 2 * size)), whole((LEN, 2 * size)), whole((LEN, D))],
-        ),
+        in_specs=[whole((LEN, D))]
+        + pair_specs(size, 0, pair) * 2
+        + [whole((1, size))] * 2
+        + [whole((LEN, D))],
+        out_specs=[whole((LEN, 2 * size)), whole((LEN, 2 * size)), whole((LEN, D))],
+        grid=(1,),
         cost_estimate=cost(4.3e9, 18e6),
-        name="ffn",
-    )(info, mid_low, *up, *down, *bias, into)
-
-
-def ffn_back_kernel(info_ref, branch_hbm, *refs):
+    )(mid_low, *pair_of(up, pair), *pair_of(down, pair), *bias, into)
+
+
+def ffn_back_kernel(branch_hbm, *refs):
     down_hbm, up_hbm, slope_hbm, refs = refs[0:6], refs[6:12], refs[12:16], refs[16:]
     pre_refs, total_ref, sum_ref, refs = refs[0:4], refs[4], refs[5], refs[6:]
     branch, down, up, slope, sems = refs
-    size = up.shape[2]
+    size = up.shape[1]
     plan = ((0, 0), (0, 1), (1, 0), (1, 1), (2, None), (3, None), (4, None), (5, None))
     first = pltpu.make_async_copy(branch_hbm, branch, sems.at[0])
     first.start()
@@ -789,8 +832,7 @@
         if which is None:
             down_part, up_part = down_hbm[piece], up_hbm[piece]
         else:
-            part = pl.ds(pl.multiple_of(info_ref[which] * size, size), size)
-            down_part, up_part = down_hbm[piece].at[part, :], up_hbm[piece].at[:, part]
+            down_part, up_part = down_hbm[piece].at[which], up_hbm[piece].at[which]
         group = [
             pltpu.make_async_copy(down_part, down.at[j], sems.at[1 + 3 * j]),
             pltpu.make_async_copy(
@@ -815,7 +857,7 @@
             d_pre = (d_act * slope[j, rows, :].astype(F32)).astype(BF16)
             pre_refs[j // 2][rows, columns] = d_pre
             sums = sums + jnp.sum(d_pre.astype(F32), axis=0, keepdims=True)
-            part = dot(d_pre, up[j], NT)
+            part = dot(d_pre, up[j])
             if j == 0:
                 total_ref[rows, :] = part
             else:
@@ -823,173 +865,243 @@
         sum_ref[j : j + 1, :] = sums
 
 
-def ffn_back(info, branch_two, down, up, slopes):
+def ffn_back(branch_two, down, up, slopes):
     size = down[2].shape[0]
     hbm = pl.BlockSpec(memory_space=pl.ANY)
     return pl.pallas_call(
         ffn_back_kernel,
         out_shape=(struct((LEN, 2 * size)),) * 4 + (struct((LEN, D), F32), struct((8, size), F32)),
+        grid=(1,),
+        in_specs=[hbm] * 17,
+        out_specs=[whole((LEN, 2 * size))] * 4 + [whole((LEN, D)), whole((8, size))],
+        scratch_shapes=[
+            pltpu.VMEM((LEN, D), BF16),
+            pltpu.VMEM((8, size, D), BF16),
+            pltpu.VMEM((8, size, D), BF16),
+            pltpu.VMEM((8, LEN, size), BF16),
+            pltpu.SemaphoreType.DMA((25,)),
+        ],
+        cost_estimate=cost(17e9, 40e6),
+    )(branch_two, *down, *up, *slopes)
+
+
+class Run(NamedTuple):
+    which: int
+    first: int
+    second: int
+    size: int
+    base: int
+    stride: int
+
+
+def unit_runs(count, size):
+    half = size // 2
+    return [Run(0, r * half // count, half + r * half // count, half // count, r * half // count, half) for r in range(count)]
+
+
+def head_runs(which, count):
+    return [Run(which, 2 * j * UNIT, (2 * j + 1) * UNIT, UNIT, 2 * j * UNIT, UNIT) for j in range(count)]
+
+
+def part_width(part):
+    return sum(2 * run.size for run in part)
+
+
+def grad_kernel(blocks, side_from, outputs, lefts, got_from, left_at, *refs):
+    n_right = 3 * lefts
+    left_hbm, right_hbm, refs = refs[:lefts], refs[lefts : lefts + n_right], refs[lefts + n_right :]
+    got_hbm, refs = (None, refs) if got_from is None else (refs[0], refs[1:])
+    out_hbm, (left, right, got, out, sems) = refs[: len(outputs)], refs[len(outputs) :]
+    count = [0]
+
+    def copy_of(source, target):
+        copy = pltpu.make_async_copy(source, target, sems.at[count[0]])
+        copy.start()
+        count[0] += 1
+        return copy
+
+    first = [
+        copy_of(left_hbm[k].at[:, left_at[side]], left.at[k, side])
+        for k in range(lefts)
+        for side in range(2)
+    ]
+    chunks, at = [], 0
+    for part, far in blocks:
+        for run in part:
+            copies = []
+            for h in range(2):
+                if far:
+                    piece, source = 1 + h, run.second if side_from else run.first
+                else:
+                    piece, source = 0, run.second if h else run.first
+                copies.append(
+                    copy_of(
+                        right_hbm[3 * run.which + piece].at[:, source : source + run.size],
+                        right.at[:, at + h * run.size : at + (h + 1) * run.size],
+                    )
+                )
+            chunks.append((run.which, at, 2 * run.size, copies))
+            at += 2 * run.size
+    if got_from is not None:
+        first.append(copy_of(got_hbm.at[:, :, got_from : got_from + at], got))
+    for copy in first:
+        copy.wait()
+    stores = []
+    for which, at, size, copies in chunks:
+        for copy in copies:
+            copy.wait()
+        columns = slice(at, at + size)
+        for side in range(2):
+            total = dot(left[which, side].reshape(D // 2, LEN), right[:, columns])
+            if got_from is not None:
+                total = total + got[side, :, columns].astype(F32)
+            out[side, :, columns] = total.astype(BF16)
+        for (start, end, side), target in zip(outputs, out_hbm):
+            if start <= at < end:
+                place = slice(at - start, at - start + size)
+                if side is None:
+                    stores.append(copy_of(out.at[:, :, columns], target.at[:, :, place]))
+                else:
+                    stores.append(copy_of(out.at[side, :, columns], target.at[:, place]))
+    for copy in stores:
+        copy.wait()
+
+
+def grad_call(info, left_t, rights, blocks, side, outputs, got=None, got_from=None):
+    width = sum(part_width(part) for part, _ in blocks)
+    hbm = pl.BlockSpec(memory_space=pl.ANY)
+    lefts = len(left_t)
+    operands = [v.reshape(4, 2, D // 8, LEN) for v in left_t] + [v for r in rights for v in r]
+    operands += [] if got is None else [got]
+    shapes = [
+        (2, D // 2, end - start) if at is None else (D // 2, end - start) for start, end, at in outputs
+    ]
+    return pl.pallas_call(
+        functools.partial(grad_kernel, blocks, side, outputs, lefts, got_from),
+        out_shape=tuple(struct(shape) for shape in shapes),
         grid_spec=pltpu.PrefetchScalarGridSpec(
             num_scalar_prefetch=1,
             grid=(1,),
-            in_specs=[hbm] * 17,
-            out_specs=[whole((LEN, 2 * size))] * 4 + [whole((LEN, D)), whole((8, size))],
+            in_specs=[hbm] * len(operands),
+            out_specs=[hbm] * len(shapes),
             scratch_shapes=[
-                pltpu.VMEM((LEN, D), BF16),
-                pltpu.VMEM((8, size, D), BF16),
-                pltpu.VMEM((8, D, size), BF16),
-                pltpu.VMEM((8, LEN, size), BF16),
-                pltpu.SemaphoreType.DMA((25,)),
+                pltpu.VMEM((lefts, 2, 4, D // 8, LEN), BF16),
+                pltpu.VMEM((LEN, width), BF16),
+                pltpu.VMEM((2, D // 2, 128 if got is None else width), BF16),
+                pltpu.VMEM((2, D // 2, width), BF16),
+                pltpu.SemaphoreType.DMA((48,)),
             ],
         ),
-        cost_estimate=cost(17e9, 40e6),
-        name="ffn_back",
-    )(info, branch_two, *down, *up, *slopes)
-
-
-def grad_columns(refs, group, size, which):
-    full, part_a, part_b = refs
-    for at in range(0, size, 2 * group):
-        yield full, at, at, 2 * group
-    for at in range(0, size, 2 * group):
-        yield part_a, at + which * group, size + at, group
-        yield part_b, at + which * group, size + at + group, group
-
-
-def grad_send_kernel(group, info_ref, left_ref, *refs):
-    *rights, out_ref = refs
-    size = rights[0].shape[1]
-    left = left_ref[...].reshape(D // 2, LEN)
-    for right, source, target, width in grad_columns(rights, group, size, 1):
-        out_ref[0, :, target : target + width] = dot(left, right[:, source : source + width]).astype(
-            BF16
-        )
-
-
-def left_spec():
-    return pl.BlockSpec((4, 1, D // 8, LEN), lambda i, info: (0, i ^ info[0], 0, 0))
-
-
-def grad_send(info, left_t, near, part_a, part_b, group):
-    size = near.shape[1]
+        cost_estimate=cost(2 * D * LEN * width, 10e6),
+    )(info, *operands)
+
+
+def column_runs(part, swap):
+    at = 0
+    for run in part:
+        for h in range(2):
+            source = at + (1 - h if swap else h) * run.size
+            yield at + h * run.size, source, run.size
+        at += 2 * run.size
+
+
+def add_kernel(part, swap, mine_ref, got_ref, out_ref):
+    rows = out_ref.shape[0]
+    mine, got = mine_ref[...].reshape(rows, -1), got_ref[...].reshape(rows, -1)
+    for at, source, size in column_runs(part, swap):
+        total = mine[:, at : at + size].astype(F32) + got[:, source : source + size].astype(F32)
+        out_ref[:, at : at + size] = total.astype(BF16)
+
+
+def block_spec(array, where, width):
+    side, column = where
+    if len(array.shape) == 3:
+        return pl.BlockSpec((1, D // 2, width), lambda *_: (side, 0, column))
+    return pl.BlockSpec((D // 2, width), lambda *_: (0, column))
+
+
+def add_parts(mine, got, part, swap):
+    width = part_width(part)
     return pl.pallas_call(
-        functools.partial(grad_send_kernel, group),
-        out_shape=struct((2, D // 2, 2 * size)),
-        grid_spec=pltpu.PrefetchScalarGridSpec(
-            num_scalar_prefetch=1,
-            grid=(2,),
-            in_specs=[left_spec()] + [whole((LEN, size))] * 3,
-            out_specs=pl.BlockSpec((1, D // 2, 2 * size), lambda i, info: (i, 0, 0)),
-        ),
-        cost_estimate=cost(4 * D * LEN * size, 10e6),
-        name="grad_send",
-    )(info, left_t.reshape(4, 2, D // 8, LEN), near, part_a, part_b)
-
-
-def grad_keep_kernel(group, info_ref, left_ref, *refs):
-    rights, got_ref, outs = refs[:3], refs[3], refs[4:]
-    size = rights[0].shape[1]
-    left = left_ref[...].reshape(D // 2, LEN)
-    for side in range(2):
-
-        @pl.when(pl.program_id(0) == side)
-        def _():
-            for right, source, target, width in grad_columns(rights, group, size, 0):
-                total = dot(left, right[:, source : source + width])
-                total = total + got_ref[0, :, target : target + width].astype(F32)
-                out_ref = outs[side + 2 * (target // size)]
-                at = target % size
-                out_ref[:, at : at + width] = total.astype(BF16)
-
-
-def grad_keep(info, left_t, own, part_a, part_b, got, group):
-    size = own.shape[1]
-    return pl.pallas_call(
-        functools.partial(grad_keep_kernel, group),
-        out_shape=(struct((D // 2, size)),) * 4,
-        grid_spec=pltpu.PrefetchScalarGridSpec(
-            num_scalar_prefetch=1,
-            grid=(2,),
-            in_specs=[left_spec()]
-            + [whole((LEN, size))] * 3
-            + [pl.BlockSpec((1, D // 2, 2 * size), lambda i, info: (i, 0, 0))],
-            out_specs=[whole((D // 2, size))] * 4,
-        ),
-        cost_estimate=cost(4 * D * LEN * size, 14e6),
-        name="grad_keep",
-    )(info, left_t.reshape(4, 2, D // 8, LEN), own, part_a, part_b, got)
-
-
-def swapped(ref, group, rows=slice(None)):
-    size = ref.shape[-1]
-    return [(at, ref[rows, at ^ group : (at ^ group) + group]) for at in range(0, size, group)]
-
-
-def add_kernel(group, swap, mine_ref, got_ref, out_ref):
-    for at in range(0, mine_ref.shape[1], group):
-        source = at ^ group if swap else at
-        total = mine_ref[:, at : at + group].astype(F32) + got_ref[:, source : source + group].astype(F32)
-        out_ref[:, at : at + group] = total.astype(BF16)
-
-
-def add_parts(mine, got, group, swap):
-    return pl.pallas_call(
-        functools.partial(add_kernel, group, swap),
-        out_shape=struct(mine.shape),
+        functools.partial(add_kernel, part, swap),
+        out_shape=struct((D // 2, width)),
+        grid=(1,),
+        in_specs=[block_spec(*v, width) for v in (mine, got)],
+        out_specs=whole((D // 2, width)),
         cost_estimate=cost(1e6, 3e6),
-        name="add_parts",
-    )(mine, got)
-
-
-def split_kernel(group, info_ref, mine_ref, x_ref, y_ref, *out_refs):
-    span = mine_ref.shape[0] // 4
+    )(mine[0], got[0])
+
+
+def split_kernel(parts, info_ref, *refs):
+    ins, out_refs = refs[: 3 * len(parts)], refs[3 * len(parts) :]
+    span = D // 8
     for k in range(4):
         rows = pl.ds(pl.multiple_of((info_ref[2] ^ k) * span, span), span)
-        for at in range(0, mine_ref.shape[1], group):
-            swap = at ^ group
-            total = mine_ref[rows, at : at + group].astype(F32)
-            total = total + x_ref[rows, swap : swap + group].astype(F32)
-            total = total + y_ref[rows, at : at + group].astype(F32)
-            out_refs[k][:, at : at + group] = total.astype(BF16)
-
-
-def split_z(info, mine, from_x, from_y, group):
-    rows, size = mine.shape
-    return pl.pallas_call(
-        functools.partial(split_kernel, group),
-        out_shape=(struct((rows // 4, size)),) * 4,
+        first = 0
+        for p, part in enumerate(parts):
+            mine, from_x, from_y = [
+                (ref[0, rows, :] if len(ref.shape) == 3 else ref[rows, :]).astype(F32)
+                for ref in ins[3 * p : 3 * p + 3]
+            ]
+            for at, source, size in column_runs(part, True):
+                total = mine[:, at : at + size] + from_y[:, at : at + size]
+                total = total + from_x[:, source : source + size]
+                out_refs[k][:, first + at : first + at + size] = total.astype(BF16)
+            first += part_width(part)
+
+
+def split_z(info, parts, sources):
+    width = sum(part_width(part) for part in parts)
+    specs = [
+        block_spec(*v, part_width(part)) for part, triple in zip(parts, sources) for v in triple
+    ]
+    out = pl.pallas_call(
+        functools.partial(split_kernel, parts),
+        out_shape=(struct((D // 8, width)),) * 4,
         grid_spec=pltpu.PrefetchScalarGridSpec(
             num_scalar_prefetch=1,
             grid=(1,),
-            in_specs=[whole((rows, size))] * 3,
-            out_specs=[whole((rows // 4, size))] * 4,
+            in_specs=specs,
+            out_specs=[whole((D // 8, width))] * 4,
         ),
         cost_estimate=cost(1e6, 4e6),
-        name="split_z",
-    )(info, mine, from_x, from_y)
-
-
-def reduce_parts(info, parts, group, y_first):
-    own_keep, own_leave, far_keep, far_leave = parts
-    if y_first:
-        from_y_leave = flip_mp(far_leave, 2)
-        from_y = flip_mp(after(far_keep, from_y_leave), 2)
-        from_x = flip_dp(add_parts(own_leave, from_y_leave, group, False), 1)
-    else:
-        from_x_far = flip_dp(far_leave, 1)
-        from_x = flip_dp(after(own_leave, from_x_far), 1)
-        from_y = flip_mp(add_parts(far_keep, from_x_far, group, True), 2)
-    mine, *others = split_z(info, own_keep, from_x, from_y, group)
-    total = mine.astype(F32)
-    for k, other in enumerate(others):
-        total = total + flip_dp(other, 2 * (k + 1)).astype(F32)
-    return total
-
-
-def natural_columns(values, group, x_at):
-    rows = values.shape[0]
-    shaped = values.reshape(rows, -1, 2, group)
-    return jnp.where(x_at == 0, shaped, shaped[:, :, ::-1]).reshape(rows, -1)
+    )(info, *[v[0] for triple in sources for v in triple])
+    return [out[0]] + [send_dp(out[k], 2 * k) for k in (1, 2, 3)]
+
+
+def finish_kernel(runs, turned, info_ref, *refs):
+    parts, outs = refs[:4], refs[4:]
+    at = 0
+    for run in runs:
+        for h in range(2):
+            columns = slice(at, at + run.size)
+            total = parts[0][:, columns].astype(F32)
+            for part in parts[1:]:
+                total = total + part[:, columns].astype(F32)
+            spot = pl.ds(pl.multiple_of(run.base + info_ref[h] * run.stride, UNIT), run.size)
+            if turned[run.which]:
+                outs[run.which][spot, :] = total.T
+            else:
+                outs[run.which][:, spot] = total
+            at += run.size
+
+
+def finish(info, values, parts, turned):
+    rows = D // 8
+    runs = tuple(run for part in parts for run in part)
+    sizes = [sum(2 * r.size for r in runs if r.which == k) for k in range(len(turned))]
+    shapes = [(size, rows) if t else (rows, size) for size, t in zip(sizes, turned)]
+    return pl.pallas_call(
+        functools.partial(finish_kernel, runs, turned),
+        out_shape=tuple(struct(shape, F32) for shape in shapes),
+        grid_spec=pltpu.PrefetchScalarGridSpec(
+            num_scalar_prefetch=1,
+            grid=(1,),
+            in_specs=[whole((rows, sum(sizes)))] * 4,
+            out_specs=[whole(shape) for shape in shapes],
+        ),
+        cost_estimate=cost(1e6, 4e6),
+    )(info, *values)
 
 
 def input_grad_kernel(one_ref, *refs):
@@ -1001,7 +1113,7 @@
 
     total = one_ref[...]
     for p in range(4):
-        total = total + dot(grads[p][...], weights[p][...], NT)
+        total = total + dot(grads[p][...], weights[p][...])
     out_ref[...] = total
     sum_ref[0:1, :] += jnp.sum(total, axis=0, keepdims=True)
 
@@ -1015,33 +1127,84 @@
         grid=(LEN // ROWS,),
         in_specs=[tile]
         + [pl.BlockSpec((ROWS, width), lambda i: (i, 0))] * 4
-        + [whole((D, width))] * 4,
+        + [whole((width, D))] * 4,
         out_specs=[tile, whole((8, D))],
         cost_estimate=cost(6.4e9, 20e6),
-        name="input_grad",
     )(grad_one, *d_qkv, *weights)
 
 
-def sum_vectors(rows, place):
-    for flip, bit, at in place:
-        size = rows.shape[0] // 2
-        keep = lax.dynamic_slice_in_dim(rows, at * size, size, 0)
-        leave = lax.dynamic_slice_in_dim(rows, (1 - at) * size, size, 0)
-        rows = keep + flip(leave, bit)
-    return rows[0]
-
-
-def by_device(parts):
-    shaped = parts.reshape(2, 2, 2, 2, 2, -1)
-    return shaped.transpose(4, 3, 2, 0, 1, 5).reshape(32, -1)
-
-
-def gather_rows(rows, order, index):
-    for flip, bit, shift in order:
-        other = flip(rows, bit)
-        low = (index >> shift) & 1
-        rows = jnp.where(low == 0, jnp.concatenate([rows, other]), jnp.concatenate([other, rows]))
-    return rows
+def exchange_kernel(sum_ref, row_ref, total_ref, rows_ref, got, sems_a, sems_b):
+    devices = GRID_DP * GRID_MP
+    me = lax.axis_index("dp") * GRID_MP + lax.axis_index("mp")
+
+    def place(index):
+        return {"dp": index // GRID_MP, "mp": index % GRID_MP}
+
+    barrier = pltpu.get_barrier_semaphore()
+
+    def greet(k, carry):
+        target = (me + k) % devices
+        pl.semaphore_signal(
+            barrier, inc=1, device_id=place(target), device_id_type=pl.DeviceIdType.MESH
+        )
+        return carry
+
+    lax.fori_loop(1, devices, greet, 0)
+    pl.semaphore_wait(barrier, devices - 1)
+
+    def copies(k):
+        target = (me + k) % devices
+        first = pltpu.make_async_remote_copy(
+            src_ref=sum_ref.at[target],
+            dst_ref=got.at[k],
+            send_sem=sems_a.at[0, k],
+            recv_sem=sems_a.at[1, k],
+            device_id=place(target),
+            device_id_type=pl.DeviceIdType.MESH,
+        )
+        second = pltpu.make_async_remote_copy(
+            src_ref=row_ref,
+            dst_ref=rows_ref.at[k],
+            send_sem=sems_b.at[0, k],
+            recv_sem=sems_b.at[1, k],
+            device_id=place(target),
+            device_id_type=pl.DeviceIdType.MESH,
+        )
+        return first, second
+
+    def start(k, carry):
+        for copy in copies(k):
+            copy.start()
+        return carry
+
+    lax.fori_loop(1, devices, start, 0)
+    rows_ref[0] = row_ref[...]
+
+    def finish_copy(k, carry):
+        for copy in copies(k):
+            copy.wait()
+        return carry
+
+    lax.fori_loop(1, devices, finish_copy, 0)
+    total_ref[...] = sum_ref[me] + jnp.sum(got[1:], axis=0)
+
+
+def exchange(sums, row):
+    devices = GRID_DP * GRID_MP
+    vmem = pl.BlockSpec(memory_space=pltpu.VMEM)
+    return pl.pallas_call(
+        exchange_kernel,
+        out_shape=(struct(sums.shape[1:], F32), struct((devices,) + row.shape, F32)),
+        in_specs=[vmem, vmem],
+        out_specs=[vmem, vmem],
+        scratch_shapes=[
+            pltpu.VMEM(sums.shape, F32),
+            pltpu.SemaphoreType.DMA((2, devices)),
+            pltpu.SemaphoreType.DMA((2, devices)),
+        ],
+        compiler_params=pltpu.CompilerParams(collective_id=0, has_side_effects=True),
+        cost_estimate=cost(1e6, 1e6),
+    )(sums, row)
 
 
 def natural_blocks(halves, x_at, mp_at):
@@ -1079,19 +1242,16 @@
 ):
     dp_at, mp_at = lax.axis_index("dp"), lax.axis_index("mp")
     x_at, z_at = dp_at % 2, dp_at // 2
-    y_at, c_at = mp_at // 2, mp_at % 2
     info = jnp.stack([x_at, 1 - x_at, z_at, mp_at]).astype(jnp.int32)
     row = lambda v: v.astype(F32)[None, :]
     width = w_qkv.shape[2]
-    flat = lambda w: w.reshape(D, -1)
-
-    w_all = fetch(w_qkv, 2, x_at, None)
-    qkv_w = [flat(w) for w in w_all]
-    out_w = fetch(w_out, 0, x_at, w_all[2])
-    up_w = fetch(w_up, 1, x_at, out_w[2])
-    down_w = fetch(w_down, 0, x_at, up_w[2])
-    qv_rows = [v.astype(F32) for v in fetch_rows(b_qv, x_at)]
-    up_rows = [v.astype(F32) for v in fetch_rows(b_up[None, :], x_at)]
+
+    heads_own, heads_first = pack_heads(info, w_qkv, w_out)
+    heads = fetch(heads_own, heads_first)
+    up_own, up_first, down_own, down_first = pack_units(info, w_up, w_down)
+    up = fetch(up_own, up_first)
+    down = fetch(down_own, down_first)
+    q_rows, v_rows, up_rows = fetch_bias([b_qv[0:1], b_qv[1:2], b_up[None, :]], x_at)
     zero = jnp.zeros((1, width // 2), F32)
 
     own_step = lax.dynamic_slice_in_dim(time_steps, mp_at, 1, 0)
@@ -1104,26 +1264,23 @@
     win_f, win_b = windows(segment_row, TILE_F), windows(segment_row, TILE_B)
 
     qkv, ctx, lse, qkv_cat = [], [], [], []
-    pairs = [(qkv_w[0],) * 2, (qkv_w[1],) * 2, qkv_w[2:4], qkv_w[4:6]]
     for p in range(4):
-        first, second = qv_rows[2 * p : 2 * p + 2]
+        first, second = 2 * p, 2 * p + 1
         bias = jnp.concatenate(
-            [first[0:1], second[0:1], zero, zero, first[1:2], second[1:2]], axis=1
+            [q_rows[first], q_rows[second], zero, zero, v_rows[first], v_rows[second]], axis=1
         )
-        parts = attend_pair(win_f, info, hidden_low, pairs[p], p >= 2, bias, hotq, hotk)
+        parts = attend_pair(win_f, hidden_low, heads, p, bias, hotq, hotk)
         for kept, part in zip((qkv, ctx, lse, qkv_cat), parts):
             kept.append(part)
     normal_one, scale_one, mid_low, mid_t, hidden_t, out_cat = first_norm(
-        info, tokens, ctx, out_w, embed_row, row(b_out), row(gain_one), row(shift_one)
-    )
-
-    up_pairs = [(up_w[0],) * 2, (up_w[1],) * 2, up_w[2:4], up_w[4:6]]
-    down_pairs = [(down_w[0],) * 2, (down_w[1],) * 2, down_w[2:4], down_w[4:6]]
+        tokens, ctx, heads, embed_row, row(b_out), row(gain_one), row(shift_one)
+    )
+
     act, slope = [], []
     ffn = jnp.broadcast_to(row(b_down), (LEN, D))
     for p in range(4):
         act_p, slope_p, ffn = ffn_pair(
-            info, mid_low, up_pairs[p], down_pairs[p], up_rows[2 * p : 2 * p + 2], ffn, p >= 2
+            mid_low, up, down, p, up_rows[2 * p : 2 * p + 2], ffn
         )
         act.append(act_p)
         slope.append(slope_p)
@@ -1131,94 +1288,137 @@
         ffn, normal_one, cotangent, row(gain_one), row(shift_one), row(gain_two), row(shift_two)
     )
 
-    ff_group = act[0].shape[1] // 2
-    sent_down = flip_mp(grad_send(info, branch_two_t, act[1], act[2], act[3], ff_group), 1)
-    *d_pre, d_mid, sums_up = ffn_back(info, branch_two, down_w, up_w, slope)
-    parts_down = grad_keep(info, branch_two_t, act[0], act[2], act[3], sent_down, ff_group)
-    g_w_down = reduce_parts(info, parts_down, ff_group, True)
-    sent_up = flip_mp(grad_send(info, mid_t, d_pre[1], d_pre[2], d_pre[3], ff_group), 1)
+    units = act[0].shape[1]
+    down_parts = [(run,) for run in unit_runs(2, units)]
+    up_parts = [down_parts[0], (down_parts[1][0], *head_runs(1, 1))]
+    qkv_part = tuple(head_runs(0, 3))
+
+    def two_way(left_t, rights, parts, cover):
+        blocks = tuple((part, far) for part in parts for far in (False, True))
+        one, two = (part_width(part) for part in parts)
+        every = 2 * (one + two)
+        (sent,) = grad_call(info, left_t, [r[1:] for r in rights], blocks, 1, ((0, every, None),))
+        got = send_mp(sent, 1)
+        covered = cover()
+        outputs = (
+            (0, one, None),
+            (one, 2 * one, None),
+            (2 * one, every, 0),
+            (2 * one, every, 1),
+        )
+        result = grad_call(
+            info, left_t, [r[:1] + r[2:] for r in rights], blocks, 0, outputs, got, 0
+        )
+        return covered, result
+
+    def first_sends(blocks):
+        own, far, keep, leave = blocks
+        return own, keep, send_mp(far, 2), send_dp(leave, 1)
+
+    def second_sends(sums, parts):
+        own, keep, from_y, from_x = sums
+        low = add_parts((own, (1, 0)), (from_y, (1, 0)), parts[0], False)
+        x_two = send_dp(low, 1)
+        low = add_parts((keep, (0, 1)), (from_x, (0, 1)), parts[1], True)
+        y_two = send_mp(low, 2)
+        here = (0, 0)
+        return (
+            ((own, here), (x_two, here), (from_y, here)),
+            ((keep, here), (from_x, here), (y_two, here)),
+        )
+
+    def ffn_part():
+        return ffn_back(branch_two, down, up, slope)
+
+    (*d_pre, d_mid, sums_up), down_blocks = two_way([branch_two_t], [act], down_parts, ffn_part)
+    down_sums = first_sends(down_blocks)
     grad_one, branch_one, branch_one_t, sums_one = first_back(
         d_mid, grad_two, normal_one, scale_one, row(gain_one)
     )
-    parts_up = grad_keep(info, mid_t, d_pre[0], d_pre[2], d_pre[3], sent_up, ff_group)
-    g_w_up = reduce_parts(info, parts_up, ff_group, False)
-    sent_out = flip_mp(grad_send(info, branch_one_t, ctx[1], ctx[2], ctx[3], UNIT), 1)
     d_qkv, qkv_sums = [None] * 4, [None] * 4
-    for p in (1, 2, 3, 0):
+
+    def back(p):
         d_qkv[p], qkv_sums[p] = attend_back_pair(
             win_b, qkv[p], hotq, hotk, branch_one, out_cat, p, ctx[p], lse[p]
         )
-        if p == 1:
-            parts_out = grad_keep(info, branch_one_t, ctx[0], ctx[2], ctx[3], sent_out, UNIT)
-            g_w_out = reduce_parts(info, parts_out, UNIT, True)
-        if p == 3:
-            sent_qkv = flip_mp(grad_send(info, hidden_t, d_qkv[1], d_qkv[2], d_qkv[3], UNIT), 1)
-    parts_qkv = grad_keep(info, hidden_t, d_qkv[0], d_qkv[2], d_qkv[3], sent_qkv, UNIT)
-    g_w_qkv = reduce_parts(info, parts_qkv, UNIT, False)
+
+    _, up_blocks = two_way([mid_t, branch_one_t], [d_pre, ctx], up_parts, lambda: back(1))
+    up_sums = first_sends(up_blocks)
+    down_last = second_sends(down_sums, down_parts)
+    back(2)
+    down_values = split_z(info, down_parts, down_last)
+    back(3)
+    up_last = second_sends(up_sums, up_parts)
+    wide = part_width(qkv_part)
+    far_only, own_only = ((qkv_part, True),), ((qkv_part, False),)
+    (sent,) = grad_call(
+        info, [hidden_t], [d_qkv[1:]], own_only + far_only, 1, ((0, 2 * wide, None),)
+    )
+    got = send_mp(sent, 1)
+    up_values = split_z(info, up_parts, up_last)
+    sides = ((0, wide, 0), (0, wide, 1))
+    far_keep, far_leave = grad_call(
+        info, [hidden_t], [[d_qkv[1]] + d_qkv[2:]], far_only, 0, sides, got, wide
+    )
+    far_x = send_dp(far_leave, 1)
+    back(0)
+    own_keep, own_leave = grad_call(
+        info, [hidden_t], [d_qkv[:1] + d_qkv[2:]], own_only, 0, sides, got, 0
+    )
+    own_x = send_dp(own_leave, 1)
+    here = (0, 0)
+    far_low = add_parts((far_keep, here), (far_x, here), qkv_part, True)
+    far_y = send_mp(far_low, 2)
     grad_tokens, sums_in = input_grad(grad_one, d_qkv, qkv_cat)
-
-    place = (
-        (flip_mp, 1, c_at),
-        (flip_mp, 2, y_at),
-        (flip_dp, 1, x_at),
-        (flip_dp, 4, z_at // 2),
-        (flip_dp, 2, z_at % 2),
-    )
-    spread = lambda v: v.reshape(8, 4, -1)
-    spread_blocks = lambda b: b.reshape(4, 8, -1).transpose(1, 0, 2)
-    rows_two = jnp.concatenate(
-        [spread(sums_two[j]) for j in range(3)]
-        + [spread_blocks(natural_blocks([sums_up[j] for j in range(8)], x_at, mp_at))],
-        axis=2,
-    )
-    rows_two = sum_vectors(by_device(rows_two), place)
-    rows_one = jnp.concatenate([spread(sums_one[j]) for j in range(3)], axis=2)
-    rows_one = sum_vectors(by_device(rows_one), place)
-    rows_qkv = []
+    qkv_values = split_z(info, (qkv_part,), (((own_keep, here), (own_x, here), (far_y, here)),))
+
+    spread = lambda v: v.reshape(GRID_DP * GRID_MP, -1)
+    spread_blocks = lambda b: b.reshape(GRID_MP, GRID_DP, -1).transpose(1, 0, 2).reshape(GRID_DP * GRID_MP, -1)
+    rows = [spread(sums[j]) for sums in (sums_two, sums_one) for j in range(3)]
+    rows.append(spread_blocks(natural_blocks([sums_up[j] for j in range(8)], x_at, mp_at)))
     for j in (0, 2):
         halves = [
             qkv_sums[p][0, (2 * j + u) * UNIT : (2 * j + u + 1) * UNIT]
             for p in range(4)
             for u in range(HALF)
         ]
-        rows_qkv.append(spread_blocks(natural_blocks(halves, x_at, mp_at)))
-    rows_qkv = sum_vectors(by_device(jnp.concatenate(rows_qkv, axis=2)), place)
-
+        rows.append(spread_blocks(natural_blocks(halves, x_at, mp_at)))
     tail_row = jnp.concatenate(
         [sums_in[0:1], jnp.broadcast_to(own_step.astype(F32)[None, :], (1, UNIT))], axis=1
     )
-    order = (
-        (flip_mp, 1, 0),
-        (flip_mp, 2, 1),
-        (flip_dp, 1, 2),
-        (flip_dp, 2, 3),
-        (flip_dp, 4, 4),
-    )
+    totals, all_rows = exchange(jnp.concatenate(rows, axis=1)[:, None, :], tail_row)
+    all_rows = all_rows[:, 0]
+    span = D // (GRID_DP * GRID_MP)
+    own = [totals[0, j * span : (j + 1) * span] for j in range(6)]
     device_at = dp_at * GRID_MP + mp_at
-    all_rows = gather_rows(tail_row, order, device_at)
-    span = D // (GRID_DP * GRID_MP)
     all_grads = all_rows[:, :D]
-    own_features = lax.dynamic_slice_in_dim(
-        time_features(all_rows[:, D]), device_at * span, span, 1
-    )
+    dims = device_at * span + jnp.arange(span, dtype=jnp.int32)
+    ladder = (dims % (D // 2)).astype(F32)
+    frequency = jnp.exp(ladder * (-math.log(10000.0) / (D // 2)))
+    angles = all_rows[:, D : D + 1] * frequency[None, :]
+    own_features = jnp.where((dims < D // 2)[None, :], jnp.sin(angles), jnp.cos(angles))
     g_w_time = jnp.dot(own_features.T, all_grads, precision=HIGHEST_PRECISION)
     g_b_time = lax.dynamic_slice_in_dim(jnp.sum(all_grads, axis=0), device_at * span, span, 0)
 
+    (g_w_qkv,) = finish(info, qkv_values, (qkv_part,), (False,))
+    (g_w_down,) = finish(info, down_values, down_parts, (True,))
+    g_w_up, g_w_out = finish(info, up_values, up_parts, (False, True))
+    up_end = totals.shape[1] - 2 * span
     return (
         out_rows,
         grad_tokens,
-        natural_columns(g_w_qkv, UNIT, x_at).reshape(-1, 3, width),
-        rows_qkv.reshape(2, 1, -1),
-        natural_columns(g_w_out, UNIT, x_at).T,
-        rows_one[:span],
-        rows_one[span : 2 * span],
-        rows_one[2 * span :],
-        natural_columns(g_w_up, ff_group, x_at),
-        rows_two[None, 3 * span :],
-        natural_columns(g_w_down, ff_group, x_at).T,
-        rows_two[:span],
-        rows_two[span : 2 * span],
-        rows_two[2 * span : 3 * span],
+        g_w_qkv.reshape(D // 8, 3, width),
+        totals[0, up_end:].reshape(2, 1, -1),
+        g_w_out,
+        own[3],
+        own[4],
+        own[5],
+        g_w_up,
+        totals[:, 6 * span : up_end],
+        g_w_down,
+        own[0],
+        own[1],
+        own[2],
         g_w_time,
         g_b_time,
     )
@@ -1245,9 +1445,12 @@
         P(),
         P(("dp", "mp"), None),
     )
+    rows = mesh.shape["dp"], mesh.shape["mp"]
+
     def body(*args):
-        whole_rows = args[0].shape[0] == LEN and (mesh.shape["dp"], mesh.shape["mp"]) == (GRID_DP, GRID_MP)
-        return (body_rows if whole_rows else body_split)(*args)
+        if args[0].shape[0] != LEN or rows != (GRID_DP, GRID_MP):
+            return body_split(*args)
+        return body_rows(*args)
 
     return jax.shard_map(
         body,

time: 646 us -> 604 us (0.935)
  the two profiles are of different devices: /device:TPU:0 before, /device:TPU:20 now
where the time goes in v3:
time: 604 us; the launch traced here: 595 us
  Pallas kernels  387 us (64%)
  waiting for transfers between devices  125 us (21%)
  starting transfers between devices  34.8 us (6%)
  local copies, waits for them, and re-layouts  28.3 us (5%)
  other arithmetic  14.8 us (2%)
    ppermute x18, waiting for transfers between devices, send_dp(): return lax.ppermute(values, 'dp', [(i, i ^ bit) for i in range(GRID_DP)])  93.7 us
    pallas_call x4, Pallas kernels, attend_back_pair(): pl.pallas_call(attend_back_kernel, out_shape=(struct((LEN, 6 * UNIT)), st...  68.5 us
    pallas_call x7, Pallas kernels, grad_call(): pl.pallas_call(functools.partial(grad_kernel, blocks, side, outputs, left...  66.1 us
    pallas_call x4, Pallas kernels, attend_pair(): pl.pallas_call(attend_kernel, out_shape=(struct((LEN, 6 * UNIT)), struct(...  53.7 us
    pallas_call x4, Pallas kernels, ffn_pair(): pl.pallas_call(ffn_kernel, out_shape=(struct((LEN, 2 * size)), struct((LE...  53.5 us
    pallas_call x1, Pallas kernels, exchange(): pl.pallas_call(exchange_kernel, out_shape=(struct(sums.shape[1:], F32), s...  35.7 us
    ppermute x23, waiting for transfers between devices, send_mp(): return lax.ppermute(values, 'mp', [(i, i ^ bit) for i in range(GRID_MP)])  31.5 us
    pallas_call x1, Pallas kernels, ffn_back(): pl.pallas_call(ffn_back_kernel, out_shape=(struct((LEN, 2 * size)),) * 4...  26.8 us
  transfers between devices with their start and end apart: 41, of which 9 were waited for; matrix products, arithmetic and copies ran while one was open for 6% of the time, Pallas kernels for 59%

profile of v3, /device:TPU:20, one launch (start us, length us, event | category | flops | bytes accessed | tf_op | source)
XLA Modules:
  0.0 594.8 jit_solution(12739264654244783660)
XLA Ops:
  3.4 4.3 shard_map.297
  9.5 5.4 shard_map.303
  24.9 13.4 %shard_map.298 = (bf16[1024,768]{1,0:T(8,128)(2,1)}, bf16[1024,256]{1,0:T(8,128)(2,1)}, f32[2,8,1024]{2,1,0:T(8,128)}, bf16[768,1024]{1,0:T(8,128)(2,1)}) custom-call(s32[2,2]{1,0:T(2,128)} %pad_add_fusion.win_ref, bf16[1024,1024]{1,0:T(8,128)(2,1)} %add_convert_fusion.x_ref, bf16[2,512,1024]{2,1,0:T(8,128)(2,1)} %get-tuple-element.109.refs_0_.refs_1_.refs_4_.refs_5_, ...), custom_call_target="tpu_custom_call" | custom-call | flops 6000000000 | bytes 8000000 | tf_op jit(solution)/shard_map/pallas_call | solution.py:511
  47.5 9.1 %collective-permute-done.8.refs_0_.refs_8_ = bf16[512,1024]{1,0:T(8,128)(2,1)} collective-permute-done((bf16[512,1024]{1,0:T(8,128)(2,1)}, bf16[512,1024]{1,0:T(8,128)(2,1)}, u32[]{:S(2)}, u32[]{:S(2)}) %collective-permute-start.8) | collective-permute-done | bytes 1048608 | tf_op jit(solution)/shard_map/ppermute | solution.py:321
  57.2 21.3 %collective-permute-done.11.refs_2_ = bf16[512,1024]{1,0:T(8,128)(2,1)S(1)} collective-permute-done((bf16[512,1024]{1,0:T(8,128)(2,1)}, bf16[512,1024]{1,0:T(8,128)(2,1)S(1)}, u32[]{:S(2)}, u32[]{:S(2)}) %collective-permute-start.11) | collective-permute-done | bytes 1048608 | tf_op jit(solution)/shard_map/ppermute | solution.py:321
  80.2 13.5 %shard_map.299 = (bf16[1024,768]{1,0:T(8,128)(2,1)}, bf16[1024,256]{1,0:T(8,128)(2,1)}, f32[2,8,1024]{2,1,0:T(8,128)}, bf16[768,1024]{1,0:T(8,128)(2,1)}) custom-call(s32[2,2]{1,0:T(2,128)} %pad_add_fusion.win_ref, bf16[1024,1024]{1,0:T(8,128)(2,1)} %add_convert_fusion.x_ref, bf16[2,512,1024]{2,1,0:T(8,128)(2,1)} %collective-permute-done.refs_0_.refs_1_.refs_6_.refs_7_, ...), custom_call_target="tpu_custom_call" | custom-call | flops 6000000000 | bytes 8000000 | tf_op jit(solution)/shard_map/pallas_call | solution.py:511
  94.8 13.3 %shard_map.300 = (bf16[1024,768]{1,0:T(8,128)(2,1)}, bf16[1024,256]{1,0:T(8,128)(2,1)}, f32[2,8,1024]{2,1,0:T(8,128)}, bf16[768,1024]{1,0:T(8,128)(2,1)}) custom-call(s32[2,2]{1,0:T(2,128)} %pad_add_fusion.win_ref, bf16[1024,1024]{1,0:T(8,128)(2,1)} %add_convert_fusion.x_ref, bf16[512,1024]{1,0:T(8,128)(2,1)} %copy-done.4, bf16[512,1024]{1,0:T(8,128)(2,1)} %copy-done.6, ...), custom_call_target="tpu_custom_call" | custom-call | flops 6000000000 | bytes 8000000 | tf_op jit(solution)/shard_map/pallas_call | solution.py:511
  108.6 13.6 %shard_map.301 = (bf16[1024,768]{1,0:T(8,128)(2,1)}, bf16[1024,256]{1,0:T(8,128)(2,1)}, f32[2,8,1024]{2,1,0:T(8,128)}, bf16[768,1024]{1,0:T(8,128)(2,1)}) custom-call(s32[2,2]{1,0:T(2,128)} %pad_add_fusion.win_ref, bf16[1024,1024]{1,0:T(8,128)(2,1)} %add_convert_fusion.x_ref, bf16[512,1024]{1,0:T(8,128)(2,1)} %copy-done.5, ...), custom_call_target="tpu_custom_call" | custom-call | flops 6000000000 | bytes 8000000 | tf_op jit(solution)/shard_map/pallas_call | solution.py:511
  122.2 10.0 %shard_map.302 = (f32[1024,1024]{1,0:T(8,128)}, f32[1024,1]{1,0:T(8,128)}, bf16[1024,1024]{1,0:T(8,128)(2,1)}, bf16[1024,1024]{1,0:T(8,128)(2,1)}, bf16[1024,102...) custom-call(bf16[1024,1024]{1,0:T(8,128)(2,1)} %tok_ref.1, bf16[1024,256]{1,0:T(8,128)(2,1)} %get-tuple-element.110.refs_0_.ctx_ref.refs_5_, ...), custom_call_target="tpu_custom_call" | custom-call | flops 2200000000 | bytes 20000000 | tf_op jit(solution)/shard_map/pallas_call | solution.py:687
  132.9 2.5 broadcast_in_dim.89.refs_6_
  135.4 13.3 %shard_map.304 = (bf16[1024,1024]{1,0:T(8,128)(2,1)}, bf16[1024,1024]{1,0:T(8,128)(2,1)}, f32[1024,1024]{1,0:T(8,128)}) custom-call(bf16[1024,1024]{1,0:T(8,128)(2,1)} %get-tuple-element.115.mid_ref, bf16[2,512,1024]{2,1,0:T(8,128)(2,1)} %get-tuple-element.118.refs_0_.refs_1_.refs_6_, bf16[2,512,1024]{2,1,0:T(8,128)(2,1)} %get-tuple-element.118.refs_0_.refs_1_.refs_6_, ...), custom_call_target="tpu_custom_call" | custom-call | flops 4300000256 | bytes 18000000 | tf_op jit(solution)/shard_map/pallas_call | solution.py:805
  148.7 13.4 %shard_map.305 = (bf16[1024,1024]{1,0:T(8,128)(2,1)}, bf16[1024,1024]{1,0:T(8,128)(2,1)}, f32[1024,1024]{1,0:T(8,128)}) custom-call(bf16[1024,1024]{1,0:T(8,128)(2,1)} %get-tuple-element.115.mid_ref, bf16[2,512,1024]{2,1,0:T(8,128)(2,1)} %collective-permute-done.16.refs_0_.refs_1_.refs_7_, ...), custom_call_target="tpu_custom_call" | custom-call | flops 4300000256 | bytes 18000000 | tf_op jit(solution)/shard_map/pallas_call | solution.py:805
  163.1 13.5 %shard_map.306 = (bf16[1024,1024]{1,0:T(8,128)(2,1)}, bf16[1024,1024]{1,0:T(8,128)(2,1)}, f32[1024,1024]{1,0:T(8,128)}) custom-call(bf16[1024,1024]{1,0:T(8,128)(2,1)} %get-tuple-element.115.mid_ref, bf16[512,1024]{1,0:T(8,128)(2,1)} %collective-permute-done.8.refs_0_.refs_8_, bf16[512,1024]{1,0:T(8,128)(2,1)} %copy-done.38, bf16[512,1024]{1,0:T(8,128)(2,1)} %copy-done.36, ...), custom_call_target="tpu_custom_call" | custom-call | flops 4300000256 | bytes 18000000 | tf_op jit(solution)/shard_map/pallas_call | solution.py:805
  176.7 13.3 %shard_map.307 = (bf16[1024,1024]{1,0:T(8,128)(2,1)}, bf16[1024,1024]{1,0:T(8,128)(2,1)}, f32[1024,1024]{1,0:T(8,128)}) custom-call(bf16[1024,1024]{1,0:T(8,128)(2,1)} %get-tuple-element.115.mid_ref, bf16[512,1024]{1,0:T(8,128)(2,1)} %collective-permute-done.9.refs_0_.refs_10_, bf16[512,1024]{1,0:T(8,128)(2,1)} %collective-permute-done.10.refs_1_.refs_11_, ...), custom_call_target="tpu_custom_call" | custom-call | flops 4300000256 | bytes 18000000 | tf_op jit(solution)/shard_map/pallas_call | solution.py:805
  189.9 10.1 %shard_map.308 = (bf16[1024,1024]{1,0:T(8,128)(2,1)}, f32[1024,1024]{1,0:T(8,128)}, bf16[1024,1024]{1,0:T(8,128)(2,1)}, bf16[1024,1024]{1,0:T(8,128)(2,1)}, f32[8,1024]{1,0:T(8,128)}) custom-call(f32[1024,1024]{1,0:T(8,128)} %get-tuple-element.123.ffn_ref, f32[1024,1024]{1,0:T(8,128)} %get-tuple-element.124.one_ref, bf16[1024,1024]{1,0:T(8,128)(2,1)} %cot_ref.1, ...), custom_call_target="tpu_custom_call" | custom-call | flops 100000000 | bytes 20000000 | tf_op jit(solution)/shard_map/pallas_call | solution.py:737
  200.1 9.0 %shard_map.329 = bf16[2,512,2048]{2,1,0:T(8,128)(2,1)} custom-call(s32[4]{0:T(128)} %pad_add_fusion.2.info_ref.left_at, bf16[4,2,128,1024]{3,2,1,0:T(8,128)(2,1)} %bitcast.137, bf16[1024,1024]{1,0:T(8,128)(2,1)} %get-tuple-element.192.refs_1_, bf16[1024,1024]{1,0:T(8,128)(2,1)} %get-tuple-element.190.refs_2_, bf16[1024,1024]{1,0:T(8,128)(2,1)} %get-tuple-element.191.refs_3_), custom_call_target="tpu_custom_call" | custom-call | flops 4294967296 | bytes 10000000 | tf_op jit(solution)/shard_map/pallas_call | solution.py:979
  209.5 26.8 %shard_map.309 = (bf16[1024,1024]{1,0:T(8,128)(2,1)}, bf16[1024,1024]{1,0:T(8,128)(2,1)}, bf16[1024,1024]{1,0:T(8,128)(2,1)}, bf16[1024,1024]{1,0:T(8,128)(2,1)}...) custom-call(bf16[1024,1024]{1,0:T(8,128)(2,1)} %get-tuple-element.126.branch_hbm, ...), custom_call_target="tpu_custom_call" | custom-call | flops 16999999488 | bytes 40000000 | tf_op jit(solution)/shard_map/pallas_call | solution.py:871
  236.2 9.4 %shard_map.310 = (f32[1024,1024]{1,0:T(8,128)}, bf16[1024,1024]{1,0:T(8,128)(2,1)}, bf16[1024,1024]{1,0:T(8,128)(2,1)}, f32[8,1024]{1,0:T(8,128)}) custom-call(f32[1024,1024]{1,0:T(8,128)} %get-tuple-element.131.part_ref, f32[1024,1024]{1,0:T(8,128)} %get-tuple-element.132.grad_ref, f32[1024,1024]{1,0:T(8,128)} %get-tuple-element.124.one_ref, ...), custom_call_target="tpu_custom_call" | custom-call | flops 100000000 | bytes 20000000 | tf_op jit(solution)/shard_map/pallas_call | solution.py:774
  245.7 10.9 %shard_map.323 = bf16[2,512,2560]{2,1,0:T(8,128)(2,1)} custom-call(s32[4]{0:T(128)} %pad_add_fusion.2.info_ref.left_at, bf16[4,2,128,1024]{3,2,1,0:T(8,128)(2,1)} %bitcast.135, bf16[4,2,128,1024]{3,2,1,0:T(8,128)(2,1)} %bitcast.139, bf16[1024,1024]{1,0:T(8,128)(2,1)} %get-tuple-element.177.refs_2_, bf16[1024,1024]{1,0:T(8,128)(2,1)} %get-tuple-element.175.refs_3_, ...), custom_call_target="tpu_custom_call" | custom-call | flops 5368709120 | bytes 10000000 | tf_op jit(solution)/shard_map/pallas_call | solution.py:979
  256.8 17.4 %shard_map.314 = (bf16[1024,768]{1,0:T(8,128)(2,1)}, f32[8,768]{1,0:T(8,128)}) custom-call(s32[2,4]{1,0:T(2,128)} %pad_add_fusion.1.win_ref, bf16[1024,768]{1,0:T(8,128)(2,1)} %get-tuple-element.146.qkv_ref, bf16[1024,128]{1,0:T(8,128)(2,1)} %get-tuple-element.299.refs_3_.hotq_ref, bf16[1024,128]{1,0:T(8,128)(2,1)} %get-tuple-element.298.refs_4_.hotk_ref, ...), custom_call_target="tpu_custom_call" | custom-call | flops 8000000000 | bytes 8000000 | tf_op jit(solution)/shard_map/pallas_call | solution.py:620
  274.1 17.0 %shard_map.313 = (bf16[1024,768]{1,0:T(8,128)(2,1)}, f32[8,768]{1,0:T(8,128)}) custom-call(s32[2,4]{1,0:T(2,128)} %pad_add_fusion.1.win_ref, bf16[1024,768]{1,0:T(8,128)(2,1)} %get-tuple-element.143.qkv_ref, bf16[1024,128]{1,0:T(8,128)(2,1)} %get-tuple-element.299.refs_3_.hotq_ref, bf16[1024,128]{1,0:T(8,128)(2,1)} %get-tuple-element.298.refs_4_.hotk_ref, ...), custom_call_target="tpu_custom_call" | custom-call | flops 8000000000 | bytes 8000000 | tf_op jit(solution)/shard_map/pallas_call | solution.py:620
  291.1 17.2 %shard_map.312 = (bf16[1024,768]{1,0:T(8,128)(2,1)}, f32[8,768]{1,0:T(8,128)}) custom-call(s32[2,4]{1,0:T(2,128)} %pad_add_fusion.1.win_ref, bf16[1024,768]{1,0:T(8,128)(2,1)} %get-tuple-element.140.qkv_ref, bf16[1024,128]{1,0:T(8,128)(2,1)} %get-tuple-element.299.refs_3_.hotq_ref, bf16[1024,128]{1,0:T(8,128)(2,1)} %get-tuple-element.298.refs_4_.hotk_ref, ...), custom_call_target="tpu_custom_call" | custom-call | flops 8000000000 | bytes 8000000 | tf_op jit(solution)/shard_map/pallas_call | solution.py:620
  308.3 7.9 %shard_map.316 = bf16[2,512,1536]{2,1,0:T(8,128)(2,1)} custom-call(s32[4]{0:T(128)} %pad_add_fusion.2.info_ref.left_at, bf16[4,2,128,1024]{3,2,1,0:T(8,128)(2,1)} %bitcast.105, bf16[1024,768]{1,0:T(8,128)(2,1)} %get-tuple-element.142.refs_1_, bf16[1024,768]{1,0:T(8,128)(2,1)} %get-tuple-element.145.refs_2_, bf16[1024,768]{1,0:T(8,128)(2,1)} %get-tuple-element.148.refs_3_), custom_call_target="tpu_custom_call" | custom-call | flops 3221225472 | bytes 10000000 | tf_op jit(solution)/shard_map/pallas_call | solution.py:979
  318.0 16.9 %shard_map.311 = (bf16[1024,768]{1,0:T(8,128)(2,1)}, f32[8,768]{1,0:T(8,128)}) custom-call(s32[2,4]{1,0:T(2,128)} %pad_add_fusion.1.win_ref, bf16[1024,768]{1,0:T(8,128)(2,1)} %get-tuple-element.135.qkv_ref, bf16[1024,128]{1,0:T(8,128)(2,1)} %get-tuple-element.299.refs_3_.hotq_ref, bf16[1024,128]{1,0:T(8,128)(2,1)} %get-tuple-element.298.refs_4_.hotk_ref, ...), custom_call_target="tpu_custom_call" | custom-call | flops 8000000000 | bytes 8000000 | tf_op jit(solution)/shard_map/pallas_call | solution.py:620
  337.9 12.6 %shard_map.315 = (f32[1024,1024]{1,0:T(8,128)}, f32[8,1024]{1,0:T(8,128)}) custom-call(f32[1024,1024]{1,0:T(8,128)} %get-tuple-element.134.one_ref, bf16[1024,768]{1,0:T(8,128)(2,1)} %get-tuple-element.139.refs_0_.refs_1_, bf16[1024,768]{1,0:T(8,128)(2,1)} %get-tuple-element.142.refs_1_, bf16[1024,768]{1,0:T(8,128)(2,1)} %get-tuple-element.145.refs_2_, ...), custom_call_target="tpu_custom_call" | custom-call | flops 6400000000 | bytes 20000000 | tf_op jit(solution)/shard_map/pallas_call | solution.py:1124
  350.5 11.3 %shard_map.330 = (bf16[2,512,512]{2,1,0:T(8,128)(2,1)}, bf16[2,512,512]{2,1,0:T(8,128)(2,1)}, bf16[512,1024]{1,0:T(8,128)(2,1)}, bf16[512,1024]{1,0:T(8,128)(2,1)}) custom-call(s32[4]{0:T(128)} %pad_add_fusion.2.info_ref.left_at, bf16[4,2,128,1024]{3,2,1,0:T(8,128)(2,1)} %bitcast.138, bf16[1024,1024]{1,0:T(8,128)(2,1)} %get-tuple-element.189.refs_1_, ...), custom_call_target="tpu_custom_call" | custom-call | flops 4294967296 | bytes 10000000 | tf_op jit(solution)/shard_map/pallas_call | solution.py:979
  363.1 13.8 %shard_map.324 = (bf16[2,512,512]{2,1,0:T(8,128)(2,1)}, bf16[2,512,512]{2,1,0:T(8,128)(2,1)}, bf16[512,1536]{1,0:T(8,128)(2,1)}, bf16[512,1536]{1,0:T(8,128)(2,1)}) custom-call(s32[4]{0:T(128)} %pad_add_fusion.2.info_ref.left_at, bf16[4,2,128,1024]{3,2,1,0:T(8,128)(2,1)} %bitcast.136, bf16[4,2,128,1024]{3,2,1,0:T(8,128)(2,1)} %bitcast.140, ...), custom_call_target="tpu_custom_call" | custom-call | flops 5368709120 | bytes 10000000 | tf_op jit(solution)/shard_map/pallas_call | solution.py:979
  383.0 6.7 %shard_map.318 = (bf16[512,768]{1,0:T(8,128)(2,1)}, bf16[512,768]{1,0:T(8,128)(2,1)}) custom-call(s32[4]{0:T(128)} %pad_add_fusion.2.info_ref.left_at, bf16[4,2,128,1024]{3,2,1,0:T(8,128)(2,1)} %bitcast.106, bf16[1024,768]{1,0:T(8,128)(2,1)} %get-tuple-element.142.refs_1_, bf16[1024,768]{1,0:T(8,128)(2,1)} %get-tuple-element.145.refs_2_, ...), custom_call_target="tpu_custom_call" | custom-call | flops 1610612736 | bytes 10000000 | tf_op jit(solution)/shard_map/pallas_call | solution.py:979
  393.4 2.1 shard_map.331
  397.6 6.7 %shard_map.317 = (bf16[512,768]{1,0:T(8,128)(2,1)}, bf16[512,768]{1,0:T(8,128)(2,1)}) custom-call(s32[4]{0:T(128)} %pad_add_fusion.2.info_ref.left_at, bf16[4,2,128,1024]{3,2,1,0:T(8,128)(2,1)} %bitcast.107, bf16[1024,768]{1,0:T(8,128)(2,1)} %get-tuple-element.139.refs_0_.refs_1_, bf16[1024,768]{1,0:T(8,128)(2,1)} %get-tuple-element.145.refs_2_, ...), custom_call_target="tpu_custom_call" | custom-call | flops 1610612736 | bytes 10000000 | tf_op jit(solution)/shard_map/pallas_call | solution.py:979
  404.2 49.5 %collective-permute-done.20.got_ref = bf16[512,768]{1,0:T(8,128)(2,1)S(1)} collective-permute-done((bf16[512,768]{1,0:T(8,128)(2,1)}, bf16[512,768]{1,0:T(8,128)(2,1)S(1)}, u32[]{:S(2)}, u32[]{:S(2)}) %collective-permute-start.20) | collective-permute-done | bytes 786464 | tf_op jit(solution)/shard_map/ppermute | solution.py:325
  454.6 2.5 shard_map.319
  457.9 2.1 shard_map.332
  461.3 2.3 shard_map.325
  464.8 2.5 shard_map.326
  470.3 35.7 %shard_map.322 = (f32[1,384]{1,0:T(1,128)}, f32[32,1,1152]{2,1,0:T(1,128)}) custom-call(f32[32,1,384]{2,1,0:T(1,128)} %broadcast_in_dim.94.sum_ref, f32[1,1152]{1,0:T(1,128)} %concatenate.247.row_ref), custom_call_target="tpu_custom_call" | custom-call | flops 1000000 | bytes 1000000 | tf_op jit(solution)/shard_map/pallas_call | solution.py:1195
  507.5 3.6 shard_map.333
  511.1 3.2 collective-permute-start.38
  516.1 3.3 shard_map.320
  520.4 2.5 collective-permute-start.24
  524.6 4.0 shard_map.327
  530.1 15.5 %collective-permute-done.23.refs_2_ = bf16[128,768]{1,0:T(8,128)(2,1)S(1)} collective-permute-done((bf16[128,768]{1,0:T(8,128)(2,1)}, bf16[128,768]{1,0:T(8,128)(2,1)S(1)}, u32[]{:S(2)}, u32[]{:S(2)}) %collective-permute-start.23) | collective-permute-done | bytes 196640 | tf_op jit(solution)/shard_map/ppermute | solution.py:325
  546.2 4.2 collective-permute-start.30
  556.3 2.8 shard_map.321
  561.2 16.7 %collective-permute-done.40.refs_3_ = bf16[128,1024]{1,0:T(8,128)(2,1)} collective-permute-done((bf16[128,1024]{1,0:T(8,128)(2,1)}, bf16[128,1024]{1,0:T(8,128)(2,1)}, u32[]{:S(2)}, u32[]{:S(2)}) %collective-permute-start.40) | collective-permute-done | bytes 262176 | tf_op jit(solution)/shard_map/ppermute | solution.py:325
  577.9 2.8 shard_map.334
  582.3 8.4 %collective-permute-done.32.refs_3_ = bf16[128,1280]{1,0:T(8,128)(2,1)S(1)} collective-permute-done((bf16[128,1280]{1,0:T(8,128)(2,1)}, bf16[128,1280]{1,0:T(8,128)(2,1)S(1)}, u32[]{:S(2)}, u32[]{:S(2)}) %collective-permute-start.32) | collective-permute-done | bytes 327712 | tf_op jit(solution)/shard_map/ppermute | solution.py:325
  591.4 2.9 shard_map.328
  (262 shorter events, 72.3 us)
Async XLA Ops:
  2.2 41.1 %collective-permute-start.4 = (bf16[1,1536]{1,0:T(2,128)(2,1)S(1)}, bf16[1,1536]{1,0:T(2,128)(2,1)S(1)}, u32[]{:S(2)}, u32[]{:S(2)}) collective-permute-start(bf16[1,1536]{1,0:T(2,128)(2,1)S(1)} %pad_maximum_fusion.2), channel_id=1, source_target_pairs={{0,2},{1,3},{2,0},{3,1},{4,6},{5,7},{6,4},{7,5},{8,10},{9,11},{10,... | collective-permute-start | bytes 9224 | tf_op jit(solution)/shard_map/ppermute | solution.py:321
  2.8 39.0 %collective-permute-start.1 = (bf16[1,1536]{1,0:T(2,128)(2,1)S(1)}, bf16[1,1536]{1,0:T(2,128)(2,1)S(1)}, u32[]{:S(2)}, u32[]{:S(2)}) collective-permute-start(bf16[1,1536]{1,0:T(2,128)(2,1)S(1)} %pad_maximum_fusion.2), channel_id=1, source_target_pairs={{0,1},{1,0},{2,3},{3,2},{4,5},{5,4},{6,7},{7,6},{8,9},{9,8},{10,11... | collective-permute-start | bytes 9224 | tf_op jit(solution)/shard_map/ppermute | solution.py:321
  7.7 36.8 %collective-permute-start.2 = (bf16[512,1024]{1,0:T(8,128)(2,1)}, bf16[512,1024]{1,0:T(8,128)(2,1)S(1)}, u32[]{:S(2)}, u32[]{:S(2)}) collective-permute-start(bf16[512,1024]{1,0:T(8,128)(2,1)} %get-tuple-element.112), channel_id=1, source_target_pairs={{0,2},{1,3},{2,0},{3,1},{4,6},{5,7},{6,4},{7,5},{8,10},{9,11},{10,... | collective-permute-start | bytes 3145736 | tf_op jit(solution)/shard_map/ppermute | solution.py:321
  9.3 70.8 %collective-permute-start = (bf16[2,512,1024]{2,1,0:T(8,128)(2,1)}, bf16[2,512,1024]{2,1,0:T(8,128)(2,1)}, u32[]{:S(2)}, u32[]{:S(2)}) collective-permute-start(bf16[2,512,1024]{2,1,0:T(8,128)(2,1)} %get-tuple-element.109.refs_0_.refs_1_.refs_4_.refs_5_), channel_id=1, source_target_pairs={{0,1},{1,0},{2,3},{3,2},{4,5},{5,4},{6,7},{7,6},{8,9},{9,8},{10,11... | collective-permute-start | bytes 6291464 | tf_op jit(solution)/shard_map/ppermute | solution.py:321
  14.9 41.7 %collective-permute-start.8 = (bf16[512,1024]{1,0:T(8,128)(2,1)}, bf16[512,1024]{1,0:T(8,128)(2,1)}, u32[]{:S(2)}, u32[]{:S(2)}) collective-permute-start(bf16[512,1024]{1,0:T(8,128)(2,1)} %get-tuple-element.116), channel_id=1, source_target_pairs={{0,2},{1,3},{2,0},{3,1},{4,6},{5,7},{6,4},{7,5},{8,10},{9,11},{10,... | collective-permute-start | bytes 3145736 | tf_op jit(solution)/shard_map/ppermute | solution.py:321
  41.8 36.7 %collective-permute-start.11 = (bf16[512,1024]{1,0:T(8,128)(2,1)}, bf16[512,1024]{1,0:T(8,128)(2,1)S(1)}, u32[]{:S(2)}, u32[]{:S(2)}) collective-permute-start(bf16[512,1024]{1,0:T(8,128)(2,1)} %get-tuple-element.117), channel_id=1, source_target_pairs={{0,2},{1,3},{2,0},{3,1},{4,6},{5,7},{6,4},{7,5},{8,10},{9,11},{10,... | collective-permute-start | bytes 3145736 | tf_op jit(solution)/shard_map/ppermute | solution.py:321
  44.5 49.1 %copy-start.4 = (bf16[512,1024]{1,0:T(8,128)(2,1)}, bf16[512,1024]{1,0:T(8,128)(2,1)S(1)}, u32[]{:S(2)}) copy-start(bf16[512,1024]{1,0:T(8,128)(2,1)S(1)} %collective-permute-done.2.refs_0_.refs_8_) | copy-start | bytes 3145732
  44.5 33.9 %collective-permute-start.6 = (bf16[512,1024]{1,0:T(8,128)(2,1)S(1)}, bf16[512,1024]{1,0:T(8,128)(2,1)S(1)}, u32[]{:S(2)}, u32[]{:S(2)}) collective-permute-start(bf16[512,1024]{1,0:T(8,128)(2,1)S(1)} %collective-permute-done.2.refs_0_.refs_8_), channel_id=1, source_target_pairs={{0,4},{4,0},{8,12},{12,8},{16,20},{20,16},{24,28},{28,24},{1,5},{5... | collective-permute-start | bytes 3145736 | tf_op jit(solution)/shard_map/ppermute | solution.py:325
  46.0 1.2 collective-permute-start.5
  46.1 34.2 %copy-start.41 = (f32[1,768]{1,0:T(1,128)}, f32[1,768]{1,0:T(1,128)S(1)}, u32[]{:S(2)}) copy-start(f32[1,768]{1,0:T(1,128)S(1)} %constant_dynamic-update-slice_fusion.5.refs_2_) | copy-start | bytes 9220
  47.2 46.5 %collective-permute-start.3 = (bf16[512,1024]{1,0:T(8,128)(2,1)S(1)}, bf16[512,1024]{1,0:T(8,128)(2,1)S(1)}, u32[]{:S(2)}, u32[]{:S(2)}) collective-permute-start(bf16[512,1024]{1,0:T(8,128)(2,1)S(1)} %collective-permute-done.2.refs_0_.refs_8_), channel_id=1, source_target_pairs={{0,1},{1,0},{2,3},{3,2},{4,5},{5,4},{6,7},{7,6},{8,9},{9,8},{10,11... | collective-permute-start | bytes 3145736 | tf_op jit(solution)/shard_map/ppermute | solution.py:321
  56.6 76.2 %collective-permute-start.16 = (bf16[2,512,1024]{2,1,0:T(8,128)(2,1)}, bf16[2,512,1024]{2,1,0:T(8,128)(2,1)}, u32[]{:S(2)}, u32[]{:S(2)}) collective-permute-start(bf16[2,512,1024]{2,1,0:T(8,128)(2,1)} %get-tuple-element.118.refs_0_.refs_1_.refs_6_), channel_id=1, source_target_pairs={{0,1},{1,0},{2,3},{3,2},{4,5},{5,4},{6,7},{7,6},{8,9},{9,8},{10,11... | collective-permute-start | bytes 6291464 | tf_op jit(solution)/shard_map/ppermute | solution.py:321
  56.6 37.1 %copy-start.34 = (f32[1,768]{1,0:T(1,128)}, f32[1,768]{1,0:T(1,128)S(1)}, u32[]{:S(2)}) copy-start(f32[1,768]{1,0:T(1,128)S(1)} %get-tuple-element.324.refs_2_) | copy-start | bytes 9220
  56.6 37.1 %copy-start.35 = (f32[1,768]{1,0:T(1,128)}, f32[1,768]{1,0:T(1,128)S(1)}, u32[]{:S(2)}) copy-start(f32[1,768]{1,0:T(1,128)S(1)} %get-tuple-element.325.refs_2_) | copy-start | bytes 9220
  78.5 70.2 %collective-permute-start.17 = (bf16[2,512,1024]{2,1,0:T(8,128)(2,1)}, bf16[2,512,1024]{2,1,0:T(8,128)(2,1)}, u32[]{:S(2)}, u32[]{:S(2)}) collective-permute-start(bf16[2,512,1024]{2,1,0:T(8,128)(2,1)} %get-tuple-element.119.refs_2_.refs_3_.refs_0_), channel_id=1, source_target_pairs={{0,1},{1,0},{2,3},{3,2},{4,5},{5,4},{6,7},{7,6},{8,9},{9,8},{10,11... | collective-permute-start | bytes 6291464 | tf_op jit(solution)/shard_map/ppermute | solution.py:321
  78.5 29.5 %collective-permute-start.9 = (bf16[512,1024]{1,0:T(8,128)(2,1)}, bf16[512,1024]{1,0:T(8,128)(2,1)}, u32[]{:S(2)}, u32[]{:S(2)}) collective-permute-start(bf16[512,1024]{1,0:T(8,128)(2,1)} %collective-permute-done.8.refs_0_.refs_8_), channel_id=1, source_target_pairs={{0,4},{4,0},{8,12},{12,8},{16,20},{20,16},{24,28},{28,24},{1,5},{5... | collective-permute-start | bytes 3145736 | tf_op jit(solution)/shard_map/ppermute | solution.py:325
  80.1 28.4 %collective-permute-start.7 = (bf16[512,1024]{1,0:T(8,128)(2,1)S(1)}, bf16[512,1024]{1,0:T(8,128)(2,1)}, u32[]{:S(2)}, u32[]{:S(2)}) collective-permute-start(bf16[512,1024]{1,0:T(8,128)(2,1)S(1)} %collective-permute-done.6.refs_0_.refs_10_), channel_id=1, source_target_pairs={{0,1},{1,0},{2,3},{3,2},{4,5},{5,4},{6,7},{7,6},{8,9},{9,8},{10,11... | collective-permute-start | bytes 3145736 | tf_op jit(solution)/shard_map/ppermute | solution.py:321
  93.7 38.5 %collective-permute-start.12 = (bf16[512,1024]{1,0:T(8,128)(2,1)}, bf16[512,1024]{1,0:T(8,128)(2,1)}, u32[]{:S(2)}, u32[]{:S(2)}) collective-permute-start(bf16[512,1024]{1,0:T(8,128)(2,1)} %copy-done.36), channel_id=1, source_target_pairs={{0,4},{4,0},{8,12},{12,8},{16,20},{20,16},{24,28},{28,24},{1,5},{5... | collective-permute-start | bytes 3145736 | tf_op jit(solution)/shard_map/ppermute | solution.py:325
  108.1 54.1 %collective-permute-start.14 = (bf16[512,1024]{1,0:T(8,128)(2,1)}, bf16[512,1024]{1,0:T(8,128)(2,1)S(1)}, u32[]{:S(2)}, u32[]{:S(2)}) collective-permute-start(bf16[512,1024]{1,0:T(8,128)(2,1)} %collective-permute-done.8.refs_0_.refs_8_), channel_id=1, source_target_pairs={{0,1},{1,0},{2,3},{3,2},{4,5},{5,4},{6,7},{7,6},{8,9},{9,8},{10,11... | collective-permute-start | bytes 3145736 | tf_op jit(solution)/shard_map/ppermute | solution.py:321
  108.5 53.6 %collective-permute-start.15 = (bf16[512,1024]{1,0:T(8,128)(2,1)S(1)}, bf16[512,1024]{1,0:T(8,128)(2,1)}, u32[]{:S(2)}, u32[]{:S(2)}) collective-permute-start(bf16[512,1024]{1,0:T(8,128)(2,1)S(1)} %copy-done.37), channel_id=1, source_target_pairs={{0,1},{1,0},{2,3},{3,2},{4,5},{5,4},{6,7},{7,6},{8,9},{9,8},{10,11... | collective-permute-start | bytes 3145736 | tf_op jit(solution)/shard_map/ppermute | solution.py:321
  132.3 44.4 %collective-permute-start.10 = (bf16[512,1024]{1,0:T(8,128)(2,1)}, bf16[512,1024]{1,0:T(8,128)(2,1)}, u32[]{:S(2)}, u32[]{:S(2)}) collective-permute-start(bf16[512,1024]{1,0:T(8,128)(2,1)} %collective-permute-done.9.refs_0_.refs_10_), channel_id=1, source_target_pairs={{0,1},{1,0},{2,3},{3,2},{4,5},{5,4},{6,7},{7,6},{8,9},{9,8},{10,11... | collective-permute-start | bytes 3145736 | tf_op jit(solution)/shard_map/ppermute | solution.py:321
  132.7 43.9 %collective-permute-start.13 = (bf16[512,1024]{1,0:T(8,128)(2,1)}, bf16[512,1024]{1,0:T(8,128)(2,1)}, u32[]{:S(2)}, u32[]{:S(2)}) collective-permute-start(bf16[512,1024]{1,0:T(8,128)(2,1)} %collective-permute-done.12.refs_2_.refs_4_), channel_id=1, source_target_pairs={{0,1},{1,0},{2,3},{3,2},{4,5},{5,4},{6,7},{7,6},{8,9},{9,8},{10,11... | collective-permute-start | bytes 3145736 | tf_op jit(solution)/shard_map/ppermute | solution.py:321
  209.0 141.5 %collective-permute-start.33 = (bf16[2,512,2048]{2,1,0:T(8,128)(2,1)}, bf16[2,512,2048]{2,1,0:T(8,128)(2,1)}, u32[]{:S(2)}, u32[]{:S(2)}) collective-permute-start(bf16[2,512,2048]{2,1,0:T(8,128)(2,1)} %shard_map.329), channel_id=1, source_target_pairs={{0,1},{1,0},{2,3},{3,2},{4,5},{5,4},{6,7},{7,6},{8,9},{9,8},{10,11... | collective-permute-start | bytes 12582920 | tf_op jit(solution)/shard_map/ppermute | solution.py:321
  256.5 106.6 %collective-permute-start.25 = (bf16[2,512,2560]{2,1,0:T(8,128)(2,1)}, bf16[2,512,2560]{2,1,0:T(8,128)(2,1)}, u32[]{:S(2)}, u32[]{:S(2)}) collective-permute-start(bf16[2,512,2560]{2,1,0:T(8,128)(2,1)} %shard_map.323), channel_id=1, source_target_pairs={{0,1},{1,0},{2,3},{3,2},{4,5},{5,4},{6,7},{7,6},{8,9},{9,8},{10,11... | collective-permute-start | bytes 15728648 | tf_op jit(solution)/shard_map/ppermute | solution.py:321
  316.2 65.1 %collective-permute-start.18 = (bf16[2,512,1536]{2,1,0:T(8,128)(2,1)}, bf16[2,512,1536]{2,1,0:T(8,128)(2,1)S(1)}, u32[]{:S(2)}, u32[]{:S(2)}) collective-permute-start(bf16[2,512,1536]{2,1,0:T(8,128)(2,1)} %shard_map.316), channel_id=1, source_target_pairs={{0,1},{1,0},{2,3},{3,2},{4,5},{5,4},{6,7},{7,6},{8,9},{9,8},{10,11... | collective-permute-start | bytes 9437192 | tf_op jit(solution)/shard_map/ppermute | solution.py:321
  361.9 31.6 %collective-permute-start.34 = (bf16[2,512,512]{2,1,0:T(8,128)(2,1)}, bf16[2,512,512]{2,1,0:T(8,128)(2,1)}, u32[]{:S(2)}, u32[]{:S(2)}) collective-permute-start(bf16[2,512,512]{2,1,0:T(8,128)(2,1)} %get-tuple-element.194), channel_id=1, source_target_pairs={{0,2},{1,3},{2,0},{3,1},{4,6},{5,7},{6,4},{7,5},{8,10},{9,11},{10,... | collective-permute-start | bytes 3145736 | tf_op jit(solution)/shard_map/ppermute | solution.py:321
  376.9 86.8 %collective-permute-start.28 = (bf16[512,1536]{1,0:T(8,128)(2,1)}, bf16[512,1536]{1,0:T(8,128)(2,1)}, u32[]{:S(2)}, u32[]{:S(2)}) collective-permute-start(bf16[512,1536]{1,0:T(8,128)(2,1)} %get-tuple-element.181), channel_id=1, source_target_pairs={{0,4},{4,0},{8,12},{12,8},{16,20},{20,16},{24,28},{28,24},{1,5},{5... | collective-permute-start | bytes 4718600 | tf_op jit(solution)/shard_map/ppermute | solution.py:325
  378.4 78.7 %collective-permute-start.36 = (bf16[512,1024]{1,0:T(8,128)(2,1)}, bf16[512,1024]{1,0:T(8,128)(2,1)}, u32[]{:S(2)}, u32[]{:S(2)}) collective-permute-start(bf16[512,1024]{1,0:T(8,128)(2,1)} %get-tuple-element.196), channel_id=1, source_target_pairs={{0,4},{4,0},{8,12},{12,8},{16,20},{20,16},{24,28},{28,24},{1,5},{5... | collective-permute-start | bytes 3145736 | tf_op jit(solution)/shard_map/ppermute | solution.py:325
  380.5 79.6 %collective-permute-start.26 = (bf16[2,512,512]{2,1,0:T(8,128)(2,1)}, bf16[2,512,512]{2,1,0:T(8,128)(2,1)}, u32[]{:S(2)}, u32[]{:S(2)}) collective-permute-start(bf16[2,512,512]{2,1,0:T(8,128)(2,1)} %get-tuple-element.179), channel_id=1, source_target_pairs={{0,2},{1,3},{2,0},{3,1},{4,6},{5,7},{6,4},{7,5},{8,10},{9,11},{10,... | collective-permute-start | bytes 3145736 | tf_op jit(solution)/shard_map/ppermute | solution.py:321
  389.7 64.1 %collective-permute-start.20 = (bf16[512,768]{1,0:T(8,128)(2,1)}, bf16[512,768]{1,0:T(8,128)(2,1)S(1)}, u32[]{:S(2)}, u32[]{:S(2)}) collective-permute-start(bf16[512,768]{1,0:T(8,128)(2,1)} %get-tuple-element.158), channel_id=1, source_target_pairs={{0,4},{4,0},{8,12},{12,8},{16,20},{20,16},{24,28},{28,24},{1,5},{5... | collective-permute-start | bytes 2359304 | tf_op jit(solution)/shard_map/ppermute | solution.py:325
  395.5 71.7 %collective-permute-start.35 = (bf16[512,512]{1,0:T(8,128)(2,1)}, bf16[512,512]{1,0:T(8,128)(2,1)S(1)}, u32[]{:S(2)}, u32[]{:S(2)}) collective-permute-start(bf16[512,512]{1,0:T(8,128)(2,1)} %shard_map.331), channel_id=1, source_target_pairs={{0,4},{4,0},{8,12},{12,8},{16,20},{20,16},{24,28},{28,24},{1,5},{5... | collective-permute-start | bytes 1572872 | tf_op jit(solution)/shard_map/ppermute | solution.py:325
  453.8 61.2 %collective-permute-start.19 = (bf16[512,768]{1,0:T(8,128)(2,1)}, bf16[512,768]{1,0:T(8,128)(2,1)S(1)}, u32[]{:S(2)}, u32[]{:S(2)}) collective-permute-start(bf16[512,768]{1,0:T(8,128)(2,1)} %get-tuple-element.156), channel_id=1, source_target_pairs={{0,4},{4,0},{8,12},{12,8},{16,20},{20,16},{24,28},{28,24},{1,5},{5... | collective-permute-start | bytes 2359304 | tf_op jit(solution)/shard_map/ppermute | solution.py:325
  457.1 57.9 %collective-permute-start.21 = (bf16[512,768]{1,0:T(8,128)(2,1)}, bf16[512,768]{1,0:T(8,128)(2,1)S(1)}, u32[]{:S(2)}, u32[]{:S(2)}) collective-permute-start(bf16[512,768]{1,0:T(8,128)(2,1)} %shard_map.319), channel_id=1, source_target_pairs={{0,2},{1,3},{2,0},{3,1},{4,6},{5,7},{6,4},{7,5},{8,10},{9,11},{10,... | collective-permute-start | bytes 2359304 | tf_op jit(solution)/shard_map/ppermute | solution.py:321
  460.1 47.4 %collective-permute-start.37 = (bf16[512,512]{1,0:T(8,128)(2,1)}, bf16[512,512]{1,0:T(8,128)(2,1)}, u32[]{:S(2)}, u32[]{:S(2)}) collective-permute-start(bf16[512,512]{1,0:T(8,128)(2,1)} %shard_map.332), channel_id=1, source_target_pairs={{0,2},{1,3},{2,0},{3,1},{4,6},{5,7},{6,4},{7,5},{8,10},{9,11},{10,... | collective-permute-start | bytes 1572872 | tf_op jit(solution)/shard_map/ppermute | solution.py:321
  463.6 56.8 %collective-permute-start.27 = (bf16[512,512]{1,0:T(8,128)(2,1)}, bf16[512,512]{1,0:T(8,128)(2,1)S(1)}, u32[]{:S(2)}, u32[]{:S(2)}) collective-permute-start(bf16[512,512]{1,0:T(8,128)(2,1)} %shard_map.325), channel_id=1, source_target_pairs={{0,4},{4,0},{8,12},{12,8},{16,20},{20,16},{24,28},{28,24},{1,5},{5... | collective-permute-start | bytes 1572872 | tf_op jit(solution)/shard_map/ppermute | solution.py:325
  467.2 40.3 %copy-start.11 = (bf16[512,512]{1,0:T(8,128)(2,1)}, bf16[512,512]{1,0:T(8,128)(2,1)S(1)}, u32[]{:S(2)}) copy-start(bf16[512,512]{1,0:T(8,128)(2,1)S(1)} %collective-permute-done.35.refs_1_) | copy-start | bytes 1572868
  467.2 56.3 %collective-permute-start.29 = (bf16[512,768]{1,0:T(8,128)(2,1)}, bf16[512,768]{1,0:T(8,128)(2,1)S(1)}, u32[]{:S(2)}, u32[]{:S(2)}) collective-permute-start(bf16[512,768]{1,0:T(8,128)(2,1)} %shard_map.326), channel_id=1, source_target_pairs={{0,2},{1,3},{2,0},{3,1},{4,6},{5,7},{6,4},{7,5},{8,10},{9,11},{10,... | collective-permute-start | bytes 2359304 | tf_op jit(solution)/shard_map/ppermute | solution.py:321
  511.1 41.4 %collective-permute-start.38 = (bf16[128,1024]{1,0:T(8,128)(2,1)}, bf16[128,1024]{1,0:T(8,128)(2,1)}, u32[]{:S(2)}, u32[]{:S(2)}) collective-permute-start(bf16[128,1024]{1,0:T(8,128)(2,1)} %get-tuple-element.198), channel_id=1, source_target_pairs={{0,8},{4,12},{8,0},{12,4},{16,24},{20,28},{24,16},{28,20},{1,9},{5... | collective-permute-start | bytes 786440 | tf_op jit(solution)/shard_map/ppermute | solution.py:325
  519.4 9.2 %collective-permute-start.22 = (bf16[128,768]{1,0:T(8,128)(2,1)}, bf16[128,768]{1,0:T(8,128)(2,1)S(1)}, u32[]{:S(2)}, u32[]{:S(2)}) collective-permute-start(bf16[128,768]{1,0:T(8,128)(2,1)} %get-tuple-element.160), channel_id=1, source_target_pairs={{0,8},{4,12},{8,0},{12,4},{16,24},{20,28},{24,16},{28,20},{1,9},{5... | collective-permute-start | bytes 589832 | tf_op jit(solution)/shard_map/ppermute | solution.py:325
  519.4 26.1 %collective-permute-start.23 = (bf16[128,768]{1,0:T(8,128)(2,1)}, bf16[128,768]{1,0:T(8,128)(2,1)S(1)}, u32[]{:S(2)}, u32[]{:S(2)}) collective-permute-start(bf16[128,768]{1,0:T(8,128)(2,1)} %get-tuple-element.161), channel_id=1, source_target_pairs={{0,16},{4,20},{8,24},{12,28},{16,0},{20,4},{24,8},{28,12},{1,17},{... | collective-permute-start | bytes 589832 | tf_op jit(solution)/shard_map/ppermute | solution.py:325
  520.4 32.0 %collective-permute-start.24 = (bf16[128,768]{1,0:T(8,128)(2,1)}, bf16[128,768]{1,0:T(8,128)(2,1)S(1)}, u32[]{:S(2)}, u32[]{:S(2)}) collective-permute-start(bf16[128,768]{1,0:T(8,128)(2,1)} %get-tuple-element.162), channel_id=1, source_target_pairs={{0,24},{4,28},{8,16},{12,20},{16,8},{20,12},{24,0},{28,4},{1,25},{... | collective-permute-start | bytes 589832 | tf_op jit(solution)/shard_map/ppermute | solution.py:325
  523.5 31.6 %copy-start.25 = (f32[32]{0:T(128)S(1)}, f32[32]{0:T(128)}, u32[]{:S(2)}) copy-start(f32[32]{0:T(128)} %slice_reduce_fusion.1) | copy-start | bytes 388
  523.6 37.6 %collective-permute-start.39 = (bf16[128,1024]{1,0:T(8,128)(2,1)}, bf16[128,1024]{1,0:T(8,128)(2,1)}, u32[]{:S(2)}, u32[]{:S(2)}) collective-permute-start(bf16[128,1024]{1,0:T(8,128)(2,1)} %get-tuple-element.199), channel_id=1, source_target_pairs={{0,16},{4,20},{8,24},{12,28},{16,0},{20,4},{24,8},{28,12},{1,17},{... | collective-permute-start | bytes 786440 | tf_op jit(solution)/shard_map/ppermute | solution.py:325
  528.6 49.3 %collective-permute-start.40 = (bf16[128,1024]{1,0:T(8,128)(2,1)}, bf16[128,1024]{1,0:T(8,128)(2,1)}, u32[]{:S(2)}, u32[]{:S(2)}) collective-permute-start(bf16[128,1024]{1,0:T(8,128)(2,1)} %get-tuple-element.200), channel_id=1, source_target_pairs={{0,24},{4,28},{8,16},{12,20},{16,8},{20,12},{24,0},{28,4},{1,25},{... | collective-permute-start | bytes 786440 | tf_op jit(solution)/shard_map/ppermute | solution.py:325
  546.2 34.5 %collective-permute-start.30 = (bf16[128,1280]{1,0:T(8,128)(2,1)}, bf16[128,1280]{1,0:T(8,128)(2,1)S(1)}, u32[]{:S(2)}, u32[]{:S(2)}) collective-permute-start(bf16[128,1280]{1,0:T(8,128)(2,1)} %get-tuple-element.183), channel_id=1, source_target_pairs={{0,8},{4,12},{8,0},{12,4},{16,24},{20,28},{24,16},{28,20},{1,9},{5... | collective-permute-start | bytes 983048 | tf_op jit(solution)/shard_map/ppermute | solution.py:325
  552.5 29.8 %collective-permute-start.31 = (bf16[128,1280]{1,0:T(8,128)(2,1)}, bf16[128,1280]{1,0:T(8,128)(2,1)S(1)}, u32[]{:S(2)}, u32[]{:S(2)}) collective-permute-start(bf16[128,1280]{1,0:T(8,128)(2,1)} %get-tuple-element.184), channel_id=1, source_target_pairs={{0,16},{4,20},{8,24},{12,28},{16,0},{20,4},{24,8},{28,12},{1,17},{... | collective-permute-start | bytes 983048 | tf_op jit(solution)/shard_map/ppermute | solution.py:325
  552.5 38.2 %collective-permute-start.32 = (bf16[128,1280]{1,0:T(8,128)(2,1)}, bf16[128,1280]{1,0:T(8,128)(2,1)S(1)}, u32[]{:S(2)}, u32[]{:S(2)}) collective-permute-start(bf16[128,1280]{1,0:T(8,128)(2,1)} %get-tuple-element.185), channel_id=1, source_target_pairs={{0,24},{4,28},{8,16},{12,20},{16,8},{20,12},{24,0},{28,4},{1,25},{... | collective-permute-start | bytes 983048 | tf_op jit(solution)/shard_map/ppermute | solution.py:325
  556.3 38.1 %copy-start.1 = (bf16[1024,1024]{1,0:T(8,128)(2,1)S(1)}, bf16[1024,1024]{1,0:T(8,128)(2,1)}, u32[]{:S(2)}) copy-start(bf16[1024,1024]{1,0:T(8,128)(2,1)} %param.33) | copy-start | bytes 6291460
  (35 other events, 332.2 us)

commit v4 on v3

--- a/solution.py
+++ b/solution.py
@@ -288,6 +288,7 @@
 BF16 = jnp.bfloat16
 TILE_F = 512
 TILE_B = 256
+TILE_U = 256
 ROWS = 256
 GRAIN = 256
 STEP = 128
@@ -311,6 +312,14 @@
 
 def struct(shape, kind=BF16):
     return jax.ShapeDtypeStruct(shape, kind)
+
+
+def far(shape, kind=BF16):
+    return pltpu.HBM(shape, kind)
+
+
+def room(mib):
+    return pltpu.CompilerParams(vmem_limit_bytes=mib * 2**20)
 
 
 def cost(flops, moved):
@@ -354,6 +363,7 @@
             in_specs=[whole((3, D, 2 * UNIT)), whole((2 * UNIT, D))],
             out_specs=[whole((HALF, 4 * UNIT, D)), whole((4 * UNIT, D))],
         ),
+        compiler_params=room(24),
         cost_estimate=cost(1e6, 5e6),
     )(info, w_qkv.transpose(1, 0, 2), w_out)
 
@@ -384,6 +394,7 @@
             ],
             out_specs=[pl.BlockSpec((1, size, D), lambda i, info: (i, 0, 0)), whole((size, D))] * 2,
         ),
+        compiler_params=room(24),
         cost_estimate=cost(1e6, 10e6),
     )(info, w_up, w_down)
 
@@ -511,10 +522,9 @@
     return pl.pallas_call(
         attend_kernel,
         out_shape=(
-            struct((LEN, 6 * UNIT)),
-            struct((LEN, 2 * UNIT)),
-            struct((HALF, 8, LEN), F32),
-            struct((6 * UNIT, D)),
+            far((LEN, 6 * UNIT)),
+            far((LEN, 2 * UNIT)),
+            far((HALF, 8, LEN), F32),
         ),
         grid_spec=pltpu.PrefetchScalarGridSpec(
             num_scalar_prefetch=1,
@@ -530,10 +540,10 @@
                 whole((LEN, 6 * UNIT)),
                 pl.BlockSpec((TILE_F, UNIT), lambda n, i, win: (i, n)),
                 pl.BlockSpec((1, 8, TILE_F), lambda n, i, win: (n, 0, i)),
-                whole((6 * UNIT, D)),
             ],
-            scratch_shapes=[pltpu.VMEM((HALF, LEN, UNIT), BF16)],
+            scratch_shapes=[pltpu.VMEM((6 * UNIT, D), BF16), pltpu.VMEM((HALF, LEN, UNIT), BF16)],
         ),
+        compiler_params=room(32),
         cost_estimate=cost(6e9, 8e6),
     )(win, hidden_low, *pair_of(heads, pair), bias, hotq, hotk)
 
@@ -544,7 +554,8 @@
     hotq_ref,
     hotk_ref,
     branch_ref,
-    wout_ref,
+    wa_ref,
+    wb_ref,
     ctx_ref,
     lse_ref,
     out_ref,
@@ -562,7 +573,9 @@
     def _():
         for r in range(LEN // ROWS):
             rows = slice(r * ROWS, (r + 1) * ROWS)
-            grads[rows, :] = dot(branch_ref[rows, :], wout_ref[...], NT).astype(BF16)
+            for u, ref in enumerate((wa_ref, wb_ref)):
+                part = dot(branch_ref[rows, :], rows_of(ref), NT)
+                grads[rows, u * UNIT : (u + 1) * UNIT] = part.astype(BF16)
 
     @pl.when(step == 0)
     def _():
@@ -616,10 +629,10 @@
         sum_ref[...] = jnp.broadcast_to(total, sum_ref.shape)
 
 
-def attend_back_pair(win, qkv, hotq, hotk, branch_one, wout_all, pair, ctx, lse):
+def attend_back_pair(win, qkv, hotq, hotk, branch_one, heads, pair, ctx, lse):
     return pl.pallas_call(
         attend_back_kernel,
-        out_shape=(struct((LEN, 6 * UNIT)), struct((8, 6 * UNIT), F32)),
+        out_shape=(far((LEN, 6 * UNIT)), struct((8, 6 * UNIT), F32)),
         grid_spec=pltpu.PrefetchScalarGridSpec(
             num_scalar_prefetch=1,
             grid=(HALF, LEN // TILE_B),
@@ -628,7 +641,7 @@
                 pl.BlockSpec((TILE_B, UNIT), lambda n, i, win: (i, 0)),
                 whole((LEN, UNIT)),
                 whole((LEN, D)),
-                pl.BlockSpec((2 * UNIT, D), lambda n, i, win: (pair, 0)),
+                *pair_specs(UNIT, 3, pair),
                 pl.BlockSpec((TILE_B, UNIT), lambda n, i, win: (i, n)),
                 pl.BlockSpec((1, 8, TILE_B), lambda n, i, win: (n, 0, i)),
             ],
@@ -641,8 +654,9 @@
                 pltpu.VMEM((LEN, UNIT), F32),
             ],
         ),
+        compiler_params=room(32),
         cost_estimate=cost(8e9, 8e6),
-    )(win, qkv, hotq, hotk, branch_one, wout_all, ctx, lse)
+    )(win, qkv, hotq, hotk, branch_one, *pair_of(heads, pair), ctx, lse)
 
 
 def norm_of(values):
@@ -674,7 +688,7 @@
     for p in range(4):
         total = total + dot(ctx_refs[p][...], wout_ref[2 * p * UNIT : 2 * (p + 1) * UNIT, :])
     normal, scale = norm_of(hidden + total)
-    normal_ref[...] = normal
+    normal_ref[...] = normal.astype(BF16)
     scale_ref[...] = scale
     mid = (normal * gain_ref[...] + shift_ref[...]).astype(BF16)
     mid_ref[...] = mid
@@ -687,12 +701,11 @@
     return pl.pallas_call(
         first_norm_kernel,
         out_shape=(
-            struct((LEN, D), F32),
-            struct((LEN, 1), F32),
-            struct((LEN, D)),
-            struct((D, LEN)),
-            struct((D, LEN)),
-            struct((D, D)),
+        far((LEN, D)),
+        far((LEN, 1), F32),
+        struct((LEN, D)),
+        far((D, LEN)),
+        far((D, LEN)),
         ),
         grid=(LEN // ROWS,),
         in_specs=[tile]
@@ -705,26 +718,79 @@
             tile,
             column,
             column,
-            whole((D, D)),
         ],
+        scratch_shapes=[pltpu.VMEM((D, D), BF16)],
+        compiler_params=room(24),
         cost_estimate=cost(2.2e9, 20e6),
     )(tokens, *contexts, *eight(heads), embed_row, b_out, gain, shift)
 
 
-def second_norm_kernel(
-    ffn_ref, one_ref, cot_ref, gain1, shift1, gain2, shift2, out_ref, grad_ref, low_ref, low_t, sum_ref
-):
+def ffn_tile(mid_ref, up_refs, down_refs, bias_refs, act_ref, slope_ref):
+    size = bias_refs[0].shape[1]
+    pres = [
+        dot(mid_ref[...], rows_of(up), NT) + bias[...] for up, bias in zip(up_refs, bias_refs)
+    ]
+    total = 0.0
+    for u in range(HALF):
+        columns = slice(u * size, (u + 1) * size)
+        pre = pres[u]
+        phi = 0.5 * (1.0 + lax.erf(pre * math.sqrt(0.5)))
+        bell = jnp.exp(-0.5 * pre * pre) * (1.0 / math.sqrt(2.0 * math.pi))
+        act = (pre * phi).astype(BF16)
+        act_ref[:, columns] = act
+        slope_ref[:, columns] = (phi + pre * bell).astype(BF16)
+        total = total + dot(act, rows_of(down_refs[u]))
+    return total
+
+
+def ffn_kernel(mid_ref, *refs):
+    *into, act_ref, slope_ref, total_ref = refs[6:]
+    total = ffn_tile(mid_ref, refs[0:2], refs[2:4], refs[4:6], act_ref, slope_ref)
+    for ref in into:
+        total = total + ref[...]
+    total_ref[...] = total
+
+
+def ffn_specs(size, pair):
+    return (
+        [pl.BlockSpec((TILE_U, D), lambda i: (i, 0))]
+        + pair_specs(size, 0, pair) * 2
+        + [whole((1, size))] * 2
+    )
+
+
+def ffn_pair(mid_low, up, down, pair, bias, into):
+    size = bias[0].shape[1]
+    tile = lambda n: pl.BlockSpec((TILE_U, n), lambda i: (i, 0))
+    return pl.pallas_call(
+        ffn_kernel,
+        out_shape=(
+            far((LEN, 2 * size)),
+            far((LEN, 2 * size)),
+            struct((LEN, D), F32),
+        ),
+        in_specs=ffn_specs(size, pair) + [tile(D)] * len(into),
+        out_specs=[tile(2 * size), tile(2 * size), tile(D)],
+        grid=(LEN // TILE_U,),
+        compiler_params=room(24),
+        cost_estimate=cost(4.3e9, 18e6),
+    )(mid_low, *pair_of(up, pair), *pair_of(down, pair), *bias, *into)
+
+
+def ffn_last_kernel(mid_ref, *refs):
+    into_ref, cot_ref, bias_ref, gain_ref, shift_ref = refs[6:11]
+    act_ref, slope_ref, out_ref, low_ref, low_t, sum_ref = refs[11:]
+
     @pl.when(pl.program_id(0) == 0)
     def _():
         sum_ref[...] = jnp.zeros_like(sum_ref)
 
-    mid = one_ref[...] * gain1[...] + shift1[...]
-    normal, scale = norm_of(mid + ffn_ref[...])
-    out_ref[...] = (normal * gain2[...] + shift2[...]).astype(BF16)
+    total = ffn_tile(mid_ref, refs[0:2], refs[2:4], refs[4:6], act_ref, slope_ref)
+    total = total + into_ref[...] + bias_ref[...]
+    normal, scale = norm_of(mid_ref[...].astype(F32) + total)
+    out_ref[...] = (normal * gain_ref[...] + shift_ref[...]).astype(BF16)
     cot = cot_ref[...].astype(F32)
-    grad = norm_back(normal, scale, cot, gain2[...])
-    grad_ref[...] = grad
-    low = grad.astype(BF16)
+    low = norm_back(normal, scale, cot, gain_ref[...]).astype(BF16)
     low_ref[...] = low
     low_t[...] = low.T
     sums = [jnp.sum(v, axis=0, keepdims=True) for v in (low.astype(F32), cot * normal, cot)]
@@ -732,97 +798,42 @@
         sum_ref[j : j + 1, :] += sums[j]
 
 
-def second_norm(ffn, normal_one, cot, *rows):
-    tile = pl.BlockSpec((ROWS, D), lambda i: (i, 0))
+def ffn_last(mid_low, up, down, pair, bias, into, cot, *rows):
+    size = bias[0].shape[1]
+    tile = lambda n: pl.BlockSpec((TILE_U, n), lambda i: (i, 0))
     return pl.pallas_call(
-        second_norm_kernel,
+        ffn_last_kernel,
         out_shape=(
-            struct((LEN, D)),
-            struct((LEN, D), F32),
+            far((LEN, 2 * size)),
+            far((LEN, 2 * size)),
+            far((LEN, D)),
             struct((LEN, D)),
             struct((D, LEN)),
             struct((8, D), F32),
         ),
-        grid=(LEN // ROWS,),
-        in_specs=[tile] * 3 + [whole((1, D))] * 4,
-        out_specs=[tile] * 3 + [pl.BlockSpec((D, ROWS), lambda i: (0, i)), whole((8, D))],
-        cost_estimate=cost(1e8, 20e6),
-    )(ffn, normal_one, cot, *rows)
-
-
-def first_back_kernel(
-    part_ref, grad_ref, one_ref, scale_ref, gain_ref, out_ref, low_ref, low_t, sum_ref
-):
-    @pl.when(pl.program_id(0) == 0)
-    def _():
-        sum_ref[...] = jnp.zeros_like(sum_ref)
-
-    d_mid = part_ref[...] + grad_ref[...]
-    normal = one_ref[...]
-    grad = norm_back(normal, scale_ref[...], d_mid, gain_ref[...])
-    out_ref[...] = grad
-    low = grad.astype(BF16)
-    low_ref[...] = low
-    low_t[...] = low.T
-    sums = [jnp.sum(v, axis=0, keepdims=True) for v in (low.astype(F32), d_mid * normal, d_mid)]
-    for j in range(3):
-        sum_ref[j : j + 1, :] += sums[j]
-
-
-def first_back(part, grad_two, normal_one, scale_one, gain):
-    tile = pl.BlockSpec((ROWS, D), lambda i: (i, 0))
-    return pl.pallas_call(
-        first_back_kernel,
-        out_shape=(struct((LEN, D), F32), struct((LEN, D)), struct((D, LEN)), struct((8, D), F32)),
-        grid=(LEN // ROWS,),
-        in_specs=[tile] * 3 + [pl.BlockSpec((ROWS, 1), lambda i: (i, 0)), whole((1, D))],
-        out_specs=[tile, tile, pl.BlockSpec((D, ROWS), lambda i: (0, i)), whole((8, D))],
-        cost_estimate=cost(1e8, 20e6),
-    )(part, grad_two, normal_one, scale_one, gain)
-
-
-def ffn_kernel(mid_ref, *refs):
-    up_refs, down_refs, bias_refs = refs[0:2], refs[2:4], refs[4:6]
-    into_ref, act_ref, slope_ref, total_ref = refs[6:]
-    size = bias_refs[0].shape[1]
-    for u in range(HALF):
-        up, down = rows_of(up_refs[u]), rows_of(down_refs[u])
-        columns = slice(u * size, (u + 1) * size)
-        for r in range(LEN // ROWS):
-            rows = slice(r * ROWS, (r + 1) * ROWS)
-            pre = dot(mid_ref[rows, :], up, NT) + bias_refs[u][...]
-            phi = 0.5 * (1.0 + lax.erf(pre * math.sqrt(0.5)))
-            bell = jnp.exp(-0.5 * pre * pre) * (1.0 / math.sqrt(2.0 * math.pi))
-            act = (pre * phi).astype(BF16)
-            act_ref[rows, columns] = act
-            slope_ref[rows, columns] = (phi + pre * bell).astype(BF16)
-            before = into_ref[rows, :] if u == 0 else total_ref[rows, :]
-            total_ref[rows, :] = before + dot(act, down)
-
-
-def ffn_pair(mid_low, up, down, pair, bias, into):
-    size = bias[0].shape[1]
-    return pl.pallas_call(
-        ffn_kernel,
-        out_shape=(
-            struct((LEN, 2 * size)),
-            struct((LEN, 2 * size)),
-            struct((LEN, D), F32),
-        ),
-        in_specs=[whole((LEN, D))]
-        + pair_specs(size, 0, pair) * 2
-        + [whole((1, size))] * 2
-        + [whole((LEN, D))],
-        out_specs=[whole((LEN, 2 * size)), whole((LEN, 2 * size)), whole((LEN, D))],
-        grid=(1,),
-        cost_estimate=cost(4.3e9, 18e6),
-    )(mid_low, *pair_of(up, pair), *pair_of(down, pair), *bias, into)
+        in_specs=ffn_specs(size, pair) + [tile(D)] * 2 + [whole((1, D))] * 3,
+        out_specs=[tile(2 * size), tile(2 * size), tile(D), tile(D)]
+        + [pl.BlockSpec((D, TILE_U), lambda i: (0, i)), whole((8, D))],
+        grid=(LEN // TILE_U,),
+        compiler_params=room(30),
+        cost_estimate=cost(4.3e9, 30e6),
+    )(
+        mid_low, *pair_of(up, pair), *pair_of(down, pair), *bias, into, cot, *rows
+    )
 
 
 def ffn_back_kernel(branch_hbm, *refs):
     down_hbm, up_hbm, slope_hbm, refs = refs[0:6], refs[6:12], refs[12:16], refs[16:]
-    pre_refs, total_ref, sum_ref, refs = refs[0:4], refs[4], refs[5], refs[6:]
-    branch, down, up, slope, sems = refs
+    one_hbm, scale_ref, gain_ref, refs = refs[0], refs[1], refs[2], refs[3:]
+    pre_hbm, sum_ref, low_ref, low_t, norm_sum_ref, refs = (
+        refs[0:4],
+        refs[4],
+        refs[5],
+        refs[6],
+        refs[7],
+        refs[8:],
+    )
+    branch, down, up, slope, total, one, sems = refs
     size = up.shape[1]
     plan = ((0, 0), (0, 1), (1, 0), (1, 1), (2, None), (3, None), (4, None), (5, None))
     first = pltpu.make_async_copy(branch_hbm, branch, sems.at[0])
@@ -833,56 +844,80 @@
             down_part, up_part = down_hbm[piece], up_hbm[piece]
         else:
             down_part, up_part = down_hbm[piece].at[which], up_hbm[piece].at[which]
+        columns = slice((j % 2) * size, (j % 2 + 1) * size)
         group = [
             pltpu.make_async_copy(down_part, down.at[j], sems.at[1 + 3 * j]),
             pltpu.make_async_copy(
-                slope_hbm[j // 2].at[:, (j % 2) * size : (j % 2 + 1) * size],
-                slope.at[j],
-                sems.at[2 + 3 * j],
+                slope_hbm[j // 2].at[:, columns], slope.at[j], sems.at[2 + 3 * j]
             ),
             pltpu.make_async_copy(up_part, up.at[j], sems.at[3 + 3 * j]),
         ]
         for copy in group:
             copy.start()
         copies.append(group)
+    last = pltpu.make_async_copy(one_hbm, one, sems.at[25])
+    last.start()
     first.wait()
+    stores = []
+    norm_sums = [0.0] * 3
     for j in range(len(plan)):
         for copy in copies[j]:
             copy.wait()
+        if j == len(plan) - 1:
+            last.wait()
         columns = slice((j % 2) * size, (j % 2 + 1) * size)
         sums = 0.0
         for r in range(LEN // ROWS):
             rows = slice(r * ROWS, (r + 1) * ROWS)
             d_act = dot(branch[rows, :], down[j], NT)
             d_pre = (d_act * slope[j, rows, :].astype(F32)).astype(BF16)
-            pre_refs[j // 2][rows, columns] = d_pre
+            slope[j, rows, :] = d_pre
             sums = sums + jnp.sum(d_pre.astype(F32), axis=0, keepdims=True)
             part = dot(d_pre, up[j])
             if j == 0:
-                total_ref[rows, :] = part
+                total[rows, :] = part
+            elif j < len(plan) - 1:
+                total[rows, :] += part
             else:
-                total_ref[rows, :] += part
+                d_mid = total[rows, :] + part + branch[rows, :].astype(F32)
+                normal = one[rows, :].astype(F32)
+                low = norm_back(normal, scale_ref[rows, :], d_mid, gain_ref[...]).astype(BF16)
+                low_ref[rows, :] = low
+                low_t[:, rows] = low.T
+                for k, v in enumerate((low.astype(F32), d_mid * normal, d_mid)):
+                    norm_sums[k] = norm_sums[k] + jnp.sum(v, axis=0, keepdims=True)
         sum_ref[j : j + 1, :] = sums
-
-
-def ffn_back(branch_two, down, up, slopes):
+        store = pltpu.make_async_copy(slope.at[j], pre_hbm[j // 2].at[:, columns], sems.at[26 + j])
+        store.start()
+        stores.append(store)
+    for k in range(3):
+        norm_sum_ref[k : k + 1, :] = norm_sums[k]
+    for store in stores:
+        store.wait()
+
+
+def ffn_back(branch_two, down, up, slopes, normal_one, scale_one, gain):
     size = down[2].shape[0]
     hbm = pl.BlockSpec(memory_space=pl.ANY)
     return pl.pallas_call(
         ffn_back_kernel,
-        out_shape=(struct((LEN, 2 * size)),) * 4 + (struct((LEN, D), F32), struct((8, size), F32)),
+        out_shape=(far((LEN, 2 * size)),) * 4
+        + (struct((8, size), F32), struct((LEN, D)), struct((D, LEN)), struct((8, D), F32)),
         grid=(1,),
-        in_specs=[hbm] * 17,
-        out_specs=[whole((LEN, 2 * size))] * 4 + [whole((LEN, D)), whole((8, size))],
+        in_specs=[hbm] * 18 + [whole((LEN, 1)), whole((1, D))],
+        out_specs=[hbm] * 4 + [whole((8, size)), whole((LEN, D)), whole((D, LEN)), whole((8, D))],
         scratch_shapes=[
             pltpu.VMEM((LEN, D), BF16),
             pltpu.VMEM((8, size, D), BF16),
             pltpu.VMEM((8, size, D), BF16),
             pltpu.VMEM((8, LEN, size), BF16),
-            pltpu.SemaphoreType.DMA((25,)),
+            pltpu.VMEM((LEN, D), F32),
+            pltpu.VMEM((LEN, D), BF16),
+            pltpu.SemaphoreType.DMA((34,)),
         ],
+        compiler_params=room(52),
         cost_estimate=cost(17e9, 40e6),
-    )(branch_two, *down, *up, *slopes)
+    )(branch_two, *down, *up, *slopes, normal_one, scale_one, gain)
 
 
 class Run(NamedTuple):
@@ -978,7 +1013,7 @@
     ]
     return pl.pallas_call(
         functools.partial(grad_kernel, blocks, side, outputs, lefts, got_from),
-        out_shape=tuple(struct(shape) for shape in shapes),
+        out_shape=tuple(far(shape) for shape in shapes),
         grid_spec=pltpu.PrefetchScalarGridSpec(
             num_scalar_prefetch=1,
             grid=(1,),
@@ -992,6 +1027,7 @@
                 pltpu.SemaphoreType.DMA((48,)),
             ],
         ),
+        compiler_params=room(32),
         cost_estimate=cost(2 * D * LEN * width, 10e6),
     )(info, *operands)
 
@@ -1028,6 +1064,7 @@
         grid=(1,),
         in_specs=[block_spec(*v, width) for v in (mine, got)],
         out_specs=whole((D // 2, width)),
+        compiler_params=room(24),
         cost_estimate=cost(1e6, 3e6),
     )(mine[0], got[0])
 
@@ -1064,6 +1101,7 @@
             in_specs=specs,
             out_specs=[whole((D // 8, width))] * 4,
         ),
+        compiler_params=room(24),
         cost_estimate=cost(1e6, 4e6),
     )(info, *[v[0] for triple in sources for v in triple])
     return [out[0]] + [send_dp(out[k], 2 * k) for k in (1, 2, 3)]
@@ -1100,37 +1138,62 @@
             in_specs=[whole((rows, sum(sizes)))] * 4,
             out_specs=[whole(shape) for shape in shapes],
         ),
+        compiler_params=room(24),
         cost_estimate=cost(1e6, 4e6),
     )(info, *values)
 
 
-def input_grad_kernel(one_ref, *refs):
-    grads, weights, out_ref, sum_ref = refs[:4], refs[4:8], refs[8], refs[9]
-
-    @pl.when(pl.program_id(0) == 0)
+def input_grad_kernel(branch_ref, *refs):
+    grads, heads, (out_ref, sum_ref, weight, sems) = refs[:4], refs[4:10], refs[10:]
+    step = pl.program_id(0)
+    plan = ((0, 0), (0, 1), (1, 0), (1, 1), (2, None), (3, None), (4, None), (5, None))
+    copies = []
+    for j, (piece, which) in enumerate(plan):
+        source = heads[piece] if which is None else heads[piece].at[which]
+        for k in range(3):
+            at = ((j // 2) * 6 + 2 * k + j % 2) * UNIT
+            copies.append(
+                pltpu.make_async_copy(
+                    source.at[k * UNIT : (k + 1) * UNIT, :],
+                    weight.at[at : at + UNIT, :],
+                    sems.at[3 * j + k],
+                )
+            )
+
+    @pl.when(step == 0)
     def _():
+        for copy in copies:
+            copy.start()
         sum_ref[...] = jnp.zeros_like(sum_ref)
 
-    total = one_ref[...]
+    total = branch_ref[...].astype(F32)
     for p in range(4):
-        total = total + dot(grads[p][...], weights[p][...])
+
+        @pl.when(step == 0)
+        def _():
+            for copy in copies[6 * p : 6 * p + 6]:
+                copy.wait()
+
+        total = total + dot(grads[p][...], weight[6 * p * UNIT : 6 * (p + 1) * UNIT, :])
     out_ref[...] = total
     sum_ref[0:1, :] += jnp.sum(total, axis=0, keepdims=True)
 
 
-def input_grad(grad_one, d_qkv, weights):
+def input_grad(branch_one, d_qkv, heads):
     tile = pl.BlockSpec((ROWS, D), lambda i: (i, 0))
     width = d_qkv[0].shape[1]
     return pl.pallas_call(
         input_grad_kernel,
-        out_shape=(struct((LEN, D), F32), struct((8, D), F32)),
+        out_shape=(far((LEN, D), F32), struct((8, D), F32)),
         grid=(LEN // ROWS,),
         in_specs=[tile]
         + [pl.BlockSpec((ROWS, width), lambda i: (i, 0))] * 4
-        + [whole((width, D))] * 4,
+        + [pl.BlockSpec(memory_space=pl.ANY)] * 6,
         out_specs=[tile, whole((8, D))],
+        scratch_shapes=[pltpu.VMEM((4 * width, D), BF16), pltpu.SemaphoreType.DMA((24,))],
+        compiler_params=room(26),
         cost_estimate=cost(6.4e9, 20e6),
-    )(grad_one, *d_qkv, *weights)
+    )(branch_one, *d_qkv, *heads)
 
 
 def exchange_kernel(sum_ref, row_ref, total_ref, rows_ref, got, sems_a, sems_b):
@@ -1263,30 +1326,36 @@
     hotq, hotk = mark_segments(segment_row)
     win_f, win_b = windows(segment_row, TILE_F), windows(segment_row, TILE_B)
 
-    qkv, ctx, lse, qkv_cat = [], [], [], []
+    qkv, ctx, lse = [], [], []
     for p in range(4):
         first, second = 2 * p, 2 * p + 1
         bias = jnp.concatenate(
             [q_rows[first], q_rows[second], zero, zero, v_rows[first], v_rows[second]], axis=1
         )
         parts = attend_pair(win_f, hidden_low, heads, p, bias, hotq, hotk)
-        for kept, part in zip((qkv, ctx, lse, qkv_cat), parts):
+        for kept, part in zip((qkv, ctx, lse), parts):
             kept.append(part)
-    normal_one, scale_one, mid_low, mid_t, hidden_t, out_cat = first_norm(
+    normal_one, scale_one, mid_low, mid_t, hidden_t = first_norm(
         tokens, ctx, heads, embed_row, row(b_out), row(gain_one), row(shift_one)
     )
 
-    act, slope = [], []
-    ffn = jnp.broadcast_to(row(b_down), (LEN, D))
-    for p in range(4):
-        act_p, slope_p, ffn = ffn_pair(
-            mid_low, up, down, p, up_rows[2 * p : 2 * p + 2], ffn
-        )
+    act, slope, ffn = [], [], ()
+    for p in range(3):
+        act_p, slope_p, *ffn = ffn_pair(mid_low, up, down, p, up_rows[2 * p : 2 * p + 2], ffn)
         act.append(act_p)
         slope.append(slope_p)
-    out_rows, grad_two, branch_two, branch_two_t, sums_two = second_norm(
-        ffn, normal_one, cotangent, row(gain_one), row(shift_one), row(gain_two), row(shift_two)
-    )
+    act_p, slope_p, out_rows, branch_two, branch_two_t, sums_two = ffn_last(
+        mid_low,
+        up,
+        down,
+        3,
+        up_rows[6:8],
+        *ffn,
+        cotangent,
+        *[row(v) for v in (b_down, gain_two, shift_two)],
+    )
+    act.append(act_p)
+    slope.append(slope_p)
 
     units = act[0].shape[1]
     down_parts = [(run,) for run in unit_runs(2, units)]
@@ -1328,23 +1397,24 @@
         )
 
     def ffn_part():
-        return ffn_back(branch_two, down, up, slope)
-
-    (*d_pre, d_mid, sums_up), down_blocks = two_way([branch_two_t], [act], down_parts, ffn_part)
+        return ffn_back(
+            branch_two, down, up, slope, normal_one, scale_one, row(gain_one)
+        )
+
+    (*d_pre, sums_up, branch_one, branch_one_t, sums_one), down_blocks = two_way(
+        [branch_two_t], [act], down_parts, ffn_part
+    )
     down_sums = first_sends(down_blocks)
-    grad_one, branch_one, branch_one_t, sums_one = first_back(
-        d_mid, grad_two, normal_one, scale_one, row(gain_one)
-    )
     d_qkv, qkv_sums = [None] * 4, [None] * 4
 
     def back(p):
         d_qkv[p], qkv_sums[p] = attend_back_pair(
-            win_b, qkv[p], hotq, hotk, branch_one, out_cat, p, ctx[p], lse[p]
+            win_b, qkv[p], hotq, hotk, branch_one, heads, p, ctx[p], lse[p]
         )
 
     _, up_blocks = two_way([mid_t, branch_one_t], [d_pre, ctx], up_parts, lambda: back(1))
+    down_last = second_sends(down_sums, down_parts)
     up_sums = first_sends(up_blocks)
-    down_last = second_sends(down_sums, down_parts)
     back(2)
     down_values = split_z(info, down_parts, down_last)
     back(3)
@@ -1362,14 +1432,14 @@
     )
     far_x = send_dp(far_leave, 1)
     back(0)
-    own_keep, own_leave = grad_call(
-        info, [hidden_t], [d_qkv[:1] + d_qkv[2:]], own_only, 0, sides, got, 0
-    )
-    own_x = send_dp(own_leave, 1)
     here = (0, 0)
     far_low = add_parts((far_keep, here), (far_x, here), qkv_part, True)
     far_y = send_mp(far_low, 2)
-    grad_tokens, sums_in = input_grad(grad_one, d_qkv, qkv_cat)
+    own_keep, own_leave = grad_call(
+        info, [hidden_t], [d_qkv[:1] + d_qkv[2:]], own_only, 0, sides, got, 0
+    )
+    own_x = send_dp(own_leave, 1)
+    grad_tokens, sums_in = input_grad(branch_one, d_qkv, heads)
     qkv_values = split_z(info, (qkv_part,), (((own_keep, here), (own_x, here), (far_y, here)),))
 
     spread = lambda v: v.reshape(GRID_DP * GRID_MP, -1)

time: 604 us -> 571 us (0.945)
  the two profiles are of different devices: /device:TPU:20 before, /device:TPU:12 now
where the time goes in v4:
time: 571 us; the launch traced here: 562 us
  Pallas kernels  320 us (56%)
  waiting for transfers between devices  120 us (21%)
  local copies, waits for them, and re-layouts  65.4 us (11%)
  starting transfers between devices  47.5 us (8%)
    ppermute x18, waiting for transfers between devices, send_dp(): return lax.ppermute(values, 'dp', [(i, i ^ bit) for i in range(GRID_DP)])  80 us
    pallas_call x4, Pallas kernels, attend_back_pair(): pl.pallas_call(attend_back_kernel, out_shape=(far((LEN, 6 * UNIT)), struc...  60.4 us
    pallas_call x4, Pallas kernels, attend_pair(): pl.pallas_call(attend_kernel, out_shape=(far((LEN, 6 * UNIT)), far((LEN,...  56.4 us
    pallas_call x7, Pallas kernels, grad_call(): pl.pallas_call(functools.partial(grad_kernel, blocks, side, outputs, left...  54.8 us
    unnamed x218, local copies, waits for them, and re-layouts  53.4 us
    ppermute x23, waiting for transfers between devices, send_mp(): return lax.ppermute(values, 'mp', [(i, i ^ bit) for i in range(GRID_MP)])  39.9 us
    pallas_call x1, Pallas kernels, exchange(): pl.pallas_call(exchange_kernel, out_shape=(struct(sums.shape[1:], F32), s...  37.7 us
    ppermute x18, starting transfers between devices, send_dp(): return lax.ppermute(values, 'dp', [(i, i ^ bit) for i in range(GRID_DP)])  36.2 us
  transfers between devices with their start and end apart: 41, of which 12 were waited for; matrix products, arithmetic and copies ran while one was open for 3% of the time, Pallas kernels for 53%

profile of v4, /device:TPU:12, one launch (start us, length us, event | category | flops | bytes accessed | tf_op | source)
XLA Modules:
  0.0 561.6 jit_solution(17370663845396128448)
XLA Ops:
  5.5 2.7 shard_map.297
  11.5 2.6 shard_map.303
  22.9 11.8 %shard_map.298 = (bf16[1024,768]{1,0:T(8,128)(2,1)}, bf16[1024,256]{1,0:T(8,128)(2,1)}, f32[2,8,1024]{2,1,0:T(8,128)}) custom-call(s32[2,2]{1,0:T(2,128)S(1)} %pad_add_fusion.win_ref, bf16[1024,1024]{1,0:T(8,128)(2,1)S(1)} %add_convert_fusion.x_ref, bf16[2,512,1024]{2,1,0:T(8,128)(2,1)} %get-tuple-element.100.refs_0_.refs_1_.refs_4_.refs_5_.wa_ref.wb_ref, ...), custom_call_target="tpu_custom_call" | custom-call | flops 6000000000 | bytes 8000000 | tf_op jit(solution)/shard_map/pallas_call | solution.py:522
  40.1 16.8 %collective-permute-done.8.refs_0_.refs_8_ = bf16[512,1024]{1,0:T(8,128)(2,1)} collective-permute-done((bf16[512,1024]{1,0:T(8,128)(2,1)}, bf16[512,1024]{1,0:T(8,128)(2,1)}, u32[]{:S(2)}, u32[]{:S(2)}) %collective-permute-start.8) | collective-permute-done | bytes 1048608 | tf_op jit(solution)/shard_map/ppermute | solution.py:330
  57.0 21.9 %collective-permute-done.11.refs_2_ = bf16[512,1024]{1,0:T(8,128)(2,1)S(1)} collective-permute-done((bf16[512,1024]{1,0:T(8,128)(2,1)}, bf16[512,1024]{1,0:T(8,128)(2,1)S(1)}, u32[]{:S(2)}, u32[]{:S(2)}) %collective-permute-start.11) | collective-permute-done | bytes 1048608 | tf_op jit(solution)/shard_map/ppermute | solution.py:330
  81.5 12.0 %shard_map.299 = (bf16[1024,768]{1,0:T(8,128)(2,1)}, bf16[1024,256]{1,0:T(8,128)(2,1)}, f32[2,8,1024]{2,1,0:T(8,128)}) custom-call(s32[2,2]{1,0:T(2,128)S(1)} %pad_add_fusion.win_ref, bf16[1024,1024]{1,0:T(8,128)(2,1)S(1)} %add_convert_fusion.x_ref, bf16[2,512,1024]{2,1,0:T(8,128)(2,1)} %collective-permute-done.refs_0_.refs_1_.refs_6_.refs_7_.wa_ref.wb_ref.refs_5_, ...), custom_call_target="tpu_custom_call" | custom-call | flops 6000000000 | bytes 8000000 | tf_op jit(solution)/shard_map/pallas_call | solution.py:522
  94.2 10.2 %shard_map.300 = (bf16[1024,768]{1,0:T(8,128)(2,1)}, bf16[1024,256]{1,0:T(8,128)(2,1)}, f32[2,8,1024]{2,1,0:T(8,128)}) custom-call(s32[2,2]{1,0:T(2,128)S(1)} %pad_add_fusion.win_ref, bf16[1024,1024]{1,0:T(8,128)(2,1)S(1)} %add_convert_fusion.x_ref, bf16[512,1024]{1,0:T(8,128)(2,1)S(1)} %collective-permute-done.2.refs_0_.refs_8_.wa_ref.refs_6_, ...), custom_call_target="tpu_custom_call" | custom-call | flops 6000000000 | bytes 8000000 | tf_op jit(solution)/shard_map/pallas_call | solution.py:522
  105.6 22.3 %shard_map.301 = (bf16[1024,768]{1,0:T(8,128)(2,1)}, bf16[1024,256]{1,0:T(8,128)(2,1)}, f32[2,8,1024]{2,1,0:T(8,128)}) custom-call(s32[2,2]{1,0:T(2,128)S(1)} %pad_add_fusion.win_ref, bf16[1024,1024]{1,0:T(8,128)(2,1)S(1)} %add_convert_fusion.x_ref, bf16[512,1024]{1,0:T(8,128)(2,1)S(1)} %collective-permute-done.6.refs_0_.refs_10_.wa_ref.refs_8_, ...), custom_call_target="tpu_custom_call" | custom-call | flops 6000000000 | bytes 8000000 | tf_op jit(solution)/shard_map/pallas_call | solution.py:522
  129.0 7.2 %shard_map.302 = (bf16[1024,1024]{1,0:T(8,128)(2,1)}, f32[1024,1]{1,0:T(8,128)}, bf16[1024,1024]{1,0:T(8,128)(2,1)S(1)}, bf16[1024,1024]{1,0:T(8,128)(2,1)}, bf16[1024,1024]{1,0:T(8,128)(2,1)}) custom-call(bf16[1024,1024]{1,0:T(8,128)(2,1)S(1)} %copy-done.3, bf16[1024,256]{1,0:T(8,128)(2,1)S(1)} %copy-done.28, bf16[1024,256]{1,0:T(8,128)(2,1)S(1)} %copy-done.32, ...), custom_call_target="tpu_custom_call" | custom-call | flops 2200000000 | bytes 20000000 | tf_op jit(solution)/shard_map/pallas_call | solution.py:701
  136.8 7.2 %shard_map.304 = (bf16[1024,1024]{1,0:T(8,128)(2,1)}, bf16[1024,1024]{1,0:T(8,128)(2,1)}, f32[1024,1024]{1,0:T(8,128)S(1)}) custom-call(bf16[1024,1024]{1,0:T(8,128)(2,1)S(1)} %get-tuple-element.106.mid_ref, bf16[2,512,1024]{2,1,0:T(8,128)(2,1)S(1)} %copy-done.52, bf16[2,512,1024]{2,1,0:T(8,128)(2,1)S(1)} %copy-done.52, ...), custom_call_target="tpu_custom_call" | custom-call | flops 4300000256 | bytes 18000000 | tf_op jit(solution)/shard_map/pallas_call | solution.py:765
  144.0 7.1 %shard_map.305 = (bf16[1024,1024]{1,0:T(8,128)(2,1)}, bf16[1024,1024]{1,0:T(8,128)(2,1)}, f32[1024,1024]{1,0:T(8,128)S(1)}) custom-call(bf16[1024,1024]{1,0:T(8,128)(2,1)S(1)} %get-tuple-element.106.mid_ref, bf16[2,512,1024]{2,1,0:T(8,128)(2,1)S(1)} %collective-permute-done.16.refs_0_.refs_1_.refs_7_, ...), custom_call_target="tpu_custom_call" | custom-call | flops 4300000256 | bytes 18000000 | tf_op jit(solution)/shard_map/pallas_call | solution.py:765
  153.1 2.9 copy-done.72
  156.1 8.5 %shard_map.306 = (bf16[1024,1024]{1,0:T(8,128)(2,1)}, bf16[1024,1024]{1,0:T(8,128)(2,1)}, f32[1024,1024]{1,0:T(8,128)S(1)}) custom-call(bf16[1024,1024]{1,0:T(8,128)(2,1)S(1)} %get-tuple-element.106.mid_ref, bf16[512,1024]{1,0:T(8,128)(2,1)} %collective-permute-done.8.refs_0_.refs_8_, bf16[512,1024]{1,0:T(8,128)(2,1)S(1)} %collective-permute-done.14.refs_1_.refs_9_, ...), custom_call_target="tpu_custom_call" | custom-call | flops 4300000256 | bytes 18000000 | tf_op jit(solution)/shard_map/pallas_call | solution.py:765
  164.7 11.1 %shard_map.307 = (bf16[1024,1024]{1,0:T(8,128)(2,1)}, bf16[1024,1024]{1,0:T(8,128)(2,1)}, bf16[1024,1024]{1,0:T(8,128)(2,1)}, bf16[1024,1024]{1,0:T(8,128)(2,1)S...) custom-call(bf16[1024,1024]{1,0:T(8,128)(2,1)S(1)} %get-tuple-element.106.mid_ref, ...), custom_call_target="tpu_custom_call" | custom-call | flops 4300000256 | bytes 30000000 | tf_op jit(solution)/shard_map/pallas_call | solution.py:804
  175.8 3.1 copy-done.83
  178.9 7.7 %shard_map.327 = bf16[2,512,2048]{2,1,0:T(8,128)(2,1)} custom-call(s32[4]{0:T(128)S(1)} %pad_add_fusion.2.info_ref.left_at, bf16[4,2,128,1024]{3,2,1,0:T(8,128)(2,1)S(1)} %bitcast.122, bf16[1024,1024]{1,0:T(8,128)(2,1)S(1)} %copy-done.73, bf16[1024,1024]{1,0:T(8,128)(2,1)S(1)} %copy-done.81, bf16[1024,1024]{1,0:T(8,128)(2,1)S(1)} %copy-done.83), custom_call_target="tpu_custom_call" | custom-call | flops 4294967296 | bytes 10000000 | tf_op jit(solution)/shard_map/pallas_call | solution.py:1014
  186.9 29.2 %shard_map.308 = (bf16[1024,1024]{1,0:T(8,128)(2,1)}, bf16[1024,1024]{1,0:T(8,128)(2,1)}, bf16[1024,1024]{1,0:T(8,128)(2,1)}, bf16[1024,1024]{1,0:T(8,128)(2,1)}...) custom-call(bf16[1024,1024]{1,0:T(8,128)(2,1)} %copy-done.85, ...), custom_call_target="tpu_custom_call" | custom-call | flops 16999999488 | bytes 40000000 | tf_op jit(solution)/shard_map/pallas_call | solution.py:902
  222.5 9.3 %shard_map.321 = bf16[2,512,2560]{2,1,0:T(8,128)(2,1)} custom-call(s32[4]{0:T(128)S(1)} %pad_add_fusion.2.info_ref.left_at, bf16[4,2,128,1024]{3,2,1,0:T(8,128)(2,1)S(1)} %bitcast.120, bf16[4,2,128,1024]{3,2,1,0:T(8,128)(2,1)S(1)} %bitcast.124, bf16[1024,1024]{1,0:T(8,128)(2,1)S(1)} %copy-done.79, bf16[1024,1024]{1,0:T(8,128)(2,1)S(1)} %copy-done.75, ...), custom_call_target="tpu_custom_call" | custom-call | flops 5368709120 | bytes 10000000 | tf_op jit(solution)/shard_map/pallas_call | solution.py:1014
  232.3 14.4 %shard_map.312 = (bf16[1024,768]{1,0:T(8,128)(2,1)}, f32[8,768]{1,0:T(8,128)S(1)}) custom-call(s32[2,4]{1,0:T(2,128)S(1)} %pad_add_fusion.1.win_ref, bf16[1024,768]{1,0:T(8,128)(2,1)S(1)} %copy-done.90, bf16[1024,128]{1,0:T(8,128)(2,1)S(1)} %copy-done.37, bf16[1024,128]{1,0:T(8,128)(2,1)S(1)} %get-tuple-element.280.refs_4_.hotk_ref, ...), custom_call_target="tpu_custom_call" | custom-call | flops 8000000000 | bytes 8000000 | tf_op jit(solution)/shard_map/pallas_call | solution.py:633
  246.8 14.2 %shard_map.311 = (bf16[1024,768]{1,0:T(8,128)(2,1)}, f32[8,768]{1,0:T(8,128)S(1)}) custom-call(s32[2,4]{1,0:T(2,128)S(1)} %pad_add_fusion.1.win_ref, bf16[1024,768]{1,0:T(8,128)(2,1)S(1)} %copy-done.89, bf16[1024,128]{1,0:T(8,128)(2,1)S(1)} %copy-done.37, bf16[1024,128]{1,0:T(8,128)(2,1)S(1)} %get-tuple-element.280.refs_4_.hotk_ref, ...), custom_call_target="tpu_custom_call" | custom-call | flops 8000000000 | bytes 8000000 | tf_op jit(solution)/shard_map/pallas_call | solution.py:633
  261.0 16.2 %shard_map.310 = (bf16[1024,768]{1,0:T(8,128)(2,1)}, f32[8,768]{1,0:T(8,128)S(1)}) custom-call(s32[2,4]{1,0:T(2,128)S(1)} %pad_add_fusion.1.win_ref, bf16[1024,768]{1,0:T(8,128)(2,1)S(1)} %copy-done.88, bf16[1024,128]{1,0:T(8,128)(2,1)S(1)} %copy-done.37, bf16[1024,128]{1,0:T(8,128)(2,1)S(1)} %get-tuple-element.280.refs_4_.hotk_ref, ...), custom_call_target="tpu_custom_call" | custom-call | flops 8000000000 | bytes 8000000 | tf_op jit(solution)/shard_map/pallas_call | solution.py:633
  278.6 6.8 %shard_map.314 = bf16[2,512,1536]{2,1,0:T(8,128)(2,1)} custom-call(s32[4]{0:T(128)S(1)} %pad_add_fusion.2.info_ref.left_at, bf16[4,2,128,1024]{3,2,1,0:T(8,128)(2,1)S(1)} %bitcast.106, bf16[1024,768]{1,0:T(8,128)(2,1)S(1)} %copy-done.20, bf16[1024,768]{1,0:T(8,128)(2,1)S(1)} %copy-done.8, bf16[1024,768]{1,0:T(8,128)(2,1)S(1)} %copy-done.6), custom_call_target="tpu_custom_call" | custom-call | flops 3221225472 | bytes 10000000 | tf_op jit(solution)/shard_map/pallas_call | solution.py:1014
  285.6 15.5 %shard_map.309 = (bf16[1024,768]{1,0:T(8,128)(2,1)}, f32[8,768]{1,0:T(8,128)S(1)}) custom-call(s32[2,4]{1,0:T(2,128)S(1)} %pad_add_fusion.1.win_ref, bf16[1024,768]{1,0:T(8,128)(2,1)S(1)} %copy-done.87, bf16[1024,128]{1,0:T(8,128)(2,1)S(1)} %copy-done.37, bf16[1024,128]{1,0:T(8,128)(2,1)S(1)} %get-tuple-element.280.refs_4_.hotk_ref, ...), custom_call_target="tpu_custom_call" | custom-call | flops 8000000000 | bytes 8000000 | tf_op jit(solution)/shard_map/pallas_call | solution.py:633
  302.6 10.9 %shard_map.313 = (f32[1024,1024]{1,0:T(8,128)}, f32[8,1024]{1,0:T(8,128)S(1)}) custom-call(bf16[1024,1024]{1,0:T(8,128)(2,1)S(1)} %copy-done.86, bf16[1024,768]{1,0:T(8,128)(2,1)S(1)} %copy-done.18, bf16[1024,768]{1,0:T(8,128)(2,1)S(1)} %copy-done.21, bf16[1024,768]{1,0:T(8,128)(2,1)S(1)} %copy-done.8, bf16[1024,768]{1,0:T(8,128)(2,1)S(1)} %copy-done.6, ...), custom_call_target="tpu_custom_call" | custom-call | flops 6400000000 | bytes 20000000 | tf_op jit(solution)/shard_map/pallas_call | solution.py:1185
  315.1 10.0 %shard_map.328 = (bf16[2,512,512]{2,1,0:T(8,128)(2,1)}, bf16[2,512,512]{2,1,0:T(8,128)(2,1)}, bf16[512,1024]{1,0:T(8,128)(2,1)}, bf16[512,1024]{1,0:T(8,128)(2,1)}) custom-call(s32[4]{0:T(128)S(1)} %pad_add_fusion.2.info_ref.left_at, bf16[4,2,128,1024]{3,2,1,0:T(8,128)(2,1)S(1)} %bitcast.123, bf16[1024,1024]{1,0:T(8,128)(2,1)S(1)} %copy-done.80, ...), custom_call_target="tpu_custom_call" | custom-call | flops 4294967296 | bytes 10000000 | tf_op jit(solution)/shard_map/pallas_call | solution.py:1014
  331.4 12.0 %shard_map.322 = (bf16[2,512,512]{2,1,0:T(8,128)(2,1)}, bf16[2,512,512]{2,1,0:T(8,128)(2,1)}, bf16[512,1536]{1,0:T(8,128)(2,1)}, bf16[512,1536]{1,0:T(8,128)(2,1)}) custom-call(s32[4]{0:T(128)S(1)} %pad_add_fusion.2.info_ref.left_at, bf16[4,2,128,1024]{3,2,1,0:T(8,128)(2,1)S(1)} %bitcast.121, bf16[4,2,128,1024]{3,2,1,0:T(8,128)(2,1)S(1)} %bitcast.125, ...), custom_call_target="tpu_custom_call" | custom-call | flops 5368709120 | bytes 10000000 | tf_op jit(solution)/shard_map/pallas_call | solution.py:1014
  346.9 4.5 shard_map.316
  363.5 4.5 shard_map.315
  368.0 52.5 %collective-permute-done.20.got_ref = bf16[512,768]{1,0:T(8,128)(2,1)} collective-permute-done((bf16[512,768]{1,0:T(8,128)(2,1)}, bf16[512,768]{1,0:T(8,128)(2,1)}, u32[]{:S(2)}, u32[]{:S(2)}) %collective-permute-start.20) | collective-permute-done | bytes 786464 | tf_op jit(solution)/shard_map/ppermute | solution.py:334
  422.1 2.4 shard_map.317
  424.9 2.1 shard_map.330
  431.0 2.3 shard_map.324
  436.9 37.7 %shard_map.320 = (f32[1,384]{1,0:T(1,128)}, f32[32,1,1152]{2,1,0:T(1,128)}) custom-call(f32[32,1,384]{2,1,0:T(1,128)} %broadcast_in_dim.92.sum_ref, f32[1,1152]{1,0:T(1,128)} %concatenate.247.row_ref), custom_call_target="tpu_custom_call" | custom-call | flops 1000000 | bytes 1000000 | tf_op jit(solution)/shard_map/pallas_call | solution.py:1258
  479.2 3.0 shard_map.331
  482.1 3.0 collective-permute-start.38
  485.3 2.0 shard_map.318
  487.4 2.5 collective-permute-start.23
  493.0 3.4 shard_map.325
  496.3 3.1 collective-permute-done.22.refs_1_
  501.9 16.1 %collective-permute-start.30 = (bf16[128,1280]{1,0:T(8,128)(2,1)}, bf16[128,1280]{1,0:T(8,128)(2,1)S(1)}, u32[]{:S(2)}, u32[]{:S(2)}) collective-permute-start(bf16[128,1280]{1,0:T(8,128)(2,1)} %get-tuple-element.165), channel_id=1, source_target_pairs={{0,8},{4,12},{8,0},{12,4},{16,24},{20,28},{24,16},{28,20},{1,9},{5... | collective-permute-start | bytes 983048 | tf_op jit(solution)/shard_map/ppermute | solution.py:334
  518.0 2.5 collective-permute-done.24.refs_3_
  524.8 2.0 fusion.1
  534.0 4.9 collective-permute-done.39.refs_2_
  538.8 7.1 %collective-permute-done.40.refs_3_ = bf16[128,1024]{1,0:T(8,128)(2,1)} collective-permute-done((bf16[128,1024]{1,0:T(8,128)(2,1)}, bf16[128,1024]{1,0:T(8,128)(2,1)}, u32[]{:S(2)}, u32[]{:S(2)}) %collective-permute-start.40) | collective-permute-done | bytes 262176 | tf_op jit(solution)/shard_map/ppermute | solution.py:334
  546.9 2.6 shard_map.332
  549.4 2.0 collective-permute-done.31.refs_2_
  551.5 7.1 %collective-permute-done.32.refs_3_ = bf16[128,1280]{1,0:T(8,128)(2,1)} collective-permute-done((bf16[128,1280]{1,0:T(8,128)(2,1)}, bf16[128,1280]{1,0:T(8,128)(2,1)}, u32[]{:S(2)}, u32[]{:S(2)}) %collective-permute-start.32) | collective-permute-done | bytes 327712 | tf_op jit(solution)/shard_map/ppermute | solution.py:334
  558.6 2.6 shard_map.326
  (388 shorter events, 95.3 us)
Async XLA Ops:
  2.2 34.7 %collective-permute-start.4 = (bf16[1,1536]{1,0:T(2,128)(2,1)S(1)}, bf16[1,1536]{1,0:T(2,128)(2,1)S(1)}, u32[]{:S(2)}, u32[]{:S(2)}) collective-permute-start(bf16[1,1536]{1,0:T(2,128)(2,1)S(1)} %pad_maximum_fusion.2), channel_id=1, source_target_pairs={{0,2},{1,3},{2,0},{3,1},{4,6},{5,7},{6,4},{7,5},{8,10},{9,11},{10,... | collective-permute-start | bytes 9224 | tf_op jit(solution)/shard_map/ppermute | solution.py:330
  2.8 32.6 %collective-permute-start.1 = (bf16[1,1536]{1,0:T(2,128)(2,1)S(1)}, bf16[1,1536]{1,0:T(2,128)(2,1)S(1)}, u32[]{:S(2)}, u32[]{:S(2)}) collective-permute-start(bf16[1,1536]{1,0:T(2,128)(2,1)S(1)} %pad_maximum_fusion.2), channel_id=1, source_target_pairs={{0,1},{1,0},{2,3},{3,2},{4,5},{5,4},{6,7},{7,6},{8,9},{9,8},{10,11... | collective-permute-start | bytes 9224 | tf_op jit(solution)/shard_map/ppermute | solution.py:330
  8.1 28.9 %collective-permute-start.2 = (bf16[512,1024]{1,0:T(8,128)(2,1)}, bf16[512,1024]{1,0:T(8,128)(2,1)S(1)}, u32[]{:S(2)}, u32[]{:S(2)}) collective-permute-start(bf16[512,1024]{1,0:T(8,128)(2,1)} %get-tuple-element.103), channel_id=1, source_target_pairs={{0,2},{1,3},{2,0},{3,1},{4,6},{5,7},{6,4},{7,5},{8,10},{9,11},{10,... | collective-permute-start | bytes 3145736 | tf_op jit(solution)/shard_map/ppermute | solution.py:330
  9.6 70.7 %collective-permute-start = (bf16[2,512,1024]{2,1,0:T(8,128)(2,1)}, bf16[2,512,1024]{2,1,0:T(8,128)(2,1)}, u32[]{:S(2)}, u32[]{:S(2)}) collective-permute-start(bf16[2,512,1024]{2,1,0:T(8,128)(2,1)} %get-tuple-element.100.refs_0_.refs_1_.refs_4_.refs_5_.wa_ref.wb_ref), channel_id=1, source_target_pairs={{0,1},{1,0},{2,3},{3,2},{4,5},{5,4},{6,7},{7,6},{8,9},{9,8},{10,11... | collective-permute-start | bytes 6291464 | tf_op jit(solution)/shard_map/ppermute | solution.py:330
  17.2 39.8 %collective-permute-start.8 = (bf16[512,1024]{1,0:T(8,128)(2,1)}, bf16[512,1024]{1,0:T(8,128)(2,1)}, u32[]{:S(2)}, u32[]{:S(2)}) collective-permute-start(bf16[512,1024]{1,0:T(8,128)(2,1)} %get-tuple-element.107), channel_id=1, source_target_pairs={{0,2},{1,3},{2,0},{3,1},{4,6},{5,7},{6,4},{7,5},{8,10},{9,11},{10,... | collective-permute-start | bytes 3145736 | tf_op jit(solution)/shard_map/ppermute | solution.py:330
  35.3 43.5 %collective-permute-start.11 = (bf16[512,1024]{1,0:T(8,128)(2,1)}, bf16[512,1024]{1,0:T(8,128)(2,1)S(1)}, u32[]{:S(2)}, u32[]{:S(2)}) collective-permute-start(bf16[512,1024]{1,0:T(8,128)(2,1)} %copy-done.59), channel_id=1, source_target_pairs={{0,2},{1,3},{2,0},{3,1},{4,6},{5,7},{6,4},{7,5},{8,10},{9,11},{10,... | collective-permute-start | bytes 3145736 | tf_op jit(solution)/shard_map/ppermute | solution.py:330
  37.1 209.7 %copy-start.23 = (bf16[512,1024]{1,0:T(8,128)(2,1)}, bf16[512,1024]{1,0:T(8,128)(2,1)S(1)}, u32[]{:S(2)}) copy-start(bf16[512,1024]{1,0:T(8,128)(2,1)S(1)} %collective-permute-done.2.refs_0_.refs_8_.wa_ref.refs_6_) | copy-start | bytes 3145732
  37.1 41.8 %collective-permute-start.6 = (bf16[512,1024]{1,0:T(8,128)(2,1)S(1)}, bf16[512,1024]{1,0:T(8,128)(2,1)S(1)}, u32[]{:S(2)}, u32[]{:S(2)}) collective-permute-start(bf16[512,1024]{1,0:T(8,128)(2,1)S(1)} %collective-permute-done.2.refs_0_.refs_8_.wa_ref.refs_6_), channel_id=1, source_target_pairs={{0,4},{4,0},{8,12},{12,8},{16,20},{20,16},{24,28},{28,24},{1,5},{5... | collective-permute-start | bytes 3145736 | tf_op jit(solution)/shard_map/ppermute | solution.py:334
  38.7 1.2 collective-permute-start.5
  39.9 53.7 %collective-permute-start.3 = (bf16[512,1024]{1,0:T(8,128)(2,1)S(1)}, bf16[512,1024]{1,0:T(8,128)(2,1)S(1)}, u32[]{:S(2)}, u32[]{:S(2)}) collective-permute-start(bf16[512,1024]{1,0:T(8,128)(2,1)S(1)} %collective-permute-done.2.refs_0_.refs_8_.wa_ref.refs_6_), channel_id=1, source_target_pairs={{0,1},{1,0},{2,3},{3,2},{4,5},{5,4},{6,7},{7,6},{8,9},{9,8},{10,11... | collective-permute-start | bytes 3145736 | tf_op jit(solution)/shard_map/ppermute | solution.py:330
  56.9 79.3 %collective-permute-start.16 = (bf16[2,512,1024]{2,1,0:T(8,128)(2,1)}, bf16[2,512,1024]{2,1,0:T(8,128)(2,1)S(1)}, u32[]{:S(2)}, u32[]{:S(2)}) collective-permute-start(bf16[2,512,1024]{2,1,0:T(8,128)(2,1)} %copy-done.51), channel_id=1, source_target_pairs={{0,1},{1,0},{2,3},{3,2},{4,5},{5,4},{6,7},{7,6},{8,9},{9,8},{10,11... | collective-permute-start | bytes 6291464 | tf_op jit(solution)/shard_map/ppermute | solution.py:330
  78.9 65.1 %collective-permute-start.17 = (bf16[2,512,1024]{2,1,0:T(8,128)(2,1)}, bf16[2,512,1024]{2,1,0:T(8,128)(2,1)S(1)}, u32[]{:S(2)}, u32[]{:S(2)}) collective-permute-start(bf16[2,512,1024]{2,1,0:T(8,128)(2,1)} %copy-done.53), channel_id=1, source_target_pairs={{0,1},{1,0},{2,3},{3,2},{4,5},{5,4},{6,7},{7,6},{8,9},{9,8},{10,11... | collective-permute-start | bytes 6291464 | tf_op jit(solution)/shard_map/ppermute | solution.py:330
  78.9 26.2 %collective-permute-start.9 = (bf16[512,1024]{1,0:T(8,128)(2,1)}, bf16[512,1024]{1,0:T(8,128)(2,1)S(1)}, u32[]{:S(2)}, u32[]{:S(2)}) collective-permute-start(bf16[512,1024]{1,0:T(8,128)(2,1)} %collective-permute-done.8.refs_0_.refs_8_), channel_id=1, source_target_pairs={{0,4},{4,0},{8,12},{12,8},{16,20},{20,16},{24,28},{28,24},{1,5},{5... | collective-permute-start | bytes 3145736 | tf_op jit(solution)/shard_map/ppermute | solution.py:334
  80.4 24.8 %collective-permute-start.7 = (bf16[512,1024]{1,0:T(8,128)(2,1)S(1)}, bf16[512,1024]{1,0:T(8,128)(2,1)S(1)}, u32[]{:S(2)}, u32[]{:S(2)}) collective-permute-start(bf16[512,1024]{1,0:T(8,128)(2,1)S(1)} %collective-permute-done.6.refs_0_.refs_10_.wa_ref.refs_8_), channel_id=1, source_target_pairs={{0,1},{1,0},{2,3},{3,2},{4,5},{5,4},{6,7},{7,6},{8,9},{9,8},{10,11... | collective-permute-start | bytes 3145736 | tf_op jit(solution)/shard_map/ppermute | solution.py:330
  93.6 42.6 %collective-permute-start.12 = (bf16[512,1024]{1,0:T(8,128)(2,1)S(1)}, bf16[512,1024]{1,0:T(8,128)(2,1)S(1)}, u32[]{:S(2)}, u32[]{:S(2)}) collective-permute-start(bf16[512,1024]{1,0:T(8,128)(2,1)S(1)} %collective-permute-done.11.refs_2_), channel_id=1, source_target_pairs={{0,4},{4,0},{8,12},{12,8},{16,20},{20,16},{24,28},{28,24},{1,5},{5... | collective-permute-start | bytes 3145736 | tf_op jit(solution)/shard_map/ppermute | solution.py:334
  105.1 59.5 %copy-start.60 = (bf16[512,1024]{1,0:T(8,128)(2,1)}, bf16[512,1024]{1,0:T(8,128)(2,1)S(1)}, u32[]{:S(2)}) copy-start(bf16[512,1024]{1,0:T(8,128)(2,1)S(1)} %collective-permute-done.9.refs_0_.refs_10_) | copy-start | bytes 3145732
  105.1 48.0 %collective-permute-start.14 = (bf16[512,1024]{1,0:T(8,128)(2,1)}, bf16[512,1024]{1,0:T(8,128)(2,1)S(1)}, u32[]{:S(2)}, u32[]{:S(2)}) collective-permute-start(bf16[512,1024]{1,0:T(8,128)(2,1)} %collective-permute-done.8.refs_0_.refs_8_), channel_id=1, source_target_pairs={{0,1},{1,0},{2,3},{3,2},{4,5},{5,4},{6,7},{7,6},{8,9},{9,8},{10,11... | collective-permute-start | bytes 3145736 | tf_op jit(solution)/shard_map/ppermute | solution.py:330
  105.1 48.0 %collective-permute-start.15 = (bf16[512,1024]{1,0:T(8,128)(2,1)S(1)}, bf16[512,1024]{1,0:T(8,128)(2,1)S(1)}, u32[]{:S(2)}, u32[]{:S(2)}) collective-permute-start(bf16[512,1024]{1,0:T(8,128)(2,1)S(1)} %collective-permute-done.11.refs_2_), channel_id=1, source_target_pairs={{0,1},{1,0},{2,3},{3,2},{4,5},{5,4},{6,7},{7,6},{8,9},{9,8},{10,11... | collective-permute-start | bytes 3145736 | tf_op jit(solution)/shard_map/ppermute | solution.py:330
  136.2 28.4 %collective-permute-start.10 = (bf16[512,1024]{1,0:T(8,128)(2,1)S(1)}, bf16[512,1024]{1,0:T(8,128)(2,1)S(1)}, u32[]{:S(2)}, u32[]{:S(2)}) collective-permute-start(bf16[512,1024]{1,0:T(8,128)(2,1)S(1)} %collective-permute-done.9.refs_0_.refs_10_), channel_id=1, source_target_pairs={{0,1},{1,0},{2,3},{3,2},{4,5},{5,4},{6,7},{7,6},{8,9},{9,8},{10,11... | collective-permute-start | bytes 3145736 | tf_op jit(solution)/shard_map/ppermute | solution.py:330
  136.3 28.3 %collective-permute-start.13 = (bf16[512,1024]{1,0:T(8,128)(2,1)S(1)}, bf16[512,1024]{1,0:T(8,128)(2,1)S(1)}, u32[]{:S(2)}, u32[]{:S(2)}) collective-permute-start(bf16[512,1024]{1,0:T(8,128)(2,1)S(1)} %collective-permute-done.12.refs_2_.refs_4_), channel_id=1, source_target_pairs={{0,1},{1,0},{2,3},{3,2},{4,5},{5,4},{6,7},{7,6},{8,9},{9,8},{10,11... | collective-permute-start | bytes 3145736 | tf_op jit(solution)/shard_map/ppermute | solution.py:330
  186.7 126.8 %collective-permute-start.33 = (bf16[2,512,2048]{2,1,0:T(8,128)(2,1)}, bf16[2,512,2048]{2,1,0:T(8,128)(2,1)}, u32[]{:S(2)}, u32[]{:S(2)}) collective-permute-start(bf16[2,512,2048]{2,1,0:T(8,128)(2,1)} %shard_map.327), channel_id=1, source_target_pairs={{0,1},{1,0},{2,3},{3,2},{4,5},{5,4},{6,7},{7,6},{8,9},{9,8},{10,11... | collective-permute-start | bytes 12582920 | tf_op jit(solution)/shard_map/ppermute | solution.py:330
  186.9 29.2 %copy-start.55 = (bf16[1024,1024]{1,0:T(8,128)(2,1)S(1)}, bf16[1024,1024]{1,0:T(8,128)(2,1)}, u32[]{:S(2)}) copy-start(bf16[1024,1024]{1,0:T(8,128)(2,1)} %get-tuple-element.154) | copy-start | bytes 6291460
  231.8 94.9 %collective-permute-start.25 = (bf16[2,512,2560]{2,1,0:T(8,128)(2,1)}, bf16[2,512,2560]{2,1,0:T(8,128)(2,1)}, u32[]{:S(2)}, u32[]{:S(2)}) collective-permute-start(bf16[2,512,2560]{2,1,0:T(8,128)(2,1)} %shard_map.321), channel_id=1, source_target_pairs={{0,1},{1,0},{2,3},{3,2},{4,5},{5,4},{6,7},{7,6},{8,9},{9,8},{10,11... | collective-permute-start | bytes 15728648 | tf_op jit(solution)/shard_map/ppermute | solution.py:330
  285.4 61.5 %collective-permute-start.18 = (bf16[2,512,1536]{2,1,0:T(8,128)(2,1)}, bf16[2,512,1536]{2,1,0:T(8,128)(2,1)S(1)}, u32[]{:S(2)}, u32[]{:S(2)}) collective-permute-start(bf16[2,512,1536]{2,1,0:T(8,128)(2,1)} %shard_map.314), channel_id=1, source_target_pairs={{0,1},{1,0},{2,3},{3,2},{4,5},{5,4},{6,7},{7,6},{8,9},{9,8},{10,11... | collective-permute-start | bytes 9437192 | tf_op jit(solution)/shard_map/ppermute | solution.py:330
  325.1 31.0 %collective-permute-start.34 = (bf16[2,512,512]{2,1,0:T(8,128)(2,1)}, bf16[2,512,512]{2,1,0:T(8,128)(2,1)}, u32[]{:S(2)}, u32[]{:S(2)}) collective-permute-start(bf16[2,512,512]{2,1,0:T(8,128)(2,1)} %get-tuple-element.176), channel_id=1, source_target_pairs={{0,2},{1,3},{2,0},{3,1},{4,6},{5,7},{6,4},{7,5},{8,10},{9,11},{10,... | collective-permute-start | bytes 3145736 | tf_op jit(solution)/shard_map/ppermute | solution.py:330
  343.5 87.2 %collective-permute-start.28 = (bf16[512,1536]{1,0:T(8,128)(2,1)}, bf16[512,1536]{1,0:T(8,128)(2,1)}, u32[]{:S(2)}, u32[]{:S(2)}) collective-permute-start(bf16[512,1536]{1,0:T(8,128)(2,1)} %get-tuple-element.163), channel_id=1, source_target_pairs={{0,4},{4,0},{8,12},{12,8},{16,20},{20,16},{24,28},{28,24},{1,5},{5... | collective-permute-start | bytes 4718600 | tf_op jit(solution)/shard_map/ppermute | solution.py:334
  345.8 78.7 %collective-permute-start.36 = (bf16[512,1024]{1,0:T(8,128)(2,1)}, bf16[512,1024]{1,0:T(8,128)(2,1)}, u32[]{:S(2)}, u32[]{:S(2)}) collective-permute-start(bf16[512,1024]{1,0:T(8,128)(2,1)} %get-tuple-element.178), channel_id=1, source_target_pairs={{0,4},{4,0},{8,12},{12,8},{16,20},{20,16},{24,28},{28,24},{1,5},{5... | collective-permute-start | bytes 3145736 | tf_op jit(solution)/shard_map/ppermute | solution.py:334
  346.3 80.8 %collective-permute-start.26 = (bf16[2,512,512]{2,1,0:T(8,128)(2,1)}, bf16[2,512,512]{2,1,0:T(8,128)(2,1)}, u32[]{:S(2)}, u32[]{:S(2)}) collective-permute-start(bf16[2,512,512]{2,1,0:T(8,128)(2,1)} %get-tuple-element.161), channel_id=1, source_target_pairs={{0,2},{1,3},{2,0},{3,1},{4,6},{5,7},{6,4},{7,5},{8,10},{9,11},{10,... | collective-permute-start | bytes 3145736 | tf_op jit(solution)/shard_map/ppermute | solution.py:330
  351.4 69.0 %collective-permute-start.20 = (bf16[512,768]{1,0:T(8,128)(2,1)}, bf16[512,768]{1,0:T(8,128)(2,1)}, u32[]{:S(2)}, u32[]{:S(2)}) collective-permute-start(bf16[512,768]{1,0:T(8,128)(2,1)} %get-tuple-element.140), channel_id=1, source_target_pairs={{0,4},{4,0},{8,12},{12,8},{16,20},{20,16},{24,28},{28,24},{1,5},{5... | collective-permute-start | bytes 2359304 | tf_op jit(solution)/shard_map/ppermute | solution.py:334
  358.6 74.7 %collective-permute-start.35 = (bf16[512,512]{1,0:T(8,128)(2,1)S(1)}, bf16[512,512]{1,0:T(8,128)(2,1)S(1)}, u32[]{:S(2)}, u32[]{:S(2)}) collective-permute-start(bf16[512,512]{1,0:T(8,128)(2,1)S(1)} %shard_map.329), channel_id=1, source_target_pairs={{0,4},{4,0},{8,12},{12,8},{16,20},{20,16},{24,28},{28,24},{1,5},{5... | collective-permute-start | bytes 1572872 | tf_op jit(solution)/shard_map/ppermute | solution.py:334
  363.5 58.6 %copy-start.26 = (bf16[512,768]{1,0:T(8,128)(2,1)S(1)}, bf16[512,768]{1,0:T(8,128)(2,1)}, u32[]{:S(2)}) copy-start(bf16[512,768]{1,0:T(8,128)(2,1)} %get-tuple-element.139.mine_ref) | copy-start | bytes 2359300
  368.0 56.9 %copy-start.14 = (bf16[512,1024]{1,0:T(8,128)(2,1)S(1)}, bf16[512,1024]{1,0:T(8,128)(2,1)}, u32[]{:S(2)}) copy-start(bf16[512,1024]{1,0:T(8,128)(2,1)} %get-tuple-element.177.mine_ref.refs_3_) | copy-start | bytes 3145732
  420.4 64.8 %collective-permute-start.19 = (bf16[512,768]{1,0:T(8,128)(2,1)}, bf16[512,768]{1,0:T(8,128)(2,1)S(1)}, u32[]{:S(2)}, u32[]{:S(2)}) collective-permute-start(bf16[512,768]{1,0:T(8,128)(2,1)} %get-tuple-element.138), channel_id=1, source_target_pairs={{0,4},{4,0},{8,12},{12,8},{16,20},{20,16},{24,28},{28,24},{1,5},{5... | collective-permute-start | bytes 2359304 | tf_op jit(solution)/shard_map/ppermute | solution.py:334
  424.5 60.8 %collective-permute-start.21 = (bf16[512,768]{1,0:T(8,128)(2,1)}, bf16[512,768]{1,0:T(8,128)(2,1)}, u32[]{:S(2)}, u32[]{:S(2)}) collective-permute-start(bf16[512,768]{1,0:T(8,128)(2,1)} %shard_map.317), channel_id=1, source_target_pairs={{0,2},{1,3},{2,0},{3,1},{4,6},{5,7},{6,4},{7,5},{8,10},{9,11},{10,... | collective-permute-start | bytes 2359304 | tf_op jit(solution)/shard_map/ppermute | solution.py:330
  427.0 48.6 %collective-permute-start.37 = (bf16[512,512]{1,0:T(8,128)(2,1)}, bf16[512,512]{1,0:T(8,128)(2,1)}, u32[]{:S(2)}, u32[]{:S(2)}) collective-permute-start(bf16[512,512]{1,0:T(8,128)(2,1)} %shard_map.330), channel_id=1, source_target_pairs={{0,2},{1,3},{2,0},{3,1},{4,6},{5,7},{6,4},{7,5},{8,10},{9,11},{10,... | collective-permute-start | bytes 1572872 | tf_op jit(solution)/shard_map/ppermute | solution.py:330
  430.6 59.2 %collective-permute-start.27 = (bf16[512,512]{1,0:T(8,128)(2,1)}, bf16[512,512]{1,0:T(8,128)(2,1)}, u32[]{:S(2)}, u32[]{:S(2)}) collective-permute-start(bf16[512,512]{1,0:T(8,128)(2,1)} %shard_map.323), channel_id=1, source_target_pairs={{0,4},{4,0},{8,12},{12,8},{16,20},{20,16},{24,28},{28,24},{1,5},{5... | collective-permute-start | bytes 1572872 | tf_op jit(solution)/shard_map/ppermute | solution.py:334
  434.2 57.3 %collective-permute-start.29 = (bf16[512,768]{1,0:T(8,128)(2,1)}, bf16[512,768]{1,0:T(8,128)(2,1)}, u32[]{:S(2)}, u32[]{:S(2)}) collective-permute-start(bf16[512,768]{1,0:T(8,128)(2,1)} %shard_map.324), channel_id=1, source_target_pairs={{0,2},{1,3},{2,0},{3,1},{4,6},{5,7},{6,4},{7,5},{8,10},{9,11},{10,... | collective-permute-start | bytes 2359304 | tf_op jit(solution)/shard_map/ppermute | solution.py:330
  482.1 39.0 %collective-permute-start.38 = (bf16[128,1024]{1,0:T(8,128)(2,1)S(1)}, bf16[128,1024]{1,0:T(8,128)(2,1)S(1)}, u32[]{:S(2)}, u32[]{:S(2)}) collective-permute-start(bf16[128,1024]{1,0:T(8,128)(2,1)S(1)} %get-tuple-element.180), channel_id=1, source_target_pairs={{0,8},{4,12},{8,0},{12,4},{16,24},{20,28},{24,16},{28,20},{1,9},{5... | collective-permute-start | bytes 786440 | tf_op jit(solution)/shard_map/ppermute | solution.py:334
  487.3 12.1 %collective-permute-start.22 = (bf16[128,768]{1,0:T(8,128)(2,1)S(1)}, bf16[128,768]{1,0:T(8,128)(2,1)S(1)}, u32[]{:S(2)}, u32[]{:S(2)}) collective-permute-start(bf16[128,768]{1,0:T(8,128)(2,1)S(1)} %get-tuple-element.142), channel_id=1, source_target_pairs={{0,8},{4,12},{8,0},{12,4},{16,24},{20,28},{24,16},{28,20},{1,9},{5... | collective-permute-start | bytes 589832 | tf_op jit(solution)/shard_map/ppermute | solution.py:334
  487.4 13.9 %collective-permute-start.23 = (bf16[128,768]{1,0:T(8,128)(2,1)S(1)}, bf16[128,768]{1,0:T(8,128)(2,1)S(1)}, u32[]{:S(2)}, u32[]{:S(2)}) collective-permute-start(bf16[128,768]{1,0:T(8,128)(2,1)S(1)} %get-tuple-element.143), channel_id=1, source_target_pairs={{0,16},{4,20},{8,24},{12,28},{16,0},{20,4},{24,8},{28,12},{1,17},{... | collective-permute-start | bytes 589832 | tf_op jit(solution)/shard_map/ppermute | solution.py:334
  489.9 30.6 %collective-permute-start.24 = (bf16[128,768]{1,0:T(8,128)(2,1)S(1)}, bf16[128,768]{1,0:T(8,128)(2,1)S(1)}, u32[]{:S(2)}, u32[]{:S(2)}) collective-permute-start(bf16[128,768]{1,0:T(8,128)(2,1)S(1)} %get-tuple-element.144), channel_id=1, source_target_pairs={{0,24},{4,28},{8,16},{12,20},{16,8},{20,12},{24,0},{28,4},{1,25},{... | collective-permute-start | bytes 589832 | tf_op jit(solution)/shard_map/ppermute | solution.py:334
  491.5 47.4 %collective-permute-start.39 = (bf16[128,1024]{1,0:T(8,128)(2,1)}, bf16[128,1024]{1,0:T(8,128)(2,1)}, u32[]{:S(2)}, u32[]{:S(2)}) collective-permute-start(bf16[128,1024]{1,0:T(8,128)(2,1)} %get-tuple-element.181), channel_id=1, source_target_pairs={{0,16},{4,20},{8,24},{12,28},{16,0},{20,4},{24,8},{28,12},{1,17},{... | collective-permute-start | bytes 786440 | tf_op jit(solution)/shard_map/ppermute | solution.py:334
  496.3 49.6 %copy-start.39 = (bf16[128,1024]{1,0:T(8,128)(2,1)S(1)}, bf16[128,1024]{1,0:T(8,128)(2,1)}, u32[]{:S(2)}) copy-start(bf16[128,1024]{1,0:T(8,128)(2,1)} %copy-done.38) | copy-start | bytes 786436
  500.1 45.8 %collective-permute-start.40 = (bf16[128,1024]{1,0:T(8,128)(2,1)}, bf16[128,1024]{1,0:T(8,128)(2,1)}, u32[]{:S(2)}, u32[]{:S(2)}) collective-permute-start(bf16[128,1024]{1,0:T(8,128)(2,1)} %get-tuple-element.182), channel_id=1, source_target_pairs={{0,24},{4,28},{8,16},{12,20},{16,8},{20,12},{24,0},{28,4},{1,25},{... | collective-permute-start | bytes 786440 | tf_op jit(solution)/shard_map/ppermute | solution.py:334
  501.9 47.5 %collective-permute-start.30 = (bf16[128,1280]{1,0:T(8,128)(2,1)}, bf16[128,1280]{1,0:T(8,128)(2,1)S(1)}, u32[]{:S(2)}, u32[]{:S(2)}) collective-permute-start(bf16[128,1280]{1,0:T(8,128)(2,1)} %get-tuple-element.165), channel_id=1, source_target_pairs={{0,8},{4,12},{8,0},{12,4},{16,24},{20,28},{24,16},{28,20},{1,9},{5... | collective-permute-start | bytes 983048 | tf_op jit(solution)/shard_map/ppermute | solution.py:334
  521.1 30.3 %collective-permute-start.31 = (bf16[128,1280]{1,0:T(8,128)(2,1)}, bf16[128,1280]{1,0:T(8,128)(2,1)}, u32[]{:S(2)}, u32[]{:S(2)}) collective-permute-start(bf16[128,1280]{1,0:T(8,128)(2,1)} %get-tuple-element.166), channel_id=1, source_target_pairs={{0,16},{4,20},{8,24},{12,28},{16,0},{20,4},{24,8},{28,12},{1,17},{... | collective-permute-start | bytes 983048 | tf_op jit(solution)/shard_map/ppermute | solution.py:334
  521.9 36.7 %collective-permute-start.32 = (bf16[128,1280]{1,0:T(8,128)(2,1)}, bf16[128,1280]{1,0:T(8,128)(2,1)}, u32[]{:S(2)}, u32[]{:S(2)}) collective-permute-start(bf16[128,1280]{1,0:T(8,128)(2,1)} %get-tuple-element.167), channel_id=1, source_target_pairs={{0,24},{4,28},{8,16},{12,20},{16,8},{20,12},{24,0},{28,4},{1,25},{... | collective-permute-start | bytes 983048 | tf_op jit(solution)/shard_map/ppermute | solution.py:334
  530.5 30.7 %copy-start.1 = (bf16[1024,1024]{1,0:T(8,128)(2,1)S(1)}, bf16[1024,1024]{1,0:T(8,128)(2,1)}, u32[]{:S(2)}) copy-start(bf16[1024,1024]{1,0:T(8,128)(2,1)} %param.33) | copy-start | bytes 6291460
  (99 other events, 761.4 us)

commit v5 on v4

--- a/solution.py
+++ b/solution.py
@@ -301,6 +301,10 @@
     return lax.dot_general(left, right, dims, preferred_element_type=F32)
 
 
+def after(values, others):
+    return lax.optimization_barrier((values, others))[0]
+
+
 def half_of(values, which, axis):
     size = values.shape[axis] // 2
     return lax.dynamic_slice_in_dim(values, which * size, size, axis)
@@ -356,14 +360,14 @@
 def pack_heads(info, w_qkv, w_out):
     return pl.pallas_call(
         pack_heads_kernel,
-        out_shape=(struct((HALF, 4 * UNIT, D)), struct((4 * UNIT, D))),
+        out_shape=(far((HALF, 4 * UNIT, D)), far((4 * UNIT, D))),
         grid_spec=pltpu.PrefetchScalarGridSpec(
             num_scalar_prefetch=1,
             grid=(1,),
             in_specs=[whole((3, D, 2 * UNIT)), whole((2 * UNIT, D))],
             out_specs=[whole((HALF, 4 * UNIT, D)), whole((4 * UNIT, D))],
         ),
-        compiler_params=room(24),
+        compiler_params=room(60),
         cost_estimate=cost(1e6, 5e6),
     )(info, w_qkv.transpose(1, 0, 2), w_out)
 
@@ -384,7 +388,7 @@
     size = w_down.shape[0] // 2
     return pl.pallas_call(
         pack_units_kernel,
-        out_shape=(struct((HALF, size, D)), struct((size, D))) * 2,
+        out_shape=(far((HALF, size, D)), far((size, D))) * 2,
         grid_spec=pltpu.PrefetchScalarGridSpec(
             num_scalar_prefetch=1,
             grid=(HALF,),
@@ -571,11 +575,10 @@
 
     @pl.when((unit == 0) & (step == 0))
     def _():
+        weight = jnp.concatenate([rows_of(wa_ref), rows_of(wb_ref)], axis=0)
         for r in range(LEN // ROWS):
             rows = slice(r * ROWS, (r + 1) * ROWS)
-            for u, ref in enumerate((wa_ref, wb_ref)):
-                part = dot(branch_ref[rows, :], rows_of(ref), NT)
-                grads[rows, u * UNIT : (u + 1) * UNIT] = part.astype(BF16)
+            grads[rows, :] = dot(branch_ref[rows, :], weight, NT).astype(BF16)
 
     @pl.when(step == 0)
     def _():
@@ -807,8 +810,8 @@
             far((LEN, 2 * size)),
             far((LEN, 2 * size)),
             far((LEN, D)),
-            struct((LEN, D)),
-            struct((D, LEN)),
+            far((LEN, D)),
+            far((D, LEN)),
             struct((8, D), F32),
         ),
         in_specs=ffn_specs(size, pair) + [tile(D)] * 2 + [whole((1, D))] * 3,
@@ -833,7 +836,7 @@
         refs[7],
         refs[8:],
     )
-    branch, down, up, slope, total, one, sems = refs
+    branch, down, up, slope, total, one, low, low_turned, sems = refs
     size = up.shape[1]
     plan = ((0, 0), (0, 1), (1, 0), (1, 1), (2, None), (3, None), (4, None), (5, None))
     first = pltpu.make_async_copy(branch_hbm, branch, sems.at[0])
@@ -881,10 +884,19 @@
             else:
                 d_mid = total[rows, :] + part + branch[rows, :].astype(F32)
                 normal = one[rows, :].astype(F32)
-                low = norm_back(normal, scale_ref[rows, :], d_mid, gain_ref[...]).astype(BF16)
-                low_ref[rows, :] = low
-                low_t[:, rows] = low.T
-                for k, v in enumerate((low.astype(F32), d_mid * normal, d_mid)):
+                part = norm_back(normal, scale_ref[rows, :], d_mid, gain_ref[...]).astype(BF16)
+                low[rows, :] = part
+                low_turned[:, rows] = part.T
+                for k, (source, target) in enumerate(
+                    (
+                        (low.at[rows, :], low_ref.at[rows, :]),
+                        (low_turned.at[:, rows], low_t.at[:, rows]),
+                    )
+                ):
+                    store = pltpu.make_async_copy(source, target, sems.at[34 + 2 * r + k])
+                    store.start()
+                    stores.append(store)
+                for k, v in enumerate((part.astype(F32), d_mid * normal, d_mid)):
                     norm_sums[k] = norm_sums[k] + jnp.sum(v, axis=0, keepdims=True)
         sum_ref[j : j + 1, :] = sums
         store = pltpu.make_async_copy(slope.at[j], pre_hbm[j // 2].at[:, columns], sems.at[26 + j])
@@ -898,14 +910,14 @@
 
 def ffn_back(branch_two, down, up, slopes, normal_one, scale_one, gain):
     size = down[2].shape[0]
-    hbm = pl.BlockSpec(memory_space=pl.ANY)
+    hbm = pl.BlockSpec(memory_space=pltpu.HBM)
     return pl.pallas_call(
         ffn_back_kernel,
         out_shape=(far((LEN, 2 * size)),) * 4
-        + (struct((8, size), F32), struct((LEN, D)), struct((D, LEN)), struct((8, D), F32)),
+        + (struct((8, size), F32), far((LEN, D)), far((D, LEN)), struct((8, D), F32)),
         grid=(1,),
         in_specs=[hbm] * 18 + [whole((LEN, 1)), whole((1, D))],
-        out_specs=[hbm] * 4 + [whole((8, size)), whole((LEN, D)), whole((D, LEN)), whole((8, D))],
+        out_specs=[hbm] * 4 + [whole((8, size)), hbm, hbm, whole((8, D))],
         scratch_shapes=[
             pltpu.VMEM((LEN, D), BF16),
             pltpu.VMEM((8, size, D), BF16),
@@ -913,7 +925,9 @@
             pltpu.VMEM((8, LEN, size), BF16),
             pltpu.VMEM((LEN, D), F32),
             pltpu.VMEM((LEN, D), BF16),
-            pltpu.SemaphoreType.DMA((34,)),
+            pltpu.VMEM((LEN, D), BF16),
+            pltpu.VMEM((D, LEN), BF16),
+            pltpu.SemaphoreType.DMA((42,)),
         ],
         compiler_params=room(52),
         cost_estimate=cost(17e9, 40e6),
@@ -955,15 +969,14 @@
         count[0] += 1
         return copy
 
-    first = [
-        copy_of(left_hbm[k].at[:, left_at[side]], left.at[k, side])
-        for k in range(lefts)
-        for side in range(2)
-    ]
+    ready = {}
     chunks, at = [], 0
     for part, far in blocks:
         for run in part:
             copies = []
+            if (run.which, 0) not in ready:
+                source = left_hbm[run.which]
+                ready[run.which, 0] = copy_of(source.at[:, left_at[0]], left.at[run.which, 0])
             for h in range(2):
                 if far:
                     piece, source = 1 + h, run.second if side_from else run.first
@@ -975,18 +988,23 @@
                         right.at[:, at + h * run.size : at + (h + 1) * run.size],
                     )
                 )
+            columns = slice(at, at + 2 * run.size)
+            if got_from is not None:
+                source = got_hbm.at[:, :, got_from + at : got_from + at + 2 * run.size]
+                copies.append(copy_of(source, got.at[:, :, columns]))
+            if (run.which, 1) not in ready:
+                source = left_hbm[run.which]
+                ready[run.which, 1] = copy_of(source.at[:, left_at[1]], left.at[run.which, 1])
             chunks.append((run.which, at, 2 * run.size, copies))
             at += 2 * run.size
-    if got_from is not None:
-        first.append(copy_of(got_hbm.at[:, :, got_from : got_from + at], got))
-    for copy in first:
-        copy.wait()
     stores = []
     for which, at, size, copies in chunks:
         for copy in copies:
             copy.wait()
         columns = slice(at, at + size)
         for side in range(2):
+            if (which, side) in ready:
+                ready.pop((which, side)).wait()
             total = dot(left[which, side].reshape(D // 2, LEN), right[:, columns])
             if got_from is not None:
                 total = total + got[side, :, columns].astype(F32)
@@ -1004,7 +1022,7 @@
 
 def grad_call(info, left_t, rights, blocks, side, outputs, got=None, got_from=None):
     width = sum(part_width(part) for part, _ in blocks)
-    hbm = pl.BlockSpec(memory_space=pl.ANY)
+    hbm = pl.BlockSpec(memory_space=pltpu.HBM)
     lefts = len(left_t)
     operands = [v.reshape(4, 2, D // 8, LEN) for v in left_t] + [v for r in rights for v in r]
     operands += [] if got is None else [got]
@@ -1027,7 +1045,7 @@
                 pltpu.SemaphoreType.DMA((48,)),
             ],
         ),
-        compiler_params=room(32),
+        compiler_params=room(60),
         cost_estimate=cost(2 * D * LEN * width, 10e6),
     )(info, *operands)
 
@@ -1101,7 +1119,7 @@
             in_specs=specs,
             out_specs=[whole((D // 8, width))] * 4,
         ),
-        compiler_params=room(24),
+        compiler_params=room(60),
         cost_estimate=cost(1e6, 4e6),
     )(info, *[v[0] for triple in sources for v in triple])
     return [out[0]] + [send_dp(out[k], 2 * k) for k in (1, 2, 3)]
@@ -1188,10 +1206,10 @@
         grid=(LEN // ROWS,),
         in_specs=[tile]
         + [pl.BlockSpec((ROWS, width), lambda i: (i, 0))] * 4
-        + [pl.BlockSpec(memory_space=pl.ANY)] * 6,
+        + [pl.BlockSpec(memory_space=pltpu.HBM)] * 6,
         out_specs=[tile, whole((8, D))],
         scratch_shapes=[pltpu.VMEM((4 * width, D), BF16), pltpu.SemaphoreType.DMA((24,))],
-        compiler_params=room(26),
+        compiler_params=room(60),
         cost_estimate=cost(6.4e9, 20e6),
     )(branch_one, *d_qkv, *heads)
 
@@ -1270,17 +1288,11 @@
     )(sums, row)
 
 
-def natural_blocks(halves, x_at, mp_at):
-    join = lambda a, b: jnp.where(x_at == 0, jnp.concatenate([a, b]), jnp.concatenate([b, a]))
-    stacked = jnp.stack(
-        [
-            join(halves[0], halves[1]),
-            join(halves[2], halves[3]),
-            join(halves[4], halves[6]),
-            join(halves[5], halves[7]),
-        ]
-    )
-    return jnp.stack([stacked[i ^ mp_at] for i in range(4)])
+def natural_order(x_at, mp_at):
+    block, half = jnp.arange(8, dtype=jnp.int32) // 2, jnp.arange(8, dtype=jnp.int32) % 2
+    away, at = block ^ mp_at, half ^ x_at
+    source = jnp.where(away < 2, 2 * away + at, 2 + away + 2 * at)
+    return (source[:, None] == jnp.arange(8, dtype=jnp.int32)[None, :]).astype(F32)
 
 
 def body_rows(
@@ -1418,20 +1430,20 @@
     back(2)
     down_values = split_z(info, down_parts, down_last)
     back(3)
-    up_last = second_sends(up_sums, up_parts)
     wide = part_width(qkv_part)
     far_only, own_only = ((qkv_part, True),), ((qkv_part, False),)
     (sent,) = grad_call(
         info, [hidden_t], [d_qkv[1:]], own_only + far_only, 1, ((0, 2 * wide, None),)
     )
     got = send_mp(sent, 1)
-    up_values = split_z(info, up_parts, up_last)
+    up_last = second_sends(after(up_sums, sent), up_parts)
     sides = ((0, wide, 0), (0, wide, 1))
     far_keep, far_leave = grad_call(
         info, [hidden_t], [[d_qkv[1]] + d_qkv[2:]], far_only, 0, sides, got, wide
     )
     far_x = send_dp(far_leave, 1)
     back(0)
+    up_values = split_z(info, up_parts, up_last)
     here = (0, 0)
     far_low = add_parts((far_keep, here), (far_x, here), qkv_part, True)
     far_y = send_mp(far_low, 2)
@@ -1442,21 +1454,29 @@
     grad_tokens, sums_in = input_grad(branch_one, d_qkv, heads)
     qkv_values = split_z(info, (qkv_part,), (((own_keep, here), (own_x, here), (far_y, here)),))
 
-    spread = lambda v: v.reshape(GRID_DP * GRID_MP, -1)
-    spread_blocks = lambda b: b.reshape(GRID_MP, GRID_DP, -1).transpose(1, 0, 2).reshape(GRID_DP * GRID_MP, -1)
-    rows = [spread(sums[j]) for sums in (sums_two, sums_one) for j in range(3)]
-    rows.append(spread_blocks(natural_blocks([sums_up[j] for j in range(8)], x_at, mp_at)))
-    for j in (0, 2):
-        halves = [
-            qkv_sums[p][0, (2 * j + u) * UNIT : (2 * j + u + 1) * UNIT]
-            for p in range(4)
-            for u in range(HALF)
-        ]
-        rows.append(spread_blocks(natural_blocks(halves, x_at, mp_at)))
+    devices = GRID_DP * GRID_MP
+    heads_sum = jnp.concatenate([v[0:1] for v in qkv_sums]).reshape(4, 3, HALF, UNIT)
+    heads_sum = heads_sum.transpose(0, 2, 1, 3).reshape(8, -1)
+    blocks = jnp.dot(
+        natural_order(x_at, mp_at),
+        jnp.concatenate([sums_up, heads_sum], axis=1),
+        precision=HIGHEST_PRECISION,
+    )
+
+    def spread(v):
+        return v.reshape(GRID_MP, GRID_DP, -1).transpose(1, 0, 2).reshape(devices, -1)
+
+    ends = (0, units // 2, units // 2 + UNIT, units // 2 + 3 * UNIT)
+    full = jnp.concatenate([sums_two[:3], sums_one[:3]]).reshape(6, devices, -1)
+    rows = [full.transpose(1, 0, 2).reshape(devices, -1), spread(blocks[:, : ends[1]])]
+    rows += [spread(blocks[:, at : at + UNIT]) for at in (ends[1], ends[3] - UNIT)]
     tail_row = jnp.concatenate(
         [sums_in[0:1], jnp.broadcast_to(own_step.astype(F32)[None, :], (1, UNIT))], axis=1
     )
     totals, all_rows = exchange(jnp.concatenate(rows, axis=1)[:, None, :], tail_row)
+    totals, all_rows, down_values, up_values = after(
+        (totals, all_rows, down_values, up_values), qkv_values[0]
+    )
     all_rows = all_rows[:, 0]
     span = D // (GRID_DP * GRID_MP)
     own = [totals[0, j * span : (j + 1) * span] for j in range(6)]

time: 571 us -> 516 us (0.904)
  the two profiles are of different devices: /device:TPU:12 before, /device:TPU:0 now
where the time goes in v5:
time: 516 us; the launch traced here: 507 us
  Pallas kernels  309 us (60%)
  waiting for transfers between devices  106 us (21%)
  starting transfers between devices  50.2 us (10%)
  local copies, waits for them, and re-layouts  32.6 us (6%)
    pallas_call x7, Pallas kernels, grad_call(): pl.pallas_call(functools.partial(grad_kernel, blocks, side, outputs, left...  61.4 us
    pallas_call x4, Pallas kernels, attend_back_pair(): pl.pallas_call(attend_back_kernel, out_shape=(far((LEN, 6 * UNIT)), struc...  58.6 us
    ppermute x23, waiting for transfers between devices, send_mp(): return lax.ppermute(values, 'mp', [(i, i ^ bit) for i in range(GRID_MP)])  55.4 us
    ppermute x18, waiting for transfers between devices, send_dp(): return lax.ppermute(values, 'dp', [(i, i ^ bit) for i in range(GRID_DP)])  50.2 us
    pallas_call x4, Pallas kernels, attend_pair(): pl.pallas_call(attend_kernel, out_shape=(far((LEN, 6 * UNIT)), far((LEN,...  43 us
    ppermute x18, starting transfers between devices, send_dp(): return lax.ppermute(values, 'dp', [(i, i ^ bit) for i in range(GRID_DP)])  36.5 us
    pallas_call x1, Pallas kernels, exchange(): pl.pallas_call(exchange_kernel, out_shape=(struct(sums.shape[1:], F32), s...  31 us
    pallas_call x1, Pallas kernels, ffn_back(): pl.pallas_call(ffn_back_kernel, out_shape=(far((LEN, 2 * size)),) * 4 + (...  28.6 us
  transfers between devices with their start and end apart: 41, of which 10 were waited for; matrix products, arithmetic and copies ran while one was open for 2% of the time, Pallas kernels for 50%

profile of v5, /device:TPU:0, one launch (start us, length us, event | category | flops | bytes accessed | tf_op | source)
XLA Modules:
  0.0 506.8 jit_solution(11172938743120145742)
XLA Ops:
  2.2 3.1 collective-permute-start.4
  5.9 4.5 shard_map.297
  14.1 3.9 shard_map.303
  25.8 10.2 %shard_map.298 = (bf16[1024,768]{1,0:T(8,128)(2,1)}, bf16[1024,256]{1,0:T(8,128)(2,1)}, f32[2,8,1024]{2,1,0:T(8,128)}) custom-call(s32[2,2]{1,0:T(2,128)S(1)} %pad_add_fusion.win_ref, bf16[1024,1024]{1,0:T(8,128)(2,1)S(1)} %add_convert_fusion.x_ref, bf16[2,512,1024]{2,1,0:T(8,128)(2,1)S(1)} %copy-done.3, bf16[2,512,1024]{2,1,0:T(8,128)(2,1)S(1)} %copy-done.3, ...), custom_call_target="tpu_custom_call" | custom-call | flops 6000000000 | bytes 8000000 | tf_op jit(solution)/shard_map/pallas_call | solution.py:526
  39.3 19.9 %collective-permute-done.8.refs_0_.refs_8_ = bf16[512,1024]{1,0:T(8,128)(2,1)} collective-permute-done((bf16[512,1024]{1,0:T(8,128)(2,1)}, bf16[512,1024]{1,0:T(8,128)(2,1)}, u32[]{:S(2)}, u32[]{:S(2)}) %collective-permute-start.8) | collective-permute-done | bytes 1048608 | tf_op jit(solution)/shard_map/ppermute | solution.py:334
  59.2 21.9 %collective-permute-done.11.refs_2_ = bf16[512,1024]{1,0:T(8,128)(2,1)S(1)} collective-permute-done((bf16[512,1024]{1,0:T(8,128)(2,1)S(1)}, bf16[512,1024]{1,0:T(8,128)(2,1)S(1)}, u32[]{:S(2)}, u32[]{:S(2)}) %collective-permute-start.11) | collective-permute-done | bytes 1048608 | tf_op jit(solution)/shard_map/ppermute | solution.py:334
  82.8 12.2 %shard_map.299 = (bf16[1024,768]{1,0:T(8,128)(2,1)}, bf16[1024,256]{1,0:T(8,128)(2,1)}, f32[2,8,1024]{2,1,0:T(8,128)}) custom-call(s32[2,2]{1,0:T(2,128)S(1)} %pad_add_fusion.win_ref, bf16[1024,1024]{1,0:T(8,128)(2,1)S(1)} %add_convert_fusion.x_ref, bf16[2,512,1024]{2,1,0:T(8,128)(2,1)} %collective-permute-done.refs_0_.refs_1_.refs_6_.refs_7_.wa_ref.wb_ref.refs_5_, ...), custom_call_target="tpu_custom_call" | custom-call | flops 6000000000 | bytes 8000000 | tf_op jit(solution)/shard_map/pallas_call | solution.py:526
  95.1 10.2 %shard_map.300 = (bf16[1024,768]{1,0:T(8,128)(2,1)}, bf16[1024,256]{1,0:T(8,128)(2,1)}, f32[2,8,1024]{2,1,0:T(8,128)}) custom-call(s32[2,2]{1,0:T(2,128)S(1)} %pad_add_fusion.win_ref, bf16[1024,1024]{1,0:T(8,128)(2,1)S(1)} %add_convert_fusion.x_ref, bf16[512,1024]{1,0:T(8,128)(2,1)S(1)} %collective-permute-done.2.refs_0_.refs_8_.wa_ref.refs_6_, ...), custom_call_target="tpu_custom_call" | custom-call | flops 6000000000 | bytes 8000000 | tf_op jit(solution)/shard_map/pallas_call | solution.py:526
  105.3 2.1 collective-permute-done.9.refs_0_.refs_10_
  107.9 10.4 %shard_map.301 = (bf16[1024,768]{1,0:T(8,128)(2,1)}, bf16[1024,256]{1,0:T(8,128)(2,1)}, f32[2,8,1024]{2,1,0:T(8,128)}) custom-call(s32[2,2]{1,0:T(2,128)S(1)} %pad_add_fusion.win_ref, bf16[1024,1024]{1,0:T(8,128)(2,1)S(1)} %add_convert_fusion.x_ref, bf16[512,1024]{1,0:T(8,128)(2,1)S(1)} %collective-permute-done.6.refs_0_.refs_10_.wa_ref.refs_8_, ...), custom_call_target="tpu_custom_call" | custom-call | flops 6000000000 | bytes 8000000 | tf_op jit(solution)/shard_map/pallas_call | solution.py:526
  119.5 6.8 %shard_map.302 = (bf16[1024,1024]{1,0:T(8,128)(2,1)}, f32[1024,1]{1,0:T(8,128)}, bf16[1024,1024]{1,0:T(8,128)(2,1)S(1)}, bf16[1024,1024]{1,0:T(8,128)(2,1)}, bf16[1024,1024]{1,0:T(8,128)(2,1)}) custom-call(bf16[1024,1024]{1,0:T(8,128)(2,1)S(1)} %copy-done.2, bf16[1024,256]{1,0:T(8,128)(2,1)S(1)} %copy-done.20, bf16[1024,256]{1,0:T(8,128)(2,1)S(1)} %copy-done.26, ...), custom_call_target="tpu_custom_call" | custom-call | flops 2200000000 | bytes 20000000 | tf_op jit(solution)/shard_map/pallas_call | solution.py:704
  126.2 3.1 collective-permute-done.12.refs_2_.refs_4_
  129.9 7.1 %shard_map.304 = (bf16[1024,1024]{1,0:T(8,128)(2,1)}, bf16[1024,1024]{1,0:T(8,128)(2,1)}, f32[1024,1024]{1,0:T(8,128)S(1)}) custom-call(bf16[1024,1024]{1,0:T(8,128)(2,1)S(1)} %get-tuple-element.120.mid_ref, bf16[2,512,1024]{2,1,0:T(8,128)(2,1)S(1)} %copy-done.39, bf16[2,512,1024]{2,1,0:T(8,128)(2,1)S(1)} %copy-done.39, ...), custom_call_target="tpu_custom_call" | custom-call | flops 4300000256 | bytes 18000000 | tf_op jit(solution)/shard_map/pallas_call | solution.py:768
  137.0 7.1 %shard_map.305 = (bf16[1024,1024]{1,0:T(8,128)(2,1)}, bf16[1024,1024]{1,0:T(8,128)(2,1)}, f32[1024,1024]{1,0:T(8,128)S(1)}) custom-call(bf16[1024,1024]{1,0:T(8,128)(2,1)S(1)} %get-tuple-element.120.mid_ref, bf16[2,512,1024]{2,1,0:T(8,128)(2,1)S(1)} %collective-permute-done.16.refs_0_.refs_1_.refs_7_, ...), custom_call_target="tpu_custom_call" | custom-call | flops 4300000256 | bytes 18000000 | tf_op jit(solution)/shard_map/pallas_call | solution.py:768
  144.1 9.1 %shard_map.306 = (bf16[1024,1024]{1,0:T(8,128)(2,1)}, bf16[1024,1024]{1,0:T(8,128)(2,1)}, f32[1024,1024]{1,0:T(8,128)S(1)}) custom-call(bf16[1024,1024]{1,0:T(8,128)(2,1)S(1)} %get-tuple-element.120.mid_ref, bf16[512,1024]{1,0:T(8,128)(2,1)} %collective-permute-done.8.refs_0_.refs_8_, bf16[512,1024]{1,0:T(8,128)(2,1)S(1)} %collective-permute-done.14.refs_1_.refs_9_, ...), custom_call_target="tpu_custom_call" | custom-call | flops 4300000256 | bytes 18000000 | tf_op jit(solution)/shard_map/pallas_call | solution.py:768
  153.3 11.5 %shard_map.307 = (bf16[1024,1024]{1,0:T(8,128)(2,1)}, bf16[1024,1024]{1,0:T(8,128)(2,1)}, bf16[1024,1024]{1,0:T(8,128)(2,1)}, bf16[1024,1024]{1,0:T(8,128)(2,1)}...) custom-call(bf16[1024,1024]{1,0:T(8,128)(2,1)S(1)} %get-tuple-element.120.mid_ref, ...), custom_call_target="tpu_custom_call" | custom-call | flops 4300000256 | bytes 30000000 | tf_op jit(solution)/shard_map/pallas_call | solution.py:807
  164.9 28.6 %shard_map.308 = (bf16[1024,1024]{1,0:T(8,128)(2,1)}, bf16[1024,1024]{1,0:T(8,128)(2,1)}, bf16[1024,1024]{1,0:T(8,128)(2,1)}, bf16[1024,1024]{1,0:T(8,128)(2,1)}...) custom-call(bf16[1024,1024]{1,0:T(8,128)(2,1)} %get-tuple-element.129.b, ...), custom_call_target="tpu_custom_call" | custom-call | flops 16999999488 | bytes 40000000 | tf_op jit(solution)/shard_map/pallas_call | solution.py:914
  193.5 10.8 %shard_map.326 = bf16[2,512,2560]{2,1,0:T(8,128)(2,1)} custom-call(s32[4]{0:T(128)} %pad_add_fusion.2.info_ref.left_at, bf16[4,2,128,1024]{3,2,1,0:T(8,128)(2,1)} %bitcast.142, bf16[4,2,128,1024]{3,2,1,0:T(8,128)(2,1)} %bitcast.144, bf16[1024,1024]{1,0:T(8,128)(2,1)} %get-tuple-element.187.refs_2_, bf16[1024,1024]{1,0:T(8,128)(2,1)} %get-tuple-element.185.refs_3_, ...), custom_call_target="tpu_custom_call" | custom-call | flops 5368709120 | bytes 10000000 | tf_op jit(solution)/shard_map/pallas_call | solution.py:1032
  204.5 9.1 %shard_map.321 = bf16[2,512,2048]{2,1,0:T(8,128)(2,1)} custom-call(s32[4]{0:T(128)} %pad_add_fusion.2.info_ref.left_at, bf16[4,2,128,1024]{3,2,1,0:T(8,128)(2,1)} %bitcast.146, bf16[1024,1024]{1,0:T(8,128)(2,1)} %get-tuple-element.173.refs_1_, bf16[1024,1024]{1,0:T(8,128)(2,1)} %get-tuple-element.171.refs_2_, bf16[1024,1024]{1,0:T(8,128)(2,1)} %get-tuple-element.172.refs_3_), custom_call_target="tpu_custom_call" | custom-call | flops 4294967296 | bytes 10000000 | tf_op jit(solution)/shard_map/pallas_call | solution.py:1032
  220.8 14.2 %shard_map.312 = (bf16[1024,768]{1,0:T(8,128)(2,1)}, f32[8,768]{1,0:T(8,128)S(1)}) custom-call(s32[2,4]{1,0:T(2,128)S(1)} %pad_add_fusion.1.win_ref, bf16[1024,768]{1,0:T(8,128)(2,1)S(1)} %copy-done.60, bf16[1024,128]{1,0:T(8,128)(2,1)S(1)} %copy-done.30, bf16[1024,128]{1,0:T(8,128)(2,1)S(1)} %get-tuple-element.272.refs_4_.hotk_ref, ...), custom_call_target="tpu_custom_call" | custom-call | flops 8000000000 | bytes 8000000 | tf_op jit(solution)/shard_map/pallas_call | solution.py:636
  235.1 14.7 %shard_map.311 = (bf16[1024,768]{1,0:T(8,128)(2,1)}, f32[8,768]{1,0:T(8,128)S(1)}) custom-call(s32[2,4]{1,0:T(2,128)S(1)} %pad_add_fusion.1.win_ref, bf16[1024,768]{1,0:T(8,128)(2,1)S(1)} %copy-done.59, bf16[1024,128]{1,0:T(8,128)(2,1)S(1)} %copy-done.30, bf16[1024,128]{1,0:T(8,128)(2,1)S(1)} %get-tuple-element.272.refs_4_.hotk_ref, ...), custom_call_target="tpu_custom_call" | custom-call | flops 8000000000 | bytes 8000000 | tf_op jit(solution)/shard_map/pallas_call | solution.py:636
  249.8 15.4 %shard_map.310 = (bf16[1024,768]{1,0:T(8,128)(2,1)}, f32[8,768]{1,0:T(8,128)S(1)}) custom-call(s32[2,4]{1,0:T(2,128)S(1)} %pad_add_fusion.1.win_ref, bf16[1024,768]{1,0:T(8,128)(2,1)S(1)} %copy-done.58, bf16[1024,128]{1,0:T(8,128)(2,1)S(1)} %copy-done.30, bf16[1024,128]{1,0:T(8,128)(2,1)S(1)} %get-tuple-element.272.refs_4_.hotk_ref, ...), custom_call_target="tpu_custom_call" | custom-call | flops 8000000000 | bytes 8000000 | tf_op jit(solution)/shard_map/pallas_call | solution.py:636
  265.2 8.3 %shard_map.314 = bf16[2,512,1536]{2,1,0:T(8,128)(2,1)} custom-call(s32[4]{0:T(128)} %pad_add_fusion.2.info_ref.left_at, bf16[4,2,128,1024]{3,2,1,0:T(8,128)(2,1)} %bitcast.123, bf16[1024,768]{1,0:T(8,128)(2,1)} %get-tuple-element.142.refs_1_, bf16[1024,768]{1,0:T(8,128)(2,1)} %get-tuple-element.145.refs_2_, bf16[1024,768]{1,0:T(8,128)(2,1)} %get-tuple-element.148.refs_3_), custom_call_target="tpu_custom_call" | custom-call | flops 3221225472 | bytes 10000000 | tf_op jit(solution)/shard_map/pallas_call | solution.py:1032
  273.6 9.2 %shard_map.322 = (bf16[2,512,512]{2,1,0:T(8,128)(2,1)}, bf16[2,512,512]{2,1,0:T(8,128)(2,1)}, bf16[512,1024]{1,0:T(8,128)(2,1)}, bf16[512,1024]{1,0:T(8,128)(2,1)}) custom-call(s32[4]{0:T(128)} %pad_add_fusion.2.info_ref.left_at, bf16[4,2,128,1024]{3,2,1,0:T(8,128)(2,1)} %bitcast.147, bf16[1024,1024]{1,0:T(8,128)(2,1)} %get-tuple-element.170.refs_1_, ...), custom_call_target="tpu_custom_call" | custom-call | flops 4294967296 | bytes 10000000 | tf_op jit(solution)/shard_map/pallas_call | solution.py:1032
  282.9 11.1 %shard_map.327 = (bf16[2,512,512]{2,1,0:T(8,128)(2,1)}, bf16[2,512,512]{2,1,0:T(8,128)(2,1)}, bf16[512,1536]{1,0:T(8,128)(2,1)}, bf16[512,1536]{1,0:T(8,128)(2,1)}) custom-call(s32[4]{0:T(128)} %pad_add_fusion.2.info_ref.left_at, bf16[4,2,128,1024]{3,2,1,0:T(8,128)(2,1)} %bitcast.143, bf16[4,2,128,1024]{3,2,1,0:T(8,128)(2,1)} %bitcast.145, ...), custom_call_target="tpu_custom_call" | custom-call | flops 5368709120 | bytes 10000000 | tf_op jit(solution)/shard_map/pallas_call | solution.py:1032
  293.9 2.1 collective-permute-start.35
  298.6 6.5 %shard_map.316 = (bf16[512,768]{1,0:T(8,128)(2,1)}, bf16[512,768]{1,0:T(8,128)(2,1)}) custom-call(s32[4]{0:T(128)} %pad_add_fusion.2.info_ref.left_at, bf16[4,2,128,1024]{3,2,1,0:T(8,128)(2,1)} %bitcast.124, bf16[1024,768]{1,0:T(8,128)(2,1)} %get-tuple-element.142.refs_1_, bf16[1024,768]{1,0:T(8,128)(2,1)} %get-tuple-element.145.refs_2_, ...), custom_call_target="tpu_custom_call" | custom-call | flops 1610612736 | bytes 10000000 | tf_op jit(solution)/shard_map/pallas_call | solution.py:1032
  306.8 2.3 collective-permute-done.26.got_ref.refs_2_
  315.6 14.2 %shard_map.309 = (bf16[1024,768]{1,0:T(8,128)(2,1)}, f32[8,768]{1,0:T(8,128)S(1)}) custom-call(s32[2,4]{1,0:T(2,128)S(1)} %pad_add_fusion.1.win_ref, bf16[1024,768]{1,0:T(8,128)(2,1)S(1)} %copy-done.57, bf16[1024,128]{1,0:T(8,128)(2,1)S(1)} %copy-done.31, bf16[1024,128]{1,0:T(8,128)(2,1)S(1)} %get-tuple-element.272.refs_4_.hotk_ref, ...), custom_call_target="tpu_custom_call" | custom-call | flops 8000000000 | bytes 8000000 | tf_op jit(solution)/shard_map/pallas_call | solution.py:636
  329.9 6.4 %shard_map.315 = (bf16[512,768]{1,0:T(8,128)(2,1)}, bf16[512,768]{1,0:T(8,128)(2,1)}) custom-call(s32[4]{0:T(128)} %pad_add_fusion.2.info_ref.left_at, bf16[4,2,128,1024]{3,2,1,0:T(8,128)(2,1)} %bitcast.125, bf16[1024,768]{1,0:T(8,128)(2,1)} %get-tuple-element.139.refs_0_.refs_1_, bf16[1024,768]{1,0:T(8,128)(2,1)} %get-tuple-element.145.refs_2_, ...), custom_call_target="tpu_custom_call" | custom-call | flops 1610612736 | bytes 10000000 | tf_op jit(solution)/shard_map/pallas_call | solution.py:1032
  336.3 34.6 %collective-permute-done.20.got_ref = bf16[512,768]{1,0:T(8,128)(2,1)} collective-permute-done((bf16[512,768]{1,0:T(8,128)(2,1)}, bf16[512,768]{1,0:T(8,128)(2,1)}, u32[]{:S(2)}, u32[]{:S(2)}) %collective-permute-start.20) | collective-permute-done | bytes 786464 | tf_op jit(solution)/shard_map/ppermute | solution.py:338
  370.9 2.0 collective-permute-start.19
  373.0 2.3 shard_map.317
  376.9 2.1 shard_map.324
  382.9 2.1 collective-permute-start.37
  384.9 12.5 %shard_map.313 = (f32[1024,1024]{1,0:T(8,128)}, f32[8,1024]{1,0:T(8,128)}) custom-call(bf16[1024,1024]{1,0:T(8,128)(2,1)} %get-tuple-element.136.branch_ref, bf16[1024,768]{1,0:T(8,128)(2,1)} %get-tuple-element.139.refs_0_.refs_1_, bf16[1024,768]{1,0:T(8,128)(2,1)} %get-tuple-element.142.refs_1_, bf16[1024,768]{1,0:T(8,128)(2,1)} %get-tuple-element.145.refs_2_, ...), custom_call_target="tpu_custom_call" | custom-call | flops 6400000000 | bytes 20000000 | tf_op jit(solution)/shard_map/pallas_call | solution.py:1203
  397.4 9.8 %collective-permute-done.29.refs_5_ = bf16[512,512]{1,0:T(8,128)(2,1)} collective-permute-done((bf16[512,512]{1,0:T(8,128)(2,1)}, bf16[512,512]{1,0:T(8,128)(2,1)}, u32[]{:S(2)}, u32[]{:S(2)}) %collective-permute-start.29) | collective-permute-done | bytes 524320 | tf_op jit(solution)/shard_map/ppermute | solution.py:334
  407.3 3.6 shard_map.325
  411.0 3.3 shard_map.318
  416.2 2.1 collective-permute-start.23
  420.4 2.5 collective-permute-start.31
  423.0 4.0 shard_map.330
  427.0 2.8 collective-permute-start.32
  429.8 10.3 %collective-permute-done.23.refs_2_ = bf16[128,768]{1,0:T(8,128)(2,1)S(1)} collective-permute-done((bf16[128,768]{1,0:T(8,128)(2,1)}, bf16[128,768]{1,0:T(8,128)(2,1)S(1)}, u32[]{:S(2)}, u32[]{:S(2)}) %collective-permute-start.23) | collective-permute-done | bytes 196640 | tf_op jit(solution)/shard_map/ppermute | solution.py:338
  441.2 13.6 %collective-permute-start.39 = (bf16[128,1280]{1,0:T(8,128)(2,1)}, bf16[128,1280]{1,0:T(8,128)(2,1)S(1)}, u32[]{:S(2)}, u32[]{:S(2)}) collective-permute-start(bf16[128,1280]{1,0:T(8,128)(2,1)} %get-tuple-element.198), channel_id=1, source_target_pairs={{0,16},{4,20},{8,24},{12,28},{16,0},{20,4},{24,8},{28,12},{1,17},{... | collective-permute-start | bytes 983048 | tf_op jit(solution)/shard_map/ppermute | solution.py:338
  457.8 31.0 %shard_map.320 = (f32[1,384]{1,0:T(1,128)}, f32[32,1,1152]{2,1,0:T(1,128)}) custom-call(f32[32,1,384]{2,1,0:T(1,128)} %broadcast_in_dim.94.sum_ref, f32[1,1152]{1,0:T(1,128)} %concatenate.43.row_ref), custom_call_target="tpu_custom_call" | custom-call | flops 1000000 | bytes 1000000 | tf_op jit(solution)/shard_map/pallas_call | solution.py:1276
  490.5 2.1 copy.55
  503.8 2.6 shard_map.332
  (321 shorter events, 64.7 us)
Async XLA Ops:
  2.2 34.0 %collective-permute-start.4 = (bf16[1,1536]{1,0:T(2,128)(2,1)S(1)}, bf16[1,1536]{1,0:T(2,128)(2,1)S(1)}, u32[]{:S(2)}, u32[]{:S(2)}) collective-permute-start(bf16[1,1536]{1,0:T(2,128)(2,1)S(1)} %pad_maximum_fusion.3), channel_id=1, source_target_pairs={{0,2},{1,3},{2,0},{3,1},{4,6},{5,7},{6,4},{7,5},{8,10},{9,11},{10,... | collective-permute-start | bytes 9224 | tf_op jit(solution)/shard_map/ppermute | solution.py:334
  5.3 31.0 %collective-permute-start.1 = (bf16[1,1536]{1,0:T(2,128)(2,1)S(1)}, bf16[1,1536]{1,0:T(2,128)(2,1)S(1)}, u32[]{:S(2)}, u32[]{:S(2)}) collective-permute-start(bf16[1,1536]{1,0:T(2,128)(2,1)S(1)} %pad_maximum_fusion.3), channel_id=1, source_target_pairs={{0,1},{1,0},{2,3},{3,2},{4,5},{5,4},{6,7},{7,6},{8,9},{9,8},{10,11... | collective-permute-start | bytes 9224 | tf_op jit(solution)/shard_map/ppermute | solution.py:334
  10.4 27.2 %collective-permute-start.2 = (bf16[512,1024]{1,0:T(8,128)(2,1)}, bf16[512,1024]{1,0:T(8,128)(2,1)S(1)}, u32[]{:S(2)}, u32[]{:S(2)}) collective-permute-start(bf16[512,1024]{1,0:T(8,128)(2,1)} %get-tuple-element.117), channel_id=1, source_target_pairs={{0,2},{1,3},{2,0},{3,1},{4,6},{5,7},{6,4},{7,5},{8,10},{9,11},{10,... | collective-permute-start | bytes 3145736 | tf_op jit(solution)/shard_map/ppermute | solution.py:334
  10.5 72.2 %collective-permute-start = (bf16[2,512,1024]{2,1,0:T(8,128)(2,1)}, bf16[2,512,1024]{2,1,0:T(8,128)(2,1)}, u32[]{:S(2)}, u32[]{:S(2)}) collective-permute-start(bf16[2,512,1024]{2,1,0:T(8,128)(2,1)} %get-tuple-element.114.refs_0_.refs_1_.refs_4_.refs_5_.wa_ref.wb_ref), channel_id=1, source_target_pairs={{0,1},{1,0},{2,3},{3,2},{4,5},{5,4},{6,7},{7,6},{8,9},{9,8},{10,11... | collective-permute-start | bytes 6291464 | tf_op jit(solution)/shard_map/ppermute | solution.py:334
  18.0 41.2 %collective-permute-start.8 = (bf16[512,1024]{1,0:T(8,128)(2,1)}, bf16[512,1024]{1,0:T(8,128)(2,1)}, u32[]{:S(2)}, u32[]{:S(2)}) collective-permute-start(bf16[512,1024]{1,0:T(8,128)(2,1)} %get-tuple-element.121), channel_id=1, source_target_pairs={{0,2},{1,3},{2,0},{3,1},{4,6},{5,7},{6,4},{7,5},{8,10},{9,11},{10,... | collective-permute-start | bytes 3145736 | tf_op jit(solution)/shard_map/ppermute | solution.py:334
  24.0 83.9 %copy-start.29 = (bf16[1024,128]{1,0:T(8,128)(2,1)}, bf16[1024,128]{1,0:T(8,128)(2,1)S(1)}, u32[]{:S(2)}) copy-start(bf16[1024,128]{1,0:T(8,128)(2,1)S(1)} %get-tuple-element.273.refs_3_.hotq_ref) | copy-start | bytes 786436
  25.8 55.3 %copy-start.40 = (bf16[2,512,1024]{2,1,0:T(8,128)(2,1)S(1)}, bf16[2,512,1024]{2,1,0:T(8,128)(2,1)}, u32[]{:S(2)}) copy-start(bf16[2,512,1024]{2,1,0:T(8,128)(2,1)} %get-tuple-element.124.refs_2_.refs_3_.refs_0_) | copy-start | bytes 6291460
  36.2 44.9 %collective-permute-start.11 = (bf16[512,1024]{1,0:T(8,128)(2,1)S(1)}, bf16[512,1024]{1,0:T(8,128)(2,1)S(1)}, u32[]{:S(2)}, u32[]{:S(2)}) collective-permute-start(bf16[512,1024]{1,0:T(8,128)(2,1)S(1)} %copy-done.76), channel_id=1, source_target_pairs={{0,2},{1,3},{2,0},{3,1},{4,6},{5,7},{6,4},{7,5},{8,10},{9,11},{10,... | collective-permute-start | bytes 3145736 | tf_op jit(solution)/shard_map/ppermute | solution.py:334
  36.3 1.2 collective-permute-start.5
  37.6 197.5 %copy-start.12 = (bf16[512,1024]{1,0:T(8,128)(2,1)}, bf16[512,1024]{1,0:T(8,128)(2,1)S(1)}, u32[]{:S(2)}) copy-start(bf16[512,1024]{1,0:T(8,128)(2,1)S(1)} %collective-permute-done.2.refs_0_.refs_8_.wa_ref.refs_6_) | copy-start | bytes 3145732
  37.6 43.5 %collective-permute-start.6 = (bf16[512,1024]{1,0:T(8,128)(2,1)S(1)}, bf16[512,1024]{1,0:T(8,128)(2,1)S(1)}, u32[]{:S(2)}, u32[]{:S(2)}) collective-permute-start(bf16[512,1024]{1,0:T(8,128)(2,1)S(1)} %collective-permute-done.2.refs_0_.refs_8_.wa_ref.refs_6_), channel_id=1, source_target_pairs={{0,4},{4,0},{8,12},{12,8},{16,20},{20,16},{24,28},{28,24},{1,5},{5... | collective-permute-start | bytes 3145736 | tf_op jit(solution)/shard_map/ppermute | solution.py:338
  39.1 55.9 %collective-permute-start.3 = (bf16[512,1024]{1,0:T(8,128)(2,1)S(1)}, bf16[512,1024]{1,0:T(8,128)(2,1)S(1)}, u32[]{:S(2)}, u32[]{:S(2)}) collective-permute-start(bf16[512,1024]{1,0:T(8,128)(2,1)S(1)} %collective-permute-done.2.refs_0_.refs_8_.wa_ref.refs_6_), channel_id=1, source_target_pairs={{0,1},{1,0},{2,3},{3,2},{4,5},{5,4},{6,7},{7,6},{8,9},{9,8},{10,11... | collective-permute-start | bytes 3145736 | tf_op jit(solution)/shard_map/ppermute | solution.py:334
  59.2 70.2 %collective-permute-start.16 = (bf16[2,512,1024]{2,1,0:T(8,128)(2,1)S(1)}, bf16[2,512,1024]{2,1,0:T(8,128)(2,1)S(1)}, u32[]{:S(2)}, u32[]{:S(2)}) collective-permute-start(bf16[2,512,1024]{2,1,0:T(8,128)(2,1)S(1)} %copy-done.39), channel_id=1, source_target_pairs={{0,1},{1,0},{2,3},{3,2},{4,5},{5,4},{6,7},{7,6},{8,9},{9,8},{10,11... | collective-permute-start | bytes 6291464 | tf_op jit(solution)/shard_map/ppermute | solution.py:334
  81.1 63.0 %copy-start.43 = (bf16[512,1024]{1,0:T(8,128)(2,1)}, bf16[512,1024]{1,0:T(8,128)(2,1)S(1)}, u32[]{:S(2)}) copy-start(bf16[512,1024]{1,0:T(8,128)(2,1)S(1)} %collective-permute-done.11.refs_2_) | copy-start | bytes 3145732
  81.1 55.9 %collective-permute-start.17 = (bf16[2,512,1024]{2,1,0:T(8,128)(2,1)S(1)}, bf16[2,512,1024]{2,1,0:T(8,128)(2,1)S(1)}, u32[]{:S(2)}, u32[]{:S(2)}) collective-permute-start(bf16[2,512,1024]{2,1,0:T(8,128)(2,1)S(1)} %copy-done.40), channel_id=1, source_target_pairs={{0,1},{1,0},{2,3},{3,2},{4,5},{5,4},{6,7},{7,6},{8,9},{9,8},{10,11... | collective-permute-start | bytes 6291464 | tf_op jit(solution)/shard_map/ppermute | solution.py:334
  81.1 26.3 %collective-permute-start.9 = (bf16[512,1024]{1,0:T(8,128)(2,1)}, bf16[512,1024]{1,0:T(8,128)(2,1)S(1)}, u32[]{:S(2)}, u32[]{:S(2)}) collective-permute-start(bf16[512,1024]{1,0:T(8,128)(2,1)} %collective-permute-done.8.refs_0_.refs_8_), channel_id=1, source_target_pairs={{0,4},{4,0},{8,12},{12,8},{16,20},{20,16},{24,28},{28,24},{1,5},{5... | collective-permute-start | bytes 3145736 | tf_op jit(solution)/shard_map/ppermute | solution.py:338
  82.7 24.8 %collective-permute-start.7 = (bf16[512,1024]{1,0:T(8,128)(2,1)S(1)}, bf16[512,1024]{1,0:T(8,128)(2,1)S(1)}, u32[]{:S(2)}, u32[]{:S(2)}) collective-permute-start(bf16[512,1024]{1,0:T(8,128)(2,1)S(1)} %collective-permute-done.6.refs_0_.refs_10_.wa_ref.refs_8_), channel_id=1, source_target_pairs={{0,1},{1,0},{2,3},{3,2},{4,5},{5,4},{6,7},{7,6},{8,9},{9,8},{10,11... | collective-permute-start | bytes 3145736 | tf_op jit(solution)/shard_map/ppermute | solution.py:334
  95.0 34.3 %collective-permute-start.12 = (bf16[512,1024]{1,0:T(8,128)(2,1)S(1)}, bf16[512,1024]{1,0:T(8,128)(2,1)S(1)}, u32[]{:S(2)}, u32[]{:S(2)}) collective-permute-start(bf16[512,1024]{1,0:T(8,128)(2,1)S(1)} %collective-permute-done.11.refs_2_), channel_id=1, source_target_pairs={{0,4},{4,0},{8,12},{12,8},{16,20},{20,16},{24,28},{28,24},{1,5},{5... | collective-permute-start | bytes 3145736 | tf_op jit(solution)/shard_map/ppermute | solution.py:338
  107.4 45.9 %copy-start.45 = (bf16[512,1024]{1,0:T(8,128)(2,1)}, bf16[512,1024]{1,0:T(8,128)(2,1)S(1)}, u32[]{:S(2)}) copy-start(bf16[512,1024]{1,0:T(8,128)(2,1)S(1)} %collective-permute-done.9.refs_0_.refs_10_) | copy-start | bytes 3145732
  107.4 36.7 %collective-permute-start.14 = (bf16[512,1024]{1,0:T(8,128)(2,1)}, bf16[512,1024]{1,0:T(8,128)(2,1)S(1)}, u32[]{:S(2)}, u32[]{:S(2)}) collective-permute-start(bf16[512,1024]{1,0:T(8,128)(2,1)} %collective-permute-done.8.refs_0_.refs_8_), channel_id=1, source_target_pairs={{0,1},{1,0},{2,3},{3,2},{4,5},{5,4},{6,7},{7,6},{8,9},{9,8},{10,11... | collective-permute-start | bytes 3145736 | tf_op jit(solution)/shard_map/ppermute | solution.py:334
  107.4 36.6 %collective-permute-start.15 = (bf16[512,1024]{1,0:T(8,128)(2,1)S(1)}, bf16[512,1024]{1,0:T(8,128)(2,1)S(1)}, u32[]{:S(2)}, u32[]{:S(2)}) collective-permute-start(bf16[512,1024]{1,0:T(8,128)(2,1)S(1)} %collective-permute-done.11.refs_2_), channel_id=1, source_target_pairs={{0,1},{1,0},{2,3},{3,2},{4,5},{5,4},{6,7},{7,6},{8,9},{9,8},{10,11... | collective-permute-start | bytes 3145736 | tf_op jit(solution)/shard_map/ppermute | solution.py:334
  129.3 23.9 %collective-permute-start.10 = (bf16[512,1024]{1,0:T(8,128)(2,1)S(1)}, bf16[512,1024]{1,0:T(8,128)(2,1)S(1)}, u32[]{:S(2)}, u32[]{:S(2)}) collective-permute-start(bf16[512,1024]{1,0:T(8,128)(2,1)S(1)} %collective-permute-done.9.refs_0_.refs_10_), channel_id=1, source_target_pairs={{0,1},{1,0},{2,3},{3,2},{4,5},{5,4},{6,7},{7,6},{8,9},{9,8},{10,11... | collective-permute-start | bytes 3145736 | tf_op jit(solution)/shard_map/ppermute | solution.py:334
  129.4 23.9 %collective-permute-start.13 = (bf16[512,1024]{1,0:T(8,128)(2,1)S(1)}, bf16[512,1024]{1,0:T(8,128)(2,1)S(1)}, u32[]{:S(2)}, u32[]{:S(2)}) collective-permute-start(bf16[512,1024]{1,0:T(8,128)(2,1)S(1)} %collective-permute-done.12.refs_2_.refs_4_), channel_id=1, source_target_pairs={{0,1},{1,0},{2,3},{3,2},{4,5},{5,4},{6,7},{7,6},{8,9},{9,8},{10,11... | collective-permute-start | bytes 3145736 | tf_op jit(solution)/shard_map/ppermute | solution.py:334
  204.3 78.6 %collective-permute-start.33 = (bf16[2,512,2560]{2,1,0:T(8,128)(2,1)}, bf16[2,512,2560]{2,1,0:T(8,128)(2,1)}, u32[]{:S(2)}, u32[]{:S(2)}) collective-permute-start(bf16[2,512,2560]{2,1,0:T(8,128)(2,1)} %shard_map.326), channel_id=1, source_target_pairs={{0,1},{1,0},{2,3},{3,2},{4,5},{5,4},{6,7},{7,6},{8,9},{9,8},{10,11... | collective-permute-start | bytes 15728648 | tf_op jit(solution)/shard_map/ppermute | solution.py:334
  213.6 60.0 %collective-permute-start.25 = (bf16[2,512,2048]{2,1,0:T(8,128)(2,1)}, bf16[2,512,2048]{2,1,0:T(8,128)(2,1)}, u32[]{:S(2)}, u32[]{:S(2)}) collective-permute-start(bf16[2,512,2048]{2,1,0:T(8,128)(2,1)} %shard_map.321), channel_id=1, source_target_pairs={{0,1},{1,0},{2,3},{3,2},{4,5},{5,4},{6,7},{7,6},{8,9},{9,8},{10,11... | collective-permute-start | bytes 12582920 | tf_op jit(solution)/shard_map/ppermute | solution.py:334
  273.5 25.1 %collective-permute-start.18 = (bf16[2,512,1536]{2,1,0:T(8,128)(2,1)}, bf16[2,512,1536]{2,1,0:T(8,128)(2,1)}, u32[]{:S(2)}, u32[]{:S(2)}) collective-permute-start(bf16[2,512,1536]{2,1,0:T(8,128)(2,1)} %shard_map.314), channel_id=1, source_target_pairs={{0,1},{1,0},{2,3},{3,2},{4,5},{5,4},{6,7},{7,6},{8,9},{9,8},{10,11... | collective-permute-start | bytes 9437192 | tf_op jit(solution)/shard_map/ppermute | solution.py:334
  282.8 26.3 %collective-permute-start.26 = (bf16[2,512,512]{2,1,0:T(8,128)(2,1)}, bf16[2,512,512]{2,1,0:T(8,128)(2,1)S(1)}, u32[]{:S(2)}, u32[]{:S(2)}) collective-permute-start(bf16[2,512,512]{2,1,0:T(8,128)(2,1)} %get-tuple-element.175), channel_id=1, source_target_pairs={{0,2},{1,3},{2,0},{3,1},{4,6},{5,7},{6,4},{7,5},{8,10},{9,11},{10,... | collective-permute-start | bytes 3145736 | tf_op jit(solution)/shard_map/ppermute | solution.py:334
  293.9 85.6 %collective-permute-start.35 = (bf16[512,1536]{1,0:T(8,128)(2,1)}, bf16[512,1536]{1,0:T(8,128)(2,1)}, u32[]{:S(2)}, u32[]{:S(2)}) collective-permute-start(bf16[512,1536]{1,0:T(8,128)(2,1)} %get-tuple-element.191), channel_id=1, source_target_pairs={{0,4},{4,0},{8,12},{12,8},{16,20},{20,16},{24,28},{28,24},{1,5},{5... | collective-permute-start | bytes 4718600 | tf_op jit(solution)/shard_map/ppermute | solution.py:338
  296.6 78.7 %collective-permute-start.28 = (bf16[512,1024]{1,0:T(8,128)(2,1)}, bf16[512,1024]{1,0:T(8,128)(2,1)}, u32[]{:S(2)}, u32[]{:S(2)}) collective-permute-start(bf16[512,1024]{1,0:T(8,128)(2,1)} %get-tuple-element.177), channel_id=1, source_target_pairs={{0,4},{4,0},{8,12},{12,8},{16,20},{20,16},{24,28},{28,24},{1,5},{5... | collective-permute-start | bytes 3145736 | tf_op jit(solution)/shard_map/ppermute | solution.py:338
  296.7 82.3 %collective-permute-start.34 = (bf16[2,512,512]{2,1,0:T(8,128)(2,1)}, bf16[2,512,512]{2,1,0:T(8,128)(2,1)}, u32[]{:S(2)}, u32[]{:S(2)}) collective-permute-start(bf16[2,512,512]{2,1,0:T(8,128)(2,1)} %get-tuple-element.190), channel_id=1, source_target_pairs={{0,2},{1,3},{2,0},{3,1},{4,6},{5,7},{6,4},{7,5},{8,10},{9,11},{10,... | collective-permute-start | bytes 3145736 | tf_op jit(solution)/shard_map/ppermute | solution.py:334
  305.2 65.7 %collective-permute-start.20 = (bf16[512,768]{1,0:T(8,128)(2,1)}, bf16[512,768]{1,0:T(8,128)(2,1)}, u32[]{:S(2)}, u32[]{:S(2)}) collective-permute-start(bf16[512,768]{1,0:T(8,128)(2,1)} %get-tuple-element.154), channel_id=1, source_target_pairs={{0,4},{4,0},{8,12},{12,8},{16,20},{20,16},{24,28},{28,24},{1,5},{5... | collective-permute-start | bytes 2359304 | tf_op jit(solution)/shard_map/ppermute | solution.py:338
  309.2 73.6 %collective-permute-start.27 = (bf16[512,512]{1,0:T(8,128)(2,1)S(1)}, bf16[512,512]{1,0:T(8,128)(2,1)}, u32[]{:S(2)}, u32[]{:S(2)}) collective-permute-start(bf16[512,512]{1,0:T(8,128)(2,1)S(1)} %shard_map.323), channel_id=1, source_target_pairs={{0,4},{4,0},{8,12},{12,8},{16,20},{20,16},{24,28},{28,24},{1,5},{5... | collective-permute-start | bytes 1572872 | tf_op jit(solution)/shard_map/ppermute | solution.py:338
  370.9 40.0 %collective-permute-start.19 = (bf16[512,768]{1,0:T(8,128)(2,1)}, bf16[512,768]{1,0:T(8,128)(2,1)}, u32[]{:S(2)}, u32[]{:S(2)}) collective-permute-start(bf16[512,768]{1,0:T(8,128)(2,1)} %get-tuple-element.152), channel_id=1, source_target_pairs={{0,4},{4,0},{8,12},{12,8},{16,20},{20,16},{24,28},{28,24},{1,5},{5... | collective-permute-start | bytes 2359304 | tf_op jit(solution)/shard_map/ppermute | solution.py:338
  375.3 35.6 %collective-permute-start.21 = (bf16[512,768]{1,0:T(8,128)(2,1)}, bf16[512,768]{1,0:T(8,128)(2,1)}, u32[]{:S(2)}, u32[]{:S(2)}) collective-permute-start(bf16[512,768]{1,0:T(8,128)(2,1)} %shard_map.317), channel_id=1, source_target_pairs={{0,2},{1,3},{2,0},{3,1},{4,6},{5,7},{6,4},{7,5},{8,10},{9,11},{10,... | collective-permute-start | bytes 2359304 | tf_op jit(solution)/shard_map/ppermute | solution.py:334
  379.0 28.3 %collective-permute-start.29 = (bf16[512,512]{1,0:T(8,128)(2,1)}, bf16[512,512]{1,0:T(8,128)(2,1)}, u32[]{:S(2)}, u32[]{:S(2)}) collective-permute-start(bf16[512,512]{1,0:T(8,128)(2,1)} %shard_map.324), channel_id=1, source_target_pairs={{0,2},{1,3},{2,0},{3,1},{4,6},{5,7},{6,4},{7,5},{8,10},{9,11},{10,... | collective-permute-start | bytes 1572872 | tf_op jit(solution)/shard_map/ppermute | solution.py:334
  381.5 36.9 %collective-permute-start.36 = (bf16[512,512]{1,0:T(8,128)(2,1)}, bf16[512,512]{1,0:T(8,128)(2,1)}, u32[]{:S(2)}, u32[]{:S(2)}) collective-permute-start(bf16[512,512]{1,0:T(8,128)(2,1)} %shard_map.328), channel_id=1, source_target_pairs={{0,4},{4,0},{8,12},{12,8},{16,20},{20,16},{24,28},{28,24},{1,5},{5... | collective-permute-start | bytes 1572872 | tf_op jit(solution)/shard_map/ppermute | solution.py:338
  382.9 37.6 %collective-permute-start.37 = (bf16[512,768]{1,0:T(8,128)(2,1)S(1)}, bf16[512,768]{1,0:T(8,128)(2,1)S(1)}, u32[]{:S(2)}, u32[]{:S(2)}) collective-permute-start(bf16[512,768]{1,0:T(8,128)(2,1)S(1)} %shard_map.329), channel_id=1, source_target_pairs={{0,2},{1,3},{2,0},{3,1},{4,6},{5,7},{6,4},{7,5},{8,10},{9,11},{10,... | collective-permute-start | bytes 2359304 | tf_op jit(solution)/shard_map/ppermute | solution.py:334
  410.9 44.0 %collective-permute-start.30 = (bf16[128,1024]{1,0:T(8,128)(2,1)}, bf16[128,1024]{1,0:T(8,128)(2,1)S(1)}, u32[]{:S(2)}, u32[]{:S(2)}) collective-permute-start(bf16[128,1024]{1,0:T(8,128)(2,1)} %get-tuple-element.179), channel_id=1, source_target_pairs={{0,8},{4,12},{8,0},{12,4},{16,24},{20,28},{24,16},{28,20},{1,9},{5... | collective-permute-start | bytes 786440 | tf_op jit(solution)/shard_map/ppermute | solution.py:338
  414.2 12.8 %collective-permute-start.22 = (bf16[128,768]{1,0:T(8,128)(2,1)}, bf16[128,768]{1,0:T(8,128)(2,1)S(1)}, u32[]{:S(2)}, u32[]{:S(2)}) collective-permute-start(bf16[128,768]{1,0:T(8,128)(2,1)} %get-tuple-element.156), channel_id=1, source_target_pairs={{0,8},{4,12},{8,0},{12,4},{16,24},{20,28},{24,16},{28,20},{1,9},{5... | collective-permute-start | bytes 589832 | tf_op jit(solution)/shard_map/ppermute | solution.py:338
  416.2 23.9 %collective-permute-start.23 = (bf16[128,768]{1,0:T(8,128)(2,1)}, bf16[128,768]{1,0:T(8,128)(2,1)S(1)}, u32[]{:S(2)}, u32[]{:S(2)}) collective-permute-start(bf16[128,768]{1,0:T(8,128)(2,1)} %get-tuple-element.157), channel_id=1, source_target_pairs={{0,16},{4,20},{8,24},{12,28},{16,0},{20,4},{24,8},{28,12},{1,17},{... | collective-permute-start | bytes 589832 | tf_op jit(solution)/shard_map/ppermute | solution.py:338
  418.3 22.9 %collective-permute-start.24 = (bf16[128,768]{1,0:T(8,128)(2,1)}, bf16[128,768]{1,0:T(8,128)(2,1)S(1)}, u32[]{:S(2)}, u32[]{:S(2)}) collective-permute-start(bf16[128,768]{1,0:T(8,128)(2,1)} %get-tuple-element.158), channel_id=1, source_target_pairs={{0,24},{4,28},{8,16},{12,20},{16,8},{20,12},{24,0},{28,4},{1,25},{... | collective-permute-start | bytes 589832 | tf_op jit(solution)/shard_map/ppermute | solution.py:338
  420.4 68.4 %copy-start.35 = (bf16[128,768]{1,0:T(8,128)(2,1)S(1)}, bf16[128,768]{1,0:T(8,128)(2,1)}, u32[]{:S(2)}) copy-start(bf16[128,768]{1,0:T(8,128)(2,1)} %get-tuple-element.155.refs_0_) | copy-start | bytes 589828
  420.4 68.4 %copy-start.37 = (s32[4]{0:T(128)S(1)}, s32[4]{0:T(128)}, u32[]{:S(2)}) copy-start(s32[4]{0:T(128)} %pad_add_fusion.2.info_ref.left_at) | copy-start | bytes 52
  420.4 72.1 %collective-permute-start.31 = (bf16[128,1024]{1,0:T(8,128)(2,1)}, bf16[128,1024]{1,0:T(8,128)(2,1)}, u32[]{:S(2)}, u32[]{:S(2)}) collective-permute-start(bf16[128,1024]{1,0:T(8,128)(2,1)} %get-tuple-element.180), channel_id=1, source_target_pairs={{0,16},{4,20},{8,24},{12,28},{16,0},{20,4},{24,8},{28,12},{1,17},{... | collective-permute-start | bytes 786440 | tf_op jit(solution)/shard_map/ppermute | solution.py:338
  427.0 65.5 %collective-permute-start.32 = (bf16[128,1024]{1,0:T(8,128)(2,1)}, bf16[128,1024]{1,0:T(8,128)(2,1)}, u32[]{:S(2)}, u32[]{:S(2)}) collective-permute-start(bf16[128,1024]{1,0:T(8,128)(2,1)} %get-tuple-element.181), channel_id=1, source_target_pairs={{0,24},{4,28},{8,16},{12,20},{16,8},{20,12},{24,0},{28,4},{1,25},{... | collective-permute-start | bytes 786440 | tf_op jit(solution)/shard_map/ppermute | solution.py:338
  440.1 52.4 %collective-permute-start.38 = (bf16[128,1280]{1,0:T(8,128)(2,1)}, bf16[128,1280]{1,0:T(8,128)(2,1)S(1)}, u32[]{:S(2)}, u32[]{:S(2)}) collective-permute-start(bf16[128,1280]{1,0:T(8,128)(2,1)} %get-tuple-element.197), channel_id=1, source_target_pairs={{0,8},{4,12},{8,0},{12,4},{16,24},{20,28},{24,16},{28,20},{1,9},{5... | collective-permute-start | bytes 983048 | tf_op jit(solution)/shard_map/ppermute | solution.py:338
  441.2 51.3 %collective-permute-start.39 = (bf16[128,1280]{1,0:T(8,128)(2,1)}, bf16[128,1280]{1,0:T(8,128)(2,1)S(1)}, u32[]{:S(2)}, u32[]{:S(2)}) collective-permute-start(bf16[128,1280]{1,0:T(8,128)(2,1)} %get-tuple-element.198), channel_id=1, source_target_pairs={{0,16},{4,20},{8,24},{12,28},{16,0},{20,4},{24,8},{28,12},{1,17},{... | collective-permute-start | bytes 983048 | tf_op jit(solution)/shard_map/ppermute | solution.py:338
  454.8 37.7 %collective-permute-start.40 = (bf16[128,1280]{1,0:T(8,128)(2,1)}, bf16[128,1280]{1,0:T(8,128)(2,1)S(1)}, u32[]{:S(2)}, u32[]{:S(2)}) collective-permute-start(bf16[128,1280]{1,0:T(8,128)(2,1)} %get-tuple-element.199), channel_id=1, source_target_pairs={{0,24},{4,28},{8,16},{12,20},{16,8},{20,12},{24,0},{28,4},{1,25},{... | collective-permute-start | bytes 983048 | tf_op jit(solution)/shard_map/ppermute | solution.py:338
  (71 other events, 786.7 us)

commit v6 on v5

--- a/solution.py
+++ b/solution.py
@@ -292,6 +292,7 @@
 ROWS = 256
 GRAIN = 256
 STEP = 128
+EXTRA = 16
 FAR = -(2.0**100)
 NN = (((1,), (0,)), ((), ()))
 NT = (((1,), (1,)), ((), ()))
@@ -303,11 +304,6 @@
 
 def after(values, others):
     return lax.optimization_barrier((values, others))[0]
-
-
-def half_of(values, which, axis):
-    size = values.shape[axis] // 2
-    return lax.dynamic_slice_in_dim(values, which * size, size, axis)
 
 
 def whole(shape):
@@ -347,29 +343,41 @@
     return [own, near, far_a, near_a, far_b, near_b]
 
 
-def pack_heads_kernel(info_ref, qkv_ref, out_ref, both_ref, first_ref):
+def pack_heads_kernel(info_ref, qkv_ref, out_ref, qv_ref, up_ref, both_ref, first_ref):
+    size = up_ref.shape[1] // 2
     for u in range(HALF):
+        at = pl.ds(pl.multiple_of(info_ref[u] * UNIT, UNIT), UNIT)
         for j in range(3):
-            at = pl.ds(pl.multiple_of(info_ref[u] * UNIT, UNIT), UNIT)
             both_ref[u, j * UNIT : (j + 1) * UNIT, :] = qkv_ref[j, :, at].T
-        at = pl.ds(pl.multiple_of(info_ref[u] * UNIT, UNIT), UNIT)
-        both_ref[u, 3 * UNIT :, :] = out_ref[at, :]
+        both_ref[u, 3 * UNIT : 4 * UNIT, :] = out_ref[at, :]
+        hidden = pl.ds(pl.multiple_of(info_ref[u] * size, UNIT), size)
+        rest = jnp.zeros((1, D - 2 * UNIT - size), F32)
+        qv = qv_ref[:, at].astype(F32)
+        parts = [qv[0:1], qv[1:2], up_ref[0:1, hidden], rest]
+        bias = jnp.broadcast_to(jnp.concatenate(parts, axis=1), (EXTRA, D))
+        both_ref[u, 4 * UNIT :, :] = bias.astype(BF16)
     first_ref[...] = both_ref[0]
 
 
-def pack_heads(info, w_qkv, w_out):
+def pack_heads(info, w_qkv, w_out, b_qv, b_up):
+    rows = 4 * UNIT + EXTRA
     return pl.pallas_call(
         pack_heads_kernel,
-        out_shape=(far((HALF, 4 * UNIT, D)), far((4 * UNIT, D))),
+        out_shape=(far((HALF, rows, D)), far((rows, D))),
         grid_spec=pltpu.PrefetchScalarGridSpec(
             num_scalar_prefetch=1,
             grid=(1,),
-            in_specs=[whole((3, D, 2 * UNIT)), whole((2 * UNIT, D))],
-            out_specs=[whole((HALF, 4 * UNIT, D)), whole((4 * UNIT, D))],
+            in_specs=[
+                whole((3, D, 2 * UNIT)),
+                whole((2 * UNIT, D)),
+                whole((2, 2 * UNIT)),
+                whole((1, b_up.shape[0])),
+            ],
+            out_specs=[whole((HALF, rows, D)), whole((rows, D))],
         ),
         compiler_params=room(60),
         cost_estimate=cost(1e6, 5e6),
-    )(info, w_qkv.transpose(1, 0, 2), w_out)
+    )(info, w_qkv.transpose(1, 0, 2), w_out, b_qv, b_up.astype(F32)[None, :])
 
 
 def pack_units_kernel(info_ref, up_ref, down_ref, up_both, up_first, down_both, down_first):
@@ -398,25 +406,9 @@
             ],
             out_specs=[pl.BlockSpec((1, size, D), lambda i, info: (i, 0, 0)), whole((size, D))] * 2,
         ),
-        compiler_params=room(24),
+        compiler_params=room(60),
         cost_estimate=cost(1e6, 10e6),
     )(info, w_up, w_down)
-
-
-def fetch_bias(own, x_at):
-    packed = jnp.concatenate(own, axis=1)
-    near, far = send_mp(packed, 1), send_mp(packed, 2)
-    near_far = send_mp(far, 1)
-    order = [(packed, x_at), (packed, 1 - x_at), (near, x_at), (near, 1 - x_at)]
-    order += [(v, at) for at in (x_at, 1 - x_at) for v in (far, near_far)]
-    pieces, start = [], 0
-    for row in own:
-        size = row.shape[1]
-        pieces.append(
-            [half_of(v[:, start : start + size], at, 1).astype(F32) for v, at in order]
-        )
-        start += size
-    return pieces
 
 
 def half_specs(rows, block):
@@ -475,7 +467,7 @@
 def attend_kernel(
     win_ref, x_ref, *refs
 ):
-    weights, (bias_ref, hotq_ref, hotk_ref, qkv_ref, ctx_ref, lse_ref, w_ref, kx) = refs[:2], refs[2:]
+    weights, biases, (hotq_ref, hotk_ref, qkv_ref, ctx_ref, lse_ref, w_ref, kx) = refs[:2], refs[2:4], refs[4:]
     unit, step = pl.program_id(0), pl.program_id(1)
 
     @pl.when((unit == 0) & (step == 0))
@@ -485,9 +477,14 @@
             for j in range(3):
                 at = (2 * j + u) * UNIT
                 w_ref[at : at + UNIT, :] = part[j * UNIT : (j + 1) * UNIT]
+        first, second = [rows_of(ref)[0:1].astype(F32) for ref in biases]
+        none = jnp.zeros((1, 2 * UNIT), F32)
+        bias = [first[:, :UNIT], second[:, :UNIT], none]
+        bias += [first[:, UNIT : 2 * UNIT], second[:, UNIT : 2 * UNIT]]
+        bias = jnp.concatenate(bias, axis=1)
         for r in range(LEN // ROWS):
             rows = slice(r * ROWS, (r + 1) * ROWS)
-            qkv_ref[rows, :] = (dot(x_ref[rows, :], w_ref[...], NT) + bias_ref[...]).astype(BF16)
+            qkv_ref[rows, :] = (dot(x_ref[rows, :], w_ref[...], NT) + bias).astype(BF16)
 
     @pl.when(step == 0)
     def _():
@@ -522,7 +519,7 @@
     variants(win_ref[1, step], TILE_F, run)
 
 
-def attend_pair(win, hidden_low, heads, pair, bias, hotq, hotk):
+def attend_pair(win, hidden_low, heads, pair, hotq, hotk):
     return pl.pallas_call(
         attend_kernel,
         out_shape=(
@@ -535,8 +532,8 @@
             grid=(HALF, LEN // TILE_F),
             in_specs=[whole((LEN, D))]
             + pair_specs(4 * UNIT, 0, pair)
+            + pair_specs(EXTRA, 4 * UNIT // EXTRA, pair)
             + [
-                whole((1, 6 * UNIT)),
                 pl.BlockSpec((TILE_F, UNIT), lambda n, i, win: (i, 0)),
                 whole((LEN, UNIT)),
             ],
@@ -549,7 +546,7 @@
         ),
         compiler_params=room(32),
         cost_estimate=cost(6e9, 8e6),
-    )(win, hidden_low, *pair_of(heads, pair), bias, hotq, hotk)
+    )(win, hidden_low, *pair_of(heads, pair) * 2, hotq, hotk)
 
 
 def attend_back_kernel(
@@ -573,13 +570,6 @@
     unit, step = pl.program_id(0), pl.program_id(1)
     scale = jnp.asarray(1.0 / math.sqrt(HEAD_DIM), BF16)
 
-    @pl.when((unit == 0) & (step == 0))
-    def _():
-        weight = jnp.concatenate([rows_of(wa_ref), rows_of(wb_ref)], axis=0)
-        for r in range(LEN // ROWS):
-            rows = slice(r * ROWS, (r + 1) * ROWS)
-            grads[rows, :] = dot(branch_ref[rows, :], weight, NT).astype(BF16)
-
     @pl.when(step == 0)
     def _():
         lane = lax.broadcasted_iota(jnp.int32, (LEN, UNIT), 1)
@@ -592,6 +582,12 @@
 
     lane = lax.broadcasted_iota(jnp.int32, (TILE_B, UNIT), 1)
     rows = pl.ds(pl.multiple_of(step * TILE_B, TILE_B), TILE_B)
+
+    @pl.when(unit == 0)
+    def _():
+        weight = jnp.concatenate([rows_of(wa_ref), rows_of(wb_ref)], axis=0)
+        grads[rows, :] = dot(branch_ref[...], weight, NT).astype(BF16)
+
     queries = qkv_ref[rows, lanes_at(unit)] * scale
     grad = grads[rows, lanes_at(unit)]
     product = (grad.astype(F32) * ctx_ref[...].astype(F32)).T
@@ -643,7 +639,7 @@
                 whole((LEN, 6 * UNIT)),
                 pl.BlockSpec((TILE_B, UNIT), lambda n, i, win: (i, 0)),
                 whole((LEN, UNIT)),
-                whole((LEN, D)),
+                pl.BlockSpec((TILE_B, D), lambda n, i, win: (jnp.where(n == 0, i, LEN // TILE_B - 1), 0)),
                 *pair_specs(UNIT, 3, pair),
                 pl.BlockSpec((TILE_B, UNIT), lambda n, i, win: (i, n)),
                 pl.BlockSpec((1, 8, TILE_B), lambda n, i, win: (n, 0, i)),
@@ -729,10 +725,11 @@
 
 
 def ffn_tile(mid_ref, up_refs, down_refs, bias_refs, act_ref, slope_ref):
-    size = bias_refs[0].shape[1]
-    pres = [
-        dot(mid_ref[...], rows_of(up), NT) + bias[...] for up, bias in zip(up_refs, bias_refs)
-    ]
+    size = act_ref.shape[1] // 2
+    pres = []
+    for up, ref in zip(up_refs, bias_refs):
+        bias = rows_of(ref)[0:1, 2 * UNIT : 2 * UNIT + size].astype(F32)
+        pres.append(dot(mid_ref[...], rows_of(up), NT) + bias)
     total = 0.0
     for u in range(HALF):
         columns = slice(u * size, (u + 1) * size)
@@ -758,12 +755,12 @@
     return (
         [pl.BlockSpec((TILE_U, D), lambda i: (i, 0))]
         + pair_specs(size, 0, pair) * 2
-        + [whole((1, size))] * 2
-    )
-
-
-def ffn_pair(mid_low, up, down, pair, bias, into):
-    size = bias[0].shape[1]
+        + pair_specs(EXTRA, 4 * UNIT // EXTRA, pair)
+    )
+
+
+def ffn_pair(mid_low, up, down, pair, heads, into):
+    size = up[2].shape[0]
     tile = lambda n: pl.BlockSpec((TILE_U, n), lambda i: (i, 0))
     return pl.pallas_call(
         ffn_kernel,
@@ -777,7 +774,7 @@
         grid=(LEN // TILE_U,),
         compiler_params=room(24),
         cost_estimate=cost(4.3e9, 18e6),
-    )(mid_low, *pair_of(up, pair), *pair_of(down, pair), *bias, *into)
+    )(mid_low, *pair_of(up, pair), *pair_of(down, pair), *pair_of(heads, pair), *into)
 
 
 def ffn_last_kernel(mid_ref, *refs):
@@ -801,8 +798,8 @@
         sum_ref[j : j + 1, :] += sums[j]
 
 
-def ffn_last(mid_low, up, down, pair, bias, into, cot, *rows):
-    size = bias[0].shape[1]
+def ffn_last(mid_low, up, down, pair, heads, into, cot, *rows):
+    size = up[2].shape[0]
     tile = lambda n: pl.BlockSpec((TILE_U, n), lambda i: (i, 0))
     return pl.pallas_call(
         ffn_last_kernel,
@@ -821,7 +818,7 @@
         compiler_params=room(30),
         cost_estimate=cost(4.3e9, 30e6),
     )(
-        mid_low, *pair_of(up, pair), *pair_of(down, pair), *bias, into, cot, *rows
+        mid_low, *pair_of(up, pair), *pair_of(down, pair), *pair_of(heads, pair), into, cot, *rows
     )
 
 
@@ -1321,13 +1318,11 @@
     row = lambda v: v.astype(F32)[None, :]
     width = w_qkv.shape[2]
 
-    heads_own, heads_first = pack_heads(info, w_qkv, w_out)
+    heads_own, heads_first = pack_heads(info, w_qkv, w_out, b_qv, b_up)
     heads = fetch(heads_own, heads_first)
     up_own, up_first, down_own, down_first = pack_units(info, w_up, w_down)
     up = fetch(up_own, up_first)
     down = fetch(down_own, down_first)
-    q_rows, v_rows, up_rows = fetch_bias([b_qv[0:1], b_qv[1:2], b_up[None, :]], x_at)
-    zero = jnp.zeros((1, width // 2), F32)
 
     own_step = lax.dynamic_slice_in_dim(time_steps, mp_at, 1, 0)
     segment_row = lax.dynamic_index_in_dim(segment_ids, mp_at, 0, keepdims=False)
@@ -1340,11 +1335,7 @@
 
     qkv, ctx, lse = [], [], []
     for p in range(4):
-        first, second = 2 * p, 2 * p + 1
-        bias = jnp.concatenate(
-            [q_rows[first], q_rows[second], zero, zero, v_rows[first], v_rows[second]], axis=1
-        )
-        parts = attend_pair(win_f, hidden_low, heads, p, bias, hotq, hotk)
+        parts = attend_pair(win_f, hidden_low, heads, p, hotq, hotk)
         for kept, part in zip((qkv, ctx, lse), parts):
             kept.append(part)
     normal_one, scale_one, mid_low, mid_t, hidden_t = first_norm(
@@ -1353,7 +1344,7 @@
 
     act, slope, ffn = [], [], ()
     for p in range(3):
-        act_p, slope_p, *ffn = ffn_pair(mid_low, up, down, p, up_rows[2 * p : 2 * p + 2], ffn)
+        act_p, slope_p, *ffn = ffn_pair(mid_low, up, down, p, heads, ffn)
         act.append(act_p)
         slope.append(slope_p)
     act_p, slope_p, out_rows, branch_two, branch_two_t, sums_two = ffn_last(
@@ -1361,7 +1352,7 @@
         up,
         down,
         3,
-        up_rows[6:8],
+        heads,
         *ffn,
         cotangent,
         *[row(v) for v in (b_down, gain_two, shift_two)],

time: 516 us -> 518 us (level)
    unnamed x163 -> x145, local copies, waits for them, and re-layouts: 22.7 us -> 18.8 us
    ppermute x23 -> x20, starting transfers between devices: 13.7 us -> 10.8 us  [send_mp(): return lax.ppermute(values, 'mp', [(i, i ^ bit) for i in range(GRID_MP)])]
    ppermute x23 -> x20, waiting for transfers between devices: 55.4 us -> 56 us  [send_mp(): return lax.ppermute(values, 'mp', [(i, i ^ bit) for i in range(GRID_MP)])]
  transfers between devices with their start and end apart: 41 -> 38, of which waited for: 10 -> 10; matrix products, arithmetic and copies ran while one was open for 2% -> 2% of each run, Pallas kernels for 50% -> 50%
where the time goes in v6:
time: 518 us; the launch traced here: 510 us
  Pallas kernels  314 us (61%)
  waiting for transfers between devices  107 us (21%)
  starting transfers between devices  49.5 us (10%)
  local copies, waits for them, and re-layouts  27.9 us (5%)
    pallas_call x7, Pallas kernels, grad_call(): pl.pallas_call(functools.partial(grad_kernel, blocks, side, outputs, left...  61.8 us
    pallas_call x4, Pallas kernels, attend_back_pair(): pl.pallas_call(attend_back_kernel, out_shape=(far((LEN, 6 * UNIT)), struc...  60.6 us
    ppermute x20, waiting for transfers between devices, send_mp(): return lax.ppermute(values, 'mp', [(i, i ^ bit) for i in range(GRID_MP)])  56 us
    ppermute x18, waiting for transfers between devices, send_dp(): return lax.ppermute(values, 'dp', [(i, i ^ bit) for i in range(GRID_DP)])  51.3 us
    pallas_call x4, Pallas kernels, attend_pair(): pl.pallas_call(attend_kernel, out_shape=(far((LEN, 6 * UNIT)), far((LEN,...  43 us
    ppermute x18, starting transfers between devices, send_dp(): return lax.ppermute(values, 'dp', [(i, i ^ bit) for i in range(GRID_DP)])  38.7 us
    pallas_call x1, Pallas kernels, exchange(): pl.pallas_call(exchange_kernel, out_shape=(struct(sums.shape[1:], F32), s...  31 us
    pallas_call x1, Pallas kernels, ffn_back(): pl.pallas_call(ffn_back_kernel, out_shape=(far((LEN, 2 * size)),) * 4 + (...  28.6 us
  transfers between devices with their start and end apart: 38, of which 10 were waited for; matrix products, arithmetic and copies ran while one was open for 2% of the time, Pallas kernels for 50%

profile of v6, /device:TPU:0, one launch (start us, length us, event | category | flops | bytes accessed | tf_op | source)
XLA Modules:
  0.0 509.9 jit_solution(16748431546059154974)
XLA Ops:
  2.7 4.4 shard_map.297
  7.1 3.0 collective-permute-start.1
  10.1 5.6 %shard_map.303 = (bf16[2,512,1024]{2,1,0:T(8,128)(2,1)}, bf16[512,1024]{1,0:T(8,128)(2,1)}, bf16[2,512,1024]{2,1,0:T(8,128)(2,1)}, bf16[512,1024]{1,0:T(8,128)(2,1)}) custom-call(s32[4]{0:T(128)} %pad_add_fusion.2.info_ref.left_at, bf16[1024,1024]{1,0:T(8,128)(2,1)} %up_ref.1, bf16[1024,1024]{1,0:T(8,128)(2,1)} %down_ref.1), custom_call_target="tpu_custom_call" | custom-call | flops 1000000 | bytes 10000000 | tf_op jit(solution)/shard_map/pallas_call | solution.py:397
  15.8 2.0 collective-permute-start.8
  22.4 12.7 %collective-permute-done.1.refs_0_.refs_2_.refs_8_.refs_4_.wa_ref.refs_6_ = bf16[528,1024]{1,0:T(8,128)(2,1)S(1)} collective-permute-done((bf16[528,1024]{1,0:T(8,128)(2,1)}, bf16[528,1024]{1,0:T(8,128)(2,1)S(1)}, u32[]{:S(2)}, u32[]{:S(2)}) %collective-permute-start.1) | collective-permute-done | bytes 1081376 | tf_op jit(solution)/shard_map/ppermute | solution.py:330
  39.2 10.1 %shard_map.298 = (bf16[1024,768]{1,0:T(8,128)(2,1)}, bf16[1024,256]{1,0:T(8,128)(2,1)}, f32[2,8,1024]{2,1,0:T(8,128)}) custom-call(s32[2,2]{1,0:T(2,128)S(1)} %pad_add_fusion.win_ref, bf16[1024,1024]{1,0:T(8,128)(2,1)S(1)} %add_convert_fusion.x_ref, bf16[2,528,1024]{2,1,0:T(8,128)(2,1)S(1)} %copy-done.2, bf16[2,528,1024]{2,1,0:T(8,128)(2,1)S(1)} %copy-done.2, ...), custom_call_target="tpu_custom_call" | custom-call | flops 6000000000 | bytes 8000000 | tf_op jit(solution)/shard_map/pallas_call | solution.py:523
  49.3 8.3 %collective-permute-done.5.refs_0_.refs_8_ = bf16[512,1024]{1,0:T(8,128)(2,1)} collective-permute-done((bf16[512,1024]{1,0:T(8,128)(2,1)}, bf16[512,1024]{1,0:T(8,128)(2,1)}, u32[]{:S(2)}, u32[]{:S(2)}) %collective-permute-start.5) | collective-permute-done | bytes 1048608 | tf_op jit(solution)/shard_map/ppermute | solution.py:330
  57.7 21.6 %collective-permute-done.8.refs_2_ = bf16[512,1024]{1,0:T(8,128)(2,1)} collective-permute-done((bf16[512,1024]{1,0:T(8,128)(2,1)}, bf16[512,1024]{1,0:T(8,128)(2,1)}, u32[]{:S(2)}, u32[]{:S(2)}) %collective-permute-start.8) | collective-permute-done | bytes 1048608 | tf_op jit(solution)/shard_map/ppermute | solution.py:330
  81.2 10.7 %shard_map.300 = (bf16[1024,768]{1,0:T(8,128)(2,1)}, bf16[1024,256]{1,0:T(8,128)(2,1)}, f32[2,8,1024]{2,1,0:T(8,128)}) custom-call(s32[2,2]{1,0:T(2,128)S(1)} %pad_add_fusion.win_ref, bf16[1024,1024]{1,0:T(8,128)(2,1)S(1)} %add_convert_fusion.x_ref, bf16[528,1024]{1,0:T(8,128)(2,1)S(1)} %collective-permute-done.1.refs_0_.refs_2_.refs_8_.refs_4_.wa_ref.refs_6_, ...), custom_call_target="tpu_custom_call" | custom-call | flops 6000000000 | bytes 8000000 | tf_op jit(solution)/shard_map/pallas_call | solution.py:523
  92.0 11.7 %shard_map.299 = (bf16[1024,768]{1,0:T(8,128)(2,1)}, bf16[1024,256]{1,0:T(8,128)(2,1)}, f32[2,8,1024]{2,1,0:T(8,128)}) custom-call(s32[2,2]{1,0:T(2,128)S(1)} %pad_add_fusion.win_ref, bf16[1024,1024]{1,0:T(8,128)(2,1)S(1)} %add_convert_fusion.x_ref, ...), custom_call_target="tpu_custom_call" | custom-call | flops 6000000000 | bytes 8000000 | tf_op jit(solution)/shard_map/pallas_call | solution.py:523
  106.1 10.4 %shard_map.301 = (bf16[1024,768]{1,0:T(8,128)(2,1)}, bf16[1024,256]{1,0:T(8,128)(2,1)}, f32[2,8,1024]{2,1,0:T(8,128)}) custom-call(s32[2,2]{1,0:T(2,128)S(1)} %pad_add_fusion.win_ref, bf16[1024,1024]{1,0:T(8,128)(2,1)S(1)} %add_convert_fusion.x_ref, bf16[528,1024]{1,0:T(8,128)(2,1)S(1)} %collective-permute-done.3.refs_0_.refs_2_.refs_10_.refs_4_.wa_ref.refs_8_, ...), custom_call_target="tpu_custom_call" | custom-call | flops 6000000000 | bytes 8000000 | tf_op jit(solution)/shard_map/pallas_call | solution.py:523
  117.5 6.8 %shard_map.302 = (bf16[1024,1024]{1,0:T(8,128)(2,1)}, f32[1024,1]{1,0:T(8,128)}, bf16[1024,1024]{1,0:T(8,128)(2,1)S(1)}, bf16[1024,1024]{1,0:T(8,128)(2,1)}, bf16[1024,1024]{1,0:T(8,128)(2,1)}) custom-call(bf16[1024,1024]{1,0:T(8,128)(2,1)S(1)} %copy-done.6, bf16[1024,256]{1,0:T(8,128)(2,1)S(1)} %copy-done.22, bf16[1024,256]{1,0:T(8,128)(2,1)S(1)} %copy-done.28, ...), custom_call_target="tpu_custom_call" | custom-call | flops 2200000000 | bytes 20000000 | tf_op jit(solution)/shard_map/pallas_call | solution.py:700
  124.3 3.2 collective-permute-done.9.refs_2_.refs_4_
  128.0 7.1 %shard_map.304 = (bf16[1024,1024]{1,0:T(8,128)(2,1)}, bf16[1024,1024]{1,0:T(8,128)(2,1)}, f32[1024,1024]{1,0:T(8,128)S(1)}) custom-call(bf16[1024,1024]{1,0:T(8,128)(2,1)S(1)} %get-tuple-element.120.mid_ref, bf16[2,512,1024]{2,1,0:T(8,128)(2,1)S(1)} %copy-done.41, bf16[2,512,1024]{2,1,0:T(8,128)(2,1)S(1)} %copy-done.41, ...), custom_call_target="tpu_custom_call" | custom-call | flops 4300000256 | bytes 18000000 | tf_op jit(solution)/shard_map/pallas_call | solution.py:765
  135.2 7.9 %shard_map.305 = (bf16[1024,1024]{1,0:T(8,128)(2,1)}, bf16[1024,1024]{1,0:T(8,128)(2,1)}, f32[1024,1024]{1,0:T(8,128)S(1)}) custom-call(bf16[1024,1024]{1,0:T(8,128)(2,1)S(1)} %get-tuple-element.120.mid_ref, bf16[2,512,1024]{2,1,0:T(8,128)(2,1)S(1)} %collective-permute-done.13.refs_0_.refs_1_.refs_7_, ...), custom_call_target="tpu_custom_call" | custom-call | flops 4300000256 | bytes 18000000 | tf_op jit(solution)/shard_map/pallas_call | solution.py:765
  143.1 9.5 %shard_map.306 = (bf16[1024,1024]{1,0:T(8,128)(2,1)}, bf16[1024,1024]{1,0:T(8,128)(2,1)}, f32[1024,1024]{1,0:T(8,128)S(1)}) custom-call(bf16[1024,1024]{1,0:T(8,128)(2,1)S(1)} %get-tuple-element.120.mid_ref, bf16[512,1024]{1,0:T(8,128)(2,1)} %collective-permute-done.5.refs_0_.refs_8_, bf16[512,1024]{1,0:T(8,128)(2,1)S(1)} %collective-permute-done.11.refs_1_.refs_9_, ...), custom_call_target="tpu_custom_call" | custom-call | flops 4300000256 | bytes 18000000 | tf_op jit(solution)/shard_map/pallas_call | solution.py:765
  152.7 11.8 %shard_map.307 = (bf16[1024,1024]{1,0:T(8,128)(2,1)}, bf16[1024,1024]{1,0:T(8,128)(2,1)}, bf16[1024,1024]{1,0:T(8,128)(2,1)}, bf16[1024,1024]{1,0:T(8,128)(2,1)}...) custom-call(bf16[1024,1024]{1,0:T(8,128)(2,1)S(1)} %get-tuple-element.120.mid_ref, ...), custom_call_target="tpu_custom_call" | custom-call | flops 4300000256 | bytes 30000000 | tf_op jit(solution)/shard_map/pallas_call | solution.py:804
  164.6 28.6 %shard_map.308 = (bf16[1024,1024]{1,0:T(8,128)(2,1)}, bf16[1024,1024]{1,0:T(8,128)(2,1)}, bf16[1024,1024]{1,0:T(8,128)(2,1)}, bf16[1024,1024]{1,0:T(8,128)(2,1)}...) custom-call(bf16[1024,1024]{1,0:T(8,128)(2,1)} %get-tuple-element.129.b, ...), custom_call_target="tpu_custom_call" | custom-call | flops 16999999488 | bytes 40000000 | tf_op jit(solution)/shard_map/pallas_call | solution.py:911
  193.2 10.8 %shard_map.326 = bf16[2,512,2560]{2,1,0:T(8,128)(2,1)} custom-call(s32[4]{0:T(128)} %pad_add_fusion.2.info_ref.left_at, bf16[4,2,128,1024]{3,2,1,0:T(8,128)(2,1)} %bitcast.140, bf16[4,2,128,1024]{3,2,1,0:T(8,128)(2,1)} %bitcast.142, bf16[1024,1024]{1,0:T(8,128)(2,1)} %get-tuple-element.187.refs_2_, bf16[1024,1024]{1,0:T(8,128)(2,1)} %get-tuple-element.185.refs_3_, ...), custom_call_target="tpu_custom_call" | custom-call | flops 5368709120 | bytes 10000000 | tf_op jit(solution)/shard_map/pallas_call | solution.py:1029
  204.1 9.3 %shard_map.321 = bf16[2,512,2048]{2,1,0:T(8,128)(2,1)} custom-call(s32[4]{0:T(128)} %pad_add_fusion.2.info_ref.left_at, bf16[4,2,128,1024]{3,2,1,0:T(8,128)(2,1)} %bitcast.144, bf16[1024,1024]{1,0:T(8,128)(2,1)} %get-tuple-element.173.refs_1_, bf16[1024,1024]{1,0:T(8,128)(2,1)} %get-tuple-element.171.refs_2_, bf16[1024,1024]{1,0:T(8,128)(2,1)} %get-tuple-element.172.refs_3_), custom_call_target="tpu_custom_call" | custom-call | flops 4294967296 | bytes 10000000 | tf_op jit(solution)/shard_map/pallas_call | solution.py:1029
  220.6 14.9 %shard_map.312 = (bf16[1024,768]{1,0:T(8,128)(2,1)}, f32[8,768]{1,0:T(8,128)S(1)}) custom-call(s32[2,4]{1,0:T(2,128)S(1)} %pad_add_fusion.1.win_ref, bf16[1024,768]{1,0:T(8,128)(2,1)S(1)} %copy-done.55, bf16[1024,128]{1,0:T(8,128)(2,1)S(1)} %copy-done.32, bf16[1024,128]{1,0:T(8,128)(2,1)S(1)} %get-tuple-element.266.refs_5_.hotk_ref, ...), custom_call_target="tpu_custom_call" | custom-call | flops 8000000000 | bytes 8000000 | tf_op jit(solution)/shard_map/pallas_call | solution.py:632
  235.6 14.9 %shard_map.311 = (bf16[1024,768]{1,0:T(8,128)(2,1)}, f32[8,768]{1,0:T(8,128)S(1)}) custom-call(s32[2,4]{1,0:T(2,128)S(1)} %pad_add_fusion.1.win_ref, bf16[1024,768]{1,0:T(8,128)(2,1)S(1)} %copy-done.54, bf16[1024,128]{1,0:T(8,128)(2,1)S(1)} %copy-done.32, bf16[1024,128]{1,0:T(8,128)(2,1)S(1)} %get-tuple-element.266.refs_5_.hotk_ref, ...), custom_call_target="tpu_custom_call" | custom-call | flops 8000000000 | bytes 8000000 | tf_op jit(solution)/shard_map/pallas_call | solution.py:632
  251.0 16.1 %shard_map.310 = (bf16[1024,768]{1,0:T(8,128)(2,1)}, f32[8,768]{1,0:T(8,128)S(1)}) custom-call(s32[2,4]{1,0:T(2,128)S(1)} %pad_add_fusion.1.win_ref, bf16[1024,768]{1,0:T(8,128)(2,1)S(1)} %copy-done.53, bf16[1024,128]{1,0:T(8,128)(2,1)S(1)} %copy-done.32, bf16[1024,128]{1,0:T(8,128)(2,1)S(1)} %get-tuple-element.266.refs_5_.hotk_ref, ...), custom_call_target="tpu_custom_call" | custom-call | flops 8000000000 | bytes 8000000 | tf_op jit(solution)/shard_map/pallas_call | solution.py:632
  267.1 8.3 %shard_map.314 = bf16[2,512,1536]{2,1,0:T(8,128)(2,1)} custom-call(s32[4]{0:T(128)} %pad_add_fusion.2.info_ref.left_at, bf16[4,2,128,1024]{3,2,1,0:T(8,128)(2,1)} %bitcast.120, bf16[1024,768]{1,0:T(8,128)(2,1)} %get-tuple-element.142.refs_1_, bf16[1024,768]{1,0:T(8,128)(2,1)} %get-tuple-element.145.refs_2_, bf16[1024,768]{1,0:T(8,128)(2,1)} %get-tuple-element.148.refs_3_), custom_call_target="tpu_custom_call" | custom-call | flops 3221225472 | bytes 10000000 | tf_op jit(solution)/shard_map/pallas_call | solution.py:1029
  275.5 9.2 %shard_map.322 = (bf16[2,512,512]{2,1,0:T(8,128)(2,1)}, bf16[2,512,512]{2,1,0:T(8,128)(2,1)}, bf16[512,1024]{1,0:T(8,128)(2,1)}, bf16[512,1024]{1,0:T(8,128)(2,1)}) custom-call(s32[4]{0:T(128)} %pad_add_fusion.2.info_ref.left_at, bf16[4,2,128,1024]{3,2,1,0:T(8,128)(2,1)} %bitcast.145, bf16[1024,1024]{1,0:T(8,128)(2,1)} %get-tuple-element.170.refs_1_, ...), custom_call_target="tpu_custom_call" | custom-call | flops 4294967296 | bytes 10000000 | tf_op jit(solution)/shard_map/pallas_call | solution.py:1029
  284.9 11.1 %shard_map.327 = (bf16[2,512,512]{2,1,0:T(8,128)(2,1)}, bf16[2,512,512]{2,1,0:T(8,128)(2,1)}, bf16[512,1536]{1,0:T(8,128)(2,1)}, bf16[512,1536]{1,0:T(8,128)(2,1)}) custom-call(s32[4]{0:T(128)} %pad_add_fusion.2.info_ref.left_at, bf16[4,2,128,1024]{3,2,1,0:T(8,128)(2,1)} %bitcast.141, bf16[4,2,128,1024]{3,2,1,0:T(8,128)(2,1)} %bitcast.143, ...), custom_call_target="tpu_custom_call" | custom-call | flops 5368709120 | bytes 10000000 | tf_op jit(solution)/shard_map/pallas_call | solution.py:1029
  295.9 3.3 collective-permute-start.32
  300.6 6.7 %shard_map.316 = (bf16[512,768]{1,0:T(8,128)(2,1)}, bf16[512,768]{1,0:T(8,128)(2,1)}) custom-call(s32[4]{0:T(128)} %pad_add_fusion.2.info_ref.left_at, bf16[4,2,128,1024]{3,2,1,0:T(8,128)(2,1)} %bitcast.121, bf16[1024,768]{1,0:T(8,128)(2,1)} %get-tuple-element.142.refs_1_, bf16[1024,768]{1,0:T(8,128)(2,1)} %get-tuple-element.145.refs_2_, ...), custom_call_target="tpu_custom_call" | custom-call | flops 1610612736 | bytes 10000000 | tf_op jit(solution)/shard_map/pallas_call | solution.py:1029
  316.9 14.9 %shard_map.309 = (bf16[1024,768]{1,0:T(8,128)(2,1)}, f32[8,768]{1,0:T(8,128)S(1)}) custom-call(s32[2,4]{1,0:T(2,128)S(1)} %pad_add_fusion.1.win_ref, bf16[1024,768]{1,0:T(8,128)(2,1)S(1)} %copy-done.52, bf16[1024,128]{1,0:T(8,128)(2,1)S(1)} %copy-done.33, bf16[1024,128]{1,0:T(8,128)(2,1)S(1)} %get-tuple-element.266.refs_5_.hotk_ref, ...), custom_call_target="tpu_custom_call" | custom-call | flops 8000000000 | bytes 8000000 | tf_op jit(solution)/shard_map/pallas_call | solution.py:632
  331.7 6.5 %shard_map.315 = (bf16[512,768]{1,0:T(8,128)(2,1)}, bf16[512,768]{1,0:T(8,128)(2,1)}) custom-call(s32[4]{0:T(128)} %pad_add_fusion.2.info_ref.left_at, bf16[4,2,128,1024]{3,2,1,0:T(8,128)(2,1)} %bitcast.122, bf16[1024,768]{1,0:T(8,128)(2,1)} %get-tuple-element.139.refs_0_.refs_1_, bf16[1024,768]{1,0:T(8,128)(2,1)} %get-tuple-element.145.refs_2_, ...), custom_call_target="tpu_custom_call" | custom-call | flops 1610612736 | bytes 10000000 | tf_op jit(solution)/shard_map/pallas_call | solution.py:1029
  338.2 35.8 %collective-permute-done.17.got_ref = bf16[512,768]{1,0:T(8,128)(2,1)} collective-permute-done((bf16[512,768]{1,0:T(8,128)(2,1)}, bf16[512,768]{1,0:T(8,128)(2,1)}, u32[]{:S(2)}, u32[]{:S(2)}) %collective-permute-start.17) | collective-permute-done | bytes 786464 | tf_op jit(solution)/shard_map/ppermute | solution.py:334
  374.1 2.0 collective-permute-start.16
  376.1 2.3 shard_map.317
  386.8 12.5 %shard_map.313 = (f32[1024,1024]{1,0:T(8,128)}, f32[8,1024]{1,0:T(8,128)}) custom-call(bf16[1024,1024]{1,0:T(8,128)(2,1)} %get-tuple-element.136.branch_ref, bf16[1024,768]{1,0:T(8,128)(2,1)} %get-tuple-element.139.refs_0_.refs_1_, bf16[1024,768]{1,0:T(8,128)(2,1)} %get-tuple-element.142.refs_1_, bf16[1024,768]{1,0:T(8,128)(2,1)} %get-tuple-element.145.refs_2_, ...), custom_call_target="tpu_custom_call" | custom-call | flops 6400000000 | bytes 20000000 | tf_op jit(solution)/shard_map/pallas_call | solution.py:1200
  399.3 11.1 %collective-permute-done.26.refs_5_ = bf16[512,512]{1,0:T(8,128)(2,1)} collective-permute-done((bf16[512,512]{1,0:T(8,128)(2,1)S(1)}, bf16[512,512]{1,0:T(8,128)(2,1)}, u32[]{:S(2)}, u32[]{:S(2)}) %collective-permute-start.26) | collective-permute-done | bytes 524320 | tf_op jit(solution)/shard_map/ppermute | solution.py:330
  410.4 3.6 shard_map.325
  414.1 3.3 shard_map.318
  417.4 2.0 collective-permute-start.19
  419.4 2.1 collective-permute-start.20
  423.6 2.5 collective-permute-start.28
  426.1 4.0 shard_map.330
  430.2 2.8 collective-permute-start.29
  433.0 10.3 %collective-permute-done.20.refs_2_ = bf16[128,768]{1,0:T(8,128)(2,1)S(1)} collective-permute-done((bf16[128,768]{1,0:T(8,128)(2,1)}, bf16[128,768]{1,0:T(8,128)(2,1)S(1)}, u32[]{:S(2)}, u32[]{:S(2)}) %collective-permute-start.20) | collective-permute-done | bytes 196640 | tf_op jit(solution)/shard_map/ppermute | solution.py:334
  444.2 13.7 %collective-permute-start.36 = (bf16[128,1280]{1,0:T(8,128)(2,1)}, bf16[128,1280]{1,0:T(8,128)(2,1)S(1)}, u32[]{:S(2)}, u32[]{:S(2)}) collective-permute-start(bf16[128,1280]{1,0:T(8,128)(2,1)} %get-tuple-element.198), channel_id=1, source_target_pairs={{0,16},{4,20},{8,24},{12,28},{16,0},{20,4},{24,8},{28,12},{1,17},{... | collective-permute-start | bytes 983048 | tf_op jit(solution)/shard_map/ppermute | solution.py:334
  461.0 31.0 %shard_map.320 = (f32[1,384]{1,0:T(1,128)}, f32[32,1,1152]{2,1,0:T(1,128)}) custom-call(f32[32,1,384]{2,1,0:T(1,128)} %broadcast_in_dim.97.sum_ref, f32[1,1152]{1,0:T(1,128)} %concatenate.23.row_ref), custom_call_target="tpu_custom_call" | custom-call | flops 1000000 | bytes 1000000 | tf_op jit(solution)/shard_map/pallas_call | solution.py:1273
  493.5 2.1 copy.55
  501.5 2.0 fusion.1
  506.9 2.6 shard_map.332
  (274 shorter events, 60.2 us)
Async XLA Ops:
  7.1 27.9 %collective-permute-start.1 = (bf16[528,1024]{1,0:T(8,128)(2,1)}, bf16[528,1024]{1,0:T(8,128)(2,1)S(1)}, u32[]{:S(2)}, u32[]{:S(2)}) collective-permute-start(bf16[528,1024]{1,0:T(8,128)(2,1)} %get-tuple-element.117), channel_id=1, source_target_pairs={{0,2},{1,3},{2,0},{3,1},{4,6},{5,7},{6,4},{7,5},{8,10},{9,11},{10,... | collective-permute-start | bytes 3244040 | tf_op jit(solution)/shard_map/ppermute | solution.py:330
  10.1 81.8 %collective-permute-start = (bf16[2,528,1024]{2,1,0:T(8,128)(2,1)}, bf16[2,528,1024]{2,1,0:T(8,128)(2,1)}, u32[]{:S(2)}, u32[]{:S(2)}) collective-permute-start(bf16[2,528,1024]{2,1,0:T(8,128)(2,1)} %get-tuple-element.114.refs_0_.refs_1_.refs_2_.refs_3_.refs_4_.refs_5_.wa_ref.wb_ref), channel_id=1, source_target_pairs={{0,1},{1,0},{2,3},{3,2},{4,5},{5,4},{6,7},{7,6},{8,9},{9,8},{10,11... | collective-permute-start | bytes 6488072 | tf_op jit(solution)/shard_map/ppermute | solution.py:330
  15.7 41.9 %collective-permute-start.5 = (bf16[512,1024]{1,0:T(8,128)(2,1)}, bf16[512,1024]{1,0:T(8,128)(2,1)}, u32[]{:S(2)}, u32[]{:S(2)}) collective-permute-start(bf16[512,1024]{1,0:T(8,128)(2,1)} %get-tuple-element.121), channel_id=1, source_target_pairs={{0,2},{1,3},{2,0},{3,1},{4,6},{5,7},{6,4},{7,5},{8,10},{9,11},{10,... | collective-permute-start | bytes 3145736 | tf_op jit(solution)/shard_map/ppermute | solution.py:330
  15.8 63.4 %collective-permute-start.8 = (bf16[512,1024]{1,0:T(8,128)(2,1)}, bf16[512,1024]{1,0:T(8,128)(2,1)}, u32[]{:S(2)}, u32[]{:S(2)}) collective-permute-start(bf16[512,1024]{1,0:T(8,128)(2,1)} %get-tuple-element.122), channel_id=1, source_target_pairs={{0,2},{1,3},{2,0},{3,1},{4,6},{5,7},{6,4},{7,5},{8,10},{9,11},{10,... | collective-permute-start | bytes 3145736 | tf_op jit(solution)/shard_map/ppermute | solution.py:330
  35.0 200.5 %copy-start.14 = (bf16[528,1024]{1,0:T(8,128)(2,1)}, bf16[528,1024]{1,0:T(8,128)(2,1)S(1)}, u32[]{:S(2)}) copy-start(bf16[528,1024]{1,0:T(8,128)(2,1)S(1)} %collective-permute-done.1.refs_0_.refs_2_.refs_8_.refs_4_.wa_ref.refs_6_) | copy-start | bytes 3244036
  35.1 44.2 %collective-permute-start.3 = (bf16[528,1024]{1,0:T(8,128)(2,1)S(1)}, bf16[528,1024]{1,0:T(8,128)(2,1)S(1)}, u32[]{:S(2)}, u32[]{:S(2)}) collective-permute-start(bf16[528,1024]{1,0:T(8,128)(2,1)S(1)} %collective-permute-done.1.refs_0_.refs_2_.refs_8_.refs_4_.wa_ref.refs_6_), channel_id=1, source_target_pairs={{0,4},{4,0},{8,12},{12,8},{16,20},{20,16},{24,28},{28,24},{1,5},{5... | collective-permute-start | bytes 3244040 | tf_op jit(solution)/shard_map/ppermute | solution.py:334
  37.0 44.0 %collective-permute-start.2 = (bf16[528,1024]{1,0:T(8,128)(2,1)S(1)}, bf16[528,1024]{1,0:T(8,128)(2,1)S(1)}, u32[]{:S(2)}, u32[]{:S(2)}) collective-permute-start(bf16[528,1024]{1,0:T(8,128)(2,1)S(1)} %collective-permute-done.1.refs_0_.refs_2_.refs_8_.refs_4_.wa_ref.refs_6_), channel_id=1, source_target_pairs={{0,1},{1,0},{2,3},{3,2},{4,5},{5,4},{6,7},{7,6},{8,9},{9,8},{10,11... | collective-permute-start | bytes 3244040 | tf_op jit(solution)/shard_map/ppermute | solution.py:330
  37.4 68.7 %copy-start.31 = (bf16[1024,128]{1,0:T(8,128)(2,1)}, bf16[1024,128]{1,0:T(8,128)(2,1)S(1)}, u32[]{:S(2)}) copy-start(bf16[1024,128]{1,0:T(8,128)(2,1)S(1)} %get-tuple-element.267.refs_4_.hotq_ref) | copy-start | bytes 786436
  57.6 69.9 %collective-permute-start.13 = (bf16[2,512,1024]{2,1,0:T(8,128)(2,1)S(1)}, bf16[2,512,1024]{2,1,0:T(8,128)(2,1)S(1)}, u32[]{:S(2)}, u32[]{:S(2)}) collective-permute-start(bf16[2,512,1024]{2,1,0:T(8,128)(2,1)S(1)} %copy-done.41), channel_id=1, source_target_pairs={{0,1},{1,0},{2,3},{3,2},{4,5},{5,4},{6,7},{7,6},{8,9},{9,8},{10,11... | collective-permute-start | bytes 6291464 | tf_op jit(solution)/shard_map/ppermute | solution.py:330
  79.2 55.9 %collective-permute-start.14 = (bf16[2,512,1024]{2,1,0:T(8,128)(2,1)S(1)}, bf16[2,512,1024]{2,1,0:T(8,128)(2,1)S(1)}, u32[]{:S(2)}, u32[]{:S(2)}) collective-permute-start(bf16[2,512,1024]{2,1,0:T(8,128)(2,1)S(1)} %copy-done.42), channel_id=1, source_target_pairs={{0,1},{1,0},{2,3},{3,2},{4,5},{5,4},{6,7},{7,6},{8,9},{9,8},{10,11... | collective-permute-start | bytes 6291464 | tf_op jit(solution)/shard_map/ppermute | solution.py:330
  79.3 73.4 %copy-start.15 = (bf16[528,1024]{1,0:T(8,128)(2,1)}, bf16[528,1024]{1,0:T(8,128)(2,1)S(1)}, u32[]{:S(2)}) copy-start(bf16[528,1024]{1,0:T(8,128)(2,1)S(1)} %collective-permute-done.3.refs_0_.refs_2_.refs_10_.refs_4_.wa_ref.refs_8_) | copy-start | bytes 3244036
  79.3 26.3 %collective-permute-start.6 = (bf16[512,1024]{1,0:T(8,128)(2,1)}, bf16[512,1024]{1,0:T(8,128)(2,1)S(1)}, u32[]{:S(2)}, u32[]{:S(2)}) collective-permute-start(bf16[512,1024]{1,0:T(8,128)(2,1)} %collective-permute-done.5.refs_0_.refs_8_), channel_id=1, source_target_pairs={{0,4},{4,0},{8,12},{12,8},{16,20},{20,16},{24,28},{28,24},{1,5},{5... | collective-permute-start | bytes 3145736 | tf_op jit(solution)/shard_map/ppermute | solution.py:334
  81.1 62.1 %copy-start.17 = (bf16[528,1024]{1,0:T(8,128)(2,1)}, bf16[528,1024]{1,0:T(8,128)(2,1)S(1)}, u32[]{:S(2)}) copy-start(bf16[528,1024]{1,0:T(8,128)(2,1)S(1)} %collective-permute-done.2.refs_1_.refs_3_.refs_9_.refs_5_.wb_ref.refs_7_) | copy-start | bytes 3244036
  81.1 24.5 %collective-permute-start.4 = (bf16[528,1024]{1,0:T(8,128)(2,1)S(1)}, bf16[528,1024]{1,0:T(8,128)(2,1)S(1)}, u32[]{:S(2)}, u32[]{:S(2)}) collective-permute-start(bf16[528,1024]{1,0:T(8,128)(2,1)S(1)} %collective-permute-done.3.refs_0_.refs_2_.refs_10_.refs_4_.wa_ref.refs_8_), channel_id=1, source_target_pairs={{0,1},{1,0},{2,3},{3,2},{4,5},{5,4},{6,7},{7,6},{8,9},{9,8},{10,11... | collective-permute-start | bytes 3244040 | tf_op jit(solution)/shard_map/ppermute | solution.py:330
  91.9 35.6 %collective-permute-start.9 = (bf16[512,1024]{1,0:T(8,128)(2,1)}, bf16[512,1024]{1,0:T(8,128)(2,1)S(1)}, u32[]{:S(2)}, u32[]{:S(2)}) collective-permute-start(bf16[512,1024]{1,0:T(8,128)(2,1)} %collective-permute-done.8.refs_2_), channel_id=1, source_target_pairs={{0,4},{4,0},{8,12},{12,8},{16,20},{20,16},{24,28},{28,24},{1,5},{5... | collective-permute-start | bytes 3145736 | tf_op jit(solution)/shard_map/ppermute | solution.py:334
  105.6 47.1 %copy-start.43 = (bf16[512,1024]{1,0:T(8,128)(2,1)}, bf16[512,1024]{1,0:T(8,128)(2,1)S(1)}, u32[]{:S(2)}) copy-start(bf16[512,1024]{1,0:T(8,128)(2,1)S(1)} %collective-permute-done.6.refs_0_.refs_10_) | copy-start | bytes 3145732
  105.6 37.5 %collective-permute-start.11 = (bf16[512,1024]{1,0:T(8,128)(2,1)}, bf16[512,1024]{1,0:T(8,128)(2,1)S(1)}, u32[]{:S(2)}, u32[]{:S(2)}) collective-permute-start(bf16[512,1024]{1,0:T(8,128)(2,1)} %collective-permute-done.5.refs_0_.refs_8_), channel_id=1, source_target_pairs={{0,1},{1,0},{2,3},{3,2},{4,5},{5,4},{6,7},{7,6},{8,9},{9,8},{10,11... | collective-permute-start | bytes 3145736 | tf_op jit(solution)/shard_map/ppermute | solution.py:330
  105.6 47.1 %copy-start.19 = (bf16[528,1024]{1,0:T(8,128)(2,1)}, bf16[528,1024]{1,0:T(8,128)(2,1)S(1)}, u32[]{:S(2)}) copy-start(bf16[528,1024]{1,0:T(8,128)(2,1)S(1)} %collective-permute-done.4.refs_1_.refs_3_.refs_11_.refs_5_.wb_ref.refs_9_) | copy-start | bytes 3244036
  105.6 37.5 %collective-permute-start.12 = (bf16[512,1024]{1,0:T(8,128)(2,1)}, bf16[512,1024]{1,0:T(8,128)(2,1)S(1)}, u32[]{:S(2)}, u32[]{:S(2)}) collective-permute-start(bf16[512,1024]{1,0:T(8,128)(2,1)} %collective-permute-done.8.refs_2_), channel_id=1, source_target_pairs={{0,1},{1,0},{2,3},{3,2},{4,5},{5,4},{6,7},{7,6},{8,9},{9,8},{10,11... | collective-permute-start | bytes 3145736 | tf_op jit(solution)/shard_map/ppermute | solution.py:330
  127.5 25.1 %collective-permute-start.7 = (bf16[512,1024]{1,0:T(8,128)(2,1)S(1)}, bf16[512,1024]{1,0:T(8,128)(2,1)S(1)}, u32[]{:S(2)}, u32[]{:S(2)}) collective-permute-start(bf16[512,1024]{1,0:T(8,128)(2,1)S(1)} %collective-permute-done.6.refs_0_.refs_10_), channel_id=1, source_target_pairs={{0,1},{1,0},{2,3},{3,2},{4,5},{5,4},{6,7},{7,6},{8,9},{9,8},{10,11... | collective-permute-start | bytes 3145736 | tf_op jit(solution)/shard_map/ppermute | solution.py:330
  127.5 25.1 %collective-permute-start.10 = (bf16[512,1024]{1,0:T(8,128)(2,1)S(1)}, bf16[512,1024]{1,0:T(8,128)(2,1)S(1)}, u32[]{:S(2)}, u32[]{:S(2)}) collective-permute-start(bf16[512,1024]{1,0:T(8,128)(2,1)S(1)} %collective-permute-done.9.refs_2_.refs_4_), channel_id=1, source_target_pairs={{0,1},{1,0},{2,3},{3,2},{4,5},{5,4},{6,7},{7,6},{8,9},{9,8},{10,11... | collective-permute-start | bytes 3145736 | tf_op jit(solution)/shard_map/ppermute | solution.py:330
  203.9 80.9 %collective-permute-start.30 = (bf16[2,512,2560]{2,1,0:T(8,128)(2,1)}, bf16[2,512,2560]{2,1,0:T(8,128)(2,1)}, u32[]{:S(2)}, u32[]{:S(2)}) collective-permute-start(bf16[2,512,2560]{2,1,0:T(8,128)(2,1)} %shard_map.326), channel_id=1, source_target_pairs={{0,1},{1,0},{2,3},{3,2},{4,5},{5,4},{6,7},{7,6},{8,9},{9,8},{10,11... | collective-permute-start | bytes 15728648 | tf_op jit(solution)/shard_map/ppermute | solution.py:330
  213.4 62.1 %collective-permute-start.22 = (bf16[2,512,2048]{2,1,0:T(8,128)(2,1)}, bf16[2,512,2048]{2,1,0:T(8,128)(2,1)}, u32[]{:S(2)}, u32[]{:S(2)}) collective-permute-start(bf16[2,512,2048]{2,1,0:T(8,128)(2,1)} %shard_map.321), channel_id=1, source_target_pairs={{0,1},{1,0},{2,3},{3,2},{4,5},{5,4},{6,7},{7,6},{8,9},{9,8},{10,11... | collective-permute-start | bytes 12582920 | tf_op jit(solution)/shard_map/ppermute | solution.py:330
  275.4 25.2 %collective-permute-start.15 = (bf16[2,512,1536]{2,1,0:T(8,128)(2,1)}, bf16[2,512,1536]{2,1,0:T(8,128)(2,1)}, u32[]{:S(2)}, u32[]{:S(2)}) collective-permute-start(bf16[2,512,1536]{2,1,0:T(8,128)(2,1)} %shard_map.314), channel_id=1, source_target_pairs={{0,1},{1,0},{2,3},{3,2},{4,5},{5,4},{6,7},{7,6},{8,9},{9,8},{10,11... | collective-permute-start | bytes 9437192 | tf_op jit(solution)/shard_map/ppermute | solution.py:330
  284.7 26.3 %collective-permute-start.23 = (bf16[2,512,512]{2,1,0:T(8,128)(2,1)}, bf16[2,512,512]{2,1,0:T(8,128)(2,1)S(1)}, u32[]{:S(2)}, u32[]{:S(2)}) collective-permute-start(bf16[2,512,512]{2,1,0:T(8,128)(2,1)} %get-tuple-element.175), channel_id=1, source_target_pairs={{0,2},{1,3},{2,0},{3,1},{4,6},{5,7},{6,4},{7,5},{8,10},{9,11},{10,... | collective-permute-start | bytes 3145736 | tf_op jit(solution)/shard_map/ppermute | solution.py:330
  295.9 86.7 %collective-permute-start.32 = (bf16[512,1536]{1,0:T(8,128)(2,1)}, bf16[512,1536]{1,0:T(8,128)(2,1)}, u32[]{:S(2)}, u32[]{:S(2)}) collective-permute-start(bf16[512,1536]{1,0:T(8,128)(2,1)} %get-tuple-element.191), channel_id=1, source_target_pairs={{0,4},{4,0},{8,12},{12,8},{16,20},{20,16},{24,28},{28,24},{1,5},{5... | collective-permute-start | bytes 4718600 | tf_op jit(solution)/shard_map/ppermute | solution.py:334
  299.8 78.6 %collective-permute-start.25 = (bf16[512,1024]{1,0:T(8,128)(2,1)}, bf16[512,1024]{1,0:T(8,128)(2,1)}, u32[]{:S(2)}, u32[]{:S(2)}) collective-permute-start(bf16[512,1024]{1,0:T(8,128)(2,1)} %get-tuple-element.177), channel_id=1, source_target_pairs={{0,4},{4,0},{8,12},{12,8},{16,20},{20,16},{24,28},{28,24},{1,5},{5... | collective-permute-start | bytes 3145736 | tf_op jit(solution)/shard_map/ppermute | solution.py:334
  299.8 81.2 %collective-permute-start.31 = (bf16[2,512,512]{2,1,0:T(8,128)(2,1)}, bf16[2,512,512]{2,1,0:T(8,128)(2,1)}, u32[]{:S(2)}, u32[]{:S(2)}) collective-permute-start(bf16[2,512,512]{2,1,0:T(8,128)(2,1)} %get-tuple-element.190), channel_id=1, source_target_pairs={{0,2},{1,3},{2,0},{3,1},{4,6},{5,7},{6,4},{7,5},{8,10},{9,11},{10,... | collective-permute-start | bytes 3145736 | tf_op jit(solution)/shard_map/ppermute | solution.py:330
  307.2 66.8 %collective-permute-start.17 = (bf16[512,768]{1,0:T(8,128)(2,1)}, bf16[512,768]{1,0:T(8,128)(2,1)}, u32[]{:S(2)}, u32[]{:S(2)}) collective-permute-start(bf16[512,768]{1,0:T(8,128)(2,1)} %get-tuple-element.154), channel_id=1, source_target_pairs={{0,4},{4,0},{8,12},{12,8},{16,20},{20,16},{24,28},{28,24},{1,5},{5... | collective-permute-start | bytes 2359304 | tf_op jit(solution)/shard_map/ppermute | solution.py:334
  312.1 73.9 %collective-permute-start.24 = (bf16[512,512]{1,0:T(8,128)(2,1)}, bf16[512,512]{1,0:T(8,128)(2,1)}, u32[]{:S(2)}, u32[]{:S(2)}) collective-permute-start(bf16[512,512]{1,0:T(8,128)(2,1)} %shard_map.323), channel_id=1, source_target_pairs={{0,4},{4,0},{8,12},{12,8},{16,20},{20,16},{24,28},{28,24},{1,5},{5... | collective-permute-start | bytes 1572872 | tf_op jit(solution)/shard_map/ppermute | solution.py:334
  331.7 44.4 %copy-start.21 = (bf16[512,768]{1,0:T(8,128)(2,1)S(1)}, bf16[512,768]{1,0:T(8,128)(2,1)}, u32[]{:S(2)}) copy-start(bf16[512,768]{1,0:T(8,128)(2,1)} %get-tuple-element.153.mine_ref) | copy-start | bytes 2359300
  374.1 40.0 %collective-permute-start.16 = (bf16[512,768]{1,0:T(8,128)(2,1)}, bf16[512,768]{1,0:T(8,128)(2,1)}, u32[]{:S(2)}, u32[]{:S(2)}) collective-permute-start(bf16[512,768]{1,0:T(8,128)(2,1)} %get-tuple-element.152), channel_id=1, source_target_pairs={{0,4},{4,0},{8,12},{12,8},{16,20},{20,16},{24,28},{28,24},{1,5},{5... | collective-permute-start | bytes 2359304 | tf_op jit(solution)/shard_map/ppermute | solution.py:334
  378.4 35.6 %collective-permute-start.18 = (bf16[512,768]{1,0:T(8,128)(2,1)}, bf16[512,768]{1,0:T(8,128)(2,1)}, u32[]{:S(2)}, u32[]{:S(2)}) collective-permute-start(bf16[512,768]{1,0:T(8,128)(2,1)} %shard_map.317), channel_id=1, source_target_pairs={{0,2},{1,3},{2,0},{3,1},{4,6},{5,7},{6,4},{7,5},{8,10},{9,11},{10,... | collective-permute-start | bytes 2359304 | tf_op jit(solution)/shard_map/ppermute | solution.py:330
  381.0 29.4 %collective-permute-start.26 = (bf16[512,512]{1,0:T(8,128)(2,1)S(1)}, bf16[512,512]{1,0:T(8,128)(2,1)}, u32[]{:S(2)}, u32[]{:S(2)}) collective-permute-start(bf16[512,512]{1,0:T(8,128)(2,1)S(1)} %shard_map.324), channel_id=1, source_target_pairs={{0,2},{1,3},{2,0},{3,1},{4,6},{5,7},{6,4},{7,5},{8,10},{9,11},{10,... | collective-permute-start | bytes 1572872 | tf_op jit(solution)/shard_map/ppermute | solution.py:330
  384.6 36.9 %collective-permute-start.33 = (bf16[512,512]{1,0:T(8,128)(2,1)}, bf16[512,512]{1,0:T(8,128)(2,1)}, u32[]{:S(2)}, u32[]{:S(2)}) collective-permute-start(bf16[512,512]{1,0:T(8,128)(2,1)} %shard_map.328), channel_id=1, source_target_pairs={{0,4},{4,0},{8,12},{12,8},{16,20},{20,16},{24,28},{28,24},{1,5},{5... | collective-permute-start | bytes 1572872 | tf_op jit(solution)/shard_map/ppermute | solution.py:334
  386.0 37.6 %collective-permute-start.34 = (bf16[512,768]{1,0:T(8,128)(2,1)S(1)}, bf16[512,768]{1,0:T(8,128)(2,1)S(1)}, u32[]{:S(2)}, u32[]{:S(2)}) collective-permute-start(bf16[512,768]{1,0:T(8,128)(2,1)S(1)} %shard_map.329), channel_id=1, source_target_pairs={{0,2},{1,3},{2,0},{3,1},{4,6},{5,7},{6,4},{7,5},{8,10},{9,11},{10,... | collective-permute-start | bytes 2359304 | tf_op jit(solution)/shard_map/ppermute | solution.py:330
  414.0 44.0 %collective-permute-start.27 = (bf16[128,1024]{1,0:T(8,128)(2,1)}, bf16[128,1024]{1,0:T(8,128)(2,1)S(1)}, u32[]{:S(2)}, u32[]{:S(2)}) collective-permute-start(bf16[128,1024]{1,0:T(8,128)(2,1)} %get-tuple-element.179), channel_id=1, source_target_pairs={{0,8},{4,12},{8,0},{12,4},{16,24},{20,28},{24,16},{28,20},{1,9},{5... | collective-permute-start | bytes 786440 | tf_op jit(solution)/shard_map/ppermute | solution.py:334
  417.4 12.8 %collective-permute-start.19 = (bf16[128,768]{1,0:T(8,128)(2,1)}, bf16[128,768]{1,0:T(8,128)(2,1)S(1)}, u32[]{:S(2)}, u32[]{:S(2)}) collective-permute-start(bf16[128,768]{1,0:T(8,128)(2,1)} %get-tuple-element.156), channel_id=1, source_target_pairs={{0,8},{4,12},{8,0},{12,4},{16,24},{20,28},{24,16},{28,20},{1,9},{5... | collective-permute-start | bytes 589832 | tf_op jit(solution)/shard_map/ppermute | solution.py:334
  419.4 23.9 %collective-permute-start.20 = (bf16[128,768]{1,0:T(8,128)(2,1)}, bf16[128,768]{1,0:T(8,128)(2,1)S(1)}, u32[]{:S(2)}, u32[]{:S(2)}) collective-permute-start(bf16[128,768]{1,0:T(8,128)(2,1)} %get-tuple-element.157), channel_id=1, source_target_pairs={{0,16},{4,20},{8,24},{12,28},{16,0},{20,4},{24,8},{28,12},{1,17},{... | collective-permute-start | bytes 589832 | tf_op jit(solution)/shard_map/ppermute | solution.py:334
  421.5 22.7 %collective-permute-start.21 = (bf16[128,768]{1,0:T(8,128)(2,1)}, bf16[128,768]{1,0:T(8,128)(2,1)S(1)}, u32[]{:S(2)}, u32[]{:S(2)}) collective-permute-start(bf16[128,768]{1,0:T(8,128)(2,1)} %get-tuple-element.158), channel_id=1, source_target_pairs={{0,24},{4,28},{8,16},{12,20},{16,8},{20,12},{24,0},{28,4},{1,25},{... | collective-permute-start | bytes 589832 | tf_op jit(solution)/shard_map/ppermute | solution.py:334
  423.6 68.3 %copy-start.37 = (bf16[128,768]{1,0:T(8,128)(2,1)S(1)}, bf16[128,768]{1,0:T(8,128)(2,1)}, u32[]{:S(2)}) copy-start(bf16[128,768]{1,0:T(8,128)(2,1)} %get-tuple-element.155.refs_0_) | copy-start | bytes 589828
  423.6 68.3 %copy-start.38 = (s32[4]{0:T(128)S(1)}, s32[4]{0:T(128)}, u32[]{:S(2)}) copy-start(s32[4]{0:T(128)} %pad_add_fusion.2.info_ref.left_at) | copy-start | bytes 52
  423.6 72.0 %collective-permute-start.28 = (bf16[128,1024]{1,0:T(8,128)(2,1)}, bf16[128,1024]{1,0:T(8,128)(2,1)}, u32[]{:S(2)}, u32[]{:S(2)}) collective-permute-start(bf16[128,1024]{1,0:T(8,128)(2,1)} %get-tuple-element.180), channel_id=1, source_target_pairs={{0,16},{4,20},{8,24},{12,28},{16,0},{20,4},{24,8},{28,12},{1,17},{... | collective-permute-start | bytes 786440 | tf_op jit(solution)/shard_map/ppermute | solution.py:334
  430.2 65.4 %collective-permute-start.29 = (bf16[128,1024]{1,0:T(8,128)(2,1)}, bf16[128,1024]{1,0:T(8,128)(2,1)}, u32[]{:S(2)}, u32[]{:S(2)}) collective-permute-start(bf16[128,1024]{1,0:T(8,128)(2,1)} %get-tuple-element.181), channel_id=1, source_target_pairs={{0,24},{4,28},{8,16},{12,20},{16,8},{20,12},{24,0},{28,4},{1,25},{... | collective-permute-start | bytes 786440 | tf_op jit(solution)/shard_map/ppermute | solution.py:334
  443.3 52.3 %collective-permute-start.35 = (bf16[128,1280]{1,0:T(8,128)(2,1)}, bf16[128,1280]{1,0:T(8,128)(2,1)S(1)}, u32[]{:S(2)}, u32[]{:S(2)}) collective-permute-start(bf16[128,1280]{1,0:T(8,128)(2,1)} %get-tuple-element.197), channel_id=1, source_target_pairs={{0,8},{4,12},{8,0},{12,4},{16,24},{20,28},{24,16},{28,20},{1,9},{5... | collective-permute-start | bytes 983048 | tf_op jit(solution)/shard_map/ppermute | solution.py:334
  444.2 51.3 %collective-permute-start.36 = (bf16[128,1280]{1,0:T(8,128)(2,1)}, bf16[128,1280]{1,0:T(8,128)(2,1)S(1)}, u32[]{:S(2)}, u32[]{:S(2)}) collective-permute-start(bf16[128,1280]{1,0:T(8,128)(2,1)} %get-tuple-element.198), channel_id=1, source_target_pairs={{0,16},{4,20},{8,24},{12,28},{16,0},{20,4},{24,8},{28,12},{1,17},{... | collective-permute-start | bytes 983048 | tf_op jit(solution)/shard_map/ppermute | solution.py:334
  458.0 37.6 %collective-permute-start.37 = (bf16[128,1280]{1,0:T(8,128)(2,1)}, bf16[128,1280]{1,0:T(8,128)(2,1)S(1)}, u32[]{:S(2)}, u32[]{:S(2)}) collective-permute-start(bf16[128,1280]{1,0:T(8,128)(2,1)} %get-tuple-element.199), channel_id=1, source_target_pairs={{0,24},{4,28},{8,16},{12,20},{16,8},{20,12},{24,0},{28,4},{1,25},{... | collective-permute-start | bytes 983048 | tf_op jit(solution)/shard_map/ppermute | solution.py:334
  460.0 43.4 %copy-start.30 = (bf16[128,1280]{1,0:T(8,128)(2,1)S(1)}, bf16[128,1280]{1,0:T(8,128)(2,1)}, u32[]{:S(2)}) copy-start(bf16[128,1280]{1,0:T(8,128)(2,1)} %get-tuple-element.201.refs_0_) | copy-start | bytes 983044
  (61 other events, 672.8 us)

commit v7 on v6

--- a/solution.py
+++ b/solution.py
@@ -1056,12 +1056,34 @@
         at += 2 * run.size
 
 
-def add_kernel(part, swap, mine_ref, got_ref, out_ref):
-    rows = out_ref.shape[0]
-    mine, got = mine_ref[...].reshape(rows, -1), got_ref[...].reshape(rows, -1)
-    for at, source, size in column_runs(part, swap):
-        total = mine[:, at : at + size].astype(F32) + got[:, source : source + size].astype(F32)
-        out_ref[:, at : at + size] = total.astype(BF16)
+def add_kernel(jobs, *refs):
+    ins, outs = refs[: 2 * len(jobs)], refs[2 * len(jobs) :]
+    for k, (part, swap) in enumerate(jobs):
+        rows = outs[k].shape[0]
+        mine, got = [ref[...].reshape(rows, -1) for ref in ins[2 * k : 2 * k + 2]]
+        for at, source, size in column_runs(part, swap):
+            total = mine[:, at : at + size].astype(F32) + got[:, source : source + size].astype(F32)
+            outs[k][:, at : at + size] = total.astype(BF16)
+
+
+def half_spec(array, where, width):
+    side, column = where
+    if len(array.shape) == 3:
+        return pl.BlockSpec((1, D // 4, width), lambda i: (side, i, column))
+    return pl.BlockSpec((D // 4, width), lambda i: (i, column))
+
+
+def add_parts(*jobs):
+    widths = [part_width(job[2]) for job in jobs]
+    return pl.pallas_call(
+        functools.partial(add_kernel, tuple(job[2:] for job in jobs)),
+        out_shape=tuple(struct((D // 2, width)) for width in widths),
+        grid=(2,),
+        in_specs=[half_spec(*v, width) for job, width in zip(jobs, widths) for v in job[:2]],
+        out_specs=[pl.BlockSpec((D // 4, width), lambda i: (i, 0)) for width in widths],
+        compiler_params=room(24),
+        cost_estimate=cost(1e6, 3e6),
+    )(*[v[0] for job in jobs for v in job[:2]])
 
 
 def block_spec(array, where, width):
@@ -1069,19 +1091,6 @@
     if len(array.shape) == 3:
         return pl.BlockSpec((1, D // 2, width), lambda *_: (side, 0, column))
     return pl.BlockSpec((D // 2, width), lambda *_: (0, column))
-
-
-def add_parts(mine, got, part, swap):
-    width = part_width(part)
-    return pl.pallas_call(
-        functools.partial(add_kernel, part, swap),
-        out_shape=struct((D // 2, width)),
-        grid=(1,),
-        in_specs=[block_spec(*v, width) for v in (mine, got)],
-        out_specs=whole((D // 2, width)),
-        compiler_params=room(24),
-        cost_estimate=cost(1e6, 3e6),
-    )(mine[0], got[0])
 
 
 def split_kernel(parts, info_ref, *refs):
@@ -1389,10 +1398,12 @@
 
     def second_sends(sums, parts):
         own, keep, from_y, from_x = sums
-        low = add_parts((own, (1, 0)), (from_y, (1, 0)), parts[0], False)
+        low, other = add_parts(
+            ((own, (1, 0)), (from_y, (1, 0)), parts[0], False),
+            ((keep, (0, 1)), (from_x, (0, 1)), parts[1], True),
+        )
         x_two = send_dp(low, 1)
-        low = add_parts((keep, (0, 1)), (from_x, (0, 1)), parts[1], True)
-        y_two = send_mp(low, 2)
+        y_two = send_mp(other, 2)
         here = (0, 0)
         return (
             ((own, here), (x_two, here), (from_y, here)),
@@ -1436,7 +1447,7 @@
     back(0)
     up_values = split_z(info, up_parts, up_last)
     here = (0, 0)
-    far_low = add_parts((far_keep, here), (far_x, here), qkv_part, True)
+    (far_low,) = add_parts(((far_keep, here), (far_x, here), qkv_part, True))
     far_y = send_mp(far_low, 2)
     own_keep, own_leave = grad_call(
         info, [hidden_t], [d_qkv[:1] + d_qkv[2:]], own_only, 0, sides, got, 0

time: 518 us -> 507 us (0.979)
  waiting for transfers between devices: 107 us -> 95.4 us
    ppermute x18, waiting for transfers between devices: 51.3 us -> 41.4 us  [send_dp(): return lax.ppermute(values, 'dp', [(i, i ^ bit) for i in range(GRID_DP)])]
    unnamed x145 -> x149, local copies, waits for them, and re-layouts: 18.8 us -> 19.7 us
  transfers between devices with their start and end apart: 38 -> 38, of which waited for: 10 -> 11; matrix products, arithmetic and copies ran while one was open for 2% -> 2% of each run, Pallas kernels for 50% -> 51%
where the time goes in v7:
time: 507 us; the launch traced here: 498 us
  Pallas kernels  312 us (62%)
  waiting for transfers between devices  95.4 us (19%)
  starting transfers between devices  51.5 us (10%)
  local copies, waits for them, and re-layouts  28.8 us (6%)
  other arithmetic  5.13 us (1%)
    pallas_call x7, Pallas kernels, grad_call(): pl.pallas_call(functools.partial(grad_kernel, blocks, side, outputs, left...  61.4 us
    pallas_call x4, Pallas kernels, attend_back_pair(): pl.pallas_call(attend_back_kernel, out_shape=(far((LEN, 6 * UNIT)), struc...  60.6 us
    ppermute x20, waiting for transfers between devices, send_mp(): return lax.ppermute(values, 'mp', [(i, i ^ bit) for i in range(GRID_MP)])  54 us
    pallas_call x4, Pallas kernels, attend_pair(): pl.pallas_call(attend_kernel, out_shape=(far((LEN, 6 * UNIT)), far((LEN,...  43 us
    ppermute x18, waiting for transfers between devices, send_dp(): return lax.ppermute(values, 'dp', [(i, i ^ bit) for i in range(GRID_DP)])  41.4 us
    ppermute x18, starting transfers between devices, send_dp(): return lax.ppermute(values, 'dp', [(i, i ^ bit) for i in range(GRID_DP)])  40.8 us
    pallas_call x1, Pallas kernels, exchange(): pl.pallas_call(exchange_kernel, out_shape=(struct(sums.shape[1:], F32), s...  30.8 us
    pallas_call x1, Pallas kernels, ffn_back(): pl.pallas_call(ffn_back_kernel, out_shape=(far((LEN, 2 * size)),) * 4 + (...  28.5 us
  transfers between devices with their start and end apart: 38, of which 11 were waited for; matrix products, arithmetic and copies ran while one was open for 2% of the time, Pallas kernels for 51%

profile of v7, /device:TPU:0, one launch (start us, length us, event | category | flops | bytes accessed | tf_op | source)
XLA Modules:
  0.0 498.3 jit_solution(11620689533359017327)
XLA Ops:
  2.7 4.4 shard_map.297
  7.1 3.0 collective-permute-start.1
  10.1 5.6 %shard_map.303 = (bf16[2,512,1024]{2,1,0:T(8,128)(2,1)}, bf16[512,1024]{1,0:T(8,128)(2,1)}, bf16[2,512,1024]{2,1,0:T(8,128)(2,1)}, bf16[512,1024]{1,0:T(8,128)(2,1)}) custom-call(s32[4]{0:T(128)} %pad_add_fusion.2.info_ref.left_at, bf16[1024,1024]{1,0:T(8,128)(2,1)} %up_ref.1, bf16[1024,1024]{1,0:T(8,128)(2,1)} %down_ref.1), custom_call_target="tpu_custom_call" | custom-call | flops 1000000 | bytes 10000000 | tf_op jit(solution)/shard_map/pallas_call | solution.py:397
  22.4 12.7 %collective-permute-done.1.refs_0_.refs_2_.refs_8_.refs_4_.wa_ref.refs_6_ = bf16[528,1024]{1,0:T(8,128)(2,1)S(1)} collective-permute-done((bf16[528,1024]{1,0:T(8,128)(2,1)}, bf16[528,1024]{1,0:T(8,128)(2,1)S(1)}, u32[]{:S(2)}, u32[]{:S(2)}) %collective-permute-start.1) | collective-permute-done | bytes 1081376 | tf_op jit(solution)/shard_map/ppermute | solution.py:330
  39.2 10.2 %shard_map.298 = (bf16[1024,768]{1,0:T(8,128)(2,1)}, bf16[1024,256]{1,0:T(8,128)(2,1)}, f32[2,8,1024]{2,1,0:T(8,128)}) custom-call(s32[2,2]{1,0:T(2,128)S(1)} %pad_add_fusion.win_ref, bf16[1024,1024]{1,0:T(8,128)(2,1)S(1)} %add_convert_fusion.x_ref, bf16[2,528,1024]{2,1,0:T(8,128)(2,1)S(1)} %copy-done.2, bf16[2,528,1024]{2,1,0:T(8,128)(2,1)S(1)} %copy-done.2, ...), custom_call_target="tpu_custom_call" | custom-call | flops 6000000000 | bytes 8000000 | tf_op jit(solution)/shard_map/pallas_call | solution.py:523
  49.3 8.3 %collective-permute-done.5.refs_0_.refs_8_ = bf16[512,1024]{1,0:T(8,128)(2,1)} collective-permute-done((bf16[512,1024]{1,0:T(8,128)(2,1)}, bf16[512,1024]{1,0:T(8,128)(2,1)}, u32[]{:S(2)}, u32[]{:S(2)}) %collective-permute-start.5) | collective-permute-done | bytes 1048608 | tf_op jit(solution)/shard_map/ppermute | solution.py:330
  57.7 21.6 %collective-permute-done.8.refs_2_ = bf16[512,1024]{1,0:T(8,128)(2,1)} collective-permute-done((bf16[512,1024]{1,0:T(8,128)(2,1)}, bf16[512,1024]{1,0:T(8,128)(2,1)}, u32[]{:S(2)}, u32[]{:S(2)}) %collective-permute-start.8) | collective-permute-done | bytes 1048608 | tf_op jit(solution)/shard_map/ppermute | solution.py:330
  81.2 10.7 %shard_map.300 = (bf16[1024,768]{1,0:T(8,128)(2,1)}, bf16[1024,256]{1,0:T(8,128)(2,1)}, f32[2,8,1024]{2,1,0:T(8,128)}) custom-call(s32[2,2]{1,0:T(2,128)S(1)} %pad_add_fusion.win_ref, bf16[1024,1024]{1,0:T(8,128)(2,1)S(1)} %add_convert_fusion.x_ref, bf16[528,1024]{1,0:T(8,128)(2,1)S(1)} %collective-permute-done.1.refs_0_.refs_2_.refs_8_.refs_4_.wa_ref.refs_6_, ...), custom_call_target="tpu_custom_call" | custom-call | flops 6000000000 | bytes 8000000 | tf_op jit(solution)/shard_map/pallas_call | solution.py:523
  91.9 11.7 %shard_map.299 = (bf16[1024,768]{1,0:T(8,128)(2,1)}, bf16[1024,256]{1,0:T(8,128)(2,1)}, f32[2,8,1024]{2,1,0:T(8,128)}) custom-call(s32[2,2]{1,0:T(2,128)S(1)} %pad_add_fusion.win_ref, bf16[1024,1024]{1,0:T(8,128)(2,1)S(1)} %add_convert_fusion.x_ref, ...), custom_call_target="tpu_custom_call" | custom-call | flops 6000000000 | bytes 8000000 | tf_op jit(solution)/shard_map/pallas_call | solution.py:523
  106.1 10.4 %shard_map.301 = (bf16[1024,768]{1,0:T(8,128)(2,1)}, bf16[1024,256]{1,0:T(8,128)(2,1)}, f32[2,8,1024]{2,1,0:T(8,128)}) custom-call(s32[2,2]{1,0:T(2,128)S(1)} %pad_add_fusion.win_ref, bf16[1024,1024]{1,0:T(8,128)(2,1)S(1)} %add_convert_fusion.x_ref, bf16[528,1024]{1,0:T(8,128)(2,1)S(1)} %collective-permute-done.3.refs_0_.refs_2_.refs_10_.refs_4_.wa_ref.refs_8_, ...), custom_call_target="tpu_custom_call" | custom-call | flops 6000000000 | bytes 8000000 | tf_op jit(solution)/shard_map/pallas_call | solution.py:523
  117.6 6.8 %shard_map.302 = (bf16[1024,1024]{1,0:T(8,128)(2,1)}, f32[1024,1]{1,0:T(8,128)}, bf16[1024,1024]{1,0:T(8,128)(2,1)S(1)}, bf16[1024,1024]{1,0:T(8,128)(2,1)}, bf16[1024,1024]{1,0:T(8,128)(2,1)}) custom-call(bf16[1024,1024]{1,0:T(8,128)(2,1)S(1)} %copy-done.6, bf16[1024,256]{1,0:T(8,128)(2,1)S(1)} %copy-done.22, bf16[1024,256]{1,0:T(8,128)(2,1)S(1)} %copy-done.28, ...), custom_call_target="tpu_custom_call" | custom-call | flops 2200000000 | bytes 20000000 | tf_op jit(solution)/shard_map/pallas_call | solution.py:700
  124.3 3.2 collective-permute-done.9.refs_2_.refs_4_
  128.0 7.1 %shard_map.304 = (bf16[1024,1024]{1,0:T(8,128)(2,1)}, bf16[1024,1024]{1,0:T(8,128)(2,1)}, f32[1024,1024]{1,0:T(8,128)S(1)}) custom-call(bf16[1024,1024]{1,0:T(8,128)(2,1)S(1)} %get-tuple-element.124.mid_ref, bf16[2,512,1024]{2,1,0:T(8,128)(2,1)S(1)} %copy-done.41, bf16[2,512,1024]{2,1,0:T(8,128)(2,1)S(1)} %copy-done.41, ...), custom_call_target="tpu_custom_call" | custom-call | flops 4300000256 | bytes 18000000 | tf_op jit(solution)/shard_map/pallas_call | solution.py:765
  135.2 8.0 %shard_map.305 = (bf16[1024,1024]{1,0:T(8,128)(2,1)}, bf16[1024,1024]{1,0:T(8,128)(2,1)}, f32[1024,1024]{1,0:T(8,128)S(1)}) custom-call(bf16[1024,1024]{1,0:T(8,128)(2,1)S(1)} %get-tuple-element.124.mid_ref, bf16[2,512,1024]{2,1,0:T(8,128)(2,1)S(1)} %collective-permute-done.13.refs_0_.refs_1_.refs_7_, ...), custom_call_target="tpu_custom_call" | custom-call | flops 4300000256 | bytes 18000000 | tf_op jit(solution)/shard_map/pallas_call | solution.py:765
  143.2 9.5 %shard_map.306 = (bf16[1024,1024]{1,0:T(8,128)(2,1)}, bf16[1024,1024]{1,0:T(8,128)(2,1)}, f32[1024,1024]{1,0:T(8,128)S(1)}) custom-call(bf16[1024,1024]{1,0:T(8,128)(2,1)S(1)} %get-tuple-element.124.mid_ref, bf16[512,1024]{1,0:T(8,128)(2,1)} %collective-permute-done.5.refs_0_.refs_8_, bf16[512,1024]{1,0:T(8,128)(2,1)S(1)} %collective-permute-done.11.refs_1_.refs_9_, ...), custom_call_target="tpu_custom_call" | custom-call | flops 4300000256 | bytes 18000000 | tf_op jit(solution)/shard_map/pallas_call | solution.py:765
  152.8 11.8 %shard_map.307 = (bf16[1024,1024]{1,0:T(8,128)(2,1)}, bf16[1024,1024]{1,0:T(8,128)(2,1)}, bf16[1024,1024]{1,0:T(8,128)(2,1)}, bf16[1024,1024]{1,0:T(8,128)(2,1)}...) custom-call(bf16[1024,1024]{1,0:T(8,128)(2,1)S(1)} %get-tuple-element.124.mid_ref, ...), custom_call_target="tpu_custom_call" | custom-call | flops 4300000256 | bytes 30000000 | tf_op jit(solution)/shard_map/pallas_call | solution.py:804
  164.6 28.5 %shard_map.308 = (bf16[1024,1024]{1,0:T(8,128)(2,1)}, bf16[1024,1024]{1,0:T(8,128)(2,1)}, bf16[1024,1024]{1,0:T(8,128)(2,1)}, bf16[1024,1024]{1,0:T(8,128)(2,1)}...) custom-call(bf16[1024,1024]{1,0:T(8,128)(2,1)} %get-tuple-element.133.b, ...), custom_call_target="tpu_custom_call" | custom-call | flops 16999999488 | bytes 40000000 | tf_op jit(solution)/shard_map/pallas_call | solution.py:911
  193.2 10.7 %shard_map.325 = bf16[2,512,2560]{2,1,0:T(8,128)(2,1)} custom-call(s32[4]{0:T(128)} %pad_add_fusion.2.info_ref.left_at, bf16[4,2,128,1024]{3,2,1,0:T(8,128)(2,1)} %bitcast.140, bf16[4,2,128,1024]{3,2,1,0:T(8,128)(2,1)} %bitcast.142, bf16[1024,1024]{1,0:T(8,128)(2,1)} %get-tuple-element.193.refs_2_, bf16[1024,1024]{1,0:T(8,128)(2,1)} %get-tuple-element.191.refs_3_, ...), custom_call_target="tpu_custom_call" | custom-call | flops 5368709120 | bytes 10000000 | tf_op jit(solution)/shard_map/pallas_call | solution.py:1029
  204.1 9.3 %shard_map.321 = bf16[2,512,2048]{2,1,0:T(8,128)(2,1)} custom-call(s32[4]{0:T(128)} %pad_add_fusion.2.info_ref.left_at, bf16[4,2,128,1024]{3,2,1,0:T(8,128)(2,1)} %bitcast.144, bf16[1024,1024]{1,0:T(8,128)(2,1)} %get-tuple-element.177.refs_1_, bf16[1024,1024]{1,0:T(8,128)(2,1)} %get-tuple-element.175.refs_2_, bf16[1024,1024]{1,0:T(8,128)(2,1)} %get-tuple-element.176.refs_3_), custom_call_target="tpu_custom_call" | custom-call | flops 4294967296 | bytes 10000000 | tf_op jit(solution)/shard_map/pallas_call | solution.py:1029
  220.6 14.9 %shard_map.312 = (bf16[1024,768]{1,0:T(8,128)(2,1)}, f32[8,768]{1,0:T(8,128)S(1)}) custom-call(s32[2,4]{1,0:T(2,128)S(1)} %pad_add_fusion.1.win_ref, bf16[1024,768]{1,0:T(8,128)(2,1)S(1)} %copy-done.55, bf16[1024,128]{1,0:T(8,128)(2,1)S(1)} %copy-done.32, bf16[1024,128]{1,0:T(8,128)(2,1)S(1)} %get-tuple-element.274.refs_5_.hotk_ref, ...), custom_call_target="tpu_custom_call" | custom-call | flops 8000000000 | bytes 8000000 | tf_op jit(solution)/shard_map/pallas_call | solution.py:632
  235.5 14.8 %shard_map.311 = (bf16[1024,768]{1,0:T(8,128)(2,1)}, f32[8,768]{1,0:T(8,128)S(1)}) custom-call(s32[2,4]{1,0:T(2,128)S(1)} %pad_add_fusion.1.win_ref, bf16[1024,768]{1,0:T(8,128)(2,1)S(1)} %copy-done.54, bf16[1024,128]{1,0:T(8,128)(2,1)S(1)} %copy-done.32, bf16[1024,128]{1,0:T(8,128)(2,1)S(1)} %get-tuple-element.274.refs_5_.hotk_ref, ...), custom_call_target="tpu_custom_call" | custom-call | flops 8000000000 | bytes 8000000 | tf_op jit(solution)/shard_map/pallas_call | solution.py:632
  251.0 16.1 %shard_map.310 = (bf16[1024,768]{1,0:T(8,128)(2,1)}, f32[8,768]{1,0:T(8,128)S(1)}) custom-call(s32[2,4]{1,0:T(2,128)S(1)} %pad_add_fusion.1.win_ref, bf16[1024,768]{1,0:T(8,128)(2,1)S(1)} %copy-done.53, bf16[1024,128]{1,0:T(8,128)(2,1)S(1)} %copy-done.32, bf16[1024,128]{1,0:T(8,128)(2,1)S(1)} %get-tuple-element.274.refs_5_.hotk_ref, ...), custom_call_target="tpu_custom_call" | custom-call | flops 8000000000 | bytes 8000000 | tf_op jit(solution)/shard_map/pallas_call | solution.py:632
  267.1 8.2 %shard_map.314 = bf16[2,512,1536]{2,1,0:T(8,128)(2,1)} custom-call(s32[4]{0:T(128)} %pad_add_fusion.2.info_ref.left_at, bf16[4,2,128,1024]{3,2,1,0:T(8,128)(2,1)} %bitcast.120, bf16[1024,768]{1,0:T(8,128)(2,1)} %get-tuple-element.146.refs_1_, bf16[1024,768]{1,0:T(8,128)(2,1)} %get-tuple-element.149.refs_2_, bf16[1024,768]{1,0:T(8,128)(2,1)} %get-tuple-element.152.refs_3_), custom_call_target="tpu_custom_call" | custom-call | flops 3221225472 | bytes 10000000 | tf_op jit(solution)/shard_map/pallas_call | solution.py:1029
  275.4 9.2 %shard_map.322 = (bf16[2,512,512]{2,1,0:T(8,128)(2,1)}, bf16[2,512,512]{2,1,0:T(8,128)(2,1)}, bf16[512,1024]{1,0:T(8,128)(2,1)}, bf16[512,1024]{1,0:T(8,128)(2,1)}) custom-call(s32[4]{0:T(128)} %pad_add_fusion.2.info_ref.left_at, bf16[4,2,128,1024]{3,2,1,0:T(8,128)(2,1)} %bitcast.145, bf16[1024,1024]{1,0:T(8,128)(2,1)} %get-tuple-element.174.refs_1_, ...), custom_call_target="tpu_custom_call" | custom-call | flops 4294967296 | bytes 10000000 | tf_op jit(solution)/shard_map/pallas_call | solution.py:1029
  284.8 3.2 collective-permute-start.24
  288.0 11.1 %shard_map.326 = (bf16[2,512,512]{2,1,0:T(8,128)(2,1)}, bf16[2,512,512]{2,1,0:T(8,128)(2,1)}, bf16[512,1536]{1,0:T(8,128)(2,1)}, bf16[512,1536]{1,0:T(8,128)(2,1)}) custom-call(s32[4]{0:T(128)} %pad_add_fusion.2.info_ref.left_at, bf16[4,2,128,1024]{3,2,1,0:T(8,128)(2,1)} %bitcast.141, bf16[4,2,128,1024]{3,2,1,0:T(8,128)(2,1)} %bitcast.143, ...), custom_call_target="tpu_custom_call" | custom-call | flops 5368709120 | bytes 10000000 | tf_op jit(solution)/shard_map/pallas_call | solution.py:1029
  300.5 6.5 %shard_map.316 = (bf16[512,768]{1,0:T(8,128)(2,1)}, bf16[512,768]{1,0:T(8,128)(2,1)}) custom-call(s32[4]{0:T(128)} %pad_add_fusion.2.info_ref.left_at, bf16[4,2,128,1024]{3,2,1,0:T(8,128)(2,1)} %bitcast.121, bf16[1024,768]{1,0:T(8,128)(2,1)} %get-tuple-element.146.refs_1_, bf16[1024,768]{1,0:T(8,128)(2,1)} %get-tuple-element.149.refs_2_, ...), custom_call_target="tpu_custom_call" | custom-call | flops 1610612736 | bytes 10000000 | tf_op jit(solution)/shard_map/pallas_call | solution.py:1029
  312.3 2.0 shard_map.323
  314.4 2.0 collective-permute-start.25
  319.4 14.9 %shard_map.309 = (bf16[1024,768]{1,0:T(8,128)(2,1)}, f32[8,768]{1,0:T(8,128)S(1)}) custom-call(s32[2,4]{1,0:T(2,128)S(1)} %pad_add_fusion.1.win_ref, bf16[1024,768]{1,0:T(8,128)(2,1)S(1)} %copy-done.52, bf16[1024,128]{1,0:T(8,128)(2,1)S(1)} %copy-done.33, bf16[1024,128]{1,0:T(8,128)(2,1)S(1)} %get-tuple-element.274.refs_5_.hotk_ref, ...), custom_call_target="tpu_custom_call" | custom-call | flops 8000000000 | bytes 8000000 | tf_op jit(solution)/shard_map/pallas_call | solution.py:632
  334.3 6.4 %shard_map.315 = (bf16[512,768]{1,0:T(8,128)(2,1)}, bf16[512,768]{1,0:T(8,128)(2,1)}) custom-call(s32[4]{0:T(128)} %pad_add_fusion.2.info_ref.left_at, bf16[4,2,128,1024]{3,2,1,0:T(8,128)(2,1)} %bitcast.122, bf16[1024,768]{1,0:T(8,128)(2,1)} %get-tuple-element.143.refs_0_.refs_1_, bf16[1024,768]{1,0:T(8,128)(2,1)} %get-tuple-element.149.refs_2_, ...), custom_call_target="tpu_custom_call" | custom-call | flops 1610612736 | bytes 10000000 | tf_op jit(solution)/shard_map/pallas_call | solution.py:1029
  340.8 22.1 %collective-permute-done.17.refs_1_ = bf16[512,768]{1,0:T(8,128)(2,1)} collective-permute-done((bf16[512,768]{1,0:T(8,128)(2,1)}, bf16[512,768]{1,0:T(8,128)(2,1)}, u32[]{:S(2)}, u32[]{:S(2)}) %collective-permute-start.17) | collective-permute-done | bytes 786464 | tf_op jit(solution)/shard_map/ppermute | solution.py:334
  367.7 2.2 shard_map.327
  369.9 2.0 collective-permute-start.33
  371.9 2.2 collective-permute-done.25.refs_1_
  374.8 12.5 %shard_map.313 = (f32[1024,1024]{1,0:T(8,128)}, f32[8,1024]{1,0:T(8,128)}) custom-call(bf16[1024,1024]{1,0:T(8,128)(2,1)} %get-tuple-element.140.branch_ref, bf16[1024,768]{1,0:T(8,128)(2,1)} %get-tuple-element.143.refs_0_.refs_1_, bf16[1024,768]{1,0:T(8,128)(2,1)} %get-tuple-element.146.refs_1_, bf16[1024,768]{1,0:T(8,128)(2,1)} %get-tuple-element.149.refs_2_, ...), custom_call_target="tpu_custom_call" | custom-call | flops 6400000000 | bytes 20000000 | tf_op jit(solution)/shard_map/pallas_call | solution.py:1209
  387.4 9.4 %collective-permute-done.26.refs_5_ = bf16[512,512]{1,0:T(8,128)(2,1)} collective-permute-done((bf16[512,512]{1,0:T(8,128)(2,1)S(1)}, bf16[512,512]{1,0:T(8,128)(2,1)}, u32[]{:S(2)}, u32[]{:S(2)}) %collective-permute-start.26) | collective-permute-done | bytes 524320 | tf_op jit(solution)/shard_map/ppermute | solution.py:330
  396.8 3.6 shard_map.324
  401.7 3.3 shard_map.318
  406.7 3.1 collective-permute-start.20
  411.1 3.1 collective-permute-start.28
  414.2 4.0 shard_map.328
  419.6 10.7 %collective-permute-done.20.refs_2_ = bf16[128,768]{1,0:T(8,128)(2,1)S(1)} collective-permute-done((bf16[128,768]{1,0:T(8,128)(2,1)}, bf16[128,768]{1,0:T(8,128)(2,1)S(1)}, u32[]{:S(2)}, u32[]{:S(2)}) %collective-permute-start.20) | collective-permute-done | bytes 196640 | tf_op jit(solution)/shard_map/ppermute | solution.py:334
  430.3 2.5 collective-permute-start.35
  432.8 13.6 %collective-permute-start.36 = (bf16[128,1280]{1,0:T(8,128)(2,1)}, bf16[128,1280]{1,0:T(8,128)(2,1)S(1)}, u32[]{:S(2)}, u32[]{:S(2)}) collective-permute-start(bf16[128,1280]{1,0:T(8,128)(2,1)} %get-tuple-element.206), channel_id=1, source_target_pairs={{0,16},{4,20},{8,24},{12,28},{16,0},{20,4},{24,8},{28,12},{1,17},{... | collective-permute-start | bytes 983048 | tf_op jit(solution)/shard_map/ppermute | solution.py:334
  449.8 30.8 %shard_map.320 = (f32[1,384]{1,0:T(1,128)}, f32[32,1,1152]{2,1,0:T(1,128)}) custom-call(f32[32,1,384]{2,1,0:T(1,128)} %broadcast_in_dim.97.sum_ref, f32[1,1152]{1,0:T(1,128)} %concatenate.23.row_ref), custom_call_target="tpu_custom_call" | custom-call | flops 1000000 | bytes 1000000 | tf_op jit(solution)/shard_map/pallas_call | solution.py:1282
  482.1 2.1 copy.55
  495.5 2.6 shard_map.330
  (276 shorter events, 63.3 us)
Async XLA Ops:
  7.1 27.9 %collective-permute-start.1 = (bf16[528,1024]{1,0:T(8,128)(2,1)}, bf16[528,1024]{1,0:T(8,128)(2,1)S(1)}, u32[]{:S(2)}, u32[]{:S(2)}) collective-permute-start(bf16[528,1024]{1,0:T(8,128)(2,1)} %get-tuple-element.121), channel_id=1, source_target_pairs={{0,2},{1,3},{2,0},{3,1},{4,6},{5,7},{6,4},{7,5},{8,10},{9,11},{10,... | collective-permute-start | bytes 3244040 | tf_op jit(solution)/shard_map/ppermute | solution.py:330
  10.1 81.8 %collective-permute-start = (bf16[2,528,1024]{2,1,0:T(8,128)(2,1)}, bf16[2,528,1024]{2,1,0:T(8,128)(2,1)}, u32[]{:S(2)}, u32[]{:S(2)}) collective-permute-start(bf16[2,528,1024]{2,1,0:T(8,128)(2,1)} %get-tuple-element.118.refs_0_.refs_1_.refs_2_.refs_3_.refs_4_.refs_5_.wa_ref.wb_ref), channel_id=1, source_target_pairs={{0,1},{1,0},{2,3},{3,2},{4,5},{5,4},{6,7},{7,6},{8,9},{9,8},{10,11... | collective-permute-start | bytes 6488072 | tf_op jit(solution)/shard_map/ppermute | solution.py:330
  15.7 41.9 %collective-permute-start.5 = (bf16[512,1024]{1,0:T(8,128)(2,1)}, bf16[512,1024]{1,0:T(8,128)(2,1)}, u32[]{:S(2)}, u32[]{:S(2)}) collective-permute-start(bf16[512,1024]{1,0:T(8,128)(2,1)} %get-tuple-element.125), channel_id=1, source_target_pairs={{0,2},{1,3},{2,0},{3,1},{4,6},{5,7},{6,4},{7,5},{8,10},{9,11},{10,... | collective-permute-start | bytes 3145736 | tf_op jit(solution)/shard_map/ppermute | solution.py:330
  15.8 63.4 %collective-permute-start.8 = (bf16[512,1024]{1,0:T(8,128)(2,1)}, bf16[512,1024]{1,0:T(8,128)(2,1)}, u32[]{:S(2)}, u32[]{:S(2)}) collective-permute-start(bf16[512,1024]{1,0:T(8,128)(2,1)} %get-tuple-element.126), channel_id=1, source_target_pairs={{0,2},{1,3},{2,0},{3,1},{4,6},{5,7},{6,4},{7,5},{8,10},{9,11},{10,... | collective-permute-start | bytes 3145736 | tf_op jit(solution)/shard_map/ppermute | solution.py:330
  35.0 200.4 %copy-start.14 = (bf16[528,1024]{1,0:T(8,128)(2,1)}, bf16[528,1024]{1,0:T(8,128)(2,1)S(1)}, u32[]{:S(2)}) copy-start(bf16[528,1024]{1,0:T(8,128)(2,1)S(1)} %collective-permute-done.1.refs_0_.refs_2_.refs_8_.refs_4_.wa_ref.refs_6_) | copy-start | bytes 3244036
  35.1 44.2 %collective-permute-start.3 = (bf16[528,1024]{1,0:T(8,128)(2,1)S(1)}, bf16[528,1024]{1,0:T(8,128)(2,1)S(1)}, u32[]{:S(2)}, u32[]{:S(2)}) collective-permute-start(bf16[528,1024]{1,0:T(8,128)(2,1)S(1)} %collective-permute-done.1.refs_0_.refs_2_.refs_8_.refs_4_.wa_ref.refs_6_), channel_id=1, source_target_pairs={{0,4},{4,0},{8,12},{12,8},{16,20},{20,16},{24,28},{28,24},{1,5},{5... | collective-permute-start | bytes 3244040 | tf_op jit(solution)/shard_map/ppermute | solution.py:334
  37.0 44.0 %collective-permute-start.2 = (bf16[528,1024]{1,0:T(8,128)(2,1)S(1)}, bf16[528,1024]{1,0:T(8,128)(2,1)S(1)}, u32[]{:S(2)}, u32[]{:S(2)}) collective-permute-start(bf16[528,1024]{1,0:T(8,128)(2,1)S(1)} %collective-permute-done.1.refs_0_.refs_2_.refs_8_.refs_4_.wa_ref.refs_6_), channel_id=1, source_target_pairs={{0,1},{1,0},{2,3},{3,2},{4,5},{5,4},{6,7},{7,6},{8,9},{9,8},{10,11... | collective-permute-start | bytes 3244040 | tf_op jit(solution)/shard_map/ppermute | solution.py:330
  37.4 68.7 %copy-start.31 = (bf16[1024,128]{1,0:T(8,128)(2,1)}, bf16[1024,128]{1,0:T(8,128)(2,1)S(1)}, u32[]{:S(2)}) copy-start(bf16[1024,128]{1,0:T(8,128)(2,1)S(1)} %get-tuple-element.275.refs_4_.hotq_ref) | copy-start | bytes 786436
  57.6 69.9 %collective-permute-start.13 = (bf16[2,512,1024]{2,1,0:T(8,128)(2,1)S(1)}, bf16[2,512,1024]{2,1,0:T(8,128)(2,1)S(1)}, u32[]{:S(2)}, u32[]{:S(2)}) collective-permute-start(bf16[2,512,1024]{2,1,0:T(8,128)(2,1)S(1)} %copy-done.41), channel_id=1, source_target_pairs={{0,1},{1,0},{2,3},{3,2},{4,5},{5,4},{6,7},{7,6},{8,9},{9,8},{10,11... | collective-permute-start | bytes 6291464 | tf_op jit(solution)/shard_map/ppermute | solution.py:330
  79.2 55.9 %collective-permute-start.14 = (bf16[2,512,1024]{2,1,0:T(8,128)(2,1)S(1)}, bf16[2,512,1024]{2,1,0:T(8,128)(2,1)S(1)}, u32[]{:S(2)}, u32[]{:S(2)}) collective-permute-start(bf16[2,512,1024]{2,1,0:T(8,128)(2,1)S(1)} %copy-done.42), channel_id=1, source_target_pairs={{0,1},{1,0},{2,3},{3,2},{4,5},{5,4},{6,7},{7,6},{8,9},{9,8},{10,11... | collective-permute-start | bytes 6291464 | tf_op jit(solution)/shard_map/ppermute | solution.py:330
  79.3 73.5 %copy-start.15 = (bf16[528,1024]{1,0:T(8,128)(2,1)}, bf16[528,1024]{1,0:T(8,128)(2,1)S(1)}, u32[]{:S(2)}) copy-start(bf16[528,1024]{1,0:T(8,128)(2,1)S(1)} %collective-permute-done.3.refs_0_.refs_2_.refs_10_.refs_4_.wa_ref.refs_8_) | copy-start | bytes 3244036
  79.3 26.3 %collective-permute-start.6 = (bf16[512,1024]{1,0:T(8,128)(2,1)}, bf16[512,1024]{1,0:T(8,128)(2,1)S(1)}, u32[]{:S(2)}, u32[]{:S(2)}) collective-permute-start(bf16[512,1024]{1,0:T(8,128)(2,1)} %collective-permute-done.5.refs_0_.refs_8_), channel_id=1, source_target_pairs={{0,4},{4,0},{8,12},{12,8},{16,20},{20,16},{24,28},{28,24},{1,5},{5... | collective-permute-start | bytes 3145736 | tf_op jit(solution)/shard_map/ppermute | solution.py:334
  81.0 62.1 %copy-start.17 = (bf16[528,1024]{1,0:T(8,128)(2,1)}, bf16[528,1024]{1,0:T(8,128)(2,1)S(1)}, u32[]{:S(2)}) copy-start(bf16[528,1024]{1,0:T(8,128)(2,1)S(1)} %collective-permute-done.2.refs_1_.refs_3_.refs_9_.refs_5_.wb_ref.refs_7_) | copy-start | bytes 3244036
  81.1 24.5 %collective-permute-start.4 = (bf16[528,1024]{1,0:T(8,128)(2,1)S(1)}, bf16[528,1024]{1,0:T(8,128)(2,1)S(1)}, u32[]{:S(2)}, u32[]{:S(2)}) collective-permute-start(bf16[528,1024]{1,0:T(8,128)(2,1)S(1)} %collective-permute-done.3.refs_0_.refs_2_.refs_10_.refs_4_.wa_ref.refs_8_), channel_id=1, source_target_pairs={{0,1},{1,0},{2,3},{3,2},{4,5},{5,4},{6,7},{7,6},{8,9},{9,8},{10,11... | collective-permute-start | bytes 3244040 | tf_op jit(solution)/shard_map/ppermute | solution.py:330
  91.9 35.6 %collective-permute-start.9 = (bf16[512,1024]{1,0:T(8,128)(2,1)}, bf16[512,1024]{1,0:T(8,128)(2,1)S(1)}, u32[]{:S(2)}, u32[]{:S(2)}) collective-permute-start(bf16[512,1024]{1,0:T(8,128)(2,1)} %collective-permute-done.8.refs_2_), channel_id=1, source_target_pairs={{0,4},{4,0},{8,12},{12,8},{16,20},{20,16},{24,28},{28,24},{1,5},{5... | collective-permute-start | bytes 3145736 | tf_op jit(solution)/shard_map/ppermute | solution.py:334
  105.6 47.2 %copy-start.43 = (bf16[512,1024]{1,0:T(8,128)(2,1)}, bf16[512,1024]{1,0:T(8,128)(2,1)S(1)}, u32[]{:S(2)}) copy-start(bf16[512,1024]{1,0:T(8,128)(2,1)S(1)} %collective-permute-done.6.refs_0_.refs_10_) | copy-start | bytes 3145732
  105.6 37.5 %collective-permute-start.11 = (bf16[512,1024]{1,0:T(8,128)(2,1)}, bf16[512,1024]{1,0:T(8,128)(2,1)S(1)}, u32[]{:S(2)}, u32[]{:S(2)}) collective-permute-start(bf16[512,1024]{1,0:T(8,128)(2,1)} %collective-permute-done.5.refs_0_.refs_8_), channel_id=1, source_target_pairs={{0,1},{1,0},{2,3},{3,2},{4,5},{5,4},{6,7},{7,6},{8,9},{9,8},{10,11... | collective-permute-start | bytes 3145736 | tf_op jit(solution)/shard_map/ppermute | solution.py:330
  105.6 47.2 %copy-start.19 = (bf16[528,1024]{1,0:T(8,128)(2,1)}, bf16[528,1024]{1,0:T(8,128)(2,1)S(1)}, u32[]{:S(2)}) copy-start(bf16[528,1024]{1,0:T(8,128)(2,1)S(1)} %collective-permute-done.4.refs_1_.refs_3_.refs_11_.refs_5_.wb_ref.refs_9_) | copy-start | bytes 3244036
  105.6 37.5 %collective-permute-start.12 = (bf16[512,1024]{1,0:T(8,128)(2,1)}, bf16[512,1024]{1,0:T(8,128)(2,1)S(1)}, u32[]{:S(2)}, u32[]{:S(2)}) collective-permute-start(bf16[512,1024]{1,0:T(8,128)(2,1)} %collective-permute-done.8.refs_2_), channel_id=1, source_target_pairs={{0,1},{1,0},{2,3},{3,2},{4,5},{5,4},{6,7},{7,6},{8,9},{9,8},{10,11... | collective-permute-start | bytes 3145736 | tf_op jit(solution)/shard_map/ppermute | solution.py:330
  127.5 25.2 %collective-permute-start.7 = (bf16[512,1024]{1,0:T(8,128)(2,1)S(1)}, bf16[512,1024]{1,0:T(8,128)(2,1)S(1)}, u32[]{:S(2)}, u32[]{:S(2)}) collective-permute-start(bf16[512,1024]{1,0:T(8,128)(2,1)S(1)} %collective-permute-done.6.refs_0_.refs_10_), channel_id=1, source_target_pairs={{0,1},{1,0},{2,3},{3,2},{4,5},{5,4},{6,7},{7,6},{8,9},{9,8},{10,11... | collective-permute-start | bytes 3145736 | tf_op jit(solution)/shard_map/ppermute | solution.py:330
  127.5 25.2 %collective-permute-start.10 = (bf16[512,1024]{1,0:T(8,128)(2,1)S(1)}, bf16[512,1024]{1,0:T(8,128)(2,1)S(1)}, u32[]{:S(2)}, u32[]{:S(2)}) collective-permute-start(bf16[512,1024]{1,0:T(8,128)(2,1)S(1)} %collective-permute-done.9.refs_2_.refs_4_), channel_id=1, source_target_pairs={{0,1},{1,0},{2,3},{3,2},{4,5},{5,4},{6,7},{7,6},{8,9},{9,8},{10,11... | collective-permute-start | bytes 3145736 | tf_op jit(solution)/shard_map/ppermute | solution.py:330
  203.9 84.1 %collective-permute-start.30 = (bf16[2,512,2560]{2,1,0:T(8,128)(2,1)}, bf16[2,512,2560]{2,1,0:T(8,128)(2,1)}, u32[]{:S(2)}, u32[]{:S(2)}) collective-permute-start(bf16[2,512,2560]{2,1,0:T(8,128)(2,1)} %shard_map.325), channel_id=1, source_target_pairs={{0,1},{1,0},{2,3},{3,2},{4,5},{5,4},{6,7},{7,6},{8,9},{9,8},{10,11... | collective-permute-start | bytes 15728648 | tf_op jit(solution)/shard_map/ppermute | solution.py:330
  213.4 62.0 %collective-permute-start.22 = (bf16[2,512,2048]{2,1,0:T(8,128)(2,1)}, bf16[2,512,2048]{2,1,0:T(8,128)(2,1)}, u32[]{:S(2)}, u32[]{:S(2)}) collective-permute-start(bf16[2,512,2048]{2,1,0:T(8,128)(2,1)} %shard_map.321), channel_id=1, source_target_pairs={{0,1},{1,0},{2,3},{3,2},{4,5},{5,4},{6,7},{7,6},{8,9},{9,8},{10,11... | collective-permute-start | bytes 12582920 | tf_op jit(solution)/shard_map/ppermute | solution.py:330
  275.3 25.2 %collective-permute-start.15 = (bf16[2,512,1536]{2,1,0:T(8,128)(2,1)}, bf16[2,512,1536]{2,1,0:T(8,128)(2,1)}, u32[]{:S(2)}, u32[]{:S(2)}) collective-permute-start(bf16[2,512,1536]{2,1,0:T(8,128)(2,1)} %shard_map.314), channel_id=1, source_target_pairs={{0,1},{1,0},{2,3},{3,2},{4,5},{5,4},{6,7},{7,6},{8,9},{9,8},{10,11... | collective-permute-start | bytes 9437192 | tf_op jit(solution)/shard_map/ppermute | solution.py:330
  284.6 26.3 %collective-permute-start.23 = (bf16[2,512,512]{2,1,0:T(8,128)(2,1)}, bf16[2,512,512]{2,1,0:T(8,128)(2,1)S(1)}, u32[]{:S(2)}, u32[]{:S(2)}) collective-permute-start(bf16[2,512,512]{2,1,0:T(8,128)(2,1)} %get-tuple-element.179), channel_id=1, source_target_pairs={{0,2},{1,3},{2,0},{3,1},{4,6},{5,7},{6,4},{7,5},{8,10},{9,11},{10,... | collective-permute-start | bytes 3145736 | tf_op jit(solution)/shard_map/ppermute | solution.py:330
  284.8 27.5 %collective-permute-start.24 = (bf16[512,1024]{1,0:T(8,128)(2,1)}, bf16[512,1024]{1,0:T(8,128)(2,1)}, u32[]{:S(2)}, u32[]{:S(2)}) collective-permute-start(bf16[512,1024]{1,0:T(8,128)(2,1)} %get-tuple-element.181), channel_id=1, source_target_pairs={{0,4},{4,0},{8,12},{12,8},{16,20},{20,16},{24,28},{28,24},{1,5},{5... | collective-permute-start | bytes 3145736 | tf_op jit(solution)/shard_map/ppermute | solution.py:334
  299.0 68.7 %collective-permute-start.32 = (bf16[512,1536]{1,0:T(8,128)(2,1)}, bf16[512,1536]{1,0:T(8,128)(2,1)}, u32[]{:S(2)}, u32[]{:S(2)}) collective-permute-start(bf16[512,1536]{1,0:T(8,128)(2,1)} %get-tuple-element.197), channel_id=1, source_target_pairs={{0,4},{4,0},{8,12},{12,8},{16,20},{20,16},{24,28},{28,24},{1,5},{5... | collective-permute-start | bytes 4718600 | tf_op jit(solution)/shard_map/ppermute | solution.py:334
  299.7 66.6 %collective-permute-start.31 = (bf16[2,512,512]{2,1,0:T(8,128)(2,1)}, bf16[2,512,512]{2,1,0:T(8,128)(2,1)}, u32[]{:S(2)}, u32[]{:S(2)}) collective-permute-start(bf16[2,512,512]{2,1,0:T(8,128)(2,1)} %get-tuple-element.196), channel_id=1, source_target_pairs={{0,2},{1,3},{2,0},{3,1},{4,6},{5,7},{6,4},{7,5},{8,10},{9,11},{10,... | collective-permute-start | bytes 3145736 | tf_op jit(solution)/shard_map/ppermute | solution.py:330
  307.0 55.9 %collective-permute-start.17 = (bf16[512,768]{1,0:T(8,128)(2,1)}, bf16[512,768]{1,0:T(8,128)(2,1)}, u32[]{:S(2)}, u32[]{:S(2)}) collective-permute-start(bf16[512,768]{1,0:T(8,128)(2,1)} %get-tuple-element.158), channel_id=1, source_target_pairs={{0,4},{4,0},{8,12},{12,8},{16,20},{20,16},{24,28},{28,24},{1,5},{5... | collective-permute-start | bytes 2359304 | tf_op jit(solution)/shard_map/ppermute | solution.py:334
  314.4 59.7 %collective-permute-start.25 = (bf16[512,512]{1,0:T(8,128)(2,1)}, bf16[512,512]{1,0:T(8,128)(2,1)}, u32[]{:S(2)}, u32[]{:S(2)}) collective-permute-start(bf16[512,512]{1,0:T(8,128)(2,1)} %get-tuple-element.182), channel_id=1, source_target_pairs={{0,4},{4,0},{8,12},{12,8},{16,20},{20,16},{24,28},{28,24},{1,5},{5... | collective-permute-start | bytes 1572872 | tf_op jit(solution)/shard_map/ppermute | solution.py:334
  340.7 60.1 %collective-permute-start.16 = (bf16[512,768]{1,0:T(8,128)(2,1)}, bf16[512,768]{1,0:T(8,128)(2,1)}, u32[]{:S(2)}, u32[]{:S(2)}) collective-permute-start(bf16[512,768]{1,0:T(8,128)(2,1)} %get-tuple-element.156), channel_id=1, source_target_pairs={{0,4},{4,0},{8,12},{12,8},{16,20},{20,16},{24,28},{28,24},{1,5},{5... | collective-permute-start | bytes 2359304 | tf_op jit(solution)/shard_map/ppermute | solution.py:334
  364.8 36.0 %collective-permute-start.18 = (bf16[512,768]{1,0:T(8,128)(2,1)}, bf16[512,768]{1,0:T(8,128)(2,1)S(1)}, u32[]{:S(2)}, u32[]{:S(2)}) collective-permute-start(bf16[512,768]{1,0:T(8,128)(2,1)} %shard_map.317), channel_id=1, source_target_pairs={{0,2},{1,3},{2,0},{3,1},{4,6},{5,7},{6,4},{7,5},{8,10},{9,11},{10,... | collective-permute-start | bytes 2359304 | tf_op jit(solution)/shard_map/ppermute | solution.py:330
  366.3 30.5 %collective-permute-start.26 = (bf16[512,512]{1,0:T(8,128)(2,1)S(1)}, bf16[512,512]{1,0:T(8,128)(2,1)}, u32[]{:S(2)}, u32[]{:S(2)}) collective-permute-start(bf16[512,512]{1,0:T(8,128)(2,1)S(1)} %get-tuple-element.183), channel_id=1, source_target_pairs={{0,2},{1,3},{2,0},{3,1},{4,6},{5,7},{6,4},{7,5},{8,10},{9,11},{10,... | collective-permute-start | bytes 1572872 | tf_op jit(solution)/shard_map/ppermute | solution.py:330
  369.9 39.9 %collective-permute-start.33 = (bf16[512,512]{1,0:T(8,128)(2,1)S(1)}, bf16[512,512]{1,0:T(8,128)(2,1)S(1)}, u32[]{:S(2)}, u32[]{:S(2)}) collective-permute-start(bf16[512,512]{1,0:T(8,128)(2,1)S(1)} %get-tuple-element.202), channel_id=1, source_target_pairs={{0,4},{4,0},{8,12},{12,8},{16,20},{20,16},{24,28},{28,24},{1,5},{5... | collective-permute-start | bytes 1572872 | tf_op jit(solution)/shard_map/ppermute | solution.py:334
  374.1 37.0 %collective-permute-start.34 = (bf16[512,768]{1,0:T(8,128)(2,1)}, bf16[512,768]{1,0:T(8,128)(2,1)S(1)}, u32[]{:S(2)}, u32[]{:S(2)}) collective-permute-start(bf16[512,768]{1,0:T(8,128)(2,1)} %get-tuple-element.203), channel_id=1, source_target_pairs={{0,2},{1,3},{2,0},{3,1},{4,6},{5,7},{6,4},{7,5},{8,10},{9,11},{10,... | collective-permute-start | bytes 2359304 | tf_op jit(solution)/shard_map/ppermute | solution.py:330
  400.4 46.0 %collective-permute-start.27 = (bf16[128,1024]{1,0:T(8,128)(2,1)}, bf16[128,1024]{1,0:T(8,128)(2,1)S(1)}, u32[]{:S(2)}, u32[]{:S(2)}) collective-permute-start(bf16[128,1024]{1,0:T(8,128)(2,1)} %get-tuple-element.185), channel_id=1, source_target_pairs={{0,8},{4,12},{8,0},{12,4},{16,24},{20,28},{24,16},{28,20},{1,9},{5... | collective-permute-start | bytes 786440 | tf_op jit(solution)/shard_map/ppermute | solution.py:334
  405.0 13.2 %collective-permute-start.19 = (bf16[128,768]{1,0:T(8,128)(2,1)}, bf16[128,768]{1,0:T(8,128)(2,1)S(1)}, u32[]{:S(2)}, u32[]{:S(2)}) collective-permute-start(bf16[128,768]{1,0:T(8,128)(2,1)} %get-tuple-element.160), channel_id=1, source_target_pairs={{0,8},{4,12},{8,0},{12,4},{16,24},{20,28},{24,16},{28,20},{1,9},{5... | collective-permute-start | bytes 589832 | tf_op jit(solution)/shard_map/ppermute | solution.py:334
  406.7 23.6 %collective-permute-start.20 = (bf16[128,768]{1,0:T(8,128)(2,1)}, bf16[128,768]{1,0:T(8,128)(2,1)S(1)}, u32[]{:S(2)}, u32[]{:S(2)}) collective-permute-start(bf16[128,768]{1,0:T(8,128)(2,1)} %get-tuple-element.161), channel_id=1, source_target_pairs={{0,16},{4,20},{8,24},{12,28},{16,0},{20,4},{24,8},{28,12},{1,17},{... | collective-permute-start | bytes 589832 | tf_op jit(solution)/shard_map/ppermute | solution.py:334
  409.8 23.1 %collective-permute-start.21 = (bf16[128,768]{1,0:T(8,128)(2,1)}, bf16[128,768]{1,0:T(8,128)(2,1)S(1)}, u32[]{:S(2)}, u32[]{:S(2)}) collective-permute-start(bf16[128,768]{1,0:T(8,128)(2,1)} %get-tuple-element.162), channel_id=1, source_target_pairs={{0,24},{4,28},{8,16},{12,20},{16,8},{20,12},{24,0},{28,4},{1,25},{... | collective-permute-start | bytes 589832 | tf_op jit(solution)/shard_map/ppermute | solution.py:334
  411.1 69.5 %copy-start.37 = (bf16[128,768]{1,0:T(8,128)(2,1)S(1)}, bf16[128,768]{1,0:T(8,128)(2,1)}, u32[]{:S(2)}) copy-start(bf16[128,768]{1,0:T(8,128)(2,1)} %get-tuple-element.159.refs_0_) | copy-start | bytes 589828
  411.1 69.5 %copy-start.38 = (s32[4]{0:T(128)S(1)}, s32[4]{0:T(128)}, u32[]{:S(2)}) copy-start(s32[4]{0:T(128)} %pad_add_fusion.2.info_ref.left_at) | copy-start | bytes 52
  411.1 73.1 %collective-permute-start.28 = (bf16[128,1024]{1,0:T(8,128)(2,1)}, bf16[128,1024]{1,0:T(8,128)(2,1)}, u32[]{:S(2)}, u32[]{:S(2)}) collective-permute-start(bf16[128,1024]{1,0:T(8,128)(2,1)} %get-tuple-element.186), channel_id=1, source_target_pairs={{0,16},{4,20},{8,24},{12,28},{16,0},{20,4},{24,8},{28,12},{1,17},{... | collective-permute-start | bytes 786440 | tf_op jit(solution)/shard_map/ppermute | solution.py:334
  418.2 66.0 %collective-permute-start.29 = (bf16[128,1024]{1,0:T(8,128)(2,1)}, bf16[128,1024]{1,0:T(8,128)(2,1)}, u32[]{:S(2)}, u32[]{:S(2)}) collective-permute-start(bf16[128,1024]{1,0:T(8,128)(2,1)} %get-tuple-element.187), channel_id=1, source_target_pairs={{0,24},{4,28},{8,16},{12,20},{16,8},{20,12},{24,0},{28,4},{1,25},{... | collective-permute-start | bytes 786440 | tf_op jit(solution)/shard_map/ppermute | solution.py:334
  430.3 53.9 %collective-permute-start.35 = (bf16[128,1280]{1,0:T(8,128)(2,1)}, bf16[128,1280]{1,0:T(8,128)(2,1)S(1)}, u32[]{:S(2)}, u32[]{:S(2)}) collective-permute-start(bf16[128,1280]{1,0:T(8,128)(2,1)} %get-tuple-element.205), channel_id=1, source_target_pairs={{0,8},{4,12},{8,0},{12,4},{16,24},{20,28},{24,16},{28,20},{1,9},{5... | collective-permute-start | bytes 983048 | tf_op jit(solution)/shard_map/ppermute | solution.py:334
  432.8 51.4 %collective-permute-start.36 = (bf16[128,1280]{1,0:T(8,128)(2,1)}, bf16[128,1280]{1,0:T(8,128)(2,1)S(1)}, u32[]{:S(2)}, u32[]{:S(2)}) collective-permute-start(bf16[128,1280]{1,0:T(8,128)(2,1)} %get-tuple-element.206), channel_id=1, source_target_pairs={{0,16},{4,20},{8,24},{12,28},{16,0},{20,4},{24,8},{28,12},{1,17},{... | collective-permute-start | bytes 983048 | tf_op jit(solution)/shard_map/ppermute | solution.py:334
  446.4 37.8 %collective-permute-start.37 = (bf16[128,1280]{1,0:T(8,128)(2,1)}, bf16[128,1280]{1,0:T(8,128)(2,1)S(1)}, u32[]{:S(2)}, u32[]{:S(2)}) collective-permute-start(bf16[128,1280]{1,0:T(8,128)(2,1)} %get-tuple-element.207), channel_id=1, source_target_pairs={{0,24},{4,28},{8,16},{12,20},{16,8},{20,12},{24,0},{28,4},{1,25},{... | collective-permute-start | bytes 983048 | tf_op jit(solution)/shard_map/ppermute | solution.py:334
  448.7 41.4 %copy-start.71 = (pred[32]{0:T(512)(128)(4,1)S(1)}, pred[32]{0:T(512)(128)(4,1)}, u32[]{:S(2)}) copy-start(pred[32]{0:T(512)(128)(4,1)} %fusion.28) | copy-start | bytes 100
  448.9 43.2 %copy-start.30 = (bf16[128,1280]{1,0:T(8,128)(2,1)S(1)}, bf16[128,1280]{1,0:T(8,128)(2,1)}, u32[]{:S(2)}) copy-start(bf16[128,1280]{1,0:T(8,128)(2,1)} %get-tuple-element.209.refs_0_) | copy-start | bytes 983044
  (63 other events, 653.9 us)
